TPU v7x, 16 devices: a whole 2x2x2 slice. The times are simulated.
16 devices in a mesh: fsdp: 16 (over z, y, x, core).
Axes of the slice: x: 2, y: 2, z: 2, core: 2. Of those that a mesh axis runs over, the one named last changes fastest.
Arguments:
- resid_in: bfloat16 [128, 257, 1280], P('fsdp')
- grad_out: bfloat16 [128, 257, 1280], P('fsdp')
- ln1_gain: float32 [1280], P('fsdp')
- ln1_bias: float32 [1280], P('fsdp')
- qkv_weight: float32 [1280, 3840], P('fsdp')
- qkv_bias: float32 [3840], P('fsdp')
- out_weight: float32 [1280, 1280], P('fsdp')
- out_bias: float32 [1280], P('fsdp')
- ln2_gain: float32 [1280], P('fsdp')
- ln2_bias: float32 [1280], P('fsdp')
- fc_weight: float32 [1280, 5120], P('fsdp')
- fc_bias: float32 [5120], P('fsdp')
- proj_weight: float32 [5120, 1280], P('fsdp')
- proj_bias: float32 [1280], P('fsdp')
Outputs:
- output 1: bfloat16 [128, 257, 1280], P('fsdp')
- output 2: bfloat16 [128, 257, 1280], P('fsdp')
- output 3: float32 [1280], P('fsdp')
- output 4: float32 [1280], P('fsdp')
- output 5: float32 [1280, 3840], P('fsdp')
- output 6: float32 [3840], P('fsdp')
- output 7: float32 [1280, 1280], P('fsdp')
- output 8: float32 [1280], P('fsdp')
- output 9: float32 [1280], P('fsdp')
- output 10: float32 [1280], P('fsdp')
- output 11: float32 [1280, 5120], P('fsdp')
- output 12: float32 [5120], P('fsdp')
- output 13: float32 [5120, 1280], P('fsdp')
- output 14: float32 [1280], P('fsdp')
All inputs are finite; a program needn't handle non-finite values.
Results may differ from a plain program's by a relative error of at most 0.02.
Values are sent between devices in bfloat16 or wider.
A program may use at most 1 GiB of HBM per device.

v0:
```python
import math
import jax
import jax.numpy as jnp
from jax import lax
from jax.sharding import PartitionSpec as P

HEADS = 16
LN_EPS = 1e-5


def layer_norm_fwd(values, gain, bias):
    mean_val = jnp.mean(values, axis=-1, keepdims=True)
    centered = values - mean_val
    inv_std = lax.rsqrt(jnp.mean(centered * centered, axis=-1, keepdims=True) + LN_EPS)
    x_hat = centered * inv_std
    return x_hat * gain + bias, x_hat, inv_std


def layer_norm_bwd(grad_norm, x_hat, inv_std, gain):
    grad_hat = grad_norm * gain
    grad_vals = inv_std * (grad_hat - jnp.mean(grad_hat, axis=-1, keepdims=True)
                           - x_hat * jnp.mean(grad_hat * x_hat, axis=-1, keepdims=True))
    return grad_vals, jnp.sum(grad_norm * x_hat, axis=(0, 1)), jnp.sum(grad_norm, axis=(0, 1))


def forward_local(full, tokens):
    (ln1_gain, ln1_bias, qkv_weight, qkv_bias, out_weight, out_bias,
     ln2_gain, ln2_bias, fc_weight, fc_bias, proj_weight, proj_bias) = full
    images, seq_len, width = tokens.shape
    head_dim = width // HEADS
    resid = tokens.astype(jnp.float32)
    normed, hat_one, inv_one = layer_norm_fwd(resid, ln1_gain, ln1_bias)
    normed_one = normed.astype(jnp.bfloat16)
    qkv_vals = (jnp.einsum("bsw,wk->bsk", normed_one, qkv_weight, preferred_element_type=jnp.float32) + qkv_bias).astype(jnp.bfloat16)
    qkv_vals = qkv_vals.reshape(images, seq_len, 3, HEADS, head_dim)
    query_heads = qkv_vals[:, :, 0]
    key_heads = qkv_vals[:, :, 1]
    value_heads = qkv_vals[:, :, 2]
    scores = jnp.einsum("bqhd,bkhd->bhqk", query_heads, key_heads, preferred_element_type=jnp.float32) * (head_dim ** -0.5)
    attn_probs = jax.nn.softmax(scores, axis=-1)
    probs_low = attn_probs.astype(jnp.bfloat16)
    mixed = jnp.einsum("bhqk,bkhd->bqhd", probs_low, value_heads, preferred_element_type=jnp.float32).astype(jnp.bfloat16).reshape(images, seq_len, width)
    middle = (resid + jnp.einsum("bsw,wv->bsv", mixed, out_weight, preferred_element_type=jnp.float32) + out_bias).astype(jnp.bfloat16)
    middle_wide = middle.astype(jnp.float32)
    normed, hat_two, inv_two = layer_norm_fwd(middle_wide, ln2_gain, ln2_bias)
    normed_two = normed.astype(jnp.bfloat16)
    pre_act = jnp.einsum("bsw,wf->bsf", normed_two, fc_weight, preferred_element_type=jnp.float32) + fc_bias
    hidden = jax.nn.gelu(pre_act, approximate=False).astype(jnp.bfloat16)
    resid_out = (middle_wide + jnp.einsum("bsf,fw->bsw", hidden, proj_weight, preferred_element_type=jnp.float32) + proj_bias).astype(jnp.bfloat16)
    saved = (hat_one, inv_one, normed_one, query_heads, key_heads, value_heads, attn_probs, probs_low,
             mixed, hat_two, inv_two, normed_two, pre_act, hidden)
    return resid_out, saved


def backward_local(weights, saved, grad_out):
    (ln1_gain, qkv_weight, out_weight, ln2_gain, fc_weight, proj_weight) = weights
    (hat_one, inv_one, normed_one, query_heads, key_heads, value_heads, attn_probs, probs_low,
     mixed, hat_two, inv_two, normed_two, pre_act, hidden) = saved
    images, seq_len, width = grad_out.shape
    head_dim = width // HEADS
    grad_wide = grad_out.astype(jnp.float32)
    d_proj_weight = jnp.einsum("bsf,bsw->fw", hidden, grad_out, preferred_element_type=jnp.float32)
    d_proj_bias = jnp.sum(grad_wide, axis=(0, 1))
    grad_hidden = jnp.einsum("bsw,fw->bsf", grad_out, proj_weight, preferred_element_type=jnp.float32)
    gauss_cdf = 0.5 * (1.0 + lax.erf(pre_act * (0.5 ** 0.5)))
    gauss_pdf = jnp.exp(-0.5 * pre_act * pre_act) * ((2.0 * math.pi) ** -0.5)
    grad_pre = grad_hidden * (gauss_cdf + pre_act * gauss_pdf)
    grad_pre_low = grad_pre.astype(jnp.bfloat16)
    d_fc_weight = jnp.einsum("bsw,bsf->wf", normed_two, grad_pre_low, preferred_element_type=jnp.float32)
    d_fc_bias = jnp.sum(grad_pre, axis=(0, 1))
    grad_norm = jnp.einsum("bsf,wf->bsw", grad_pre_low, fc_weight, preferred_element_type=jnp.float32)
    grad_ln, d_ln2_gain, d_ln2_bias = layer_norm_bwd(grad_norm, hat_two, inv_two, ln2_gain)
    grad_middle = grad_wide + grad_ln
    grad_middle_low = grad_middle.astype(jnp.bfloat16)
    d_out_weight = jnp.einsum("bsw,bsv->wv", mixed, grad_middle_low, preferred_element_type=jnp.float32)
    d_out_bias = jnp.sum(grad_middle, axis=(0, 1))
    grad_mixed = jnp.einsum("bsv,wv->bsw", grad_middle_low, out_weight, preferred_element_type=jnp.float32)
    grad_mixed = grad_mixed.astype(jnp.bfloat16).reshape(images, seq_len, HEADS, head_dim)
    grad_probs = jnp.einsum("bqhd,bkhd->bhqk", grad_mixed, value_heads, preferred_element_type=jnp.float32)
    grad_value = jnp.einsum("bhqk,bqhd->bkhd", probs_low, grad_mixed, preferred_element_type=jnp.float32)
    grad_scores = attn_probs * (grad_probs - jnp.sum(grad_probs * attn_probs, axis=-1, keepdims=True)) * (head_dim ** -0.5)
    grad_scores = grad_scores.astype(jnp.bfloat16)
    grad_query = jnp.einsum("bhqk,bkhd->bqhd", grad_scores, key_heads, preferred_element_type=jnp.float32)
    grad_key = jnp.einsum("bhqk,bqhd->bkhd", grad_scores, query_heads, preferred_element_type=jnp.float32)
    grad_qkv = jnp.stack([grad_query, grad_key, grad_value], axis=2).reshape(images, seq_len, 3 * width)
    grad_qkv_low = grad_qkv.astype(jnp.bfloat16)
    d_qkv_weight = jnp.einsum("bsw,bsk->wk", normed_one, grad_qkv_low, preferred_element_type=jnp.float32)
    d_qkv_bias = jnp.sum(grad_qkv, axis=(0, 1))
    grad_norm = jnp.einsum("bsk,wk->bsw", grad_qkv_low, qkv_weight, preferred_element_type=jnp.float32)
    grad_ln, d_ln1_gain, d_ln1_bias = layer_norm_bwd(grad_norm, hat_one, inv_one, ln1_gain)
    grad_in = (grad_middle + grad_ln).astype(jnp.bfloat16)
    return grad_in, (d_ln1_gain, d_ln1_bias, d_qkv_weight, d_qkv_bias, d_out_weight, d_out_bias,
                     d_ln2_gain, d_ln2_bias, d_fc_weight, d_fc_bias, d_proj_weight, d_proj_bias)


def solution(mesh):
    specs = (P("fsdp"),) * 14

    def gather_bf16(shards):
        return tuple(lax.all_gather(shard.astype(jnp.bfloat16), "fsdp", axis=0, tiled=True) for shard in shards)

    def device_step(resid_in, grad_out, *shards):
        full = gather_bf16(shards)
        resid_out, saved = forward_local(full, resid_in)
        needed, resid_out = lax.optimization_barrier(
            ((shards[0], shards[2], shards[4], shards[6], shards[8], shards[10]), resid_out))
        weights = gather_bf16(needed)
        grad_in, grads = backward_local(weights, saved, grad_out)
        grad_shards = tuple(lax.psum_scatter(grad, "fsdp", scatter_dimension=0, tiled=True) for grad in grads)
        return (resid_out, grad_in) + grad_shards

    return jax.shard_map(device_step, mesh=mesh, in_specs=specs, out_specs=specs, check_vma=False)
```

profile of v0, /device:TPU:0, one launch (start us, length us, event | category | flops | bytes accessed | tf_op | source)
XLA Modules:
  0.0 1904.6 jit_solution(10505752507581790584)
XLA Ops:
  7.2 2.2 convert_element_type.147
  9.5 1.7 convert_element_type.154
  11.3 2.4 convert_element_type.164
  13.7 2.4 convert_element_type.168
  20.2 0.7 convert_element_type.165
  20.9 0.7 convert_element_type.148
  23.3 36.3 %all-reduce.20 = (bf16[3840]{0:T(1024)(128)(2,1)S(1)}, bf16[1280]{0:T(1024)(128)(2,1)S(1)}, bf16[1280]{0:T(1024)(128)(2,1)S(1)}, bf16[1280]{0:T(1024)(128)(2,1)S...) all-reduce(bf16[3840]{0:T(1024)(128)(2,1)S(1)} %dynamic-update-slic, ...), channel_id=1, replica_groups=mesh['fsdp'=16] {'fsdp'}, use_global_device_ids=true, to_apply=%add.2 | all-reduce | flops 16640 | bytes 66560
  59.6 3.9 convert_reduce_fusion.1
  63.5 4.4 fusion.69
  71.0 34.0 %add_convert_fusion = bf16[8,257,3840]{2,1,0:T(8,128)(2,1)} fusion(f32[3840]{0:T(1024)S(1)} %convert_element_type.149, bf16[1280,3840]{1,0:T(8,128)(2,1)} %all-gather.9.cloned.1.call-done, f32[1280]{0:T(1024)S(1)} %convert_element_type.145, f32[1280]{0:T(1024)S(1)} %convert_element_type.143, f32[8,257]{1,0:T(8,128)S(1)} %add_rsqrt_fusion.1, ...), kind=kOutput, calls=%fused_computation.39 | convolution fusion | flops 20242882560 | bytes 30925888 | tf_op jit(solution)/shard_map/bsw,wk->bsk/dot_general | solution.py:34
  105.0 45.1 %reshape.128 = bf16[8,257,3,16,80]{4,3,2,1,0:T(8,128)(2,1)} reshape(bf16[8,257,3840]{2,1,0:T(8,128)(2,1)} %add_convert_fusion) | data formatting | bytes 31580160 | tf_op jit(solution)/shard_map/reshape | solution.py:35
  150.1 17.1 fusion.123
  167.3 13.9 copy.103
  181.2 14.0 copy.104
  195.1 23.9 %fusion.91 = f32[8,16,257,257]{2,3,1,0:T(8,128)} fusion(bf16[8,257,1,16,80]{1,4,3,0,2:T(8,128)(2,1)} %copy.104, bf16[8,257,1,16,80]{1,4,3,0,2:T(8,128)(2,1)} %copy.103), kind=kOutput, calls=%fused_computation.112 | convolution fusion | flops 1352683520 | bytes 44343808 | tf_op jit(solution)/shard_map/bqhd,bkhd->bhqk/dot_general | solution.py:39
  219.1 52.7 %fusion.124 = (f32[8,16,257]{2,1,0:T(8,128)S(1)}, f32[8,16,257,257]{2,3,1,0:T(8,128)}) fusion(f32[8,16,257,257]{2,3,1,0:T(8,128)} %fusion.91), kind=kOutput, calls=%fused_computation.144 | output fusion | flops 33817344 | bytes 67765760 | tf_op jit(solution)/shard_map/sub | solution.py:40
  271.8 14.0 copy.102
  285.7 23.5 %fusion.98 = bf16[8,16,80,257]{3,2,1,0:T(8,128)(2,1)} fusion(bf16[8,257,1,16,80]{1,4,3,0,2:T(8,128)(2,1)} %copy.102, f32[8,16,257,257]{2,3,1,0:T(8,128)} %get-tuple-element.105, f32[8,16,257]{2,1,0:T(8,128)S(1)} %get-tuple-element.104), kind=kOutput, calls=%fused_computation.119 | convolution fusion | flops 1372223744 | bytes 44475392 | tf_op jit(solution)/shard_map/bhqk,bkhd->bqhd/dot_general | solution.py:42
  309.3 14.4 convert_reduce_fusion
  323.8 2.4 copy-done
  326.2 1.6 fusion.60
  327.8 52.7 %fusion.77 = (u8[257,5120]{1,0:T(8,128)(4,1)S(1)}, u8[257,5120]{1,0:T(8,128)(4,1)S(1)}, f32[8,257,5120]{2,1,0:T(8,128)}) fusion(f32[5120]{0:T(1024)S(1)} %copy-done.11, bf16[1280,5120]{1,0:T(8,128)(2,1)} %all-gather.13.cloned.1.call-done, bf16[8,257,1280]{2,1,0:T(8,128)(2,1)} %copy-done, f32[1280]{0:T(1024)S(1)} %copy-done.24, f32[1280]{0:T(1024)S(1)} %copy-done.22, ...), kind=kOutput, calls=%fused_computation.101 | convolution fusion | flops 27108937728 | bytes 63156288 | tf_op jit(solution)/shard_map/bsw,wf->bsf/dot_general | solution.py:47
  380.6 102.5 %fusion.6 = bf16[8,257,5120]{2,1,0:T(8,128)(2,1)} fusion(f32[8,257,5120]{2,1,0:T(8,128)} %get-tuple-element.108, f32[5120]{0:T(1024)S(1)} %copy-done.11, u8[257,5120]{1,0:T(8,128)(4,1)S(1)} %get-tuple-element.71, u8[257,5120]{1,0:T(8,128)(4,1)S(1)} %get-tuple-element.70), kind=kLoop, calls=%fused_computation.13 | loop fusion | flops 747397120 | bytes 65812480 | tf_op jit(solution)/shard_map/convert_element_type | solution.py:48
  483.2 37.1 %fusion.73 = bf16[8,257,1280]{2,1,0:T(8,128)(2,1)} fusion(bf16[8,257,1280]{2,1,0:T(8,128)(2,1)} %copy-done, bf16[8,257,5120]{2,1,0:T(8,128)(2,1)} %fusion.6, bf16[5120,1280]{1,0:T(8,128)(2,1)} %all-gather.15.cloned.1.call-done, f32[1280]{0:T(1024)S(1)} %copy-done.30), kind=kOutput, calls=%fused_computation.97 | convolution fusion | flops 26958929920 | bytes 44692480 | tf_op jit(solution)/shard_map/bsf,fw->bsw/dot_general | solution.py:49
  520.2 1.0 convert_element_type.173
  521.3 1.0 convert_element_type.175
  522.4 1.7 convert_element_type.179
  524.7 33.4 %all-reduce.19 = (bf16[1280]{0:T(1024)(128)(2,1)S(1)}, bf16[1280]{0:T(1024)(128)(2,1)S(1)}) all-reduce(bf16[1280]{0:T(1024)(128)(2,1)S(1)} %dynamic-update-slice.8, bf16[1280]{0:T(1024)(128)(2,1)S(1)} %dynamic-update-slice.9), channel_id=1, replica_groups=mesh['fsdp'=16] {'fsdp'}, use_global_device_ids=true, to_apply=%add.8 | all-reduce | flops 2560 | bytes 10240
  558.7 2.2 convert_element_type.184
  560.9 26.4 %all-gather.17.cloned.1.call-done = bf16[5120,1280]{1,0:T(8,128)(2,1)} async-done(((bf16[320,1280]{1,0:T(8,128)(2,1)}), bf16[5120,1280]{1,0:T(8,128)(2,1)}) %all-gather.17.cloned.1.call-update) | async-done | bytes 13107216 | tf_op jit(solution)/shard_map/all_gather | solution.py:100
  587.3 52.5 %fusion.125 = (f32[5120]{0:T(1024)}, bf16[8,257,5120]{2,1,0:T(8,128)(2,1)}) fusion(f32[8,257,5120]{2,1,0:T(8,128)} %get-tuple-element.108, f32[5120]{0:T(1024)S(1)} %copy-done.11, bf16[8,257,1280]{2,0,1:T(8,128)(2,1)} %param.15, bf16[5120,1280]{1,0:T(8,128)(2,1)} %all-gather.17.cloned.1.call-done), kind=kOutput, calls=%fused_computation.145 | convolution fusion | flops 27074719744 | bytes 81571840 | tf_op jit(solution)/shard_map/bsw,fw->bsf/dot_general | solution.py:64
  639.8 14.2 all-gather.19.cloned.1.call-done
  654.1 39.8 %fusion.59 = (f32[1280]{0:T(1024)}, f32[8,257]{1,0:T(8,128)S(1)}, f32[8,257]{1,0:T(8,128)S(1)}, f32[1280]{0:T(1024)}, f32[8,257,1280]{2,1,0:T(8,128)}) fusion(bf16[8,257,1280]{2,1,0:T(8,128)(2,1)} %copy-done, f32[8,257]{1,0:T(8,128)S(1)} %copy-done.13, f32[8,257]{1,0:T(8,128)S(1)} %copy-done.6, f32[1280]{0:T(1024)S(1)} %convert_element_type.177, ...), kind=kOutput, calls=%fused_computation.83 | convolution fusion | flops 26974711808 | bytes 49998976 | tf_op jit(solution)/shard_map/bsf,wf->bsw/dot_general | solution.py:71
  693.9 15.2 fusion.122
  709.1 12.5 convolution_convert_fusion
  721.6 9.5 copy.99
  731.1 24.0 %fusion.95 = f32[8,16,257,257]{2,3,1,0:T(8,128)} fusion(bf16[8,257,16,80]{1,3,2,0:T(8,128)(2,1)} %bitcast.93, bf16[8,257,1,16,80]{1,4,3,0,2:T(8,128)(2,1)} %copy.102), kind=kOutput, calls=%fused_computation.116 | convolution fusion | flops 1352683520 | bytes 44343808 | tf_op jit(solution)/shard_map/bqhd,bkhd->bhqk/dot_general | solution.py:79
  755.1 71.2 %fusion.87 = f32[8,257,1,16,80]{1,4,3,0,2:T(8,128)} fusion(f32[8,16,257,257]{2,3,1,0:T(8,128)} %fusion.95, bf16[8,257,1,16,80]{1,4,3,0,2:T(8,128)(2,1)} %copy.103, f32[8,16,257,257]{2,3,1,0:T(8,128)} %get-tuple-element.105, f32[8,16,257]{2,1,0:T(8,128)S(1)} %copy-done.4), kind=kOutput, calls=%fused_computation.110 | convolution fusion | flops 1411896576 | bytes 83555840 | tf_op jit(solution)/shard_map/bhqk,bqhd->bkhd/dot_general | solution.py:84
  826.3 77.4 %fusion.84 = f32[8,257,1,16,80]{1,4,3,0,2:T(8,128)} fusion(f32[8,16,257,257]{2,3,1,0:T(8,128)} %fusion.95, bf16[8,257,1,16,80]{1,4,3,0,2:T(8,128)(2,1)} %copy.104, f32[8,16,257,257]{2,3,1,0:T(8,128)} %get-tuple-element.105, f32[8,16,257]{2,1,0:T(8,128)S(1)} %copy-done.4), kind=kOutput, calls=%fused_computation.109 | convolution fusion | flops 1411896576 | bytes 83555840 | tf_op jit(solution)/shard_map/bhqk,bkhd->bqhd/dot_general | solution.py:83
  903.7 27.0 %fusion.81 = f32[8,257,1,16,80]{1,4,3,0,2:T(8,128)} fusion(bf16[8,257,16,80]{1,3,2,0:T(8,128)(2,1)} %bitcast.94, f32[8,16,257,257]{2,3,1,0:T(8,128)} %get-tuple-element.105, f32[8,16,257]{2,1,0:T(8,128)S(1)} %copy-done.4), kind=kOutput, calls=%fused_computation.108 | convolution fusion | flops 1369592064 | bytes 49738752 | tf_op jit(solution)/shard_map/bhqk,bqhd->bkhd/dot_general | solution.py:80
  930.7 15.8 fusion.20
  946.5 0.7 reduce_sum.177
  947.2 25.4 %fusion.21 = bf16[8,257,3,16,80]{1,4,3,0,2:T(8,128)(2,1)} fusion(f32[8,257,1,16,80]{1,4,3,0,2:T(8,128)} %fusion.81, f32[8,257,1,16,80]{1,4,3,0,2:T(8,128)} %fusion.87, f32[8,257,1,16,80]{1,4,3,0,2:T(8,128)} %fusion.84), kind=kLoop, calls=%fused_computation.38 | loop fusion | flops 15790080 | bytes 47370240 | tf_op jit(solution)/shard_map/convert_element_type | solution.py:86
  972.6 40.5 %copy.100 = bf16[8,257,3,16,80]{4,3,2,1,0:T(8,128)(2,1)} copy(bf16[8,257,3,16,80]{1,4,3,0,2:T(8,128)(2,1)} %fusion.21) | data formatting | bytes 31580160 | tf_op jit(solution)/shard_map/convert_element_type | solution.py:86
  1013.1 37.3 %reshape.130 = bf16[8,257,3840]{2,1,0:T(8,128)(2,1)} reshape(bf16[8,257,3,16,80]{4,3,2,1,0:T(8,128)(2,1)} %copy.100) | data formatting | bytes 31580160 | tf_op jit(solution)/shard_map/convert_element_type | solution.py:86
  1050.4 33.4 %fusion.68 = (f32[1280]{0:T(1024)}, f32[8,257]{1,0:T(8,128)}, f32[8,257]{1,0:T(8,128)}, f32[1280]{0:T(1024)}, f32[8,257,1280]{2,1,0:T(8,128)}) fusion(f32[8,257]{1,0:T(8,128)S(1)} %copy-done.16, f32[8,257]{1,0:T(8,128)S(1)} %copy-done.9, bf16[8,257,1280]{2,0,1:T(8,128)(2,1)} %param.14, f32[1280]{0:T(1024)S(1)} %copy-done.18, ...), kind=kOutput, calls=%fused_computation.92 | convolution fusion | flops 20237611008 | bytes 41458816 | tf_op jit(solution)/shard_map/bsk,wk->bsw/dot_general | solution.py:89
  1083.9 16.7 convolution_bitcast_fusion.3
  1100.7 39.0 %convolution_bitcast_fusion.2 = f32[1280,3840]{1,0:T(8,128)} fusion(bf16[8,257,3840]{2,1,0:T(8,128)(2,1)} %reshape.130, f32[1280]{0:T(1024)S(1)} %copy-done.29, f32[1280]{0:T(1024)S(1)} %copy-done.27, f32[8,257]{1,0:T(8,128)S(1)} %copy-done.16, f32[8,257]{1,0:T(8,128)S(1)} %copy-done.9, bf16[8,257,1280]{2,0,1:T(8,128)(2,1)} %param.14), kind=kOutput, calls=%fused_computation.46 | convolution fusion | flops 20227092480 | bytes 40740928 | tf_op jit(solution)/shard_map/bsw,bsk->wk/dot_general | solution.py:87
  1139.8 40.2 %convolution_bitcast_fusion = f32[5120,1280]{1,0:T(8,128)} fusion(bf16[8,257,5120]{2,1,0:T(8,128)(2,1)} %fusion.6, bf16[8,257,1280]{2,0,1:T(8,128)(2,1)} %param.15), kind=kOutput, calls=%fused_computation.42 | convolution fusion | flops 26948403200 | bytes 52531200 | tf_op jit(solution)/shard_map/bsf,bsw->fw/dot_general | solution.py:62
  1180.8 40.2 %convolution_bitcast_fusion.1 = f32[1280,5120]{1,0:T(8,128)} fusion(bf16[8,257,5120]{2,1,0:T(8,128)(2,1)} %get-tuple-element.112, bf16[8,257,1280]{2,1,0:T(8,128)(2,1)} %copy-done, f32[1280]{0:T(1024)S(1)} %copy-done.25, f32[1280]{0:T(1024)S(1)} %copy-done.23, f32[8,257]{1,0:T(8,128)S(1)} %copy-done.14, f32[8,257]{1,0:T(8,128)S(1)} %copy-done.7), kind=kOutput, calls=%fused_computation.43 | convolution fusion | flops 26964193280 | bytes 52557888 | tf_op jit(solution)/shard_map/bsw,bsf->wf/dot_general | solution.py:69
  1221.1 6.1 copy.87
  1227.3 9.0 fusion.67
  1236.2 3.4 copy.88
  1239.6 1.3 dynamic-slice
  1240.9 1.3 dynamic-slice.1
  1242.2 1.3 dynamic-slice.3
  1243.4 1.3 dynamic-slice.4
  1244.7 1.3 dynamic-slice.5
  1246.0 1.3 dynamic-slice.7
  1247.3 1.3 dynamic-slice.6
  1248.6 1.3 dynamic-slice.2
  1250.0 99.0 %reduce-scatter.5.cloned.1.call-done = f32[80,3840]{1,0:T(8,128)} async-done(((f32[1280,3840]{1,0:T(8,128)}), f32[80,3840]{1,0:T(8,128)}) %reduce-scatter.5.cloned.1.call-update) | async-done | bytes 1228816 | tf_op jit(solution)/shard_map/reduce_scatter | solution.py:109
  1348.9 275.2 %reduce-scatter.11.cloned.1.call-done = f32[320,1280]{1,0:T(8,128)} async-done(((f32[5120,1280]{1,0:T(8,128)}), f32[320,1280]{1,0:T(8,128)}) %reduce-scatter.11.cloned.1.call-update) | async-done | bytes 1638416 | tf_op jit(solution)/shard_map/reduce_scatter | solution.py:109
  1624.1 273.5 %reduce-scatter.9.cloned.1.call-done = f32[80,5120]{1,0:T(8,128)} async-done(((f32[1280,5120]{1,0:T(8,128)}), f32[80,5120]{1,0:T(8,128)}) %reduce-scatter.9.cloned.1.call-update) | async-done | bytes 1638416 | tf_op jit(solution)/shard_map/reduce_scatter | solution.py:109
  (151 shorter events, 11.5 us)
Async XLA Ops:
  7.2 63.8 %all-gather.9.cloned.1.call-start = ((), (), s32[]{:S(2)}) async-start(), calls=%async_computation.4 | async-start | bytes 10444800 | tf_op jit(solution)/shard_map/all_gather | solution.py:100
  9.4 299.9 %all-gather.11.cloned.1.call-start = ((), (), s32[]{:S(2)}) async-start(), calls=%async_computation.5 | async-start | bytes 3481600 | tf_op jit(solution)/shard_map/all_gather | solution.py:100
  11.2 316.6 %all-gather.13.cloned.1.call-start = ((), (), s32[]{:S(2)}) async-start(), calls=%async_computation.6 | async-start | bytes 13926400 | tf_op jit(solution)/shard_map/all_gather | solution.py:100
  13.7 469.5 %all-gather.15.cloned.1.call-start = ((), (), s32[]{:S(2)}) async-start(), calls=%async_computation.7 | async-start | bytes 13926400 | tf_op jit(solution)/shard_map/all_gather | solution.py:100
  16.2 571.1 %all-gather.17.cloned.1.call-start = ((), (), s32[]{:S(2)}) async-start(), calls=%async_computation.8 | async-start | bytes 13926400 | tf_op jit(solution)/shard_map/all_gather | solution.py:100
  59.6 45.4 %copy-start.26 = (f32[1280]{0:T(1024)}, f32[1280]{0:T(1024)S(1)}, u32[]{:S(2)}) copy-start(f32[1280]{0:T(1024)S(1)} %convert_element_type.143) | copy-start | bytes 15364
  59.6 45.4 %copy-start.28 = (f32[1280]{0:T(1024)}, f32[1280]{0:T(1024)S(1)}, u32[]{:S(2)}) copy-start(f32[1280]{0:T(1024)S(1)} %convert_element_type.145) | copy-start | bytes 15364
  63.5 41.5 %copy-start.8 = (f32[8,257]{1,0:T(8,128)}, f32[8,257]{1,0:T(8,128)S(1)}, u32[]{:S(2)}) copy-start(f32[8,257]{1,0:T(8,128)S(1)} %broadcast_multiply_fusion.5) | copy-start | bytes 24676
  68.0 37.0 %copy-start.15 = (f32[8,257]{1,0:T(8,128)}, f32[8,257]{1,0:T(8,128)S(1)}, u32[]{:S(2)}) copy-start(f32[8,257]{1,0:T(8,128)S(1)} %add_rsqrt_fusion.1) | copy-start | bytes 24676
  271.8 37.5 %copy-start.3 = (f32[8,16,257]{2,1,0:T(8,128)}, f32[8,16,257]{2,1,0:T(8,128)S(1)}, u32[]{:S(2)}) copy-start(f32[8,16,257]{2,1,0:T(8,128)S(1)} %get-tuple-element.104) | copy-start | bytes 394756
  285.7 23.6 %copy-start.31 = (f32[1280]{0:T(1024)S(1)}, f32[1280]{0:T(1024)}, u32[]{:S(2)}) copy-start(f32[1280]{0:T(1024)} %convert_element_type.156) | copy-start | bytes 15364
  309.3 18.5 copy-start.11
  309.3 18.5 copy-start.22
  309.3 18.5 copy-start.24
  323.7 2.4 copy-start
  323.8 56.8 %copy-start.5 = (f32[8,257]{1,0:T(8,128)}, f32[8,257]{1,0:T(8,128)S(1)}, u32[]{:S(2)}) copy-start(f32[8,257]{1,0:T(8,128)S(1)} %broadcast_multiply_fusion.4) | copy-start | bytes 24676
  327.8 52.8 %copy-start.12 = (f32[8,257]{1,0:T(8,128)}, f32[8,257]{1,0:T(8,128)S(1)}, u32[]{:S(2)}) copy-start(f32[8,257]{1,0:T(8,128)S(1)} %add_rsqrt_fusion) | copy-start | bytes 24676
  380.6 102.6 %copy-start.30 = (f32[1280]{0:T(1024)S(1)}, f32[1280]{0:T(1024)}, u32[]{:S(2)}) copy-start(f32[1280]{0:T(1024)} %convert_element_type.170) | copy-start | bytes 15364
  483.1 37.1 %copy-start.1 = (f32[320,1280]{1,0:T(8,128)S(1)}, f32[320,1280]{1,0:T(8,128)}, u32[]{:S(2)}) copy-start(f32[320,1280]{1,0:T(8,128)} %param.26) | copy-start | bytes 4915204
  483.1 38.2 %copy-start.2 = (f32[80,5120]{1,0:T(8,128)S(1)}, f32[80,5120]{1,0:T(8,128)}, u32[]{:S(2)}) copy-start(f32[80,5120]{1,0:T(8,128)} %param.24) | copy-start | bytes 4915204
  483.1 41.0 %copy-start.32 = (f32[80]{0:T(128)S(1)}, f32[80]{0:T(128)}, u32[]{:S(2)}) copy-start(f32[80]{0:T(128)} %param.22) | copy-start | bytes 964
  483.1 41.0 %copy-start.33 = (f32[80]{0:T(128)S(1)}, f32[80]{0:T(128)}, u32[]{:S(2)}) copy-start(f32[80]{0:T(128)} %param.16) | copy-start | bytes 964
  521.2 132.8 %all-gather.19.cloned.1.call-start = ((), (), s32[]{:S(2)}) async-start(), calls=%async_computation.9 | async-start | bytes 13926400 | tf_op jit(solution)/shard_map/all_gather | solution.py:100
  522.3 186.8 %all-gather.21.cloned.1.call-start = ((), (), s32[]{:S(2)}) async-start(), calls=%async_computation.10 | async-start | bytes 3481600 | tf_op jit(solution)/shard_map/all_gather | solution.py:100
  524.1 526.3 %all-gather.23.cloned.1.call-start = ((), (), s32[]{:S(2)}) async-start(), calls=%async_computation.11 | async-start | bytes 10444800 | tf_op jit(solution)/shard_map/all_gather | solution.py:100
  560.9 93.2 %copy-start.6 = (f32[8,257]{1,0:T(8,128)S(1)}, f32[8,257]{1,0:T(8,128)}, u32[]{:S(2)}) copy-start(f32[8,257]{1,0:T(8,128)} %copy-done.5) | copy-start | bytes 24676
  560.9 93.2 %copy-start.13 = (f32[8,257]{1,0:T(8,128)S(1)}, f32[8,257]{1,0:T(8,128)}, u32[]{:S(2)}) copy-start(f32[8,257]{1,0:T(8,128)} %copy-done.12) | copy-start | bytes 24676
  560.9 678.7 %all-reduce.23.cloned.1.call-start = ((), (), s32[]{:S(2)}) async-start(), calls=%async_computation.16 | async-start | bytes 172032
  731.1 24.0 %copy-start.4 = (f32[8,16,257]{2,1,0:T(8,128)S(1)}, f32[8,16,257]{2,1,0:T(8,128)}, u32[]{:S(2)}) copy-start(f32[8,16,257]{2,1,0:T(8,128)} %copy-done.3) | copy-start | bytes 394756
  1013.1 37.3 %copy-start.9 = (f32[8,257]{1,0:T(8,128)S(1)}, f32[8,257]{1,0:T(8,128)}, u32[]{:S(2)}) copy-start(f32[8,257]{1,0:T(8,128)} %copy-done.8) | copy-start | bytes 24676
  1013.1 37.3 %copy-start.16 = (f32[8,257]{1,0:T(8,128)S(1)}, f32[8,257]{1,0:T(8,128)}, u32[]{:S(2)}) copy-start(f32[8,257]{1,0:T(8,128)} %copy-done.15) | copy-start | bytes 24676
  1013.1 37.3 %copy-start.18 = (f32[1280]{0:T(1024)S(1)}, f32[1280]{0:T(1024)}, u32[]{:S(2)}) copy-start(f32[1280]{0:T(1024)} %convert_element_type.186) | copy-start | bytes 15364
  1083.8 16.9 copy-start.27
  1083.8 16.9 copy-start.29
  1083.8 166.2 %reduce-scatter.7.cloned.1.call-start = ((), (), s32[]{:S(2)}) async-start(), calls=%async_computation.13 | async-start | bytes 6963200 | tf_op jit(solution)/shard_map/reduce_scatter | solution.py:109
  1100.6 248.3 %reduce-scatter.5.cloned.1.call-start = ((), (), s32[]{:S(2)}) async-start(), calls=%async_computation.12 | async-start | bytes 20889600 | tf_op jit(solution)/shard_map/reduce_scatter | solution.py:109
  1139.8 484.3 %reduce-scatter.11.cloned.1.call-start = ((), (), s32[]{:S(2)}) async-start(), calls=%async_computation.15 | async-start | bytes 27852800 | tf_op jit(solution)/shard_map/reduce_scatter | solution.py:109
  1180.0 0.7 copy-start.7
  1180.0 0.7 copy-start.14
  1180.0 0.7 copy-start.23
  1180.0 0.7 copy-start.25
  1180.1 717.5 %reduce-scatter.9.cloned.1.call-start = ((), (), s32[]{:S(2)}) async-start(), calls=%async_computation.14 | async-start | bytes 27852800 | tf_op jit(solution)/shard_map/reduce_scatter | solution.py:109
  1221.0 6.2 copy-start.21
  1221.0 6.2 copy-start.20
  1221.0 6.2 copy-start.10
  1221.0 6.2 copy-start.17
  1221.0 6.2 copy-start.19
  1221.1 6.2 slice-start
  1221.1 6.1 slice-start.1
Sparse Core Ops, SparseCore 0:
  10.8 57.3 all-gather.8
  71.0 31.8 all-gather.10
  105.7 64.0 all-gather.12
  172.5 64.0 all-gather.14
  521.4 65.9 all-gather.16
  590.0 64.0 all-gather.18
  656.9 31.9 all-gather.20
  691.7 53.3 all-gather.22
  1083.9 67.5 all-reduce.22
  1154.2 72.6 reduce-scatter.6
  1232.4 116.4 reduce-scatter.4
  1351.6 272.4 reduce-scatter.10
  1626.9 270.5 reduce-scatter.8
where the time goes:
time: 1910 us; the launch traced here: 1900 us
  waiting for transfers between devices  688 us (36%)
  matrix products  660 us (35%)
  other arithmetic  254 us (13%)
  local copies, waits for them, and re-layouts  217 us (11%)
  blocking collectives  69.7 us (4%)
    reduce_scatter x4, waiting for transfers between devices, device_step(): lax.psum_scatter(grad, 'fsdp', scatter_dimension=0, tiled=True)  648 us
    convert_element_type x1, other arithmetic, forward_local(): hidden = jax.nn.gelu(pre_act, approximate=False).astype(jnp.bfloat16)  102 us
    convert_element_type x2, local copies, waits for them, and re-layouts, backward_local(): grad_qkv_low = grad_qkv.astype(jnp.bfloat16)  77.8 us
    dot_general x1, matrix products, backward_local(): jnp.einsum('bhqk,bkhd->bqhd', grad_scores, key_heads, preferred_element_t...  77.4 us
    dot_general x1, matrix products, backward_local(): jnp.einsum('bhqk,bqhd->bkhd', grad_scores, query_heads, preferred_element...  71.2 us
    unnamed x2, blocking collectives  69.7 us
    unnamed x105, local copies, waits for them, and re-layouts  67 us
    dot_general x1, matrix products, forward_local(): jnp.einsum('bsw,wf->bsf', normed_two, fc_weight, preferred_element_type=j...  52.7 us
  transfers between devices with their start and end apart: 13, of which 5 were waited for; matrix products, arithmetic and copies ran while one was open for 55% of the time, Pallas kernels for 0%

commit v1 on v0

v1 whole, which is shorter than its diff:
```python
import math
import jax, jax.numpy as jnp
from jax import lax
from jax.experimental import pallas as pl
from jax.experimental.pallas import tpu as pltpu
from jax.sharding import PartitionSpec as P

BF, F32 = jnp.bfloat16, jnp.float32
IMAGES, SEQ, WIDTH, FFN, HEADS, HEAD = 8, 257, 1280, 5120, 16, 80
MAIN = SEQ - 1
TOKENS = IMAGES * SEQ
TAIL = IMAGES * MAIN
LN_EPS = 1e-5
VMEM_MAX = 67043328
LANES = WIDTH // 128
ROWS = 32


def dot(a, b):
    return jnp.dot(a, b, preferred_element_type=F32)


def dot_nt(a, b):
    return lax.dot_general(a, b, (((1,), (1,)), ((), ())), preferred_element_type=F32)


def dot_tn(a, b):
    return lax.dot_general(a, b, (((0,), (0,)), ((), ())), preferred_element_type=F32)


def col_sum(v):
    return jnp.sum(v, axis=0, keepdims=True)


def col_max(v):
    return jnp.max(v, axis=0, keepdims=True)


def row_sum(v):
    return jnp.sum(v, axis=-1, keepdims=True)


def whole(*shape, **kw):
    return pl.BlockSpec(shape, lambda *i: (0,) * len(shape), **kw)


def norm_stats(values):
    mean = row_sum(values) * (1.0 / WIDTH)
    centered = values - mean
    inv = lax.rsqrt(row_sum(centered * centered) * (1.0 / WIDTH) + LN_EPS)
    return centered * inv, inv


def row_tiles(body, step=128):
    def loop(i, carry):
        body(pl.multiple_of(i * step, step), step)
        return carry
    lax.fori_loop(0, TAIL // step, loop, 0)
    body(TAIL, IMAGES)


def to_image_order(wide, place, step=128):
    per = MAIN // step
    def loop(i, carry):
        first = (i % per) * (step * IMAGES) + i // per
        rows = [wide[c, pl.ds(first, step, stride=IMAGES), :] for c in range(LANES)]
        place(pl.multiple_of(i * step, step), step, jnp.concatenate(rows, axis=1))
        return carry
    lax.fori_loop(0, IMAGES * per, loop, 0)
    place(TAIL, IMAGES, joined(wide, TAIL, IMAGES))


def from_image_order(values, wide):
    def loop(i, carry):
        rows = values[pl.ds(pl.multiple_of(i * 128, 128), 128), :]
        for c in range(LANES):
            wide[c, pl.ds((i % 2) * (128 * IMAGES) + i // 2, 128, stride=IMAGES), :] = rows[:, c * 128:(c + 1) * 128]
        return carry
    lax.fori_loop(0, 2 * IMAGES, loop, 0)
    put(wide, TAIL, IMAGES, values[pl.ds(TAIL, IMAGES), :])


def joined(wide, r, n):
    return jnp.concatenate([wide[c, pl.ds(r, n), :] for c in range(LANES)], axis=1)


def put(wide, r, n, values):
    for c in range(LANES):
        wide[c, pl.ds(r, n), :] = values[:, c * 128:(c + 1) * 128]


QKV_N = 768


def qkv_kernel(x_ref, gain_ref, bias_ref, w_ref, wb_ref, xim_ref, h_ref, qkv_ref, wide):
    @pl.when(pl.program_id(0) == 0)
    def _():
        def widen(r, n):
            put(wide, r, n, x_ref[pl.ds(r, n), :].astype(F32))
        row_tiles(widen)
        gain, bias = gain_ref[...], bias_ref[...]

        def place(r, n, values):
            xim_ref[pl.ds(r, n), :] = values.astype(BF)
            hat, _ = norm_stats(values)
            h_ref[pl.ds(r, n), :] = (hat * gain + bias).astype(BF)
        to_image_order(wide, place, ROWS)
    qkv_ref[...] = (dot(h_ref[...], w_ref[...]) + wb_ref[...]).astype(BF)


def qkv_call(x, gain, bias, w, wb):
    full = whole(TOKENS, WIDTH)
    vec = whole(1, WIDTH)
    return pl.pallas_call(
        qkv_kernel,
        grid=(3 * WIDTH // QKV_N,),
        in_specs=[whole(TOKENS, WIDTH, pipeline_mode=pl.Buffered(1)), vec, vec,
                  pl.BlockSpec((WIDTH, QKV_N), lambda i: (0, i)), pl.BlockSpec((1, QKV_N), lambda i: (0, i))],
        out_specs=[full, full, pl.BlockSpec((TOKENS, QKV_N), lambda i: (0, i))],
        out_shape=[jax.ShapeDtypeStruct((TOKENS, WIDTH), BF), jax.ShapeDtypeStruct((TOKENS, WIDTH), BF),
                   jax.ShapeDtypeStruct((TOKENS, 3 * WIDTH), BF)],
        scratch_shapes=[pltpu.VMEM((LANES, TOKENS, 128), F32)],
        compiler_params=pltpu.CompilerParams(dimension_semantics=("arbitrary",), vmem_limit_bytes=VMEM_MAX),
        cost_estimate=pl.CostEstimate(flops=2 * TOKENS * WIDTH * 3 * WIDTH, bytes_accessed=60_000_000, transcendentals=0),
        name="qkv",
    )(x, gain, bias, w, wb)


MLP_F = 256
CDF_P = 0.33
CDF_C = (0.1326322871417956, 0.11939570820799192, 0.18103829560051796, -0.08904113226212501,
         0.33075919469138065, -0.22023738432274684, 0.0454530347223348)


def gelu_pair(u):
    bell = jnp.exp(u * u * -0.5)
    t = 1.0 / (1.0 + CDF_P * jnp.abs(u))
    poly = CDF_C[6]
    for c in CDF_C[5::-1]:
        poly = poly * t + c
    tail = poly * t * bell
    cdf = jnp.where(u < 0.0, tail, 1.0 - tail)
    return u * cdf, cdf + u * bell * ((2.0 * math.pi) ** -0.5)


def mlp_kernel(r_hbm, dy_hbm, gain_ref, bias_ref, pb_ref, fc_ref, proj_ref, fcb_ref,
               y_hbm, dr_hbm, dr16_hbm, dfc_ref, dproj_ref, dfcb_ref, small_ref,
               n2, dy, y_acc, dn_acc, g, du, ua, ub, da, db, sem):
    step, last = pl.program_id(0), pl.num_programs(0) - 1

    @pl.when(step == 0)
    def _():
        cp = pltpu.make_async_copy(dy_hbm, n2, sem)
        cp.start()
        cp.wait()

        def widen(r, n):
            put(dn_acc, r, n, n2[pl.ds(r, n), :].astype(F32))
        row_tiles(widen)
        cp = pltpu.make_async_copy(r_hbm, n2, sem)
        cp.start()

        def place(r, n, values):
            dy[pl.ds(r, n), :] = values.astype(BF)
        to_image_order(dn_acc, place)
        cp.wait()
        gain, bias = gain_ref[...], bias_ref[...]

        def norm(r, n):
            hat, _ = norm_stats(n2[pl.ds(r, n), :].astype(F32))
            n2[pl.ds(r, n), :] = (hat * gain + bias).astype(BF)
            y_acc[pl.ds(r, n), :] = jnp.zeros((n, WIDTH), F32)
            put(dn_acc, r, n, jnp.zeros((n, WIDTH), F32))
        row_tiles(norm, ROWS)

    fcb = fcb_ref[...]
    bias_sum = jnp.zeros((8, MLP_F), F32)
    tiles = [(b * MAIN, MAIN) for b in range(IMAGES - 1)] + [((IMAGES - 1) * MAIN, MAIN + IMAGES)]
    pairs = ((ua, da), (ub, db))

    def products(k):
        r, n = tiles[k]
        u_s, d_s = pairs[k % 2]
        u_s[0:n, :] = dot(n2[r:r + n, :], fc_ref[...])
        d_s[0:n, :] = dot_nt(dy[r:r + n, :], proj_ref[...])

    def pointwise(k, total):
        r, n = tiles[k]
        u_s, d_s = pairs[k % 2]
        value, slope = gelu_pair(u_s[0:n, :] + fcb)
        g[r:r + n, :] = value.astype(BF)
        grad = d_s[0:n, :] * slope
        du[r:r + n, :] = grad.astype(BF)
        return total + jnp.sum(grad.reshape(n // 8, 8, MLP_F), axis=0)

    products(0)
    for k in range(1, IMAGES):
        products(k)
        bias_sum = pointwise(k - 1, bias_sum)
    bias_sum = pointwise(IMAGES - 1, bias_sum)
    dfcb_ref[...] = col_sum(bias_sum)
    y_acc[...] += dot(g[...], proj_ref[...])
    for c in range(LANES // 2):
        part = dot_nt(du[...], fc_ref[c * 256:(c + 1) * 256, :])
        dn_acc[2 * c] += part[:, :128]
        dn_acc[2 * c + 1] += part[:, 128:]
    dproj_ref[...] = dot_tn(g[...], dy[...])
    dfc_ref[...] = dot_tn(n2[...], du[...])

    @pl.when(step == last)
    def _():
        cp = pltpu.make_async_copy(r_hbm, n2, sem)
        cp.start()
        cp.wait()
        gain, pb = gain_ref[...], pb_ref[...]
        small_ref[...] = jnp.zeros_like(small_ref)

        def rows_sum(v):
            return jnp.sum(v.reshape(v.shape[0] // 8, 8, WIDTH), axis=0)

        def back(r, n):
            wide_r = n2[pl.ds(r, n), :].astype(F32)
            hat, inv = norm_stats(wide_r)
            dn = joined(dn_acc, r, n)
            wide_dy = dy[pl.ds(r, n), :].astype(F32)
            small_ref[0:8, :] += rows_sum(dn * hat)
            small_ref[8:16, :] += rows_sum(dn)
            small_ref[16:24, :] += rows_sum(wide_dy)
            dhat = dn * gain
            m1 = row_sum(dhat) * (1.0 / WIDTH)
            m2 = row_sum(dhat * hat) * (1.0 / WIDTH)
            dr = wide_dy + inv * (dhat - m1 - hat * m2)
            put(dn_acc, r, n, dr)
            small_ref[24:32, :] += rows_sum(dr)
            y_acc[pl.ds(r, n), :] += wide_r + pb
            n2[pl.ds(r, n), :] = dr.astype(BF)
        row_tiles(back, ROWS)
        copies = [pltpu.make_async_copy(dn_acc, dr_hbm, sem), pltpu.make_async_copy(n2, dr16_hbm, sem)]
        for cp in copies:
            cp.start()
        for cp in copies:
            cp.wait()
        from_image_order(y_acc, dn_acc)

        def narrow(r, n):
            dy[pl.ds(r, n), :] = joined(dn_acc, r, n).astype(BF)
        row_tiles(narrow)
        cp = pltpu.make_async_copy(dy, y_hbm, sem)
        cp.start()
        cp.wait()


def mlp_call(r, dy, gain, bias, pb, fc, proj, fcb):
    hbm = pl.BlockSpec(memory_space=pl.ANY)
    vec = whole(1, WIDTH)
    n = fc.shape[1]
    return pl.pallas_call(
        mlp_kernel,
        grid=(n // MLP_F,),
        in_specs=[hbm, hbm, vec, vec, vec, pl.BlockSpec((WIDTH, MLP_F), lambda i: (0, i)),
                  pl.BlockSpec((MLP_F, WIDTH), lambda i: (i, 0)), pl.BlockSpec((1, MLP_F), lambda i: (0, i))],
        out_specs=[hbm, hbm, hbm, pl.BlockSpec((WIDTH, MLP_F), lambda i: (0, i)), pl.BlockSpec((MLP_F, WIDTH), lambda i: (i, 0)),
                   pl.BlockSpec((1, MLP_F), lambda i: (0, i)), whole(32, WIDTH)],
        out_shape=[jax.ShapeDtypeStruct((TOKENS, WIDTH), BF), jax.ShapeDtypeStruct((LANES, TOKENS, 128), F32),
                   jax.ShapeDtypeStruct((TOKENS, WIDTH), BF), jax.ShapeDtypeStruct((WIDTH, n), F32), jax.ShapeDtypeStruct((n, WIDTH), F32),
                   jax.ShapeDtypeStruct((1, n), F32), jax.ShapeDtypeStruct((32, WIDTH), F32)],
        scratch_shapes=[pltpu.VMEM((TOKENS, WIDTH), BF), pltpu.VMEM((TOKENS, WIDTH), BF),
                        pltpu.VMEM((TOKENS, WIDTH), F32), pltpu.VMEM((LANES, TOKENS, 128), F32),
                        pltpu.VMEM((TOKENS, MLP_F), BF), pltpu.VMEM((TOKENS, MLP_F), BF)]
                       + [pltpu.VMEM((MAIN + IMAGES, MLP_F), F32)] * 4 + [pltpu.SemaphoreType.DMA],
        compiler_params=pltpu.CompilerParams(dimension_semantics=("arbitrary",), vmem_limit_bytes=VMEM_MAX),
        cost_estimate=pl.CostEstimate(flops=12 * TOKENS * WIDTH * n, bytes_accessed=150_000_000, transcendentals=TOKENS * n),
        name="mlp",
    )(r, dy, gain, bias, pb, fc, proj, fcb)


SCALE = HEAD ** -0.5


def window(h):
    first = min(HEAD * h // 128 * 128, WIDTH - 256)
    wide = 128 if HEAD * h + HEAD <= first + 128 else 256
    return first, wide, HEAD * h - first


def lane_mask(h):
    first, wide, off = window(h)
    lane = lax.broadcasted_iota(jnp.int32, (MAIN, wide), 1)
    return (lane >= off) & (lane < off + HEAD)


def head_rows():
    lane = lax.broadcasted_iota(jnp.int32, (HEADS, WIDTH), 1)
    row = lax.broadcasted_iota(jnp.int32, (HEADS, WIDTH), 0)
    return jnp.where((lane >= row * HEAD) & (lane < row * HEAD + HEAD), 1.0, 0.0).astype(F32)


def tail_softmax(s, s_self):
    m = jnp.maximum(jnp.max(s, axis=1, keepdims=True), s_self)
    e = jnp.exp((s - m) * SCALE)
    e_self = jnp.exp((s_self - m) * SCALE)
    inv = 1.0 / (row_sum(e) + e_self)
    return e * inv, e_self * inv


def attn_kernel(qkv_ref, qkvt_ref, x_ref, xt_ref, w_ref, wb_ref, o_hbm, r_hbm, max_ref, inv_ref,
                tails, o_tail, o_t, ptail, o_buf, r_buf, sems):
    b, last = pl.program_id(0), pl.num_programs(0) - 1
    slot = b % 2

    @pl.when(b == 0)
    def _():
        tails[...] = qkvt_ref[...].astype(F32)

    heads = head_rows()
    q_t = heads * tails[pl.ds(b, 1), 0:WIDTH]
    k_t = heads * tails[pl.ds(b, 1), WIDTH:2 * WIDTH]
    v_t = heads * tails[pl.ds(b, 1), 2 * WIDTH:3 * WIDTH]
    q, k, v = qkv_ref[:, 0:WIDTH], qkv_ref[:, WIDTH:2 * WIDTH], qkv_ref[:, 2 * WIDTH:3 * WIDTH]

    p, p_self = tail_softmax(dot_nt(q_t.astype(BF), k), row_sum(q_t * k_t))
    mixed = dot(p.astype(BF), v) * heads + p_self.astype(BF).astype(F32) * v_t
    o_tail[pl.ds(b, 1), :] = col_sum(mixed)

    s_tail = dot_nt(k_t.astype(BF), q)
    v_turned = v.T
    for h in range(HEADS):
        first, wide, _ = window(h)
        q_h = jnp.where(lane_mask(h), qkv_ref[:, first:first + wide], jnp.zeros((), BF))
        s = dot_nt(qkv_ref[:, WIDTH + first:WIDTH + first + wide], q_h)
        top = jnp.maximum(col_max(s), s_tail[h:h + 1, :])
        e = jnp.exp((s - top) * SCALE)
        e_tail = jnp.exp((s_tail[h:h + 1, :] - top) * SCALE)
        inv = 1.0 / (col_sum(e) + e_tail)
        max_ref[0, h:h + 1, :] = top
        inv_ref[0, h:h + 1, :] = inv
        ptail[h:h + 1, :] = e_tail * inv
        o_t[HEAD * h:HEAD * h + HEAD, :] = dot(v_turned[HEAD * h:HEAD * h + HEAD, :], (e * inv).astype(BF))

    @pl.when(b >= 2)
    def _():
        out_copy(o_buf, o_hbm, slot, b - 2, sems, 0).wait()
        out_copy(r_buf, r_hbm, slot, b - 2, sems, 1).wait()

    o = (o_t[...].T + dot_tn(ptail[...].astype(BF), v_t.astype(BF))).astype(BF)
    o_buf[slot] = o
    r_buf[slot] = (x_ref[...].astype(F32) + dot(o, w_ref[...]) + wb_ref[...]).astype(BF)
    out_copy(o_buf, o_hbm, slot, b, sems, 0).start()
    out_copy(r_buf, r_hbm, slot, b, sems, 1).start()

    @pl.when(b == last)
    def _():
        for buf, hbm, n in ((o_buf, o_hbm, 0), (r_buf, r_hbm, 1)):
            out_copy(buf, hbm, 1 - slot, b - 1, sems, n).wait()
        o = o_tail[...].astype(BF)
        o_buf[1 - slot, 0:IMAGES, :] = o
        r_buf[1 - slot, 0:IMAGES, :] = (xt_ref[...].astype(F32) + dot(o, w_ref[...]) + wb_ref[...]).astype(BF)
        copies = [pltpu.make_async_copy(buf.at[1 - slot, pl.ds(0, IMAGES)], hbm.at[pl.ds(TAIL, IMAGES)], sems.at[n, 1 - slot])
                  for buf, hbm, n in ((o_buf, o_hbm, 0), (r_buf, r_hbm, 1))]
        for cp in copies:
            cp.start()
        for cp in copies:
            cp.wait()
        for buf, hbm, n in ((o_buf, o_hbm, 0), (r_buf, r_hbm, 1)):
            out_copy(buf, hbm, slot, b, sems, n).wait()


def out_copy(buf, hbm, slot, b, sems, n):
    return pltpu.make_async_copy(buf.at[slot], hbm.at[pl.ds(pl.multiple_of(b * MAIN, MAIN), MAIN)], sems.at[n, slot])


def attn_call(qkv, xim, w, wb):
    hbm = pl.BlockSpec(memory_space=pl.ANY)
    main = lambda n: pl.BlockSpec((MAIN, n), lambda i: (i, 0))
    tail = lambda n: pl.BlockSpec((IMAGES, n), lambda i: (TAIL // IMAGES, 0))
    stat = pl.BlockSpec((1, HEADS, MAIN), lambda i: (i, 0, 0))
    return pl.pallas_call(
        attn_kernel,
        grid=(IMAGES,),
        in_specs=[main(3 * WIDTH), tail(3 * WIDTH), main(WIDTH), tail(WIDTH),
                  whole(WIDTH, WIDTH), whole(1, WIDTH)],
        out_specs=[hbm, hbm, stat, stat],
        out_shape=[jax.ShapeDtypeStruct((TOKENS, WIDTH), BF), jax.ShapeDtypeStruct((TOKENS, WIDTH), BF),
                   jax.ShapeDtypeStruct((IMAGES, HEADS, MAIN), F32), jax.ShapeDtypeStruct((IMAGES, HEADS, MAIN), F32)],
        scratch_shapes=[pltpu.VMEM((IMAGES, 3 * WIDTH), F32), pltpu.VMEM((IMAGES, WIDTH), F32),
                        pltpu.VMEM((WIDTH, MAIN), F32), pltpu.VMEM((HEADS, MAIN), F32),
                        pltpu.VMEM((2, MAIN, WIDTH), BF), pltpu.VMEM((2, MAIN, WIDTH), BF), pltpu.SemaphoreType.DMA((2, 2))],
        compiler_params=pltpu.CompilerParams(dimension_semantics=("arbitrary",), vmem_limit_bytes=VMEM_MAX),
        cost_estimate=pl.CostEstimate(flops=30_000_000_000, bytes_accessed=50_000_000, transcendentals=8_400_000),
        name="attn",
    )(qkv, qkv, xim, xim, w, wb)


def outb_kernel(dr_ref, o_ref, w_ref, do_ref, dw_ref):
    n = 256
    c = pl.program_id(0)
    do_ref[...] = dot_nt(dr_ref[...], w_ref[...]).astype(BF)
    dw_ref[...] = dot_tn(o_ref[...], dr_ref[:, pl.ds(pl.multiple_of(c * n, n), n)])


def outb_call(dr, o, w):
    n = 256
    full = whole(TOKENS, WIDTH)
    return pl.pallas_call(
        outb_kernel,
        grid=(WIDTH // n,),
        in_specs=[full, full, pl.BlockSpec((n, WIDTH), lambda i: (i, 0))],
        out_specs=[pl.BlockSpec((TOKENS, n), lambda i: (0, i)), pl.BlockSpec((WIDTH, n), lambda i: (0, i))],
        out_shape=[jax.ShapeDtypeStruct((TOKENS, WIDTH), BF), jax.ShapeDtypeStruct((WIDTH, WIDTH), F32)],
        compiler_params=pltpu.CompilerParams(dimension_semantics=("arbitrary",), vmem_limit_bytes=VMEM_MAX),
        cost_estimate=pl.CostEstimate(flops=4 * TOKENS * WIDTH * WIDTH, bytes_accessed=30_000_000, transcendentals=0),
        name="outb",
    )(dr, o, w)


def attn_back_kernel(qkv_ref, qkvt_ref, do_ref, dot_ref, max_ref, inv_ref, dqkv_hbm, dwb_ref,
                     tails, do_tails, grad_tails, dq_t, dk, dv, ds_tail, buf, sems):
    b, last = pl.program_id(0), pl.num_programs(0) - 1
    slot = b % 2

    @pl.when(b == 0)
    def _():
        tails[...] = qkvt_ref[...].astype(F32)
        do_tails[...] = dot_ref[...].astype(F32)
        dwb_ref[...] = jnp.zeros_like(dwb_ref)

    heads = head_rows()
    q_t = heads * tails[pl.ds(b, 1), 0:WIDTH]
    k_t = heads * tails[pl.ds(b, 1), WIDTH:2 * WIDTH]
    v_t = heads * tails[pl.ds(b, 1), 2 * WIDTH:3 * WIDTH]
    do_t = heads * do_tails[pl.ds(b, 1), :]
    q, k, v = qkv_ref[:, 0:WIDTH], qkv_ref[:, WIDTH:2 * WIDTH], qkv_ref[:, 2 * WIDTH:3 * WIDTH]
    do = do_ref[...]
    q_t16, k_t16, v_t16, do_t16 = (z.astype(BF) for z in (q_t, k_t, v_t, do_t))

    p, p_self = tail_softmax(dot_nt(q_t16, k), row_sum(q_t * k_t))
    dp, dp_self = dot_nt(do_t16, v), row_sum(do_t * v_t)
    inner = row_sum(p * dp) + p_self * dp_self
    ds16 = (p * (dp - inner) * SCALE).astype(BF)
    ds_self = (p_self * (dp_self - inner) * SCALE).astype(BF).astype(F32)
    grad_q = col_sum(dot(ds16, k) * heads + ds_self * k_t)
    grad_k = ds_self * q_t
    grad_v = p_self.astype(BF).astype(F32) * do_t
    dk[...] = dot_tn(ds16, q_t16)
    dv[...] = dot_tn(p.astype(BF), do_t16)

    p_tail = jnp.exp((dot_nt(k_t16, q) - max_ref[0]) * SCALE) * inv_ref[0]
    dp_tail = dot_nt(v_t16, do)
    inner_tail = p_tail * dp_tail

    k_turned = k.T
    for h in range(HEADS):
        first, wide, _ = window(h)
        here = slice(first, first + wide)
        mask = lane_mask(h)
        q_h = jnp.where(mask, qkv_ref[:, here], jnp.zeros((), BF))
        do_h = jnp.where(mask, do_ref[:, here], jnp.zeros((), BF))
        s = dot_nt(qkv_ref[:, WIDTH + first:WIDTH + first + wide], q_h)
        dp = dot_nt(qkv_ref[:, 2 * WIDTH + first:2 * WIDTH + first + wide], do_h)
        p = jnp.exp((s - max_ref[0, h:h + 1, :]) * SCALE) * inv_ref[0, h:h + 1, :]
        inner = col_sum(p * dp) + inner_tail[h:h + 1, :]
        ds = (p * (dp - inner) * SCALE).astype(BF)
        dv[:, here] += dot(p.astype(BF), do_h)
        dk[:, here] += dot(ds, q_h)
        dq_t[HEAD * h:HEAD * h + HEAD, :] = dot(k_turned[HEAD * h:HEAD * h + HEAD, :], ds)
        ds_tail[h:h + 1, :] = p_tail[h:h + 1, :] * (dp_tail[h:h + 1, :] - inner) * SCALE

    ds_tail16 = ds_tail[...].astype(BF)
    grad_k = col_sum(grad_k + dot(ds_tail16, q) * heads)
    grad_v = col_sum(grad_v + dot(p_tail.astype(BF), do) * heads)

    @pl.when(b >= 2)
    def _():
        out_copy(buf, dqkv_hbm, slot, b - 2, sems, 0).wait()

    grad = dq_t[...].T + dot_tn(ds_tail16, k_t16)
    for n, (main, tail) in enumerate(((grad, grad_q), (dk[...], grad_k), (dv[...], grad_v))):
        here = slice(n * WIDTH, (n + 1) * WIDTH)
        buf[slot, :, here] = main.astype(BF)
        grad_tails[pl.ds(b, 1), here] = tail
        dwb_ref[:, here] += col_sum(main) + tail
    out_copy(buf, dqkv_hbm, slot, b, sems, 0).start()

    @pl.when(b == last)
    def _():
        out_copy(buf, dqkv_hbm, 1 - slot, b - 1, sems, 0).wait()
        buf[1 - slot, 0:IMAGES, :] = grad_tails[...].astype(BF)
        cp = pltpu.make_async_copy(buf.at[1 - slot, pl.ds(0, IMAGES)], dqkv_hbm.at[pl.ds(TAIL, IMAGES)], sems.at[0, 1 - slot])
        cp.start()
        cp.wait()
        out_copy(buf, dqkv_hbm, slot, b, sems, 0).wait()


def attn_back_call(qkv, do, top, inv):
    hbm = pl.BlockSpec(memory_space=pl.ANY)
    main = lambda n: pl.BlockSpec((MAIN, n), lambda i: (i, 0))
    tail = lambda n: pl.BlockSpec((IMAGES, n), lambda i: (TAIL // IMAGES, 0))
    stat = pl.BlockSpec((1, HEADS, MAIN), lambda i: (i, 0, 0))
    return pl.pallas_call(
        attn_back_kernel,
        grid=(IMAGES,),
        in_specs=[main(3 * WIDTH), tail(3 * WIDTH), main(WIDTH), tail(WIDTH), stat, stat],
        out_specs=[hbm, whole(1, 3 * WIDTH)],
        out_shape=[jax.ShapeDtypeStruct((TOKENS, 3 * WIDTH), BF), jax.ShapeDtypeStruct((1, 3 * WIDTH), F32)],
        scratch_shapes=[pltpu.VMEM((IMAGES, 3 * WIDTH), F32), pltpu.VMEM((IMAGES, WIDTH), F32),
                        pltpu.VMEM((IMAGES, 3 * WIDTH), F32), pltpu.VMEM((WIDTH, MAIN), F32),
                        pltpu.VMEM((MAIN, WIDTH), F32), pltpu.VMEM((MAIN, WIDTH), F32), pltpu.VMEM((HEADS, MAIN), F32),
                        pltpu.VMEM((2, MAIN, 3 * WIDTH), BF), pltpu.SemaphoreType.DMA((1, 2))],
        compiler_params=pltpu.CompilerParams(dimension_semantics=("arbitrary",), vmem_limit_bytes=VMEM_MAX),
        cost_estimate=pl.CostEstimate(flops=60_000_000_000, bytes_accessed=50_000_000, transcendentals=8_400_000),
        name="attn_back",
    )(qkv, qkv, do, do, top, inv)


def qkvb_kernel(xim_hbm, dr_hbm, gain_ref, h_ref, dqkv_ref, w_ref, dx_hbm, dw_ref, small_ref, acc, dr, xd, sems):
    c, last = pl.program_id(0), pl.num_programs(0) - 1
    loads = [pltpu.make_async_copy(dr_hbm, dr, sems.at[0]), pltpu.make_async_copy(xim_hbm, xd, sems.at[1])]

    @pl.when(c == 0)
    def _():
        for cp in loads:
            cp.start()
        acc[...] = jnp.zeros_like(acc)
    acc[...] += dot_nt(dqkv_ref[...], w_ref[...])
    dw_ref[...] = dot_tn(h_ref[...], dqkv_ref[...])

    @pl.when(c == last)
    def _():
        for cp in loads:
            cp.wait()
        gain = gain_ref[...]
        small_ref[...] = jnp.zeros_like(small_ref)

        def back(r, n):
            hat, inv = norm_stats(xd[pl.ds(r, n), :].astype(F32))
            dn = acc[pl.ds(r, n), :]
            small_ref[0:8, :] += jnp.sum((dn * hat).reshape(n // 8, 8, WIDTH), axis=0)
            small_ref[8:16, :] += jnp.sum(dn.reshape(n // 8, 8, WIDTH), axis=0)
            dhat = dn * gain
            m1 = row_sum(dhat) * (1.0 / WIDTH)
            m2 = row_sum(dhat * hat) * (1.0 / WIDTH)
            acc[pl.ds(r, n), :] = joined(dr, r, n) + inv * (dhat - m1 - hat * m2)
        row_tiles(back, ROWS)
        from_image_order(acc, dr)

        def narrow(r, n):
            xd[pl.ds(r, n), :] = joined(dr, r, n).astype(BF)
        row_tiles(narrow)
        cp = pltpu.make_async_copy(xd, dx_hbm, sems.at[1])
        cp.start()
        cp.wait()


def qkvb_call(xim, dr, gain, h, dqkv, w):
    hbm = pl.BlockSpec(memory_space=pl.ANY)
    return pl.pallas_call(
        qkvb_kernel,
        grid=(3 * WIDTH // QKV_N,),
        in_specs=[hbm, hbm, whole(1, WIDTH),
                  whole(TOKENS, WIDTH, pipeline_mode=pl.Buffered(1)),
                  pl.BlockSpec((TOKENS, QKV_N), lambda i: (0, i)), pl.BlockSpec((WIDTH, QKV_N), lambda i: (0, i))],
        out_specs=[hbm, pl.BlockSpec((WIDTH, QKV_N), lambda i: (0, i)), whole(16, WIDTH)],
        out_shape=[jax.ShapeDtypeStruct((TOKENS, WIDTH), BF), jax.ShapeDtypeStruct((WIDTH, 3 * WIDTH), F32),
                   jax.ShapeDtypeStruct((16, WIDTH), F32)],
        scratch_shapes=[pltpu.VMEM((TOKENS, WIDTH), F32), pltpu.VMEM((LANES, TOKENS, 128), F32), pltpu.VMEM((TOKENS, WIDTH), BF),
                        pltpu.SemaphoreType.DMA((2,))],
        compiler_params=pltpu.CompilerParams(dimension_semantics=("arbitrary",), vmem_limit_bytes=VMEM_MAX),
        cost_estimate=pl.CostEstimate(flops=4 * TOKENS * WIDTH * 3 * WIDTH, bytes_accessed=80_000_000, transcendentals=0),
        name="qkvb",
    )(xim, dr, gain, h, dqkv, w)


PARTS = 16
VECTORS = (80, 80, 240, 80, 80, 80, 320, 80)


def solution(mesh):
    specs = (P("fsdp"),) * 14

    def gather(shard):
        return lax.all_gather(shard.astype(BF), "fsdp", axis=0, tiled=True)

    def scatter(grad):
        return lax.psum_scatter(grad, "fsdp", scatter_dimension=0, tiled=True)

    def device_step(resid_in, grad_out, ln1_gain, ln1_bias, qkv_weight, qkv_bias, out_weight, out_bias,
                    ln2_gain, ln2_bias, fc_weight, fc_bias, proj_weight, proj_bias):
        wq, wo, wf, wp = (gather(w) for w in (qkv_weight, out_weight, fc_weight, proj_weight))
        packed = jnp.concatenate([ln1_gain, ln1_bias, qkv_bias, out_bias, ln2_gain, ln2_bias, fc_bias, proj_bias])
        packed = gather(packed[None]).astype(F32)
        cuts = [sum(VECTORS[:i]) for i in range(len(VECTORS) + 1)]
        g1, b1, bq, bo, g2, b2, bf, bp = (packed[:, a:b].reshape(1, -1) for a, b in zip(cuts, cuts[1:]))

        x = resid_in.transpose(1, 0, 2).reshape(TOKENS, WIDTH)
        dy = grad_out.transpose(1, 0, 2).reshape(TOKENS, WIDTH)
        xim, h, qkv = qkv_call(x, g1, b1, wq, bq)
        o, r, top, inv = attn_call(qkv, xim, wo, bo)
        y, dr, dr16, dwf, dwp, dbf, small2 = mlp_call(r, dy, g2, b2, bp, wf, wp, bf)
        do, dwo = outb_call(dr16, o, wo)
        dqkv, dbq = attn_back_call(qkv, do, top, inv)
        dx, dwq, small1 = qkvb_call(xim, dr, g1, h, dqkv, wq)

        turned = dwp.reshape(PARTS, 4, 80, WIDTH).transpose(0, 2, 1, 3).reshape(WIDTH, 4 * WIDTH)
        s1 = scatter(dwf[:, :3 * WIDTH])
        s2 = scatter(jnp.concatenate([dwf[:, 3 * WIDTH:], turned[:, :2 * WIDTH]], axis=1))
        s3 = scatter(jnp.concatenate([turned[:, 2 * WIDTH:], dwo], axis=1))
        dwf = jnp.concatenate([s1, s2[:, :WIDTH]], axis=1)
        dwp = jnp.concatenate([s2[:, WIDTH:], s3[:, :2 * WIDTH]], axis=1).reshape(80, 4, WIDTH).transpose(1, 0, 2).reshape(320, WIDTH)
        dwo = s3[:, 2 * WIDTH:]
        dwq = scatter(dwq)
        rows = lambda a, i: jnp.sum(a[8 * i:8 * i + 8], axis=0)
        vectors = (rows(small1, 0), rows(small1, 1), dbq[0], rows(small2, 3), rows(small2, 0), rows(small2, 1), dbf[0], rows(small2, 2))
        packed = jnp.concatenate([v.reshape(PARTS, -1) for v in vectors], axis=1)
        packed = scatter(packed)[0]
        dg1, db1, dbq, dbo, dg2, db2, dbf, dbp = (packed[a:b] for a, b in zip(cuts, cuts[1:]))
        unturn = lambda t: t.reshape(SEQ, IMAGES, WIDTH).transpose(1, 0, 2)
        return (unturn(y), unturn(dx), dg1, db1, dwq, dbq, dwo, dbo, dg2, db2, dwf, dbf, dwp, dbp)

    return jax.shard_map(device_step, mesh=mesh, in_specs=specs, out_specs=specs, check_vma=False)
```

time: 1910 us -> 1310 us (0.69)
  matrix products: 660 us -> 0 us
  Pallas kernels: 0 us -> 511 us
  other arithmetic: 254 us -> 44 us
  local copies, waits for them, and re-layouts: 217 us -> 111 us
  waiting for transfers between devices: 688 us -> 604 us
  blocking collectives: 69.7 us -> 15.2 us
    dot_general x18 -> x0, matrix products: 660 us -> none  [the longest x1 77.4 us: backward_local(): jnp.einsum('bhqk,bkhd->bqhd', grad_scores, key_heads, preferred_element_t...]
    pallas_call x0 -> x6, Pallas kernels: none -> 511 us  [the longest x1 258 us: mlp_call(): pl.pallas_call(mlp_kernel, grid=(n // MLP_F,), in_specs=[hbm, hbm, vec, v...]
    reduce_scatter x4, waiting for transfers between devices: 648 us -> 475 us  [scatter(): return lax.psum_scatter(grad, 'fsdp', scatter_dimension=0, tiled=True)]
    convert_element_type x31 -> x4, other arithmetic: 160 us -> 7.36 us  [gather(): return lax.all_gather(shard.astype(BF), 'fsdp', axis=0, tiled=True)]
    convert_element_type x2 -> x0, local copies, waits for them, and re-layouts: 77.8 us -> none  [backward_local(): grad_qkv_low = grad_qkv.astype(jnp.bfloat16)]
    unnamed x2 -> x0, blocking collectives: 69.7 us -> none
    all_gather x8 -> x4, waiting for transfers between devices: 40.6 us -> 109 us  [gather(): return lax.all_gather(shard.astype(BF), 'fsdp', axis=0, tiled=True)]
    sub x1 -> x0, other arithmetic: 52.7 us -> none  [forward_local(): attn_probs = jax.nn.softmax(scores, axis=-1)]
  transfers between devices with their start and end apart: 13 -> 9, of which waited for: 5 -> 8; matrix products, arithmetic and copies ran while one was open for 55% -> 5% of each run, Pallas kernels for 0% -> 7%
where the time goes in v1:
time: 1310 us; the launch traced here: 1300 us
  waiting for transfers between devices  604 us (46%)
  Pallas kernels  511 us (39%)
  local copies, waits for them, and re-layouts  111 us (8%)
  other arithmetic  44 us (3%)
  blocking collectives  15.2 us (1%)
  between operations  14.5 us (1%)
    reduce_scatter x4, waiting for transfers between devices, scatter(): return lax.psum_scatter(grad, 'fsdp', scatter_dimension=0, tiled=True)  475 us
    pallas_call x1, Pallas kernels, mlp_call(): pl.pallas_call(mlp_kernel, grid=(n // MLP_F,), in_specs=[hbm, hbm, vec, v...  258 us
    all_gather x4, waiting for transfers between devices, gather(): return lax.all_gather(shard.astype(BF), 'fsdp', axis=0, tiled=True)  109 us
    pallas_call x1, Pallas kernels, qkvb_call(): pl.pallas_call(qkvb_kernel, grid=(3 * WIDTH // QKV_N,), in_specs=[hbm, hb...  77.5 us
    pallas_call x1, Pallas kernels, attn_back_call(): pl.pallas_call(attn_back_kernel, grid=(IMAGES,), in_specs=[main(3 * WIDTH...  63.7 us
    pallas_call x1, Pallas kernels, attn_call(): pl.pallas_call(attn_kernel, grid=(IMAGES,), in_specs=[main(3 * WIDTH), ta...  47.8 us
    pallas_call x1, Pallas kernels, qkv_call(): pl.pallas_call(qkv_kernel, grid=(3 * WIDTH // QKV_N,), in_specs=[whole(TO...  43.1 us
    transpose x1, local copies, waits for them, and re-layouts, device_step(): dwp.reshape(PARTS, 4, 80, WIDTH).transpose(0, 2, 1, 3)  30.1 us
  transfers between devices with their start and end apart: 9, of which 8 were waited for; matrix products, arithmetic and copies ran while one was open for 5% of the time, Pallas kernels for 7%

profile of v1, /device:TPU:0, one launch (start us, length us, event | category | flops | bytes accessed | tf_op | source)
XLA Modules:
  0.0 1300.4 jit_solution(78678706389261524)
XLA Ops:
  7.3 2.3 convert_element_type.25
  9.7 1.7 convert_element_type.26
  11.4 2.4 convert_element_type.27
  13.9 0.0 all-gather.12.cloned.1.call-start
  13.9 1.0 convert_element_type.28
  15.2 0.1 concatenate.50
  15.3 15.2 %all-gather = bf16[16,1,1040]{2,1,0:T(2,128)(2,1)S(1)} all-gather(bf16[1,1,1040]{2,1,0:T(2,128)(2,1)S(1)} %bitcast.57), channel_id=1, replica_groups=mesh['fsdp'=16] {'fsdp'}, dimensions={0}, use_global_device_ids=true | all-gather | bytes 35360 | tf_op jit(solution)/shard_map/all_gather | solution.py:581
  30.4 0.1 slice.154
  30.5 0.1 fusion.1
  30.6 0.7 reshape.219.gain_ref
  31.3 0.7 reshape.220.bias_ref
  31.9 0.7 reshape.221.wb_ref
  32.6 0.7 reshape.222.wb_ref
  33.3 0.7 reshape.224.gain_ref
  34.0 0.7 reshape.225.bias_ref
  34.7 0.7 reshape.226.pb_ref
  35.3 0.7 reshape.227.fcb_ref
  36.0 31.6 %all-gather.6.cloned.1.call-done.w_ref = bf16[1280,3840]{1,0:T(8,128)(2,1)} async-done(((bf16[80,3840]{1,0:T(8,128)(2,1)}), bf16[1280,3840]{1,0:T(8,128)(2,1)}) %all-gather.6.cloned.1.call-update) | async-done | bytes 9830416 | tf_op jit(solution)/shard_map/all_gather | solution.py:581
  67.6 43.1 %qkv.1 = (bf16[2056,1280]{1,0:T(8,128)(2,1)}, bf16[2056,1280]{1,0:T(8,128)(2,1)}, bf16[2056,3840]{1,0:T(8,128)(2,1)}) custom-call(bf16[2056,1280]{1,0:T(8,128)(2,1)} %bitcast.59, f32[1,1280]{1,0:T(1,128)} %reshape.219.gain_ref, f32[1,1280]{1,0:T(1,128)} %reshape.220.bias_ref, bf16[1280,3840]{1,0:T(8,128)(2,1)} %all-gather.6.cloned.1.call-done.w_ref, ...), custom_call_target="tpu_custom_call" | custom-call | flops 20211302400 | bytes 60000000 | tf_op jit(solution)/shard_map/qkv/pallas_call | solution.py:114
  110.7 47.8 %attn.1 = (bf16[2056,1280]{1,0:T(8,128)(2,1)}, bf16[2056,1280]{1,0:T(8,128)(2,1)}, f32[8,16,256]{2,1,0:T(8,128)}, f32[8,16,256]{2,1,0:T(8,128)}) custom-call(bf16[2056,3840]{1,0:T(8,128)(2,1)} %get-tuple-element.35.qkv_ref.qkvt_ref, bf16[2056,3840]{1,0:T(8,128)(2,1)} %get-tuple-element.35.qkv_ref.qkvt_ref, ...), custom_call_target="tpu_custom_call" | custom-call | flops 30000001024 | bytes 50000000 | tf_op jit(solution)/shard_map/attn/pallas_call | solution.py:377
  158.5 11.0 all-gather.10.cloned.1.call-done.fc_ref
  169.5 66.7 %all-gather.12.cloned.1.call-done.proj_ref = bf16[5120,1280]{1,0:T(8,128)(2,1)} async-done(((bf16[320,1280]{1,0:T(8,128)(2,1)}), bf16[5120,1280]{1,0:T(8,128)(2,1)}) %all-gather.12.cloned.1.call-update) | async-done | bytes 13107216 | tf_op jit(solution)/shard_map/all_gather | solution.py:581
  236.2 257.9 %mlp.1 = (bf16[2056,1280]{1,0:T(8,128)(2,1)}, f32[10,2056,128]{2,1,0:T(8,128)}, bf16[2056,1280]{1,0:T(8,128)(2,1)}, f32[1280,5120]{1,0:T(8,128)}, f32[5120,1280]...) custom-call(bf16[2056,1280]{1,0:T(8,128)(2,1)} %get-tuple-element.37.r_hbm, bf16[2056,1280]{1,0:T(8,128)(2,1)} %bitcast.60, ...), custom_call_target="tpu_custom_call" | custom-call | flops 161690419200 | bytes 150000000 | tf_op jit(solution)/shard_map/mlp/pallas_call | solution.py:257
  494.1 30.1 %copy.30 = f32[16,80,4,1280]{3,2,1,0:T(4,128)} copy(f32[16,80,4,1280]{3,1,2,0:T(8,128)} %bitcast.51) | data formatting | bytes 52428800 | tf_op jit(solution)/shard_map/transpose | solution.py:603
  524.2 21.8 %copy.33 = f32[160,8,4,1280]{3,1,2,0:T(8,128)} copy(f32[160,8,4,1280]{3,2,1,0:T(4,128)} %bitcast.50) | data formatting | bytes 52428800
  546.0 18.8 %fusion = (f32[1280,2560]{1,0:T(8,128)}, f32[1280,2560]{1,0:T(8,128)}) fusion(f32[1280,5120]{1,0:T(8,128)} %bitcast.49), kind=kLoop, calls=%fused_computation.24 | loop fusion | bytes 52428800 | tf_op jit(solution)/shard_map/slice | solution.py:605
  564.8 6.0 slice.143
  570.8 21.4 %outb.1 = (bf16[2056,1280]{1,0:T(8,128)(2,1)}, f32[1280,1280]{1,0:T(8,128)}) custom-call(bf16[2056,1280]{1,0:T(8,128)(2,1)} %get-tuple-element.41.dr_ref, bf16[2056,1280]{1,0:T(8,128)(2,1)} %get-tuple-element.42.o_ref, bf16[1280,1280]{1,0:T(8,128)(2,1)} %all-gather.8.cloned.1.call-done.w_ref), custom_call_target="tpu_custom_call" | custom-call | flops 13474201600 | bytes 30000000 | tf_op jit(solution)/shard_map/outb/pallas_call | solution.py:404
  592.2 63.7 %attn_back.1 = (bf16[2056,3840]{1,0:T(8,128)(2,1)}, f32[1,3840]{1,0:T(1,128)}) custom-call(bf16[2056,3840]{1,0:T(8,128)(2,1)} %get-tuple-element.35.qkv_ref.qkvt_ref, bf16[2056,3840]{1,0:T(8,128)(2,1)} %get-tuple-element.35.qkv_ref.qkvt_ref, bf16[2056,1280]{1,0:T(8,128)(2,1)} %get-tuple-element.43.do_ref.dot_ref, ...), custom_call_target="tpu_custom_call" | custom-call | flops 60000002048 | bytes 50000000 | tf_op jit(solution)/shard_map/attn_back/pallas_call | solution.py:499
  655.9 77.5 %qkvb.1 = (bf16[2056,1280]{1,0:T(8,128)(2,1)}, f32[1280,3840]{1,0:T(8,128)}, f32[16,1280]{1,0:T(8,128)}) custom-call(bf16[2056,1280]{1,0:T(8,128)(2,1)} %get-tuple-element.36.x_ref.xt_ref.xim_hbm, f32[10,2056,128]{2,1,0:T(8,128)} %get-tuple-element.39.dr_hbm, f32[1,1280]{1,0:T(1,128)} %reshape.219.gain_ref, bf16[2056,1280]{1,0:T(8,128)(2,1)} %get-tuple-element.40.h_ref, ...), custom_call_target="tpu_custom_call" | custom-call | flops 40422604800 | bytes 80000000 | tf_op jit(solution)/shard_map/qkvb/pallas_call | solution.py:556
  733.4 0.8 slice_reduce_fusion.4
  734.2 0.1 reshape.230
  734.3 0.1 reshape.231
  734.4 0.8 reduce
  735.1 0.1 reshape_squeeze.6
  735.2 0.9 slice_reduce_fusion
  736.1 0.1 reshape.232
  736.2 0.1 reshape.233
  736.2 0.1 reshape.234
  736.3 0.1 reshape.235
  736.4 0.5 broadcast.5
  736.9 1.4 reduce.6
  738.3 0.1 reshape_squeeze.7
  738.4 0.7 concatenate.51
  739.2 15.0 %pad_maximum_fusion.1 = f32[1280,3840]{1,0:T(8,128)} fusion(f32[1280,2560]{1,0:T(8,128)} %get-tuple-element.62, f32[1280,1280]{1,0:T(8,128)} %slice.143), kind=kLoop, calls=%fused_computation.1 | loop fusion | flops 4915200 | bytes 39321600 | tf_op jit(solution)/shard_map/concatenate | solution.py:605
  754.3 15.1 %pad_maximum_fusion = f32[1280,3840]{1,0:T(8,128)} fusion(f32[1280,1280]{1,0:T(8,128)} %get-tuple-element.54, f32[1280,2560]{1,0:T(8,128)} %get-tuple-element.63), kind=kLoop, calls=%fused_computation | loop fusion | flops 4915200 | bytes 39321600 | tf_op jit(solution)/shard_map/concatenate | solution.py:606
  769.4 15.1 %slice.142 = f32[1280,3840]{1,0:T(8,128)} slice(f32[1280,5120]{1,0:T(8,128)} %get-tuple-element.55), slice={[0:1280], [0:3840]} | slice | bytes 39321600 | tf_op jit(solution)/shard_map/slice | solution.py:604
  784.6 0.7 reduce-scatter.5.cloned.1.call-update
  785.3 19.0 %all-reduce.3.cloned.1.call-done = f32[16,1040]{1,0:T(8,128)} async-done(((f32[16,1040]{1,0:T(8,128)}), f32[16,1040]{1,0:T(8,128)}) %all-reduce.3.cloned.1.call-update) | async-done | bytes 66576
  804.2 1.3 dynamic-slice.3
  805.6 1.4 dynamic-slice_reduce_fusion
  807.0 1.4 dynamic-slice_bitcast_fusion
  808.4 116.8 %reduce-scatter.11.cloned.1.call-done = f32[80,3840]{1,0:T(8,128)} async-done(((f32[1280,3840]{1,0:T(8,128)}), f32[80,3840]{1,0:T(8,128)}) %reduce-scatter.11.cloned.1.call-update) | async-done | bytes 1228816 | tf_op jit(solution)/shard_map/reduce_scatter | solution.py:584
  925.2 1.2 slice.164
  926.4 121.3 %reduce-scatter.7.cloned.1.call-done = f32[80,3840]{1,0:T(8,128)} async-done(((f32[1280,3840]{1,0:T(8,128)}), f32[80,3840]{1,0:T(8,128)}) %reduce-scatter.7.cloned.1.call-update) | async-done | bytes 1228816 | tf_op jit(solution)/shard_map/reduce_scatter | solution.py:584
  1047.7 1.2 slice.165
  1048.9 0.1 pad_maximum_fusion.3
  1049.1 0.8 reshape.238
  1049.9 1.5 copy.31
  1051.3 1.0 slice.163
  1052.4 1.8 slice.161
  1054.2 116.2 %reduce-scatter.9.cloned.1.call-done = f32[80,3840]{1,0:T(8,128)} async-done(((f32[1280,3840]{1,0:T(8,128)}), f32[80,3840]{1,0:T(8,128)}) %reduce-scatter.9.cloned.1.call-update) | async-done | bytes 1228816 | tf_op jit(solution)/shard_map/reduce_scatter | solution.py:584
  1170.3 2.6 pad_maximum_fusion.2
  1172.9 120.6 %reduce-scatter.5.cloned.1.call-done = f32[80,3840]{1,0:T(8,128)} async-done(((f32[1280,3840]{1,0:T(8,128)}), f32[80,3840]{1,0:T(8,128)}) %reduce-scatter.5.cloned.1.call-update) | async-done | bytes 1228816 | tf_op jit(solution)/shard_map/reduce_scatter | solution.py:584
  (44 shorter events, 0.5 us)
Async XLA Ops:
  7.2 6.8 copy-start
  7.2 7.8 copy-start.1
  7.2 7.8 copy-start.8
  7.2 7.8 copy-start.3
  7.2 7.8 copy-start.2
  7.2 7.9 copy-start.5
  7.2 7.9 copy-start.4
  7.3 7.9 copy-start.7
  7.3 7.9 copy-start.6
  7.3 60.3 %all-gather.6.cloned.1.call-start = ((), (), s32[]{:S(2)}) async-start(), calls=%async_computation.4 | async-start | bytes 10444800 | tf_op jit(solution)/shard_map/all_gather | solution.py:581
  9.6 101.0 %all-gather.8.cloned.1.call-start = ((), (), s32[]{:S(2)}) async-start(), calls=%async_computation.5 | async-start | bytes 3481600 | tf_op jit(solution)/shard_map/all_gather | solution.py:581
  11.4 158.1 %all-gather.10.cloned.1.call-start = ((), (), s32[]{:S(2)}) async-start(), calls=%async_computation.6 | async-start | bytes 13926400 | tf_op jit(solution)/shard_map/all_gather | solution.py:581
  13.9 222.3 %all-gather.12.cloned.1.call-start = ((), (), s32[]{:S(2)}) async-start(), calls=%async_computation.7 | async-start | bytes 13926400 | tf_op jit(solution)/shard_map/all_gather | solution.py:581
  14.9 789.3 %all-reduce.3.cloned.1.call-start = ((), (), s32[]{:S(2)}) async-start(), calls=%async_computation.12 | async-start | bytes 147456
  739.2 186.0 %reduce-scatter.11.cloned.1.call-start = ((), (), s32[]{:S(2)}) async-start(), calls=%async_computation.11 | async-start | bytes 20889600 | tf_op jit(solution)/shard_map/reduce_scatter | solution.py:584
  754.2 293.5 %reduce-scatter.7.cloned.1.call-start = ((), (), s32[]{:S(2)}) async-start(), calls=%async_computation.9 | async-start | bytes 20889600 | tf_op jit(solution)/shard_map/reduce_scatter | solution.py:584
  769.4 401.0 %reduce-scatter.9.cloned.1.call-start = ((), (), s32[]{:S(2)}) async-start(), calls=%async_computation.10 | async-start | bytes 20889600 | tf_op jit(solution)/shard_map/reduce_scatter | solution.py:584
  784.5 509.0 %reduce-scatter.5.cloned.1.call-start = ((), (), s32[]{:S(2)}) async-start(), calls=%async_computation.8 | async-start | bytes 20889600 | tf_op jit(solution)/shard_map/reduce_scatter | solution.py:584
Sparse Core Ops, SparseCore 0:
  10.9 56.6 all-gather.5
  70.4 32.1 all-gather.7
  105.4 64.0 all-gather.9
  172.1 64.0 all-gather.11
  739.3 64.9 all-reduce.2
  809.0 116.1 reduce-scatter.10
  930.1 117.5 reduce-scatter.6
  1052.7 117.5 reduce-scatter.8
  1175.8 117.5 reduce-scatter.4

commit v2 on v1

--- a/solution.py
+++ b/solution.py
@@ -1,3 +1,4 @@
+import itertools
 import math
 import jax, jax.numpy as jnp
 from jax import lax
@@ -40,8 +41,24 @@
     return jnp.sum(v, axis=-1, keepdims=True)
 
 
+def eights(v):
+    return jnp.sum(v.reshape(v.shape[0] // 8, 8, v.shape[1]), axis=0)
+
+
 def whole(*shape, **kw):
     return pl.BlockSpec(shape, lambda *i: (0,) * len(shape), **kw)
+
+
+def by_cols(rows, cols, at=lambda i: i):
+    return pl.BlockSpec((rows, cols), lambda i: (0, at(i)))
+
+
+def by_rows(rows, cols, at=lambda i: i):
+    return pl.BlockSpec((rows, cols), lambda i: (at(i), 0))
+
+
+def steps(first, wide):
+    return slice(first * wide, (first + 1) * wide)
 
 
 def norm_stats(values):
@@ -74,7 +91,7 @@
     def loop(i, carry):
         rows = values[pl.ds(pl.multiple_of(i * 128, 128), 128), :]
         for c in range(LANES):
-            wide[c, pl.ds((i % 2) * (128 * IMAGES) + i // 2, 128, stride=IMAGES), :] = rows[:, c * 128:(c + 1) * 128]
+            wide[c, pl.ds((i % 2) * (128 * IMAGES) + i // 2, 128, stride=IMAGES), :] = rows[:, steps(c, 128)]
         return carry
     lax.fori_loop(0, 2 * IMAGES, loop, 0)
     put(wide, TAIL, IMAGES, values[pl.ds(TAIL, IMAGES), :])
@@ -86,7 +103,125 @@
 
 def put(wide, r, n, values):
     for c in range(LANES):
-        wide[c, pl.ds(r, n), :] = values[:, c * 128:(c + 1) * 128]
+        wide[c, pl.ds(r, n), :] = values[:, steps(c, 128)]
+
+
+def norm_back(dn, hat, inv, gain):
+    dhat = dn * gain
+    m1 = row_sum(dhat) * (1.0 / WIDTH)
+    m2 = row_sum(dhat * hat) * (1.0 / WIDTH)
+    return inv * (dhat - m1 - hat * m2)
+
+
+SLOTS = 3
+ORDERS = ((2, 1, 0), (1, 0, 2), (0, 2, 1))
+
+
+class Exchange:
+    def __init__(self, rows, cols, cuts, along):
+        self.rows, self.cols = rows, cols
+        self.blocks = (2, 2, 2, 2, rows, cols)
+        self.parts = [((slice(a, b), slice(None)) if along == 0 else (slice(None), slice(a, b))) for a, b in zip(cuts, cuts[1:])]
+        self.shapes = [((b - a, cols) if along == 0 else (rows, b - a)) for a, b in zip(cuts, cuts[1:])]
+
+    def scratch(self):
+        two = (2, 2, 2)
+        out = [pltpu.VMEM((2, *self.blocks), F32), pltpu.VMEM((SLOTS, *two, self.rows, self.cols), F32)]
+        for axes in (2, 1, 0):
+            out += [pltpu.VMEM((SLOTS, *two[:axes], *shape), F32) for shape in self.shapes]
+        return out + [pltpu.SemaphoreType.DMA((10, SLOTS)), pltpu.SemaphoreType.DMA((10, SLOTS))]
+
+    COUNT = 13
+
+    def bind(self, refs):
+        self.local, self.pair = refs[0], refs[1]
+        self.held = [None, refs[2:5], refs[5:8], refs[8:11]]
+        self.send, self.recv = refs[11], refs[12]
+        me = lax.axis_index("fsdp")
+        self.core = me % 2
+        self.at = (me // 8, (me // 4) % 2, (me // 2) % 2)
+        self.other_core = me + 1 - 2 * self.core
+        self.other = [me + step - 2 * step * place for step, place in zip((8, 4, 2), self.at)]
+        return self
+
+    def neighbours(self):
+        return (self.other_core, *self.other)
+
+    def remote(self, src, dst, sem, slot, device):
+        return pltpu.make_async_remote_copy(src_ref=src, dst_ref=dst, send_sem=self.send.at[sem, slot], recv_sem=self.recv.at[sem, slot],
+                                            device_id=(device,), device_id_type=pl.DeviceIdType.MESH)
+
+    def index(self, stage, part, side, rest=None):
+        order = ORDERS[part]
+        left = [a for a in range(3) if a not in order[:stage - 1]]
+        axis = order[stage - 1]
+        where = self.at[axis] if side else 1 - self.at[axis]
+        return tuple(where if a == axis else slice(None) for a in left)
+
+    def copy(self, stage, part, c):
+        slot = c % SLOTS
+        if stage == 0:
+            return self.remote(self.local.at[c % 2, :, :, :, 1 - self.core], self.pair.at[slot], 0, slot, self.other_core)
+        source = self.pair if stage == 1 else self.held[stage - 1][part]
+        tail = self.parts[part] if stage == 1 else ()
+        return self.remote(source.at[(slot, *self.index(stage, part, False), *tail)], self.held[stage][part].at[slot],
+                           3 * stage - 2 + part, slot, self.other[ORDERS[part][stage - 1]])
+
+    def start(self, stage, c):
+        for part in range(1 if stage == 0 else 3):
+            self.copy(stage, part, c).start()
+
+    def wait(self, stage, c):
+        for part in range(1 if stage == 0 else 3):
+            self.copy(stage, part, c).wait()
+
+    def add(self, stage, c):
+        slot = c % SLOTS
+        if stage == 0:
+            for chip in itertools.product(range(2), repeat=3):
+                self.pair[(slot, *chip)] += self.local[(c % 2, *chip, self.core)]
+            return
+        for part in range(3):
+            source = self.pair if stage == 1 else self.held[stage - 1][part]
+            tail = self.parts[part] if stage == 1 else ()
+            for place in itertools.product(range(2), repeat=3 - stage):
+                free = iter(place)
+                kept = tuple(next(free) if isinstance(i, slice) else i for i in self.index(stage, part, True))
+                self.held[stage][part][(slot, *place)] += source[(slot, *kept, *tail)]
+
+    def result(self, c, out_ref):
+        for part in range(3):
+            out_ref[self.parts[part]] = self.held[3][part][c % SLOTS]
+
+
+def meet(exchange):
+    barrier = pltpu.get_barrier_semaphore()
+    for device in exchange.neighbours():
+        pl.semaphore_signal(barrier, inc=1, device_id=(device,), device_id_type=pl.DeviceIdType.MESH)
+    pl.semaphore_wait(barrier, 4)
+
+
+def advance(exchanges, t, chunks, outs):
+    for stage in (3, 2, 1, 0):
+        c = t - 2 - stage
+
+        @pl.when((c >= 0) & (c < chunks))
+        def _():
+            for exchange, out in zip(exchanges, outs):
+                exchange.wait(stage, c)
+                exchange.add(stage, c)
+                if stage < 3:
+                    exchange.start(stage + 1, c)
+                else:
+                    exchange.result(c, out)
+
+    @pl.when((t >= 1) & (t <= chunks))
+    def _():
+        for exchange in exchanges:
+            exchange.start(0, t - 1)
+
+
+DRAIN = 5
 
 
 QKV_N = 768
@@ -115,8 +250,8 @@
         qkv_kernel,
         grid=(3 * WIDTH // QKV_N,),
         in_specs=[whole(TOKENS, WIDTH, pipeline_mode=pl.Buffered(1)), vec, vec,
-                  pl.BlockSpec((WIDTH, QKV_N), lambda i: (0, i)), pl.BlockSpec((1, QKV_N), lambda i: (0, i))],
-        out_specs=[full, full, pl.BlockSpec((TOKENS, QKV_N), lambda i: (0, i))],
+                  by_cols(WIDTH, QKV_N), by_cols(1, QKV_N)],
+        out_specs=[full, full, by_cols(TOKENS, QKV_N)],
         out_shape=[jax.ShapeDtypeStruct((TOKENS, WIDTH), BF), jax.ShapeDtypeStruct((TOKENS, WIDTH), BF),
                    jax.ShapeDtypeStruct((TOKENS, 3 * WIDTH), BF)],
         scratch_shapes=[pltpu.VMEM((LANES, TOKENS, 128), F32)],
@@ -126,7 +261,12 @@
     )(x, gain, bias, w, wb)
 
 
+PARTS = 16
 MLP_F = 256
+UNITS = MLP_F // PARTS
+MLP_STEPS = FFN // MLP_F
+FC_SUM = Exchange(WIDTH // PARTS, MLP_F, (0, 24, 48, 80), 0)
+PROJ_SUM = Exchange(UNITS, WIDTH, (0, 512, 896, 1280), 1)
 CDF_P = 0.33
 CDF_C = (0.1326322871417956, 0.11939570820799192, 0.18103829560051796, -0.08904113226212501,
          0.33075919469138065, -0.22023738432274684, 0.0454530347223348)
@@ -145,11 +285,13 @@
 
 def mlp_kernel(r_hbm, dy_hbm, gain_ref, bias_ref, pb_ref, fc_ref, proj_ref, fcb_ref,
                y_hbm, dr_hbm, dr16_hbm, dfc_ref, dproj_ref, dfcb_ref, small_ref,
-               n2, dy, y_acc, dn_acc, g, du, ua, ub, da, db, sem):
-    step, last = pl.program_id(0), pl.num_programs(0) - 1
+               n2, dy, y_acc, dn_acc, g, du, ua, ub, da, db, sem, *comm):
+    step = pl.program_id(0)
+    by_row, by_col = FC_SUM.bind(comm[:Exchange.COUNT]), PROJ_SUM.bind(comm[Exchange.COUNT:])
 
     @pl.when(step == 0)
     def _():
+        meet(by_row)
         cp = pltpu.make_async_copy(dy_hbm, n2, sem)
         cp.start()
         cp.wait()
@@ -162,116 +304,127 @@
 
         def place(r, n, values):
             dy[pl.ds(r, n), :] = values.astype(BF)
-        to_image_order(dn_acc, place)
+        to_image_order(dn_acc, place, ROWS)
         cp.wait()
-        gain, bias = gain_ref[...], bias_ref[...]
+        gain, bias, pb = gain_ref[...], bias_ref[...], pb_ref[...]
 
         def norm(r, n):
-            hat, _ = norm_stats(n2[pl.ds(r, n), :].astype(F32))
+            wide_r = n2[pl.ds(r, n), :].astype(F32)
+            hat, _ = norm_stats(wide_r)
             n2[pl.ds(r, n), :] = (hat * gain + bias).astype(BF)
-            y_acc[pl.ds(r, n), :] = jnp.zeros((n, WIDTH), F32)
+            y_acc[pl.ds(r, n), :] = wide_r + pb
             put(dn_acc, r, n, jnp.zeros((n, WIDTH), F32))
         row_tiles(norm, ROWS)
-
-    fcb = fcb_ref[...]
-    bias_sum = jnp.zeros((8, MLP_F), F32)
-    tiles = [(b * MAIN, MAIN) for b in range(IMAGES - 1)] + [((IMAGES - 1) * MAIN, MAIN + IMAGES)]
-    pairs = ((ua, da), (ub, db))
-
-    def products(k):
-        r, n = tiles[k]
-        u_s, d_s = pairs[k % 2]
-        u_s[0:n, :] = dot(n2[r:r + n, :], fc_ref[...])
-        d_s[0:n, :] = dot_nt(dy[r:r + n, :], proj_ref[...])
-
-    def pointwise(k, total):
-        r, n = tiles[k]
-        u_s, d_s = pairs[k % 2]
-        value, slope = gelu_pair(u_s[0:n, :] + fcb)
-        g[r:r + n, :] = value.astype(BF)
-        grad = d_s[0:n, :] * slope
-        du[r:r + n, :] = grad.astype(BF)
-        return total + jnp.sum(grad.reshape(n // 8, 8, MLP_F), axis=0)
-
-    products(0)
-    for k in range(1, IMAGES):
-        products(k)
-        bias_sum = pointwise(k - 1, bias_sum)
-    bias_sum = pointwise(IMAGES - 1, bias_sum)
-    dfcb_ref[...] = col_sum(bias_sum)
-    y_acc[...] += dot(g[...], proj_ref[...])
-    for c in range(LANES // 2):
-        part = dot_nt(du[...], fc_ref[c * 256:(c + 1) * 256, :])
-        dn_acc[2 * c] += part[:, :128]
-        dn_acc[2 * c + 1] += part[:, 128:]
-    dproj_ref[...] = dot_tn(g[...], dy[...])
-    dfc_ref[...] = dot_tn(n2[...], du[...])
-
-    @pl.when(step == last)
+        small_ref[...] = jnp.zeros_like(small_ref)
+
+    advance((by_row, by_col), step, MLP_STEPS, (dfc_ref, dproj_ref))
+
+    @pl.when(step < MLP_STEPS)
+    def _():
+        fcb = fcb_ref[...]
+        fc, proj = fc_ref[...], proj_ref[...].reshape(MLP_F, WIDTH)
+        bias_sum = jnp.zeros((8, MLP_F), F32)
+        tiles = [(b * MAIN, MAIN) for b in range(IMAGES - 1)] + [((IMAGES - 1) * MAIN, MAIN + IMAGES)]
+        pairs = ((ua, da), (ub, db))
+
+        def products(k):
+            r, n = tiles[k]
+            u_s, d_s = pairs[k % 2]
+            u_s[0:n, :] = dot(n2[r:r + n, :], fc)
+            d_s[0:n, :] = dot_nt(dy[r:r + n, :], proj)
+
+        def pointwise(k, total):
+            r, n = tiles[k]
+            u_s, d_s = pairs[k % 2]
+            value, slope = gelu_pair(u_s[0:n, :] + fcb)
+            g[r:r + n, :] = value.astype(BF)
+            grad = d_s[0:n, :] * slope
+            du[r:r + n, :] = grad.astype(BF)
+            return total + eights(grad)
+
+        products(0)
+        for k in range(1, IMAGES):
+            products(k)
+            bias_sum = pointwise(k - 1, bias_sum)
+        bias_sum = pointwise(IMAGES - 1, bias_sum)
+        dfcb_ref[...] = col_sum(bias_sum)
+        y_acc[...] += dot(g[...], proj)
+        for c in range(LANES // 2):
+            part = dot_nt(du[...], fc_ref[steps(c, 256), :])
+            dn_acc[2 * c] += part[:, :128]
+            dn_acc[2 * c + 1] += part[:, 128:]
+        by_col.local[step % 2] = dot_tn(g[...], dy[...]).reshape(by_col.blocks)
+        by_row.local[step % 2] = dot_tn(n2[...], du[...]).reshape(by_row.blocks)
+
+    out_copies = [pltpu.make_async_copy(dn_acc, dr_hbm, sem), pltpu.make_async_copy(n2, dr16_hbm, sem)]
+    y_copy = pltpu.make_async_copy(dy, y_hbm, sem)
+
+    @pl.when(step == MLP_STEPS)
     def _():
         cp = pltpu.make_async_copy(r_hbm, n2, sem)
         cp.start()
         cp.wait()
-        gain, pb = gain_ref[...], pb_ref[...]
-        small_ref[...] = jnp.zeros_like(small_ref)
-
-        def rows_sum(v):
-            return jnp.sum(v.reshape(v.shape[0] // 8, 8, WIDTH), axis=0)
+        gain = gain_ref[...]
 
         def back(r, n):
-            wide_r = n2[pl.ds(r, n), :].astype(F32)
-            hat, inv = norm_stats(wide_r)
+            hat, inv = norm_stats(n2[pl.ds(r, n), :].astype(F32))
             dn = joined(dn_acc, r, n)
             wide_dy = dy[pl.ds(r, n), :].astype(F32)
-            small_ref[0:8, :] += rows_sum(dn * hat)
-            small_ref[8:16, :] += rows_sum(dn)
-            small_ref[16:24, :] += rows_sum(wide_dy)
-            dhat = dn * gain
-            m1 = row_sum(dhat) * (1.0 / WIDTH)
-            m2 = row_sum(dhat * hat) * (1.0 / WIDTH)
-            dr = wide_dy + inv * (dhat - m1 - hat * m2)
+            dr = wide_dy + norm_back(dn, hat, inv, gain)
             put(dn_acc, r, n, dr)
-            small_ref[24:32, :] += rows_sum(dr)
-            y_acc[pl.ds(r, n), :] += wide_r + pb
             n2[pl.ds(r, n), :] = dr.astype(BF)
+            for i, v in enumerate((dn * hat, dn, wide_dy, dr)):
+                small_ref[steps(i, 8), :] += eights(v)
         row_tiles(back, ROWS)
-        copies = [pltpu.make_async_copy(dn_acc, dr_hbm, sem), pltpu.make_async_copy(n2, dr16_hbm, sem)]
-        for cp in copies:
+        for cp in out_copies:
             cp.start()
-        for cp in copies:
+
+    @pl.when(step == MLP_STEPS + 1)
+    def _():
+        for cp in out_copies:
             cp.wait()
         from_image_order(y_acc, dn_acc)
 
+    @pl.when(step == MLP_STEPS + 2)
+    def _():
         def narrow(r, n):
             dy[pl.ds(r, n), :] = joined(dn_acc, r, n).astype(BF)
         row_tiles(narrow)
-        cp = pltpu.make_async_copy(dy, y_hbm, sem)
-        cp.start()
-        cp.wait()
+        y_copy.start()
+
+    @pl.when(step == MLP_STEPS + 3)
+    def _():
+        y_copy.wait()
 
 
 def mlp_call(r, dy, gain, bias, pb, fc, proj, fcb):
     hbm = pl.BlockSpec(memory_space=pl.ANY)
     vec = whole(1, WIDTH)
-    n = fc.shape[1]
+    now = lambda i: jnp.minimum(i, MLP_STEPS - 1)
+    done = lambda i: jnp.maximum(i - DRAIN, 0)
     return pl.pallas_call(
         mlp_kernel,
-        grid=(n // MLP_F,),
-        in_specs=[hbm, hbm, vec, vec, vec, pl.BlockSpec((WIDTH, MLP_F), lambda i: (0, i)),
-                  pl.BlockSpec((MLP_F, WIDTH), lambda i: (i, 0)), pl.BlockSpec((1, MLP_F), lambda i: (0, i))],
-        out_specs=[hbm, hbm, hbm, pl.BlockSpec((WIDTH, MLP_F), lambda i: (0, i)), pl.BlockSpec((MLP_F, WIDTH), lambda i: (i, 0)),
-                   pl.BlockSpec((1, MLP_F), lambda i: (0, i)), whole(32, WIDTH)],
+        grid=(MLP_STEPS + DRAIN,),
+        in_specs=[hbm, hbm, vec, vec, vec, by_cols(WIDTH, MLP_F, now),
+                  pl.BlockSpec((PARTS, None, UNITS, WIDTH), lambda i: (0, now(i), 0, 0)),
+                  by_cols(1, MLP_F, now)],
+        out_specs=[hbm, hbm, hbm, by_cols(WIDTH // PARTS, MLP_F, done),
+                   by_rows(UNITS, WIDTH, done),
+                   by_cols(1, MLP_F, now), whole(32, WIDTH)],
         out_shape=[jax.ShapeDtypeStruct((TOKENS, WIDTH), BF), jax.ShapeDtypeStruct((LANES, TOKENS, 128), F32),
-                   jax.ShapeDtypeStruct((TOKENS, WIDTH), BF), jax.ShapeDtypeStruct((WIDTH, n), F32), jax.ShapeDtypeStruct((n, WIDTH), F32),
-                   jax.ShapeDtypeStruct((1, n), F32), jax.ShapeDtypeStruct((32, WIDTH), F32)],
+                   jax.ShapeDtypeStruct((TOKENS, WIDTH), BF), jax.ShapeDtypeStruct((WIDTH // PARTS, FFN), F32),
+                   jax.ShapeDtypeStruct((FFN // PARTS, WIDTH), F32),
+                   jax.ShapeDtypeStruct((1, FFN), F32), jax.ShapeDtypeStruct((32, WIDTH), F32)],
         scratch_shapes=[pltpu.VMEM((TOKENS, WIDTH), BF), pltpu.VMEM((TOKENS, WIDTH), BF),
                         pltpu.VMEM((TOKENS, WIDTH), F32), pltpu.VMEM((LANES, TOKENS, 128), F32),
                         pltpu.VMEM((TOKENS, MLP_F), BF), pltpu.VMEM((TOKENS, MLP_F), BF)]
-                       + [pltpu.VMEM((MAIN + IMAGES, MLP_F), F32)] * 4 + [pltpu.SemaphoreType.DMA],
-        compiler_params=pltpu.CompilerParams(dimension_semantics=("arbitrary",), vmem_limit_bytes=VMEM_MAX),
-        cost_estimate=pl.CostEstimate(flops=12 * TOKENS * WIDTH * n, bytes_accessed=150_000_000, transcendentals=TOKENS * n),
+                       + [pltpu.VMEM((MAIN + IMAGES, MLP_F), F32)] * 4 + [pltpu.SemaphoreType.DMA]
+                       + FC_SUM.scratch() + PROJ_SUM.scratch(),
+        compiler_params=pltpu.CompilerParams(dimension_semantics=("arbitrary",), vmem_limit_bytes=VMEM_MAX, collective_id=0,
+                                             has_side_effects=True),
+        cost_estimate=pl.CostEstimate(flops=12 * TOKENS * WIDTH * FFN, bytes_accessed=150_000_000, transcendentals=TOKENS * FFN),
         name="mlp",
-    )(r, dy, gain, bias, pb, fc, proj, fcb)
+    )(r, dy, gain, bias, pb, fc, proj.reshape(PARTS, MLP_STEPS, UNITS, WIDTH), fcb)
 
 
 SCALE = HEAD ** -0.5
@@ -313,10 +466,8 @@
         tails[...] = qkvt_ref[...].astype(F32)
 
     heads = head_rows()
-    q_t = heads * tails[pl.ds(b, 1), 0:WIDTH]
-    k_t = heads * tails[pl.ds(b, 1), WIDTH:2 * WIDTH]
-    v_t = heads * tails[pl.ds(b, 1), 2 * WIDTH:3 * WIDTH]
-    q, k, v = qkv_ref[:, 0:WIDTH], qkv_ref[:, WIDTH:2 * WIDTH], qkv_ref[:, 2 * WIDTH:3 * WIDTH]
+    q_t, k_t, v_t = (heads * tails[pl.ds(b, 1), steps(i, WIDTH)] for i in range(3))
+    q, k, v = (qkv_ref[:, steps(i, WIDTH)] for i in range(3))
 
     p, p_self = tail_softmax(dot_nt(q_t.astype(BF), k), row_sum(q_t * k_t))
     mixed = dot(p.astype(BF), v) * heads + p_self.astype(BF).astype(F32) * v_t
@@ -335,7 +486,7 @@
         max_ref[0, h:h + 1, :] = top
         inv_ref[0, h:h + 1, :] = inv
         ptail[h:h + 1, :] = e_tail * inv
-        o_t[HEAD * h:HEAD * h + HEAD, :] = dot(v_turned[HEAD * h:HEAD * h + HEAD, :], (e * inv).astype(BF))
+        o_t[steps(h, HEAD), :] = dot(v_turned[steps(h, HEAD), :], (e * inv).astype(BF))
 
     @pl.when(b >= 2)
     def _():
@@ -371,8 +522,8 @@
 
 def attn_call(qkv, xim, w, wb):
     hbm = pl.BlockSpec(memory_space=pl.ANY)
-    main = lambda n: pl.BlockSpec((MAIN, n), lambda i: (i, 0))
-    tail = lambda n: pl.BlockSpec((IMAGES, n), lambda i: (TAIL // IMAGES, 0))
+    main = lambda n: by_rows(MAIN, n)
+    tail = lambda n: by_rows(IMAGES, n, lambda i: TAIL // IMAGES)
     stat = pl.BlockSpec((1, HEADS, MAIN), lambda i: (i, 0, 0))
     return pl.pallas_call(
         attn_kernel,
@@ -404,8 +555,8 @@
     return pl.pallas_call(
         outb_kernel,
         grid=(WIDTH // n,),
-        in_specs=[full, full, pl.BlockSpec((n, WIDTH), lambda i: (i, 0))],
-        out_specs=[pl.BlockSpec((TOKENS, n), lambda i: (0, i)), pl.BlockSpec((WIDTH, n), lambda i: (0, i))],
+        in_specs=[full, full, by_rows(n, WIDTH)],
+        out_specs=[by_cols(TOKENS, n), by_cols(WIDTH, n)],
         out_shape=[jax.ShapeDtypeStruct((TOKENS, WIDTH), BF), jax.ShapeDtypeStruct((WIDTH, WIDTH), F32)],
         compiler_params=pltpu.CompilerParams(dimension_semantics=("arbitrary",), vmem_limit_bytes=VMEM_MAX),
         cost_estimate=pl.CostEstimate(flops=4 * TOKENS * WIDTH * WIDTH, bytes_accessed=30_000_000, transcendentals=0),
@@ -425,11 +576,9 @@
         dwb_ref[...] = jnp.zeros_like(dwb_ref)
 
     heads = head_rows()
-    q_t = heads * tails[pl.ds(b, 1), 0:WIDTH]
-    k_t = heads * tails[pl.ds(b, 1), WIDTH:2 * WIDTH]
-    v_t = heads * tails[pl.ds(b, 1), 2 * WIDTH:3 * WIDTH]
+    q_t, k_t, v_t = (heads * tails[pl.ds(b, 1), steps(i, WIDTH)] for i in range(3))
     do_t = heads * do_tails[pl.ds(b, 1), :]
-    q, k, v = qkv_ref[:, 0:WIDTH], qkv_ref[:, WIDTH:2 * WIDTH], qkv_ref[:, 2 * WIDTH:3 * WIDTH]
+    q, k, v = (qkv_ref[:, steps(i, WIDTH)] for i in range(3))
     do = do_ref[...]
     q_t16, k_t16, v_t16, do_t16 = (z.astype(BF) for z in (q_t, k_t, v_t, do_t))
 
@@ -462,7 +611,7 @@
         ds = (p * (dp - inner) * SCALE).astype(BF)
         dv[:, here] += dot(p.astype(BF), do_h)
         dk[:, here] += dot(ds, q_h)
-        dq_t[HEAD * h:HEAD * h + HEAD, :] = dot(k_turned[HEAD * h:HEAD * h + HEAD, :], ds)
+        dq_t[steps(h, HEAD), :] = dot(k_turned[steps(h, HEAD), :], ds)
         ds_tail[h:h + 1, :] = p_tail[h:h + 1, :] * (dp_tail[h:h + 1, :] - inner) * SCALE
 
     ds_tail16 = ds_tail[...].astype(BF)
@@ -475,7 +624,7 @@
 
     grad = dq_t[...].T + dot_tn(ds_tail16, k_t16)
     for n, (main, tail) in enumerate(((grad, grad_q), (dk[...], grad_k), (dv[...], grad_v))):
-        here = slice(n * WIDTH, (n + 1) * WIDTH)
+        here = steps(n, WIDTH)
         buf[slot, :, here] = main.astype(BF)
         grad_tails[pl.ds(b, 1), here] = tail
         dwb_ref[:, here] += col_sum(main) + tail
@@ -493,8 +642,8 @@
 
 def attn_back_call(qkv, do, top, inv):
     hbm = pl.BlockSpec(memory_space=pl.ANY)
-    main = lambda n: pl.BlockSpec((MAIN, n), lambda i: (i, 0))
-    tail = lambda n: pl.BlockSpec((IMAGES, n), lambda i: (TAIL // IMAGES, 0))
+    main = lambda n: by_rows(MAIN, n)
+    tail = lambda n: by_rows(IMAGES, n, lambda i: TAIL // IMAGES)
     stat = pl.BlockSpec((1, HEADS, MAIN), lambda i: (i, 0, 0))
     return pl.pallas_call(
         attn_back_kernel,
@@ -534,12 +683,9 @@
         def back(r, n):
             hat, inv = norm_stats(xd[pl.ds(r, n), :].astype(F32))
             dn = acc[pl.ds(r, n), :]
-            small_ref[0:8, :] += jnp.sum((dn * hat).reshape(n // 8, 8, WIDTH), axis=0)
-            small_ref[8:16, :] += jnp.sum(dn.reshape(n // 8, 8, WIDTH), axis=0)
-            dhat = dn * gain
-            m1 = row_sum(dhat) * (1.0 / WIDTH)
-            m2 = row_sum(dhat * hat) * (1.0 / WIDTH)
-            acc[pl.ds(r, n), :] = joined(dr, r, n) + inv * (dhat - m1 - hat * m2)
+            for i, v in enumerate((dn * hat, dn)):
+                small_ref[steps(i, 8), :] += eights(v)
+            acc[pl.ds(r, n), :] = joined(dr, r, n) + norm_back(dn, hat, inv, gain)
         row_tiles(back, ROWS)
         from_image_order(acc, dr)
 
@@ -558,8 +704,8 @@
         grid=(3 * WIDTH // QKV_N,),
         in_specs=[hbm, hbm, whole(1, WIDTH),
                   whole(TOKENS, WIDTH, pipeline_mode=pl.Buffered(1)),
-                  pl.BlockSpec((TOKENS, QKV_N), lambda i: (0, i)), pl.BlockSpec((WIDTH, QKV_N), lambda i: (0, i))],
-        out_specs=[hbm, pl.BlockSpec((WIDTH, QKV_N), lambda i: (0, i)), whole(16, WIDTH)],
+                  by_cols(TOKENS, QKV_N), by_cols(WIDTH, QKV_N)],
+        out_specs=[hbm, by_cols(WIDTH, QKV_N), whole(16, WIDTH)],
         out_shape=[jax.ShapeDtypeStruct((TOKENS, WIDTH), BF), jax.ShapeDtypeStruct((WIDTH, 3 * WIDTH), F32),
                    jax.ShapeDtypeStruct((16, WIDTH), F32)],
         scratch_shapes=[pltpu.VMEM((TOKENS, WIDTH), F32), pltpu.VMEM((LANES, TOKENS, 128), F32), pltpu.VMEM((TOKENS, WIDTH), BF),
@@ -570,8 +716,17 @@
     )(xim, dr, gain, h, dqkv, w)
 
 
-PARTS = 16
 VECTORS = (80, 80, 240, 80, 80, 80, 320, 80)
+
+
+def to_steps(v):
+    rows = v.shape[0]
+    return v.reshape(rows, PARTS, MLP_STEPS, UNITS).swapaxes(1, 2).reshape(rows, FFN)
+
+
+def from_steps(v):
+    rows = v.shape[0]
+    return v.reshape(rows, MLP_STEPS, PARTS, UNITS).swapaxes(1, 2).reshape(rows, FFN)
 
 
 def solution(mesh):
@@ -585,7 +740,7 @@
 
     def device_step(resid_in, grad_out, ln1_gain, ln1_bias, qkv_weight, qkv_bias, out_weight, out_bias,
                     ln2_gain, ln2_bias, fc_weight, fc_bias, proj_weight, proj_bias):
-        wq, wo, wf, wp = (gather(w) for w in (qkv_weight, out_weight, fc_weight, proj_weight))
+        wq, wo, wf, wp = (gather(w) for w in (qkv_weight, out_weight, to_steps(fc_weight.astype(BF)), proj_weight))
         packed = jnp.concatenate([ln1_gain, ln1_bias, qkv_bias, out_bias, ln2_gain, ln2_bias, fc_bias, proj_bias])
         packed = gather(packed[None]).astype(F32)
         cuts = [sum(VECTORS[:i]) for i in range(len(VECTORS) + 1)]
@@ -595,21 +750,18 @@
         dy = grad_out.transpose(1, 0, 2).reshape(TOKENS, WIDTH)
         xim, h, qkv = qkv_call(x, g1, b1, wq, bq)
         o, r, top, inv = attn_call(qkv, xim, wo, bo)
-        y, dr, dr16, dwf, dwp, dbf, small2 = mlp_call(r, dy, g2, b2, bp, wf, wp, bf)
+        y, dr, dr16, dwf, dwp, dbf, small2 = mlp_call(r, dy, g2, b2, bp, wf, wp, to_steps(bf))
         do, dwo = outb_call(dr16, o, wo)
         dqkv, dbq = attn_back_call(qkv, do, top, inv)
         dx, dwq, small1 = qkvb_call(xim, dr, g1, h, dqkv, wq)
 
-        turned = dwp.reshape(PARTS, 4, 80, WIDTH).transpose(0, 2, 1, 3).reshape(WIDTH, 4 * WIDTH)
-        s1 = scatter(dwf[:, :3 * WIDTH])
-        s2 = scatter(jnp.concatenate([dwf[:, 3 * WIDTH:], turned[:, :2 * WIDTH]], axis=1))
-        s3 = scatter(jnp.concatenate([turned[:, 2 * WIDTH:], dwo], axis=1))
-        dwf = jnp.concatenate([s1, s2[:, :WIDTH]], axis=1)
-        dwp = jnp.concatenate([s2[:, WIDTH:], s3[:, :2 * WIDTH]], axis=1).reshape(80, 4, WIDTH).transpose(1, 0, 2).reshape(320, WIDTH)
-        dwo = s3[:, 2 * WIDTH:]
+        dwf, dbf = from_steps(dwf), from_steps(dbf)
+        dwo = scatter(dwo)
         dwq = scatter(dwq)
-        rows = lambda a, i: jnp.sum(a[8 * i:8 * i + 8], axis=0)
-        vectors = (rows(small1, 0), rows(small1, 1), dbq[0], rows(small2, 3), rows(small2, 0), rows(small2, 1), dbf[0], rows(small2, 2))
+        fold = lambda a: list(jnp.sum(a.reshape(-1, 8, WIDTH), axis=1))
+        small1 = fold(small1)
+        *ln2_sums, proj_bias_sum, out_bias_sum = fold(small2)
+        vectors = (*small1, dbq, out_bias_sum, *ln2_sums, dbf, proj_bias_sum)
         packed = jnp.concatenate([v.reshape(PARTS, -1) for v in vectors], axis=1)
         packed = scatter(packed)[0]
         dg1, db1, dbq, dbo, dg2, db2, dbf, dbp = (packed[a:b] for a, b in zip(cuts, cuts[1:]))

time: 1310 us -> 970 us (0.74)
  waiting for transfers between devices: 604 us -> 359 us
  local copies, waits for them, and re-layouts: 111 us -> 28.9 us
  other arithmetic: 44 us -> 10.4 us
  Pallas kernels: 511 us -> 534 us
    reduce_scatter x4 -> x2, waiting for transfers between devices: 475 us -> 193 us  [scatter(): return lax.psum_scatter(grad, 'fsdp', scatter_dimension=0, tiled=True)]
    slice x7 -> x0, local copies, waits for them, and re-layouts: 45 us -> none  [the longest x1 18.8 us: device_step(): turned[:, :2 * WIDTH]]
    unnamed x10 -> x8, waiting for transfers between devices: 19.8 us -> 58.6 us
    concatenate x4 -> x0, other arithmetic: 32.7 us -> none  [the longest x1 15.1 us: device_step(): s3 = scatter(jnp.concatenate([turned[:, 2 * WIDTH:], dwo], axis=1))]
    transpose x2 -> x4, local copies, waits for them, and re-layouts: 31.6 us -> 2.22 us  [the longest x2 1.83 us: from_steps(): v.reshape(rows, MLP_STEPS, PARTS, UNITS).swapaxes(1, 2).reshape(rows, FFN)]
    pallas_call x2, Pallas kernels: 279 us -> 301 us  [the longest x1 280 us: mlp_call(): pl.pallas_call(mlp_kernel, grid=(MLP_STEPS + DRAIN,), in_specs=[hbm, hbm,...]
  transfers between devices with their start and end apart: 9 -> 7, of which waited for: 8 -> 6; matrix products, arithmetic and copies ran while one was open for 5% -> 3% of each run, Pallas kernels for 7% -> 9%
where the time goes in v2:
time: 970 us; the launch traced here: 962 us
  Pallas kernels  534 us (55%)
  waiting for transfers between devices  359 us (37%)
  local copies, waits for them, and re-layouts  28.9 us (3%)
  blocking collectives  15 us (2%)
  between operations  14.9 us (2%)
  other arithmetic  10.4 us (1%)
    pallas_call x1, Pallas kernels, mlp_call(): pl.pallas_call(mlp_kernel, grid=(MLP_STEPS + DRAIN,), in_specs=[hbm, hbm,...  280 us
    reduce_scatter x2, waiting for transfers between devices, scatter(): return lax.psum_scatter(grad, 'fsdp', scatter_dimension=0, tiled=True)  193 us
    all_gather x4, waiting for transfers between devices, gather(): return lax.all_gather(shard.astype(BF), 'fsdp', axis=0, tiled=True)  106 us
    pallas_call x1, Pallas kernels, qkvb_call(): pl.pallas_call(qkvb_kernel, grid=(3 * WIDTH // QKV_N,), in_specs=[hbm, hb...  77.6 us
    pallas_call x1, Pallas kernels, attn_back_call(): pl.pallas_call(attn_back_kernel, grid=(IMAGES,), in_specs=[main(3 * WIDTH...  63.7 us
    unnamed x8, waiting for transfers between devices  58.6 us
    pallas_call x1, Pallas kernels, attn_call(): pl.pallas_call(attn_kernel, grid=(IMAGES,), in_specs=[main(3 * WIDTH), ta...  47.8 us
    pallas_call x1, Pallas kernels, qkv_call(): pl.pallas_call(qkv_kernel, grid=(3 * WIDTH // QKV_N,), in_specs=[whole(TO...  43.4 us
  transfers between devices with their start and end apart: 7, of which 6 were waited for; matrix products, arithmetic and copies ran while one was open for 3% of the time, Pallas kernels for 9%

profile of v2, /device:TPU:0, one launch (start us, length us, event | category | flops | bytes accessed | tf_op | source)
XLA Modules:
  0.0 961.7 jit_solution(9310372386595935426)
XLA Ops:
  7.2 0.0 all-gather.6.cloned.1.call-start
  7.2 2.2 convert_element_type.25
  9.4 0.0 all-gather.8.cloned.1.call-start
  9.5 1.7 convert_element_type.26
  11.3 0.0 all-gather.10.cloned.1.call-start
  11.4 1.8 copy.40
  13.2 0.4 copy.41
  13.5 1.3 copy.42
  14.9 0.0 all-gather.12.cloned.1.call-start
  15.0 2.4 convert_element_type.28
  17.4 0.0 all-reduce.3.cloned.1.call-start
  17.6 0.1 concatenate.38
  17.7 15.0 %all-gather = bf16[16,1,1040]{2,1,0:T(2,128)(2,1)S(1)} all-gather(bf16[1,1,1040]{2,1,0:T(2,128)(2,1)S(1)} %bitcast.68), channel_id=1, replica_groups=mesh['fsdp'=16] {'fsdp'}, dimensions={0}, use_global_device_ids=true | all-gather | bytes 35360 | tf_op jit(solution)/shard_map/all_gather | solution.py:736
  32.7 0.1 slice.98
  32.7 0.1 fusion
  32.8 0.7 reshape.216.gain_ref
  33.5 0.7 reshape.217.bias_ref
  34.2 0.7 reshape.218.wb_ref
  34.9 0.7 reshape.219.wb_ref
  35.6 0.7 reshape.221.gain_ref
  36.2 0.7 reshape.222.bias_ref
  36.9 0.7 reshape.223.pb_ref
  37.6 0.1 reshape_reshape.6
  37.7 0.7 reshape.227.fcb_ref
  38.4 28.9 %all-gather.6.cloned.1.call-done.w_ref = bf16[1280,3840]{1,0:T(8,128)(2,1)} async-done(((bf16[80,3840]{1,0:T(8,128)(2,1)}), bf16[1280,3840]{1,0:T(8,128)(2,1)}) %all-gather.6.cloned.1.call-update) | async-done | bytes 9830416 | tf_op jit(solution)/shard_map/all_gather | solution.py:736
  67.4 43.4 %qkv.1 = (bf16[2056,1280]{1,0:T(8,128)(2,1)}, bf16[2056,1280]{1,0:T(8,128)(2,1)}, bf16[2056,3840]{1,0:T(8,128)(2,1)}) custom-call(bf16[2056,1280]{1,0:T(8,128)(2,1)} %bitcast.71, f32[1,1280]{1,0:T(1,128)} %reshape.216.gain_ref, f32[1,1280]{1,0:T(1,128)} %reshape.217.bias_ref, bf16[1280,3840]{1,0:T(8,128)(2,1)} %all-gather.6.cloned.1.call-done.w_ref, ...), custom_call_target="tpu_custom_call" | custom-call | flops 20211302400 | bytes 60000000 | tf_op jit(solution)/shard_map/qkv/pallas_call | solution.py:249
  110.7 47.8 %attn.1 = (bf16[2056,1280]{1,0:T(8,128)(2,1)}, bf16[2056,1280]{1,0:T(8,128)(2,1)}, f32[8,16,256]{2,1,0:T(8,128)}, f32[8,16,256]{2,1,0:T(8,128)}) custom-call(bf16[2056,3840]{1,0:T(8,128)(2,1)} %get-tuple-element.35.qkv_ref.qkvt_ref, bf16[2056,3840]{1,0:T(8,128)(2,1)} %get-tuple-element.35.qkv_ref.qkvt_ref, ...), custom_call_target="tpu_custom_call" | custom-call | flops 30000001024 | bytes 50000000 | tf_op jit(solution)/shard_map/attn/pallas_call | solution.py:528
  158.5 10.7 %all-gather.10.cloned.1.call-done.fc_ref = bf16[1280,5120]{1,0:T(8,128)(2,1)} async-done(((bf16[80,5120]{1,0:T(8,128)(2,1)}), bf16[1280,5120]{1,0:T(8,128)(2,1)}) %all-gather.10.cloned.1.call-update) | async-done | bytes 13107216 | tf_op jit(solution)/shard_map/all_gather | solution.py:736
  169.3 66.8 %all-gather.12.cloned.1.call-done = bf16[5120,1280]{1,0:T(8,128)(2,1)} async-done(((bf16[320,1280]{1,0:T(8,128)(2,1)}), bf16[5120,1280]{1,0:T(8,128)(2,1)}) %all-gather.12.cloned.1.call-update) | async-done | bytes 13107216 | tf_op jit(solution)/shard_map/all_gather | solution.py:736
  236.1 279.8 %mlp.1 = (bf16[2056,1280]{1,0:T(8,128)(2,1)}, f32[10,2056,128]{2,1,0:T(8,128)}, bf16[2056,1280]{1,0:T(8,128)(2,1)}, f32[80,5120]{1,0:T(8,128)}, f32[320,1280]{1,...) custom-call(bf16[2056,1280]{1,0:T(8,128)(2,1)} %get-tuple-element.37.r_hbm, bf16[2056,1280]{1,0:T(8,128)(2,1)} %bitcast.72, ...), custom_call_target="tpu_custom_call" | custom-call | flops 161690419200 | bytes 150000000 | tf_op jit(solution)/shard_map/mlp/pallas_call | solution.py:405
  515.9 21.5 %outb.1 = (bf16[2056,1280]{1,0:T(8,128)(2,1)}, f32[1280,1280]{1,0:T(8,128)}) custom-call(bf16[2056,1280]{1,0:T(8,128)(2,1)} %get-tuple-element.41.dr_ref, bf16[2056,1280]{1,0:T(8,128)(2,1)} %get-tuple-element.42.o_ref, bf16[1280,1280]{1,0:T(8,128)(2,1)} %all-gather.8.cloned.1.call-done.w_ref), custom_call_target="tpu_custom_call" | custom-call | flops 13474201600 | bytes 30000000 | tf_op jit(solution)/shard_map/outb/pallas_call | solution.py:555
  537.4 63.7 %attn_back.1 = (bf16[2056,3840]{1,0:T(8,128)(2,1)}, f32[1,3840]{1,0:T(1,128)}) custom-call(bf16[2056,3840]{1,0:T(8,128)(2,1)} %get-tuple-element.35.qkv_ref.qkvt_ref, bf16[2056,3840]{1,0:T(8,128)(2,1)} %get-tuple-element.35.qkv_ref.qkvt_ref, bf16[2056,1280]{1,0:T(8,128)(2,1)} %get-tuple-element.43.do_ref.dot_ref, ...), custom_call_target="tpu_custom_call" | custom-call | flops 60000002048 | bytes 50000000 | tf_op jit(solution)/shard_map/attn_back/pallas_call | solution.py:648
  601.1 77.6 %qkvb.1 = (bf16[2056,1280]{1,0:T(8,128)(2,1)}, f32[1280,3840]{1,0:T(8,128)}, f32[16,1280]{1,0:T(8,128)}) custom-call(bf16[2056,1280]{1,0:T(8,128)(2,1)} %get-tuple-element.36.x_ref.xt_ref.xim_hbm, f32[10,2056,128]{2,1,0:T(8,128)} %get-tuple-element.39.dr_hbm, f32[1,1280]{1,0:T(1,128)} %reshape.216.gain_ref, bf16[2056,1280]{1,0:T(8,128)(2,1)} %get-tuple-element.40.h_ref, ...), custom_call_target="tpu_custom_call" | custom-call | flops 40422604800 | bytes 80000000 | tf_op jit(solution)/shard_map/qkvb/pallas_call | solution.py:702
  678.7 0.9 bitcast_reduce_fusion.1
  679.6 0.1 reshape_unstack.18
  679.7 0.1 reshape_unstack.19
  679.8 0.8 reduce.2
  680.6 0.1 reshape.231
  680.6 1.0 bitcast_reduce_fusion
  681.6 0.1 slice_reduce_fusion
  681.7 0.1 reshape_unstack.20
  681.7 0.1 reshape_unstack.21
  681.8 0.1 reshape_unstack.22
  681.9 0.1 reshape_unstack.23
  682.0 0.5 broadcast.11
  682.5 1.4 reduce.18
  683.9 0.1 reshape.233
  684.0 0.1 copy.44
  684.1 0.1 reshape_reshape.7
  684.2 0.7 concatenate.39
  684.9 0.0 reduce-scatter.5.cloned.1.call-start
  685.0 0.5 reduce-scatter.5.cloned.1.call-update
  685.6 0.7 reduce-scatter.3.cloned.1.call-update
  686.3 2.0 copy.45
  688.3 1.8 copy.46
  690.0 3.0 copy.47
  693.0 57.3 %all-reduce.3.cloned.1.call-done = f32[16,1040]{1,0:T(8,128)} async-done(((f32[16,1040]{1,0:T(8,128)}), f32[16,1040]{1,0:T(8,128)}) %all-reduce.3.cloned.1.call-update) | async-done | bytes 66576
  750.4 1.3 dynamic-slice.3
  751.7 1.4 dynamic-slice_reduce_fusion
  753.1 1.4 dynamic-slice_bitcast_fusion
  754.5 71.4 %reduce-scatter.5.cloned.1.call-done = f32[80,1280]{1,0:T(8,128)} async-done(((f32[1280,1280]{1,0:T(8,128)}), f32[80,1280]{1,0:T(8,128)}) %reduce-scatter.5.cloned.1.call-update) | async-done | bytes 409616 | tf_op jit(solution)/shard_map/reduce_scatter | solution.py:739
  825.9 122.1 %reduce-scatter.3.cloned.1.call-done = f32[80,3840]{1,0:T(8,128)} async-done(((f32[1280,3840]{1,0:T(8,128)}), f32[80,3840]{1,0:T(8,128)}) %reduce-scatter.3.cloned.1.call-update) | async-done | bytes 1228816 | tf_op jit(solution)/shard_map/reduce_scatter | solution.py:739
  947.9 5.3 copy.54
  953.3 1.2 copy.55
  (36 shorter events, 0.3 us)
Async XLA Ops:
  7.2 60.2 %all-gather.6.cloned.1.call-start = ((), (), s32[]{:S(2)}) async-start(), calls=%async_computation.2 | async-start | bytes 10444800 | tf_op jit(solution)/shard_map/all_gather | solution.py:736
  9.4 101.3 %all-gather.8.cloned.1.call-start = ((), (), s32[]{:S(2)}) async-start(), calls=%async_computation.3 | async-start | bytes 3481600 | tf_op jit(solution)/shard_map/all_gather | solution.py:736
  11.2 6.2 copy-start.1
  11.2 6.3 copy-start.8
  11.2 6.3 copy-start.2
  11.2 6.3 copy-start.3
  11.3 6.3 copy-start.4
  11.3 6.3 copy-start.5
  11.3 6.3 copy-start.6
  11.3 6.3 copy-start.7
  11.3 157.9 %all-gather.10.cloned.1.call-start = ((), (), s32[]{:S(2)}) async-start(), calls=%async_computation.4 | async-start | bytes 13926400 | tf_op jit(solution)/shard_map/all_gather | solution.py:736
  14.9 221.2 %all-gather.12.cloned.1.call-start = ((), (), s32[]{:S(2)}) async-start(), calls=%async_computation.5 | async-start | bytes 13926400 | tf_op jit(solution)/shard_map/all_gather | solution.py:736
  17.4 733.0 %all-reduce.3.cloned.1.call-start = ((), (), s32[]{:S(2)}) async-start(), calls=%async_computation.8 | async-start | bytes 147456
  684.9 140.9 %reduce-scatter.5.cloned.1.call-start = ((), (), s32[]{:S(2)}) async-start(), calls=%async_computation.7 | async-start | bytes 6963200 | tf_op jit(solution)/shard_map/reduce_scatter | solution.py:739
  685.5 262.4 %reduce-scatter.3.cloned.1.call-start = ((), (), s32[]{:S(2)}) async-start(), calls=%async_computation.6 | async-start | bytes 20889600 | tf_op jit(solution)/shard_map/reduce_scatter | solution.py:739
  947.9 5.3 copy-start
Sparse Core Ops, SparseCore 0:
  10.8 56.5 all-gather.5
  70.2 32.1 all-gather.7
  105.2 64.0 all-gather.9
  171.9 64.1 all-gather.11
  685.1 65.2 all-reduce.2
  753.1 72.7 reduce-scatter.4
  831.4 116.4 reduce-scatter.2

commit v3 on v2

v3 whole, which is shorter than its diff:
```python
import itertools
import math
import jax, jax.numpy as jnp
from jax import lax
from jax.experimental import pallas as pl
from jax.experimental.pallas import tpu as pltpu
from jax.sharding import PartitionSpec as P

BF, F32 = jnp.bfloat16, jnp.float32
IMAGES, SEQ, WIDTH, FFN, HEADS, HEAD = 8, 257, 1280, 5120, 16, 80
MAIN = SEQ - 1
TOKENS = IMAGES * SEQ
TAIL = IMAGES * MAIN
LN_EPS = 1e-5
VMEM_MAX = 67043328
LANE, SUBLANE, QUAD, QKV = 128, 8, 4, 3 * WIDTH
LANES = WIDTH // LANE
ROWS = 32


def dot(a, b):
    return jnp.dot(a, b, preferred_element_type=F32)


def dot_nt(a, b):
    return lax.dot_general(a, b, (((1,), (1,)), ((), ())), preferred_element_type=F32)


def dot_tn(a, b):
    return lax.dot_general(a, b, (((0,), (0,)), ((), ())), preferred_element_type=F32)


def col_sum(v):
    return jnp.sum(v, axis=0, keepdims=True)


def col_max(v):
    return jnp.max(v, axis=0, keepdims=True)


def row_sum(v):
    return jnp.sum(v, axis=-1, keepdims=True)


def row_mean(v):
    return row_sum(v) * (1.0 / WIDTH)


def clear(*refs):
    for ref in refs:
        ref[...] = jnp.zeros_like(ref)


def step_id():
    return pl.program_id(0)


def cost(flops, bytes_accessed, transcendentals=0):
    return pl.CostEstimate(flops=flops, bytes_accessed=bytes_accessed, transcendentals=transcendentals)


def eights(v):
    return jnp.sum(v.reshape(v.shape[0] // SUBLANE, SUBLANE, v.shape[1]), axis=0)


def whole(*shape, **kw):
    return pl.BlockSpec(shape, lambda *i: (0,) * len(shape), **kw)


def by_cols(rows, cols, at=lambda i: i):
    return pl.BlockSpec((rows, cols), lambda i: (0, at(i)))


def by_rows(rows, cols, at=lambda i: i):
    return pl.BlockSpec((rows, cols), lambda i: (at(i), 0))


def steps(first, wide):
    return slice(first * wide, (first + 1) * wide)


def norm_stats(values):
    mean = row_mean(values)
    centered = values - mean
    inv = lax.rsqrt(row_mean(centered * centered) + LN_EPS)
    return centered * inv, inv


def row_tiles(body, step=LANE):
    def loop(i, carry):
        body(pl.multiple_of(i * step, step), step)
        return carry
    lax.fori_loop(0, TAIL // step, loop, 0)
    body(TAIL, IMAGES)


def to_image_order(wide, place, step=LANE):
    per = MAIN // step
    def loop(i, carry):
        first = (i % per) * (step * IMAGES) + i // per
        rows = [wide[c, pl.ds(first, step, stride=IMAGES), :] for c in range(LANES)]
        place(pl.multiple_of(i * step, step), step, jnp.concatenate(rows, axis=1))
        return carry
    lax.fori_loop(0, IMAGES * per, loop, 0)
    place(TAIL, IMAGES, joined(wide, TAIL, IMAGES))


def from_image_order(values, wide):
    def loop(i, carry):
        rows = values[pl.ds(pl.multiple_of(i * LANE, LANE), LANE), :]
        for c in range(LANES):
            wide[c, pl.ds((i % 2) * (LANE * IMAGES) + i // 2, LANE, stride=IMAGES), :] = rows[:, steps(c, LANE)]
        return carry
    lax.fori_loop(0, 2 * IMAGES, loop, 0)
    put(wide, TAIL, IMAGES, values[pl.ds(TAIL, IMAGES), :])


def joined(wide, r, n):
    return jnp.concatenate([wide[c, pl.ds(r, n), :] for c in range(LANES)], axis=1)


def put(wide, r, n, values):
    for c in range(LANES):
        wide[c, pl.ds(r, n), :] = values[:, steps(c, LANE)]


def norm_back(dn, hat, inv, gain):
    dhat = dn * gain
    m1 = row_mean(dhat)
    m2 = row_mean(dhat * hat)
    return inv * (dhat - m1 - hat * m2)


ORDERS = ((2, 1, 0), (1, 0, 2), (0, 2, 1))


class Links:
    def find(self, send, recv):
        self.send, self.recv = send, recv
        me = lax.axis_index("fsdp")
        self.core = me % 2
        self.at = (me // SUBLANE, (me // QUAD) % 2, (me // 2) % 2)
        self.other_core = me + 1 - 2 * self.core
        self.other = [me + step - 2 * step * place for step, place in zip((SUBLANE, QUAD, 2), self.at)]
        return self

    def meet(self):
        barrier = pltpu.get_barrier_semaphore()
        devices = (self.other_core, *self.other)
        for device in devices:
            pl.semaphore_signal(barrier, inc=1, device_id=(device,), device_id_type=pl.DeviceIdType.MESH)
        pl.semaphore_wait(barrier, len(devices))

    def remote(self, src, dst, sem, device):
        return pltpu.make_async_remote_copy(src_ref=src, dst_ref=dst, send_sem=self.send.at[sem], recv_sem=self.recv.at[sem],
                                            device_id=(device,), device_id_type=pl.DeviceIdType.MESH)


class Gather(Links):
    COUNT = 2

    def __init__(self, rows, cols, cuts):
        self.rows, self.cols, self.cuts = rows, cols, cuts
        self.full_shape = jax.ShapeDtypeStruct((2, 2, 2, 2, rows, cols), BF)

    def scratch(self):
        return [pltpu.SemaphoreType.DMA((SEMS,))] * self.COUNT

    def bind(self, own, full, sems):
        self.own, self.full = own, full
        return self.find(*sems)

    def region(self, part, known, arrived=False):
        done = ORDERS[part][:known]
        place = [slice(None) if a in done else self.at[a] for a in range(3)]
        if arrived:
            place[done[-1]] = 1 - self.at[done[-1]]
        return (*place, self.core, slice(None), pl.ds(self.cuts[part], self.cuts[part + 1] - self.cuts[part]))

    def hop(self, stage, part):
        where = self.full.at[self.region(part, stage - 1)]
        source = self.own.at[self.region(part, 0)[-2:]] if stage == 1 else where
        return self.remote(source, where, QUAD * stage + part, self.other[ORDERS[part][stage - 1]])

    def forward(self, stage, part):
        if stage == 0:
            return self.remote(self.own, self.full.at[(*self.at, self.core)], 0, self.other_core)
        where = self.full.at[self.region(part, stage, True)]
        return self.remote(where, where, QUAD * (stage + 3) + part, self.other_core)

    def keep(self):
        return pltpu.make_async_copy(self.own, self.full.at[(*self.at, self.core)], self.send.at[1])

    def begin(self):
        for part in range(3):
            self.hop(1, part).start()
        self.forward(0, 0).start()
        self.keep().start()

    def turn(self, stage):
        if stage == 1:
            self.keep().wait()
        for part in range(3):
            self.hop(stage, part).wait()
            if stage < 3:
                self.hop(stage + 1, part).start()
        for part in range(3):
            self.forward(stage, part).start()

    def end(self):
        self.forward(0, 0).wait()
        for stage in range(1, QUAD):
            for part in range(3):
                self.forward(stage, part).wait()


SEMS = 28


class Exchange(Links):
    def __init__(self, rows, cols, cuts, along, stride=1, spare=0):
        self.rows, self.cols, self.stride = rows, cols, stride
        self.slots, self.locals = 3 * stride + spare, 1 + stride
        self.blocks = (2, 2, 2, 2, rows, cols)
        self.parts = [((slice(a, b), slice(None)) if along == 0 else (slice(None), slice(a, b))) for a, b in zip(cuts, cuts[1:])]
        self.shapes = [((b - a, cols) if along == 0 else (rows, b - a)) for a, b in zip(cuts, cuts[1:])]

    def scratch(self):
        two = (2, 2, 2)
        out = [pltpu.VMEM((self.locals, *self.blocks), F32), pltpu.VMEM((self.slots, *two, self.rows, self.cols), F32)]
        for axes in (2, 1, 0):
            out += [pltpu.VMEM((self.slots, *two[:axes], *shape), F32) for shape in self.shapes]
        return out + [pltpu.SemaphoreType.DMA((10, self.slots))] * 2

    COUNT = 13

    def bind(self, refs):
        self.local, self.pair = refs[0], refs[1]
        self.held = [None, refs[2:5], refs[5:SUBLANE], refs[SUBLANE:11]]
        return self.find(*refs[11:])

    def index(self, stage, part, side):
        order = ORDERS[part]
        left = [a for a in range(3) if a not in order[:stage - 1]]
        axis = order[stage - 1]
        where = self.at[axis] if side else 1 - self.at[axis]
        return tuple(where if a == axis else slice(None) for a in left)

    def copy(self, stage, part, c):
        slot = c % self.slots
        if stage == 0:
            return self.remote(self.local.at[c % self.locals, :, :, :, 1 - self.core], self.pair.at[slot], (0, slot), self.other_core)
        source = self.pair if stage == 1 else self.held[stage - 1][part]
        tail = self.parts[part] if stage == 1 else ()
        return self.remote(source.at[(slot, *self.index(stage, part, False), *tail)], self.held[stage][part].at[slot],
                           (3 * stage - 2 + part, slot), self.other[ORDERS[part][stage - 1]])

    def start(self, stage, c):
        for part in range(1 if stage == 0 else 3):
            self.copy(stage, part, c).start()

    def wait(self, stage, c):
        for part in range(1 if stage == 0 else 3):
            self.copy(stage, part, c).wait()

    def add(self, stage, c):
        slot = c % self.slots
        if stage == 0:
            for chip in itertools.product(range(2), repeat=3):
                self.pair[(slot, *chip)] += self.local[(c % self.locals, *chip, self.core)]
            return
        for part in range(3):
            source = self.pair if stage == 1 else self.held[stage - 1][part]
            tail = self.parts[part] if stage == 1 else ()
            for place in itertools.product(range(2), repeat=3 - stage):
                free = iter(place)
                kept = tuple(next(free) if isinstance(i, slice) else i for i in self.index(stage, part, True))
                self.held[stage][part][(slot, *place)] += source[(slot, *kept, *tail)]

    def result(self, c, out_ref):
        for part in range(3):
            out_ref[self.parts[part]] = self.held[3][part][c % self.slots]

    def put_local(self, c, values):
        self.local[c % self.locals] = values.reshape(self.blocks)


def comm_params(n):
    return pltpu.CompilerParams(dimension_semantics=("arbitrary",), vmem_limit_bytes=VMEM_MAX, collective_id=n, has_side_effects=True)


def advance(exchanges, t, exists, emit):
    for stage in (3, 2, 1, 0):
        c = t - 1 - (stage + 1) * exchanges[0].stride

        @pl.when(exists(c))
        def _():
            for n, exchange in enumerate(exchanges):
                exchange.wait(stage, c)
                exchange.add(stage, c)
                if stage < 3:
                    exchange.start(stage + 1, c)
                else:
                    emit(n, exchange, c)

    @pl.when(exists(t - 1))
    def _():
        for exchange in exchanges:
            exchange.start(0, t - 1)


def first_chunks(n):
    return lambda c: (c >= 0) & (c < n)


DRAIN = 5


QKV_N = 768


def qkv_kernel(x_ref, gain_ref, bias_ref, w_ref, wb_ref, xim_ref, ht_ref, qkv_ref, wide, h_ref):
    @pl.when(step_id() == 0)
    def _():
        def widen(r, n):
            put(wide, r, n, x_ref[pl.ds(r, n), :].astype(F32))
        row_tiles(widen)
        gain, bias = gain_ref[...], bias_ref[...]

        def place(r, n, values):
            xim_ref[pl.ds(r, n), :] = values.astype(BF)
            hat, _ = norm_stats(values)
            h_ref[pl.ds(r, n), :] = (hat * gain + bias).astype(BF)
        to_image_order(wide, place, ROWS)
        for b in range(IMAGES):
            ht_ref[:, steps(b, MAIN)] = h_ref[steps(b, MAIN), :].T
        ht_ref[:, TAIL:TOKENS] = h_ref[TAIL:TOKENS, :].T
    qkv_ref[...] = (dot(h_ref[...], w_ref[...]) + wb_ref[...]).astype(BF)


def qkv_call(x, gain, bias, w, wb):
    full = whole(TOKENS, WIDTH)
    vec = whole(1, WIDTH)
    return pl.pallas_call(
        qkv_kernel,
        grid=(QKV // QKV_N,),
        in_specs=[whole(TOKENS, WIDTH, pipeline_mode=pl.Buffered(1)), vec, vec,
                  by_cols(WIDTH, QKV_N), by_cols(1, QKV_N)],
        out_specs=[full, whole(WIDTH, TOKENS), by_cols(TOKENS, QKV_N)],
        out_shape=[jax.ShapeDtypeStruct((TOKENS, WIDTH), BF), jax.ShapeDtypeStruct((WIDTH, TOKENS), BF),
                   jax.ShapeDtypeStruct((TOKENS, QKV), BF)],
        scratch_shapes=[pltpu.VMEM((LANES, TOKENS, LANE), F32), pltpu.VMEM((TOKENS, WIDTH), BF)],
        compiler_params=pltpu.CompilerParams(dimension_semantics=("arbitrary",), vmem_limit_bytes=VMEM_MAX),
        cost_estimate=cost(2 * TOKENS * WIDTH * QKV, 60_000_000),
        name="qkv",
    )(x, gain, bias, w, wb)


PARTS = 16
MLP_F = MAIN
UNITS = MLP_F // PARTS
MLP_STEPS = FFN // MLP_F
ROW_CUTS = (0, 24, 48, 80)
FC_SUM = Exchange(WIDTH // PARTS, MLP_F, ROW_CUTS, 0)
PROJ_SUM = Exchange(UNITS, WIDTH, (0, 512, 896, 1280), 1)
CDF_P = 0.33
CDF_C = (0.1326322871417956, 0.11939570820799192, 0.18103829560051796, -0.08904113226212501,
         0.33075919469138065, -0.22023738432274684, 0.0454530347223348)


def gelu_pair(u):
    bell = jnp.exp(u * u * -0.5)
    t = 1.0 / (1.0 + CDF_P * jnp.abs(u))
    poly = CDF_C[6]
    for c in CDF_C[5::-1]:
        poly = poly * t + c
    tail = poly * t * bell
    cdf = jnp.where(u < 0.0, tail, 1.0 - tail)
    return u * cdf, cdf + u * bell * ((2.0 * math.pi) ** -0.5)


def mlp_kernel(r_hbm, dy_hbm, gain_ref, bias_ref, pb_ref, fc_ref, proj_ref, fcb_ref,
               y_hbm, dr_hbm, dr16_hbm, dfc_ref, dproj_ref, dfcb_ref, small_ref,
               n2, dy, y_acc, dn_acc, g, du, ua, ub, da, db, sem, *comm):
    step = step_id()
    by_row, by_col = FC_SUM.bind(comm[:Exchange.COUNT]), PROJ_SUM.bind(comm[Exchange.COUNT:])

    @pl.when(step == 0)
    def _():
        by_row.meet()
        cp = pltpu.make_async_copy(dy_hbm, n2, sem)
        cp.start()
        cp.wait()

        def widen(r, n):
            put(dn_acc, r, n, n2[pl.ds(r, n), :].astype(F32))
        row_tiles(widen)
        cp = pltpu.make_async_copy(r_hbm, n2, sem)
        cp.start()

        def place(r, n, values):
            dy[pl.ds(r, n), :] = values.astype(BF)
        to_image_order(dn_acc, place, ROWS)
        cp.wait()
        gain, bias, pb = gain_ref[...], bias_ref[...], pb_ref[...]

        def norm(r, n):
            wide_r = n2[pl.ds(r, n), :].astype(F32)
            hat, _ = norm_stats(wide_r)
            n2[pl.ds(r, n), :] = (hat * gain + bias).astype(BF)
            y_acc[pl.ds(r, n), :] = wide_r + pb
            put(dn_acc, r, n, jnp.zeros((n, WIDTH), F32))
        row_tiles(norm, ROWS)
        clear(small_ref)

    outs = (dfc_ref, dproj_ref)
    advance((by_row, by_col), step, first_chunks(MLP_STEPS), lambda n, exchange, c: exchange.result(c, outs[n]))

    @pl.when(step < MLP_STEPS)
    def _():
        fcb = fcb_ref[...]
        fc, proj = fc_ref[...], proj_ref[...].reshape(MLP_F, WIDTH)
        bias_sum = jnp.zeros((SUBLANE, MLP_F), F32)
        tiles = [(b * MAIN, MAIN) for b in range(IMAGES - 1)] + [((IMAGES - 1) * MAIN, MAIN + IMAGES)]
        pairs = ((ua, da), (ub, db))

        def products(k):
            r, n = tiles[k]
            u_s, d_s = pairs[k % 2]
            u_s[0:n, :] = dot(n2[r:r + n, :], fc)
            d_s[0:n, :] = dot_nt(dy[r:r + n, :], proj)

        def pointwise(k, total):
            r, n = tiles[k]
            u_s, d_s = pairs[k % 2]
            value, slope = gelu_pair(u_s[0:n, :] + fcb)
            g[r:r + n, :] = value.astype(BF)
            grad = d_s[0:n, :] * slope
            du[r:r + n, :] = grad.astype(BF)
            return total + eights(grad)

        products(0)
        for k in range(1, IMAGES):
            products(k)
            bias_sum = pointwise(k - 1, bias_sum)
        bias_sum = pointwise(IMAGES - 1, bias_sum)
        dfcb_ref[...] = col_sum(bias_sum)
        y_acc[...] += dot(g[...], proj)
        for c in range(LANES // 2):
            part = dot_nt(du[...], fc_ref[steps(c, MAIN), :])
            dn_acc[2 * c] += part[:, :LANE]
            dn_acc[2 * c + 1] += part[:, LANE:]
        by_col.put_local(step, dot_tn(g[...], dy[...]))
        by_row.put_local(step, dot_tn(n2[...], du[...]))

    out_copies = [pltpu.make_async_copy(dn_acc, dr_hbm, sem), pltpu.make_async_copy(n2, dr16_hbm, sem)]
    y_copy = pltpu.make_async_copy(dy, y_hbm, sem)

    @pl.when(step == MLP_STEPS)
    def _():
        cp = pltpu.make_async_copy(r_hbm, n2, sem)
        cp.start()
        cp.wait()
        gain = gain_ref[...]

        def back(r, n):
            hat, inv = norm_stats(n2[pl.ds(r, n), :].astype(F32))
            dn = joined(dn_acc, r, n)
            wide_dy = dy[pl.ds(r, n), :].astype(F32)
            dr = wide_dy + norm_back(dn, hat, inv, gain)
            put(dn_acc, r, n, dr)
            n2[pl.ds(r, n), :] = dr.astype(BF)
            for i, v in enumerate((dn * hat, dn, wide_dy, dr)):
                small_ref[steps(i, SUBLANE), :] += eights(v)
        row_tiles(back, ROWS)
        for cp in out_copies:
            cp.start()

    @pl.when(step == MLP_STEPS + 1)
    def _():
        for cp in out_copies:
            cp.wait()
        from_image_order(y_acc, dn_acc)

    @pl.when(step == MLP_STEPS + 2)
    def _():
        def narrow(r, n):
            dy[pl.ds(r, n), :] = joined(dn_acc, r, n).astype(BF)
        row_tiles(narrow)
        y_copy.start()

    @pl.when(step == MLP_STEPS + 3)
    def _():
        y_copy.wait()


def mlp_call(r, dy, gain, bias, pb, fc, proj, fcb):
    hbm = pl.BlockSpec(memory_space=pl.ANY)
    vec = whole(1, WIDTH)
    now = lambda i: jnp.minimum(i, MLP_STEPS - 1)
    done = lambda i: jnp.maximum(i - DRAIN, 0)
    return pl.pallas_call(
        mlp_kernel,
        grid=(MLP_STEPS + DRAIN,),
        in_specs=[hbm, hbm, vec, vec, vec, by_cols(WIDTH, MLP_F, now),
                  pl.BlockSpec((PARTS, None, UNITS, WIDTH), lambda i: (0, now(i), 0, 0)),
                  by_cols(1, MLP_F, now)],
        out_specs=[hbm, hbm, hbm, by_cols(WIDTH // PARTS, MLP_F, done),
                   by_rows(UNITS, WIDTH, done),
                   by_cols(1, MLP_F, now), whole(32, WIDTH)],
        out_shape=[jax.ShapeDtypeStruct((TOKENS, WIDTH), BF), jax.ShapeDtypeStruct((LANES, TOKENS, LANE), F32),
                   jax.ShapeDtypeStruct((TOKENS, WIDTH), BF), jax.ShapeDtypeStruct((WIDTH // PARTS, FFN), F32),
                   jax.ShapeDtypeStruct((FFN // PARTS, WIDTH), F32),
                   jax.ShapeDtypeStruct((1, FFN), F32), jax.ShapeDtypeStruct((32, WIDTH), F32)],
        scratch_shapes=[pltpu.VMEM((TOKENS, WIDTH), BF), pltpu.VMEM((TOKENS, WIDTH), BF),
                        pltpu.VMEM((TOKENS, WIDTH), F32), pltpu.VMEM((LANES, TOKENS, LANE), F32),
                        pltpu.VMEM((TOKENS, MLP_F), BF), pltpu.VMEM((TOKENS, MLP_F), BF)]
                       + [pltpu.VMEM((MAIN + IMAGES, MLP_F), F32)] * QUAD + [pltpu.SemaphoreType.DMA]
                       + FC_SUM.scratch() + PROJ_SUM.scratch(),
        compiler_params=comm_params(0),
        cost_estimate=cost(12 * TOKENS * WIDTH * FFN, 150_000_000, TOKENS * FFN),
        name="mlp",
    )(r, dy, gain, bias, pb, fc, proj.reshape(PARTS, MLP_STEPS, UNITS, WIDTH), fcb)


SCALE = HEAD ** -0.5


def window(h):
    first = min(HEAD * h // LANE * LANE, WIDTH - MAIN)
    wide = LANE if HEAD * h + HEAD <= first + LANE else MAIN
    return first, wide, HEAD * h - first


def lane_mask(h):
    first, wide, off = window(h)
    lane = lax.broadcasted_iota(jnp.int32, (MAIN, wide), 1)
    return (lane >= off) & (lane < off + HEAD)


def thirds(ref, rows=slice(None)):
    return [ref[rows, steps(i, WIDTH)] for i in range(3)]


def head_rows():
    lane = lax.broadcasted_iota(jnp.int32, (HEADS, WIDTH), 1)
    row = lax.broadcasted_iota(jnp.int32, (HEADS, WIDTH), 0)
    return (lane // HEAD == row).astype(F32)


def tail_softmax(s, s_self):
    m = jnp.maximum(jnp.max(s, axis=1, keepdims=True), s_self)
    e = jnp.exp((s - m) * SCALE)
    e_self = jnp.exp((s_self - m) * SCALE)
    inv = 1.0 / (row_sum(e) + e_self)
    return e * inv, e_self * inv


def attn_kernel(qkv_ref, qkvt_ref, x_ref, xt_ref, w_ref, wb_ref, o_hbm, r_hbm, max_ref, inv_ref,
                tails, o_tail, o_t, ptail, o_buf, r_buf, sems):
    b, last = step_id(), pl.num_programs(0) - 1
    slot = b % 2

    @pl.when(b == 0)
    def _():
        tails[...] = qkvt_ref[...].astype(F32)

    heads = head_rows()
    q_t, k_t, v_t = (heads * z for z in thirds(tails, pl.ds(b, 1)))
    q, k, v = thirds(qkv_ref)

    p, p_self = tail_softmax(dot_nt(q_t.astype(BF), k), row_sum(q_t * k_t))
    mixed = dot(p.astype(BF), v) * heads + p_self.astype(BF).astype(F32) * v_t
    o_tail[pl.ds(b, 1), :] = col_sum(mixed)

    s_tail = dot_nt(k_t.astype(BF), q)
    v_turned = v.T
    for h in range(HEADS):
        first, wide, _ = window(h)
        q_h = jnp.where(lane_mask(h), qkv_ref[:, first:first + wide], jnp.zeros((), BF))
        s = dot_nt(qkv_ref[:, pl.ds(WIDTH + first, wide)], q_h)
        top = jnp.maximum(col_max(s), s_tail[steps(h, 1), :])
        e = jnp.exp((s - top) * SCALE)
        e_tail = jnp.exp((s_tail[steps(h, 1), :] - top) * SCALE)
        inv = 1.0 / (col_sum(e) + e_tail)
        max_ref[0, steps(h, 1), :] = top
        inv_ref[0, steps(h, 1), :] = inv
        ptail[steps(h, 1), :] = e_tail * inv
        o_t[steps(h, HEAD), :] = dot(v_turned[steps(h, HEAD), :], (e * inv).astype(BF))

    @pl.when(b >= 2)
    def _():
        out_copy(o_buf, o_hbm, slot, b - 2, sems, 0).wait()
        out_copy(r_buf, r_hbm, slot, b - 2, sems, 1).wait()

    o = (o_t[...].T + dot_tn(ptail[...].astype(BF), v_t.astype(BF))).astype(BF)
    o_buf[slot] = o
    r_buf[slot] = (x_ref[...].astype(F32) + dot(o, w_ref[...]) + wb_ref[...]).astype(BF)
    out_copy(o_buf, o_hbm, slot, b, sems, 0).start()
    out_copy(r_buf, r_hbm, slot, b, sems, 1).start()

    @pl.when(b == last)
    def _():
        for buf, hbm, n in ((o_buf, o_hbm, 0), (r_buf, r_hbm, 1)):
            out_copy(buf, hbm, 1 - slot, b - 1, sems, n).wait()
        o = o_tail[...].astype(BF)
        o_buf[1 - slot, 0:IMAGES, :] = o
        r_buf[1 - slot, 0:IMAGES, :] = (xt_ref[...].astype(F32) + dot(o, w_ref[...]) + wb_ref[...]).astype(BF)
        copies = [pltpu.make_async_copy(buf.at[1 - slot, pl.ds(0, IMAGES)], hbm.at[pl.ds(TAIL, IMAGES)], sems.at[n, 1 - slot])
                  for buf, hbm, n in ((o_buf, o_hbm, 0), (r_buf, r_hbm, 1))]
        for cp in copies:
            cp.start()
        for cp in copies:
            cp.wait()
        for buf, hbm, n in ((o_buf, o_hbm, 0), (r_buf, r_hbm, 1)):
            out_copy(buf, hbm, slot, b, sems, n).wait()


def out_copy(buf, hbm, slot, b, sems, n):
    return pltpu.make_async_copy(buf.at[slot], hbm.at[pl.ds(pl.multiple_of(b * MAIN, MAIN), MAIN)], sems.at[n, slot])


def attn_call(qkv, xim, w, wb):
    hbm = pl.BlockSpec(memory_space=pl.ANY)
    main = lambda n: by_rows(MAIN, n)
    tail = lambda n: by_rows(IMAGES, n, lambda i: TAIL // IMAGES)
    stat = pl.BlockSpec((1, HEADS, MAIN), lambda i: (i, 0, 0))
    return pl.pallas_call(
        attn_kernel,
        grid=(IMAGES,),
        in_specs=[main(QKV), tail(QKV), main(WIDTH), tail(WIDTH),
                  whole(WIDTH, WIDTH), whole(1, WIDTH)],
        out_specs=[hbm, hbm, stat, stat],
        out_shape=[jax.ShapeDtypeStruct((TOKENS, WIDTH), BF), jax.ShapeDtypeStruct((TOKENS, WIDTH), BF),
                   jax.ShapeDtypeStruct((IMAGES, HEADS, MAIN), F32), jax.ShapeDtypeStruct((IMAGES, HEADS, MAIN), F32)],
        scratch_shapes=[pltpu.VMEM((IMAGES, QKV), F32), pltpu.VMEM((IMAGES, WIDTH), F32),
                        pltpu.VMEM((WIDTH, MAIN), F32), pltpu.VMEM((HEADS, MAIN), F32),
                        pltpu.VMEM((2, MAIN, WIDTH), BF), pltpu.VMEM((2, MAIN, WIDTH), BF), pltpu.SemaphoreType.DMA((2, 2))],
        compiler_params=pltpu.CompilerParams(dimension_semantics=("arbitrary",), vmem_limit_bytes=VMEM_MAX),
        cost_estimate=cost(30_000_000_000, 50_000_000, 8_400_000),
        name="attn",
    )(qkv, qkv, xim, xim, w, wb)


def outb_kernel(dr_ref, o_ref, w_ref, do_ref, dw_ref):
    n = MAIN
    c = step_id()
    do_ref[...] = dot_nt(dr_ref[...], w_ref[...]).astype(BF)
    dw_ref[...] = dot_tn(o_ref[...], dr_ref[:, pl.ds(pl.multiple_of(c * n, n), n)])


def outb_call(dr, o, w):
    n = MAIN
    full = whole(TOKENS, WIDTH)
    return pl.pallas_call(
        outb_kernel,
        grid=(WIDTH // n,),
        in_specs=[full, full, by_rows(n, WIDTH)],
        out_specs=[by_cols(TOKENS, n), by_cols(WIDTH, n)],
        out_shape=[jax.ShapeDtypeStruct((TOKENS, WIDTH), BF), jax.ShapeDtypeStruct((WIDTH, WIDTH), F32)],
        compiler_params=pltpu.CompilerParams(dimension_semantics=("arbitrary",), vmem_limit_bytes=VMEM_MAX),
        cost_estimate=cost(QUAD * TOKENS * WIDTH * WIDTH, 30_000_000),
        name="outb",
    )(dr, o, w)


def attn_back_kernel(qkv_ref, qkvt_ref, do_ref, dot_ref, max_ref, inv_ref, dw_ref, dqkv_hbm, dwb_ref, dwout_ref,
                     tails, do_tails, grad_tails, dq_t, dk, dv, ds_tail, buf, sems, *comm):
    b = step_id()
    by_row = FC_SUM.bind(comm)

    @pl.when(b == 0)
    def _():
        by_row.meet()
    advance((by_row,), b, first_chunks(OUT_STEPS), lambda n, exchange, c: exchange.result(c, dwout_ref))

    @pl.when(b < OUT_STEPS)
    def _():
        by_row.put_local(b, dw_ref[...])

    @pl.when(b < IMAGES)
    def _():
        image_back(b, qkv_ref, qkvt_ref, do_ref, dot_ref, max_ref, inv_ref, dqkv_hbm, dwb_ref,
                   tails, do_tails, grad_tails, dq_t, dk, dv, ds_tail, buf, sems)


OUT_STEPS = WIDTH // MAIN


def image_back(b, qkv_ref, qkvt_ref, do_ref, dot_ref, max_ref, inv_ref, dqkv_hbm, dwb_ref,
               tails, do_tails, grad_tails, dq_t, dk, dv, ds_tail, buf, sems):
    last = IMAGES - 1
    slot = b % 2

    @pl.when(b == 0)
    def _():
        tails[...] = qkvt_ref[...].astype(F32)
        do_tails[...] = dot_ref[...].astype(F32)
        clear(dwb_ref)

    heads = head_rows()
    q_t, k_t, v_t = (heads * z for z in thirds(tails, pl.ds(b, 1)))
    do_t = heads * do_tails[pl.ds(b, 1), :]
    q, k, v = thirds(qkv_ref)
    do = do_ref[...]
    q_t16, k_t16, v_t16, do_t16 = (z.astype(BF) for z in (q_t, k_t, v_t, do_t))

    p, p_self = tail_softmax(dot_nt(q_t16, k), row_sum(q_t * k_t))
    dp, dp_self = dot_nt(do_t16, v), row_sum(do_t * v_t)
    inner = row_sum(p * dp) + p_self * dp_self
    ds16 = (p * (dp - inner) * SCALE).astype(BF)
    ds_self = (p_self * (dp_self - inner) * SCALE).astype(BF).astype(F32)
    grad_q = col_sum(dot(ds16, k) * heads + ds_self * k_t)
    grad_k = ds_self * q_t
    grad_v = p_self.astype(BF).astype(F32) * do_t
    dk[...] = dot_tn(ds16, q_t16)
    dv[...] = dot_tn(p.astype(BF), do_t16)

    p_tail = jnp.exp((dot_nt(k_t16, q) - max_ref[0]) * SCALE) * inv_ref[0]
    dp_tail = dot_nt(v_t16, do)
    inner_tail = p_tail * dp_tail

    k_turned = k.T
    for h in range(HEADS):
        first, wide, _ = window(h)
        here = slice(first, first + wide)
        mask = lane_mask(h)
        q_h = jnp.where(mask, qkv_ref[:, here], jnp.zeros((), BF))
        do_h = jnp.where(mask, do_ref[:, here], jnp.zeros((), BF))
        s = dot_nt(qkv_ref[:, pl.ds(WIDTH + first, wide)], q_h)
        dp = dot_nt(qkv_ref[:, pl.ds(2 * WIDTH + first, wide)], do_h)
        p = jnp.exp((s - max_ref[0, steps(h, 1), :]) * SCALE) * inv_ref[0, steps(h, 1), :]
        inner = col_sum(p * dp) + inner_tail[steps(h, 1), :]
        ds = (p * (dp - inner) * SCALE).astype(BF)
        dv[:, here] += dot(p.astype(BF), do_h)
        dk[:, here] += dot(ds, q_h)
        dq_t[steps(h, HEAD), :] = dot(k_turned[steps(h, HEAD), :], ds)
        ds_tail[steps(h, 1), :] = p_tail[steps(h, 1), :] * (dp_tail[steps(h, 1), :] - inner) * SCALE

    ds_tail16 = ds_tail[...].astype(BF)
    grad_k = col_sum(grad_k + dot(ds_tail16, q) * heads)
    grad_v = col_sum(grad_v + dot(p_tail.astype(BF), do) * heads)

    @pl.when(b >= 2)
    def _():
        out_copy(buf, dqkv_hbm, slot, b - 2, sems, 0).wait()

    grad = dq_t[...].T + dot_tn(ds_tail16, k_t16)
    for n, (main, tail) in enumerate(((grad, grad_q), (dk[...], grad_k), (dv[...], grad_v))):
        here = steps(n, WIDTH)
        buf[slot, :, here] = main.astype(BF)
        grad_tails[pl.ds(b, 1), here] = tail
        dwb_ref[:, here] += col_sum(main) + tail
    out_copy(buf, dqkv_hbm, slot, b, sems, 0).start()

    @pl.when(b == last)
    def _():
        out_copy(buf, dqkv_hbm, 1 - slot, b - 1, sems, 0).wait()
        buf[1 - slot, 0:IMAGES, :] = grad_tails[...].astype(BF)
        cp = pltpu.make_async_copy(buf.at[1 - slot, pl.ds(0, IMAGES)], dqkv_hbm.at[pl.ds(TAIL, IMAGES)], sems.at[0, 1 - slot])
        cp.start()
        cp.wait()
        out_copy(buf, dqkv_hbm, slot, b, sems, 0).wait()


def attn_back_call(qkv, do, top, inv, dw):
    hbm = pl.BlockSpec(memory_space=pl.ANY)
    image = lambda i: jnp.minimum(i, IMAGES - 1)
    main = lambda n: by_rows(MAIN, n, image)
    tail = lambda n: by_rows(IMAGES, n, lambda i: TAIL // IMAGES)
    stat = pl.BlockSpec((1, HEADS, MAIN), lambda i: (image(i), 0, 0))
    return pl.pallas_call(
        attn_back_kernel,
        grid=(OUT_STEPS + DRAIN,),
        in_specs=[main(QKV), tail(QKV), main(WIDTH), tail(WIDTH), stat, stat,
                  by_cols(WIDTH, MAIN, lambda i: jnp.minimum(i, OUT_STEPS - 1))],
        out_specs=[hbm, whole(1, QKV), by_cols(WIDTH // PARTS, MAIN, lambda i: jnp.maximum(i - DRAIN, 0))],
        out_shape=[jax.ShapeDtypeStruct((TOKENS, QKV), BF), jax.ShapeDtypeStruct((1, QKV), F32),
                   jax.ShapeDtypeStruct((WIDTH // PARTS, WIDTH), F32)],
        scratch_shapes=[pltpu.VMEM((IMAGES, QKV), F32), pltpu.VMEM((IMAGES, WIDTH), F32),
                        pltpu.VMEM((IMAGES, QKV), F32), pltpu.VMEM((WIDTH, MAIN), F32),
                        pltpu.VMEM((MAIN, WIDTH), F32), pltpu.VMEM((MAIN, WIDTH), F32), pltpu.VMEM((HEADS, MAIN), F32),
                        pltpu.VMEM((2, MAIN, QKV), BF), pltpu.SemaphoreType.DMA((1, 2))] + FC_SUM.scratch(),
        compiler_params=comm_params(1),
        cost_estimate=cost(60_000_000_000, 50_000_000, 8_400_000),
        name="attn_back",
    )(qkv, qkv, do, do, top, inv, dw)


QB_N = MAIN
QB_STEPS = QKV // QB_N
QKV_SUM = Exchange(WIDTH // PARTS, QB_N, ROW_CUTS, 0, 2, 1)
VECTOR_CHUNK = QB_STEPS + 2
QB_GRID = VECTOR_CHUNK + 2 + QUAD * QKV_SUM.stride
VECTOR_ROWS = 16


def qkvb_kernel(xim_hbm, dr_hbm, gain_ref, vec_ref, ht_ref, dqkv_ref, w_ref, dx_hbm, dw_ref, out_vec_ref,
                acc, dr, xd, vec, vec_out, sums, sems, *comm):
    t = step_id()
    by_row = QKV_SUM.bind(comm)
    loads = [pltpu.make_async_copy(dr_hbm, dr, sems.at[0]), pltpu.make_async_copy(xim_hbm, xd, sems.at[1])]
    store = pltpu.make_async_copy(xd, dx_hbm, sems.at[1])

    @pl.when(t == 0)
    def _():
        by_row.meet()
        for cp in loads:
            cp.start()
        clear(acc, sums, vec)
        vec[:VECTOR_ROWS, :] = vec_ref[...]

    def emit(n, exchange, c):
        @pl.when(c < QB_STEPS)
        def _():
            exchange.result(c, dw_ref)

        @pl.when(c == VECTOR_CHUNK)
        def _():
            exchange.result(c, vec_out)
            out_vec_ref[...] = vec_out[:, :LANE].T[:VECTOR_ROWS, :]
    advance((by_row,), t, lambda c: ((c >= 0) & (c < QB_STEPS)) | (c == VECTOR_CHUNK), emit)

    @pl.when(t < QB_STEPS)
    def _():
        by_row.put_local(t, dot(ht_ref[...], dqkv_ref[...]))
        acc[...] += dot_nt(dqkv_ref[...], w_ref[...])

    @pl.when(t == QB_STEPS)
    def _():
        for cp in loads:
            cp.wait()

    def back(r, n):
        hat, inv = norm_stats(xd[pl.ds(r, n), :].astype(F32))
        dn = acc[pl.ds(r, n), :]
        for i, v in enumerate((dn * hat, dn)):
            sums[steps(i, SUBLANE), :] += eights(v)
        acc[pl.ds(r, n), :] = joined(dr, r, n) + norm_back(dn, hat, inv, gain_ref[...])

    @pl.when((t >= QB_STEPS) & (t <= VECTOR_CHUNK))
    def _():
        part = (t - QB_STEPS) * BACK_TILES

        def loop(i, carry):
            @pl.when(part + i < TAIL // ROWS)
            def _():
                back(pl.multiple_of((part + i) * ROWS, ROWS), ROWS)
            return carry
        lax.fori_loop(0, BACK_TILES, loop, 0)

    @pl.when(t == VECTOR_CHUNK)
    def _():
        back(TAIL, IMAGES)
        for i in range(2):
            vec[VECTOR_ROWS - 2 + i:VECTOR_ROWS - 1 + i, :] = col_sum(sums[steps(i, SUBLANE), :])
        turned = vec[...].T
        by_row.put_local(t, jnp.concatenate([turned, jnp.zeros_like(turned)], axis=1))

    @pl.when(t == VECTOR_CHUNK + 1)
    def _():
        from_image_order(acc, dr)

    @pl.when(t == VECTOR_CHUNK + 2)
    def _():
        def narrow(r, n):
            xd[pl.ds(r, n), :] = joined(dr, r, n).astype(BF)
        row_tiles(narrow)
        store.start()

    @pl.when(t == QB_GRID - 1)
    def _():
        store.wait()


BACK_TILES = -(-TAIL // ROWS // 3)


def qkvb_call(xim, dr, gain, vec, ht, dqkv, w):
    hbm = pl.BlockSpec(memory_space=pl.ANY)
    now = lambda i: jnp.minimum(i, QB_STEPS - 1)
    return pl.pallas_call(
        qkvb_kernel,
        grid=(QB_GRID,),
        in_specs=[hbm, hbm, whole(1, WIDTH), whole(VECTOR_ROWS, WIDTH),
                  whole(WIDTH, TOKENS, pipeline_mode=pl.Buffered(1)), by_cols(TOKENS, QB_N, now), by_cols(WIDTH, QB_N, now)],
        out_specs=[hbm, by_cols(WIDTH // PARTS, QB_N, lambda i: jnp.clip(i - 1 - QUAD * QKV_SUM.stride, 0, QB_STEPS - 1)),
                   whole(VECTOR_ROWS, WIDTH // PARTS)],
        out_shape=[jax.ShapeDtypeStruct((TOKENS, WIDTH), BF), jax.ShapeDtypeStruct((WIDTH // PARTS, QKV), F32),
                   jax.ShapeDtypeStruct((VECTOR_ROWS, WIDTH // PARTS), F32)],
        scratch_shapes=[pltpu.VMEM((TOKENS, WIDTH), F32), pltpu.VMEM((LANES, TOKENS, LANE), F32), pltpu.VMEM((TOKENS, WIDTH), BF),
                        pltpu.VMEM((LANE, WIDTH), F32), pltpu.VMEM((WIDTH // PARTS, QB_N), F32), pltpu.VMEM((16, WIDTH), F32), pltpu.SemaphoreType.DMA((2,))]
                       + QKV_SUM.scratch(),
        compiler_params=comm_params(2),
        cost_estimate=cost(QUAD * TOKENS * WIDTH * QKV, 80_000_000),
        name="qkvb",
    )(xim, dr, gain, vec, ht, dqkv, w)


VECTORS = (80, 80, 240, 80, 80, 80, 320, 80)


def to_steps(v):
    rows = v.shape[0]
    return v.reshape(rows, PARTS, MLP_STEPS, UNITS).swapaxes(1, 2).reshape(rows, FFN)


def from_steps(v):
    rows = v.shape[0]
    return v.reshape(rows, MLP_STEPS, PARTS, UNITS).swapaxes(1, 2).reshape(rows, FFN)


def solution(mesh):
    specs = (P("fsdp"),) * 14

    def gather(shard):
        return lax.all_gather(shard.astype(BF), "fsdp", axis=0, tiled=True)

    def device_step(resid_in, grad_out, ln1_gain, ln1_bias, qkv_weight, qkv_bias, out_weight, out_bias,
                    ln2_gain, ln2_bias, fc_weight, fc_bias, proj_weight, proj_bias):
        wq, wo, wf, wp = (gather(w) for w in (qkv_weight, out_weight, to_steps(fc_weight.astype(BF)), proj_weight))
        packed = jnp.concatenate([ln1_gain, ln1_bias, qkv_bias, out_bias, ln2_gain, ln2_bias, fc_bias, proj_bias])
        packed = gather(packed[None]).astype(F32)
        cuts = [sum(VECTORS[:i]) for i in range(len(VECTORS) + 1)]
        g1, b1, bq, bo, g2, b2, bf, bp = (packed[:, a:b].reshape(1, -1) for a, b in zip(cuts, cuts[1:]))

        x = resid_in.transpose(1, 0, 2).reshape(TOKENS, WIDTH)
        dy = grad_out.transpose(1, 0, 2).reshape(TOKENS, WIDTH)
        xim, ht, qkv = qkv_call(x, g1, b1, wq, bq)
        o, r, top, inv = attn_call(qkv, xim, wo, bo)
        y, dr, dr16, dwf, dwp, dbf, small = mlp_call(r, dy, g2, b2, bp, wf, wp, to_steps(bf))
        do, dwo = outb_call(dr16, o, wo)
        dqkv, dbq, dwo = attn_back_call(qkv, do, top, inv, dwo)
        owned = lambda v: v.reshape(PARTS, -1, WIDTH // PARTS).swapaxes(0, 1).reshape(-1, WIDTH)
        vec = jnp.concatenate([jnp.sum(small.reshape(4, 8, WIDTH), axis=1), owned(dbq), owned(from_steps(dbf))])
        vec = jnp.pad(vec, ((0, VECTOR_ROWS - len(vec)), (0, 0)))
        dx, dwq, vec = qkvb_call(xim, dr, g1, vec, ht, dqkv, wq)
        dg2, db2, dbp, dbo = vec[:4]
        dbq, dbf = vec[4:7].reshape(-1), vec[7:11].reshape(-1)
        dg1, db1 = vec[VECTOR_ROWS - 2:]
        dwf = from_steps(dwf)
        unturn = lambda t: t.reshape(SEQ, IMAGES, WIDTH).transpose(1, 0, 2)
        return (unturn(y), unturn(dx), dg1, db1, dwq, dbq, dwo, dbo, dg2, db2, dwf, dbf, dwp, dbp)

    return jax.shard_map(device_step, mesh=mesh, in_specs=specs, out_specs=specs, check_vma=False)
```

time: 970 us -> 755 us (0.78)
  waiting for transfers between devices: 359 us -> 105 us
  Pallas kernels: 534 us -> 568 us
    reduce_scatter x2 -> x0, waiting for transfers between devices: 193 us -> none  [scatter(): return lax.psum_scatter(grad, 'fsdp', scatter_dimension=0, tiled=True)]
    unnamed x8 -> x4, waiting for transfers between devices: 58.6 us -> 0.07 us
    pallas_call x4, Pallas kernels: 232 us -> 267 us  [the longest x1 102 us: qkvb_call(): pl.pallas_call(qkvb_kernel, grid=(QB_GRID,), in_specs=[hbm, hbm, whole(1,...]
  transfers between devices with their start and end apart: 7 -> 4, of which waited for: 6 -> 3; matrix products, arithmetic and copies ran while one was open for 3% -> 2% of each run, Pallas kernels for 9% -> 12%
where the time goes in v3:
time: 755 us; the launch traced here: 745 us
  Pallas kernels  568 us (75%)
  waiting for transfers between devices  105 us (14%)
  local copies, waits for them, and re-layouts  32.4 us (4%)
  blocking collectives  15 us (2%)
  between operations  14.6 us (2%)
  other arithmetic  10.1 us (1%)
    pallas_call x1, Pallas kernels, mlp_call(): pl.pallas_call(mlp_kernel, grid=(MLP_STEPS + DRAIN,), in_specs=[hbm, hbm,...  280 us
    all_gather x4, waiting for transfers between devices, gather(): return lax.all_gather(shard.astype(BF), 'fsdp', axis=0, tiled=True)  105 us
    pallas_call x1, Pallas kernels, qkvb_call(): pl.pallas_call(qkvb_kernel, grid=(QB_GRID,), in_specs=[hbm, hbm, whole(1,...  102 us
    pallas_call x1, Pallas kernels, attn_back_call(): pl.pallas_call(attn_back_kernel, grid=(OUT_STEPS + DRAIN,), in_specs=[mai...  72 us
    pallas_call x1, Pallas kernels, attn_call(): pl.pallas_call(attn_kernel, grid=(IMAGES,), in_specs=[main(QKV), tail(QKV...  47.8 us
    pallas_call x1, Pallas kernels, qkv_call(): pl.pallas_call(qkv_kernel, grid=(QKV // QKV_N,), in_specs=[whole(TOKENS,...  44.7 us
    pallas_call x1, Pallas kernels, outb_call(): pl.pallas_call(outb_kernel, grid=(WIDTH // n,), in_specs=[full, full, by_...  21.6 us
    unnamed x34, local copies, waits for them, and re-layouts  16 us
  transfers between devices with their start and end apart: 4, of which 3 were waited for; matrix products, arithmetic and copies ran while one was open for 2% of the time, Pallas kernels for 12%

profile of v3, /device:TPU:0, one launch (start us, length us, event | category | flops | bytes accessed | tf_op | source)
XLA Modules:
  0.0 745.3 jit_solution(16672508054496871822)
XLA Ops:
  7.2 0.0 all-gather.6.cloned.1.call-start
  7.2 2.2 convert_element_type.27
  9.4 0.0 all-gather.6.cloned.1.call-update
  9.4 0.0 all-gather.8.cloned.1.call-start
  9.5 1.7 convert_element_type.28
  11.2 0.0 all-gather.8.cloned.1.call-update
  11.2 0.0 copy-start.4
  11.2 0.0 copy-start.5
  11.3 0.0 copy-start.8
  11.3 0.0 copy-start.9
  11.3 0.0 all-gather.10.cloned.1.call-start
  11.4 1.8 copy.42
  13.2 0.4 copy.43
  13.5 1.3 copy.44
  14.9 0.0 all-gather.10.cloned.1.call-update
  14.9 0.0 all-gather.12.cloned.1.call-start
  15.0 2.4 convert_element_type.30
  17.4 0.0 all-gather.12.cloned.1.call-update
  17.5 0.1 concatenate.38
  17.7 15.0 %all-gather = bf16[16,1,1040]{2,1,0:T(2,128)(2,1)S(1)} all-gather(bf16[1,1,1040]{2,1,0:T(2,128)(2,1)S(1)} %bitcast.72), channel_id=1, replica_groups=mesh['fsdp'=16] {'fsdp'}, dimensions={0}, use_global_device_ids=true | all-gather | bytes 35360 | tf_op jit(solution)/shard_map/all_gather | solution.py:917
  32.6 0.1 slice.50
  32.7 0.1 fusion
  32.8 0.7 reshape.217.gain_ref
  33.5 0.7 reshape.218.bias_ref
  34.1 0.7 reshape.219.wb_ref
  34.8 0.7 reshape.220.wb_ref
  35.5 0.7 reshape.222.gain_ref
  36.2 0.7 reshape.223.bias_ref
  36.8 0.7 reshape.224.pb_ref
  37.5 0.1 reshape_reshape.6
  37.7 0.7 reshape.228.fcb_ref
  38.4 28.9 %all-gather.6.cloned.1.call-done.w_ref = bf16[1280,3840]{1,0:T(8,128)(2,1)} async-done(((bf16[80,3840]{1,0:T(8,128)(2,1)}), bf16[1280,3840]{1,0:T(8,128)(2,1)}) %all-gather.6.cloned.1.call-update) | async-done | bytes 9830416 | tf_op jit(solution)/shard_map/all_gather | solution.py:917
  67.3 44.7 %qkv.1 = (bf16[2056,1280]{1,0:T(8,128)(2,1)}, bf16[1280,2056]{1,0:T(8,128)(2,1)}, bf16[2056,3840]{1,0:T(8,128)(2,1)}) custom-call(bf16[2056,1280]{1,0:T(8,128)(2,1)} %bitcast.74, f32[1,1280]{1,0:T(1,128)} %reshape.217.gain_ref, f32[1,1280]{1,0:T(1,128)} %reshape.218.bias_ref, bf16[1280,3840]{1,0:T(8,128)(2,1)} %all-gather.6.cloned.1.call-done.w_ref, ...), custom_call_target="tpu_custom_call" | custom-call | flops 20211302400 | bytes 60000000 | tf_op jit(solution)/shard_map/qkv/pallas_call | solution.py:344
  112.0 47.8 %attn.1 = (bf16[2056,1280]{1,0:T(8,128)(2,1)}, bf16[2056,1280]{1,0:T(8,128)(2,1)}, f32[8,16,256]{2,1,0:T(8,128)}, f32[8,16,256]{2,1,0:T(8,128)}) custom-call(bf16[2056,3840]{1,0:T(8,128)(2,1)} %get-tuple-element.36.qkv_ref.qkvt_ref, bf16[2056,3840]{1,0:T(8,128)(2,1)} %get-tuple-element.36.qkv_ref.qkvt_ref, ...), custom_call_target="tpu_custom_call" | custom-call | flops 30000001024 | bytes 50000000 | tf_op jit(solution)/shard_map/attn/pallas_call | solution.py:628
  159.8 9.4 %all-gather.10.cloned.1.call-done.fc_ref = bf16[1280,5120]{1,0:T(8,128)(2,1)} async-done(((bf16[80,5120]{1,0:T(8,128)(2,1)}), bf16[1280,5120]{1,0:T(8,128)(2,1)}) %all-gather.10.cloned.1.call-update) | async-done | bytes 13107216 | tf_op jit(solution)/shard_map/all_gather | solution.py:917
  169.3 66.7 %all-gather.12.cloned.1.call-done = bf16[5120,1280]{1,0:T(8,128)(2,1)} async-done(((bf16[320,1280]{1,0:T(8,128)(2,1)}), bf16[5120,1280]{1,0:T(8,128)(2,1)}) %all-gather.12.cloned.1.call-update) | async-done | bytes 13107216 | tf_op jit(solution)/shard_map/all_gather | solution.py:917
  236.0 279.8 %mlp.1 = (bf16[2056,1280]{1,0:T(8,128)(2,1)}, f32[10,2056,128]{2,1,0:T(8,128)}, bf16[2056,1280]{1,0:T(8,128)(2,1)}, f32[80,5120]{1,0:T(8,128)}, f32[320,1280]{1,...) custom-call(bf16[2056,1280]{1,0:T(8,128)(2,1)} %get-tuple-element.38.r_hbm, bf16[2056,1280]{1,0:T(8,128)(2,1)} %bitcast.75, ...), custom_call_target="tpu_custom_call" | custom-call | flops 161690419200 | bytes 150000000 | tf_op jit(solution)/shard_map/mlp/pallas_call | solution.py:502
  515.8 21.6 %outb.1 = (bf16[2056,1280]{1,0:T(8,128)(2,1)}, f32[1280,1280]{1,0:T(8,128)}) custom-call(bf16[2056,1280]{1,0:T(8,128)(2,1)} %get-tuple-element.42.dr_ref, bf16[2056,1280]{1,0:T(8,128)(2,1)} %get-tuple-element.43.o_ref, bf16[1280,1280]{1,0:T(8,128)(2,1)} %all-gather.8.cloned.1.call-done.w_ref), custom_call_target="tpu_custom_call" | custom-call | flops 13474201600 | bytes 30000000 | tf_op jit(solution)/shard_map/outb/pallas_call | solution.py:655
  537.4 72.0 %attn_back.1 = (bf16[2056,3840]{1,0:T(8,128)(2,1)}, f32[1,3840]{1,0:T(1,128)}, f32[80,1280]{1,0:T(8,128)}) custom-call(bf16[2056,3840]{1,0:T(8,128)(2,1)} %get-tuple-element.36.qkv_ref.qkvt_ref, bf16[2056,3840]{1,0:T(8,128)(2,1)} %get-tuple-element.36.qkv_ref.qkvt_ref, bf16[2056,1280]{1,0:T(8,128)(2,1)} %get-tuple-element.44.do_ref.dot_ref, ...), custom_call_target="tpu_custom_call" | custom-call | flops 60000002048 | bytes 50000000 | tf_op jit(solution)/shard_map/attn_back/pallas_call | solution.py:772
  609.3 0.8 reduce
  610.1 0.1 reshape.231
  610.2 0.1 reshape.232
  610.3 0.5 broadcast.14
  610.8 1.4 reduce.4
  612.2 0.1 reshape.233
  612.3 0.1 copy.47
  612.4 0.1 reshape_reshape.7
  612.5 0.1 reshape.234
  612.6 1.0 bitcast_reduce_fusion
  613.6 0.7 select_maximum_fusion.vec_ref
  614.3 102.1 %qkvb.1 = (bf16[2056,1280]{1,0:T(8,128)(2,1)}, f32[80,3840]{1,0:T(8,128)}, f32[16,80]{1,0:T(8,128)}) custom-call(bf16[2056,1280]{1,0:T(8,128)(2,1)} %get-tuple-element.37.x_ref.xt_ref.xim_hbm, f32[10,2056,128]{2,1,0:T(8,128)} %get-tuple-element.40.dr_hbm, f32[1,1280]{1,0:T(1,128)} %reshape.217.gain_ref, f32[16,1280]{1,0:T(8,128)} %select_maximum_fusion.vec_ref, ...), custom_call_target="tpu_custom_call" | custom-call | flops 40422604800 | bytes 80000000 | tf_op jit(solution)/shard_map/qkvb/pallas_call | solution.py:882
  716.4 0.7 slice.47
  717.1 1.4 slice_bitcast_fusion
  718.4 0.7 slice.46
  719.1 0.7 reshape.239
  719.8 0.6 reshape.236
  720.4 2.0 copy.49
  722.4 1.8 copy.50
  724.2 3.1 copy.51
  727.3 5.3 copy.60
  732.7 2.7 copy.61
  735.3 1.0 copy.62
  736.4 0.8 copy.63
  737.1 1.2 copy.64
  (36 shorter events, 0.1 us)
Async XLA Ops:
  7.2 60.1 %all-gather.6.cloned.1.call-start = ((), (), s32[]{:S(2)}) async-start(), calls=%async_computation | async-start | bytes 10444800 | tf_op jit(solution)/shard_map/all_gather | solution.py:917
  9.4 102.6 %all-gather.8.cloned.1.call-start = ((), (), s32[]{:S(2)}) async-start(), calls=%async_computation.1 | async-start | bytes 3481600 | tf_op jit(solution)/shard_map/all_gather | solution.py:917
  11.2 6.2 copy-start.3
  11.2 6.2 copy-start.10
  11.2 6.2 copy-start.4
  11.2 6.2 copy-start.5
  11.3 6.2 copy-start.6
  11.3 6.2 copy-start.7
  11.3 6.2 copy-start.8
  11.3 6.2 copy-start.9
  11.3 158.0 %all-gather.10.cloned.1.call-start = ((), (), s32[]{:S(2)}) async-start(), calls=%async_computation.2 | async-start | bytes 13926400 | tf_op jit(solution)/shard_map/all_gather | solution.py:917
  14.9 221.1 %all-gather.12.cloned.1.call-start = ((), (), s32[]{:S(2)}) async-start(), calls=%async_computation.3 | async-start | bytes 13926400 | tf_op jit(solution)/shard_map/all_gather | solution.py:917
  724.2 8.4 %slice-start = ((s8[5263360]{0:T(1024)(128)(4,1)}), s8[1069056]{0:T(1024)(128)(4,1)S(1)}, s32[]{:S(2)}) async-start(s8[5263360]{0:T(1024)(128)(4,1)} %bitcast.60), calls=%async_computation.4 | async-start | bytes 2138112
  727.3 5.4 slice-start.1
  732.6 2.7 copy-start.1
  732.6 3.7 copy-start.2
  732.7 4.5 copy-start
Sparse Core Ops, SparseCore 0:
  10.8 56.4 all-gather.5
  70.1 32.1 all-gather.7
  105.1 64.0 all-gather.9
  171.9 64.0 all-gather.11

commit v4 on v3

--- a/solution.py
+++ b/solution.py
@@ -14,6 +14,7 @@
 LN_EPS = 1e-5
 VMEM_MAX = 67043328
 LANE, SUBLANE, QUAD, QKV = 128, 8, 4, 3 * WIDTH
+ALL = ...
 LANES = WIDTH // LANE
 ROWS = 32
 
@@ -48,7 +49,7 @@
 
 def clear(*refs):
     for ref in refs:
-        ref[...] = jnp.zeros_like(ref)
+        ref[ALL] = jnp.zeros_like(ref)
 
 
 def step_id():
@@ -84,6 +85,9 @@
     centered = values - mean
     inv = lax.rsqrt(row_mean(centered * centered) + LN_EPS)
     return centered * inv, inv
+
+
+BLOCKS = [slice(a, b) for a, b in ((0, 512), (512, 1024), (1024, 1536), (1536, TOKENS))]
 
 
 def row_tiles(body, step=LANE):
@@ -161,6 +165,7 @@
 
     def __init__(self, rows, cols, cuts):
         self.rows, self.cols, self.cuts = rows, cols, cuts
+        self.parts = range(len(cuts) - 1)
         self.full_shape = jax.ShapeDtypeStruct((2, 2, 2, 2, rows, cols), BF)
 
     def scratch(self):
@@ -192,7 +197,7 @@
         return pltpu.make_async_copy(self.own, self.full.at[(*self.at, self.core)], self.send.at[1])
 
     def begin(self):
-        for part in range(3):
+        for part in self.parts:
             self.hop(1, part).start()
         self.forward(0, 0).start()
         self.keep().start()
@@ -200,17 +205,17 @@
     def turn(self, stage):
         if stage == 1:
             self.keep().wait()
-        for part in range(3):
+        for part in self.parts:
             self.hop(stage, part).wait()
             if stage < 3:
                 self.hop(stage + 1, part).start()
-        for part in range(3):
+        for part in self.parts:
             self.forward(stage, part).start()
 
     def end(self):
         self.forward(0, 0).wait()
         for stage in range(1, QUAD):
-            for part in range(3):
+            for part in self.parts:
                 self.forward(stage, part).wait()
 
 
@@ -316,47 +321,130 @@
 DRAIN = 5
 
 
+PARTS = 16
+SHARD = WIDTH // PARTS
+VECTOR_ROWS = 16
+QKV_ALL = Gather(SHARD, QKV, (0, 1280, 2560, 3840))
+OUT_ALL = Gather(SHARD, WIDTH, (0, 384, 768, 1280))
+FC_ALL = Gather(SHARD, FFN, (0, 1664, 3328, 5120))
+PROJ_ALL = Gather(FFN // PARTS, WIDTH, (0, 384, 896, 1280))
+VECTOR_ALL = Gather(SHARD, LANE, (0, LANE))
+
+
+def open_kernel(x_hbm, rows_ref, wq_ref, wo_ref, xim_hbm, h_hbm, ht_hbm, vec_ref, wq_full, wo_full,
+                x, wide, h, ht, rows, vec_own, vec_full, wq_own, wo_own, sems, *comm):
+    loads = pltpu.make_async_copy(x_hbm, x, sems.at[0])
+    loads.start()
+    clear(rows)
+    rows[:VECTOR_ROWS, :] = rows_ref[ALL]
+    vec_own[ALL] = rows[ALL].T[:SHARD, :].astype(BF)
+    wq_own[ALL] = wq_ref[ALL].astype(BF)
+    wo_own[ALL] = wo_ref[ALL].astype(BF)
+    pairs = [comm[2 * i:2 * i + 2] for i in range(3)]
+    vectors = VECTOR_ALL.bind(vec_own, vec_full, pairs[0])
+    weights = QKV_ALL.bind(wq_own, wq_full, pairs[1]), OUT_ALL.bind(wo_own, wo_full, pairs[2])
+    gathers = (vectors, *weights)
+    vectors.meet()
+    for gather in gathers:
+        gather.begin()
+    loads.wait()
+
+    def widen(r, n):
+        put(wide, r, n, x[pl.ds(r, n), :].astype(F32))
+    row_tiles(widen)
+    for gather in gathers:
+        gather.turn(1)
+
+    def place(r, n, values):
+        x[pl.ds(r, n), :] = values.astype(BF)
+    to_image_order(wide, place)
+    for gather in gathers:
+        gather.turn(2)
+    vectors.turn(3)
+    vectors.end()
+    vec_ref[ALL] = vec_full[ALL].reshape(WIDTH, LANE).astype(F32).T[:VECTOR_ROWS, :]
+    gain, bias = vec_ref[0:1, :], vec_ref[1:2, :]
+
+    def norm(r, n):
+        hat, _ = norm_stats(x[pl.ds(r, n), :].astype(F32))
+        h[pl.ds(r, n), :] = (hat * gain + bias).astype(BF)
+    row_tiles(norm, ROWS)
+    for b in range(IMAGES):
+        ht[:, steps(b, MAIN)] = h[steps(b, MAIN), :].T
+    ht[:, TAIL:TOKENS] = h[TAIL:TOKENS, :].T
+    stores = [pltpu.make_async_copy(src, dst, sems.at[i]) for i, (src, dst) in enumerate(((x, xim_hbm), (h, h_hbm), (ht, ht_hbm)))]
+    for cp in stores:
+        cp.start()
+    for gather in weights:
+        gather.turn(3)
+    for gather in weights:
+        gather.end()
+    for cp in stores:
+        cp.wait()
+
+
+def open_call(x, rows, wq, wo):
+    hbm, vmem = pl.BlockSpec(memory_space=pl.ANY), pl.BlockSpec(memory_space=pltpu.VMEM)
+    return pl.pallas_call(
+        open_kernel,
+        in_specs=[hbm, vmem, vmem, vmem],
+        out_specs=[hbm, hbm, hbm, vmem, hbm, hbm],
+        out_shape=[jax.ShapeDtypeStruct((TOKENS, WIDTH), BF), jax.ShapeDtypeStruct((TOKENS, WIDTH), BF),
+                   jax.ShapeDtypeStruct((WIDTH, TOKENS), BF), jax.ShapeDtypeStruct((VECTOR_ROWS, WIDTH), F32),
+                   QKV_ALL.full_shape, OUT_ALL.full_shape],
+        scratch_shapes=[pltpu.VMEM((TOKENS, WIDTH), BF), pltpu.VMEM((LANES, TOKENS, LANE), F32), pltpu.VMEM((TOKENS, WIDTH), BF),
+                        pltpu.VMEM((WIDTH, TOKENS), BF), pltpu.VMEM((LANE, LANE), F32), pltpu.VMEM((SHARD, LANE), BF),
+                        pltpu.VMEM(VECTOR_ALL.full_shape.shape, BF), pltpu.VMEM((SHARD, QKV), BF), pltpu.VMEM((SHARD, WIDTH), BF),
+                        pltpu.SemaphoreType.DMA((3,))] + VECTOR_ALL.scratch() + QKV_ALL.scratch() + OUT_ALL.scratch(),
+        compiler_params=pltpu.CompilerParams(vmem_limit_bytes=VMEM_MAX, collective_id=3, has_side_effects=True),
+        cost_estimate=cost(1_000_000_000, 60_000_000),
+        name="open",
+    )(x, rows, wq, wo)
+
+
 QKV_N = 768
 
 
-def qkv_kernel(x_ref, gain_ref, bias_ref, w_ref, wb_ref, xim_ref, ht_ref, qkv_ref, wide, h_ref):
-    @pl.when(step_id() == 0)
-    def _():
-        def widen(r, n):
-            put(wide, r, n, x_ref[pl.ds(r, n), :].astype(F32))
-        row_tiles(widen)
-        gain, bias = gain_ref[...], bias_ref[...]
-
-        def place(r, n, values):
-            xim_ref[pl.ds(r, n), :] = values.astype(BF)
-            hat, _ = norm_stats(values)
-            h_ref[pl.ds(r, n), :] = (hat * gain + bias).astype(BF)
-        to_image_order(wide, place, ROWS)
-        for b in range(IMAGES):
-            ht_ref[:, steps(b, MAIN)] = h_ref[steps(b, MAIN), :].T
-        ht_ref[:, TAIL:TOKENS] = h_ref[TAIL:TOKENS, :].T
-    qkv_ref[...] = (dot(h_ref[...], w_ref[...]) + wb_ref[...]).astype(BF)
-
-
-def qkv_call(x, gain, bias, w, wb):
-    full = whole(TOKENS, WIDTH)
-    vec = whole(1, WIDTH)
+def qkv_kernel(h_ref, w_ref, wb_ref, own_ref, qkv_ref, full, *sems):
+    t, last = step_id(), pl.num_programs(0) - 1
+    gather = FC_ALL.bind(own_ref, full, sems)
+
+    @pl.when(t == 0)
+    def _():
+        gather.meet()
+        gather.begin()
+
+    @pl.when(t == 1)
+    def _():
+        gather.turn(1)
+
+    @pl.when(t == 3)
+    def _():
+        gather.turn(2)
+    for rows in BLOCKS:
+        qkv_ref[rows, :] = (dot(h_ref[rows, :], w_ref[ALL]) + wb_ref[ALL]).astype(BF)
+
+    @pl.when(t == last)
+    def _():
+        gather.turn(3)
+        gather.end()
+
+
+def qkv_call(h, w, wb, own):
+    hbm = pl.BlockSpec(memory_space=pl.ANY)
     return pl.pallas_call(
         qkv_kernel,
         grid=(QKV // QKV_N,),
-        in_specs=[whole(TOKENS, WIDTH, pipeline_mode=pl.Buffered(1)), vec, vec,
-                  by_cols(WIDTH, QKV_N), by_cols(1, QKV_N)],
-        out_specs=[full, whole(WIDTH, TOKENS), by_cols(TOKENS, QKV_N)],
-        out_shape=[jax.ShapeDtypeStruct((TOKENS, WIDTH), BF), jax.ShapeDtypeStruct((WIDTH, TOKENS), BF),
-                   jax.ShapeDtypeStruct((TOKENS, QKV), BF)],
-        scratch_shapes=[pltpu.VMEM((LANES, TOKENS, LANE), F32), pltpu.VMEM((TOKENS, WIDTH), BF)],
-        compiler_params=pltpu.CompilerParams(dimension_semantics=("arbitrary",), vmem_limit_bytes=VMEM_MAX),
+        in_specs=[whole(TOKENS, WIDTH, pipeline_mode=pl.Buffered(1)), by_cols(WIDTH, QKV_N), by_cols(1, QKV_N), whole(SHARD, FFN)],
+        out_specs=[by_cols(TOKENS, QKV_N), hbm],
+        out_shape=[jax.ShapeDtypeStruct((TOKENS, QKV), BF), FC_ALL.full_shape],
+        scratch_shapes=FC_ALL.scratch(),
+        compiler_params=comm_params(QUAD),
         cost_estimate=cost(2 * TOKENS * WIDTH * QKV, 60_000_000),
         name="qkv",
-    )(x, gain, bias, w, wb)
-
-
-PARTS = 16
+    )(h, w, wb, own)
+
+
 MLP_F = MAIN
 UNITS = MLP_F // PARTS
 MLP_STEPS = FFN // MLP_F
@@ -402,7 +490,7 @@
             dy[pl.ds(r, n), :] = values.astype(BF)
         to_image_order(dn_acc, place, ROWS)
         cp.wait()
-        gain, bias, pb = gain_ref[...], bias_ref[...], pb_ref[...]
+        gain, bias, pb = gain_ref[ALL], bias_ref[ALL], pb_ref[ALL]
 
         def norm(r, n):
             wide_r = n2[pl.ds(r, n), :].astype(F32)
@@ -418,8 +506,8 @@
 
     @pl.when(step < MLP_STEPS)
     def _():
-        fcb = fcb_ref[...]
-        fc, proj = fc_ref[...], proj_ref[...].reshape(MLP_F, WIDTH)
+        fcb = fcb_ref[ALL]
+        fc, proj = fc_ref[ALL], proj_ref[ALL].reshape(MLP_F, WIDTH)
         bias_sum = jnp.zeros((SUBLANE, MLP_F), F32)
         tiles = [(b * MAIN, MAIN) for b in range(IMAGES - 1)] + [((IMAGES - 1) * MAIN, MAIN + IMAGES)]
         pairs = ((ua, da), (ub, db))
@@ -444,14 +532,14 @@
             products(k)
             bias_sum = pointwise(k - 1, bias_sum)
         bias_sum = pointwise(IMAGES - 1, bias_sum)
-        dfcb_ref[...] = col_sum(bias_sum)
-        y_acc[...] += dot(g[...], proj)
+        dfcb_ref[ALL] = col_sum(bias_sum)
+        y_acc[ALL] += dot(g[ALL], proj)
         for c in range(LANES // 2):
-            part = dot_nt(du[...], fc_ref[steps(c, MAIN), :])
+            part = dot_nt(du[ALL], fc_ref[steps(c, MAIN), :])
             dn_acc[2 * c] += part[:, :LANE]
             dn_acc[2 * c + 1] += part[:, LANE:]
-        by_col.put_local(step, dot_tn(g[...], dy[...]))
-        by_row.put_local(step, dot_tn(n2[...], du[...]))
+        by_col.put_local(step, dot_tn(g[ALL], dy[ALL]))
+        by_row.put_local(step, dot_tn(n2[ALL], du[ALL]))
 
     out_copies = [pltpu.make_async_copy(dn_acc, dr_hbm, sem), pltpu.make_async_copy(n2, dr16_hbm, sem)]
     y_copy = pltpu.make_async_copy(dy, y_hbm, sem)
@@ -461,7 +549,7 @@
         cp = pltpu.make_async_copy(r_hbm, n2, sem)
         cp.start()
         cp.wait()
-        gain = gain_ref[...]
+        gain = gain_ref[ALL]
 
         def back(r, n):
             hat, inv = norm_stats(n2[pl.ds(r, n), :].astype(F32))
@@ -556,14 +644,30 @@
     return e * inv, e_self * inv
 
 
-def attn_kernel(qkv_ref, qkvt_ref, x_ref, xt_ref, w_ref, wb_ref, o_hbm, r_hbm, max_ref, inv_ref,
-                tails, o_tail, o_t, ptail, o_buf, r_buf, sems):
+def attn_kernel(qkv_ref, qkvt_ref, x_ref, xt_ref, w_ref, wb_ref, proj_ref, o_hbm, r_hbm, max_ref, inv_ref, full,
+                tails, o_tail, o_t, ptail, o_buf, r_buf, sems, own, *comm):
     b, last = step_id(), pl.num_programs(0) - 1
     slot = b % 2
+    gather = PROJ_ALL.bind(own, full, comm)
 
     @pl.when(b == 0)
     def _():
-        tails[...] = qkvt_ref[...].astype(F32)
+        tails[ALL] = qkvt_ref[ALL].astype(F32)
+        own[ALL] = proj_ref[ALL].astype(BF)
+        gather.meet()
+        gather.begin()
+
+    @pl.when(b == 1)
+    def _():
+        gather.turn(1)
+
+    @pl.when(b == 3)
+    def _():
+        gather.turn(2)
+
+    @pl.when(b == last)
+    def _():
+        gather.turn(3)
 
     heads = head_rows()
     q_t, k_t, v_t = (heads * z for z in thirds(tails, pl.ds(b, 1)))
@@ -593,9 +697,9 @@
         out_copy(o_buf, o_hbm, slot, b - 2, sems, 0).wait()
         out_copy(r_buf, r_hbm, slot, b - 2, sems, 1).wait()
 
-    o = (o_t[...].T + dot_tn(ptail[...].astype(BF), v_t.astype(BF))).astype(BF)
+    o = (o_t[ALL].T + dot_tn(ptail[ALL].astype(BF), v_t.astype(BF))).astype(BF)
     o_buf[slot] = o
-    r_buf[slot] = (x_ref[...].astype(F32) + dot(o, w_ref[...]) + wb_ref[...]).astype(BF)
+    r_buf[slot] = (x_ref[ALL].astype(F32) + dot(o, w_ref[ALL]) + wb_ref[ALL]).astype(BF)
     out_copy(o_buf, o_hbm, slot, b, sems, 0).start()
     out_copy(r_buf, r_hbm, slot, b, sems, 1).start()
 
@@ -603,9 +707,9 @@
     def _():
         for buf, hbm, n in ((o_buf, o_hbm, 0), (r_buf, r_hbm, 1)):
             out_copy(buf, hbm, 1 - slot, b - 1, sems, n).wait()
-        o = o_tail[...].astype(BF)
+        o = o_tail[ALL].astype(BF)
         o_buf[1 - slot, 0:IMAGES, :] = o
-        r_buf[1 - slot, 0:IMAGES, :] = (xt_ref[...].astype(F32) + dot(o, w_ref[...]) + wb_ref[...]).astype(BF)
+        r_buf[1 - slot, 0:IMAGES, :] = (xt_ref[ALL].astype(F32) + dot(o, w_ref[ALL]) + wb_ref[ALL]).astype(BF)
         copies = [pltpu.make_async_copy(buf.at[1 - slot, pl.ds(0, IMAGES)], hbm.at[pl.ds(TAIL, IMAGES)], sems.at[n, 1 - slot])
                   for buf, hbm, n in ((o_buf, o_hbm, 0), (r_buf, r_hbm, 1))]
         for cp in copies:
@@ -614,13 +718,14 @@
             cp.wait()
         for buf, hbm, n in ((o_buf, o_hbm, 0), (r_buf, r_hbm, 1)):
             out_copy(buf, hbm, slot, b, sems, n).wait()
+        gather.end()
 
 
 def out_copy(buf, hbm, slot, b, sems, n):
     return pltpu.make_async_copy(buf.at[slot], hbm.at[pl.ds(pl.multiple_of(b * MAIN, MAIN), MAIN)], sems.at[n, slot])
 
 
-def attn_call(qkv, xim, w, wb):
+def attn_call(qkv, xim, w, wb, proj):
     hbm = pl.BlockSpec(memory_space=pl.ANY)
     main = lambda n: by_rows(MAIN, n)
     tail = lambda n: by_rows(IMAGES, n, lambda i: TAIL // IMAGES)
@@ -629,24 +734,26 @@
         attn_kernel,
         grid=(IMAGES,),
         in_specs=[main(QKV), tail(QKV), main(WIDTH), tail(WIDTH),
-                  whole(WIDTH, WIDTH), whole(1, WIDTH)],
-        out_specs=[hbm, hbm, stat, stat],
+                  whole(WIDTH, WIDTH), whole(1, WIDTH), whole(*proj.shape)],
+        out_specs=[hbm, hbm, stat, stat, hbm],
         out_shape=[jax.ShapeDtypeStruct((TOKENS, WIDTH), BF), jax.ShapeDtypeStruct((TOKENS, WIDTH), BF),
-                   jax.ShapeDtypeStruct((IMAGES, HEADS, MAIN), F32), jax.ShapeDtypeStruct((IMAGES, HEADS, MAIN), F32)],
+                   jax.ShapeDtypeStruct((IMAGES, HEADS, MAIN), F32), jax.ShapeDtypeStruct((IMAGES, HEADS, MAIN), F32),
+                   PROJ_ALL.full_shape],
         scratch_shapes=[pltpu.VMEM((IMAGES, QKV), F32), pltpu.VMEM((IMAGES, WIDTH), F32),
                         pltpu.VMEM((WIDTH, MAIN), F32), pltpu.VMEM((HEADS, MAIN), F32),
-                        pltpu.VMEM((2, MAIN, WIDTH), BF), pltpu.VMEM((2, MAIN, WIDTH), BF), pltpu.SemaphoreType.DMA((2, 2))],
-        compiler_params=pltpu.CompilerParams(dimension_semantics=("arbitrary",), vmem_limit_bytes=VMEM_MAX),
+                        pltpu.VMEM((2, MAIN, WIDTH), BF), pltpu.VMEM((2, MAIN, WIDTH), BF), pltpu.SemaphoreType.DMA((2, 2)),
+                        pltpu.VMEM(proj.shape, BF)] + PROJ_ALL.scratch(),
+        compiler_params=comm_params(5),
         cost_estimate=cost(30_000_000_000, 50_000_000, 8_400_000),
         name="attn",
-    )(qkv, qkv, xim, xim, w, wb)
+    )(qkv, qkv, xim, xim, w, wb, proj)
 
 
 def outb_kernel(dr_ref, o_ref, w_ref, do_ref, dw_ref):
     n = MAIN
     c = step_id()
-    do_ref[...] = dot_nt(dr_ref[...], w_ref[...]).astype(BF)
-    dw_ref[...] = dot_tn(o_ref[...], dr_ref[:, pl.ds(pl.multiple_of(c * n, n), n)])
+    do_ref[ALL] = dot_nt(dr_ref[ALL], w_ref[ALL]).astype(BF)
+    dw_ref[ALL] = dot_tn(o_ref[ALL], dr_ref[:, pl.ds(pl.multiple_of(c * n, n), n)])
 
 
 def outb_call(dr, o, w):
@@ -676,7 +783,7 @@
 
     @pl.when(b < OUT_STEPS)
     def _():
-        by_row.put_local(b, dw_ref[...])
+        by_row.put_local(b, dw_ref[ALL])
 
     @pl.when(b < IMAGES)
     def _():
@@ -694,15 +801,15 @@
 
     @pl.when(b == 0)
     def _():
-        tails[...] = qkvt_ref[...].astype(F32)
-        do_tails[...] = dot_ref[...].astype(F32)
+        tails[ALL] = qkvt_ref[ALL].astype(F32)
+        do_tails[ALL] = dot_ref[ALL].astype(F32)
         clear(dwb_ref)
 
     heads = head_rows()
     q_t, k_t, v_t = (heads * z for z in thirds(tails, pl.ds(b, 1)))
     do_t = heads * do_tails[pl.ds(b, 1), :]
     q, k, v = thirds(qkv_ref)
-    do = do_ref[...]
+    do = do_ref[ALL]
     q_t16, k_t16, v_t16, do_t16 = (z.astype(BF) for z in (q_t, k_t, v_t, do_t))
 
     p, p_self = tail_softmax(dot_nt(q_t16, k), row_sum(q_t * k_t))
@@ -713,8 +820,8 @@
     grad_q = col_sum(dot(ds16, k) * heads + ds_self * k_t)
     grad_k = ds_self * q_t
     grad_v = p_self.astype(BF).astype(F32) * do_t
-    dk[...] = dot_tn(ds16, q_t16)
-    dv[...] = dot_tn(p.astype(BF), do_t16)
+    dk[ALL] = dot_tn(ds16, q_t16)
+    dv[ALL] = dot_tn(p.astype(BF), do_t16)
 
     p_tail = jnp.exp((dot_nt(k_t16, q) - max_ref[0]) * SCALE) * inv_ref[0]
     dp_tail = dot_nt(v_t16, do)
@@ -737,7 +844,7 @@
         dq_t[steps(h, HEAD), :] = dot(k_turned[steps(h, HEAD), :], ds)
         ds_tail[steps(h, 1), :] = p_tail[steps(h, 1), :] * (dp_tail[steps(h, 1), :] - inner) * SCALE
 
-    ds_tail16 = ds_tail[...].astype(BF)
+    ds_tail16 = ds_tail[ALL].astype(BF)
     grad_k = col_sum(grad_k + dot(ds_tail16, q) * heads)
     grad_v = col_sum(grad_v + dot(p_tail.astype(BF), do) * heads)
 
@@ -745,8 +852,8 @@
     def _():
         out_copy(buf, dqkv_hbm, slot, b - 2, sems, 0).wait()
 
-    grad = dq_t[...].T + dot_tn(ds_tail16, k_t16)
-    for n, (main, tail) in enumerate(((grad, grad_q), (dk[...], grad_k), (dv[...], grad_v))):
+    grad = dq_t[ALL].T + dot_tn(ds_tail16, k_t16)
+    for n, (main, tail) in enumerate(((grad, grad_q), (dk[ALL], grad_k), (dv[ALL], grad_v))):
         here = steps(n, WIDTH)
         buf[slot, :, here] = main.astype(BF)
         grad_tails[pl.ds(b, 1), here] = tail
@@ -756,7 +863,7 @@
     @pl.when(b == last)
     def _():
         out_copy(buf, dqkv_hbm, 1 - slot, b - 1, sems, 0).wait()
-        buf[1 - slot, 0:IMAGES, :] = grad_tails[...].astype(BF)
+        buf[1 - slot, 0:IMAGES, :] = grad_tails[ALL].astype(BF)
         cp = pltpu.make_async_copy(buf.at[1 - slot, pl.ds(0, IMAGES)], dqkv_hbm.at[pl.ds(TAIL, IMAGES)], sems.at[0, 1 - slot])
         cp.start()
         cp.wait()
@@ -792,7 +899,6 @@
 QKV_SUM = Exchange(WIDTH // PARTS, QB_N, ROW_CUTS, 0, 2, 1)
 VECTOR_CHUNK = QB_STEPS + 2
 QB_GRID = VECTOR_CHUNK + 2 + QUAD * QKV_SUM.stride
-VECTOR_ROWS = 16
 
 
 def qkvb_kernel(xim_hbm, dr_hbm, gain_ref, vec_ref, ht_ref, dqkv_ref, w_ref, dx_hbm, dw_ref, out_vec_ref,
@@ -808,7 +914,7 @@
         for cp in loads:
             cp.start()
         clear(acc, sums, vec)
-        vec[:VECTOR_ROWS, :] = vec_ref[...]
+        vec[:VECTOR_ROWS, :] = vec_ref[ALL]
 
     def emit(n, exchange, c):
         @pl.when(c < QB_STEPS)
@@ -818,13 +924,13 @@
         @pl.when(c == VECTOR_CHUNK)
         def _():
             exchange.result(c, vec_out)
-            out_vec_ref[...] = vec_out[:, :LANE].T[:VECTOR_ROWS, :]
+            out_vec_ref[ALL] = vec_out[:, :LANE].T[:VECTOR_ROWS, :]
     advance((by_row,), t, lambda c: ((c >= 0) & (c < QB_STEPS)) | (c == VECTOR_CHUNK), emit)
 
     @pl.when(t < QB_STEPS)
     def _():
-        by_row.put_local(t, dot(ht_ref[...], dqkv_ref[...]))
-        acc[...] += dot_nt(dqkv_ref[...], w_ref[...])
+        by_row.put_local(t, dot(ht_ref[ALL], dqkv_ref[ALL]))
+        acc[ALL] += dot_nt(dqkv_ref[ALL], w_ref[ALL])
 
     @pl.when(t == QB_STEPS)
     def _():
@@ -836,7 +942,7 @@
         dn = acc[pl.ds(r, n), :]
         for i, v in enumerate((dn * hat, dn)):
             sums[steps(i, SUBLANE), :] += eights(v)
-        acc[pl.ds(r, n), :] = joined(dr, r, n) + norm_back(dn, hat, inv, gain_ref[...])
+        acc[pl.ds(r, n), :] = joined(dr, r, n) + norm_back(dn, hat, inv, gain_ref[ALL])
 
     @pl.when((t >= QB_STEPS) & (t <= VECTOR_CHUNK))
     def _():
@@ -854,7 +960,7 @@
         back(TAIL, IMAGES)
         for i in range(2):
             vec[VECTOR_ROWS - 2 + i:VECTOR_ROWS - 1 + i, :] = col_sum(sums[steps(i, SUBLANE), :])
-        turned = vec[...].T
+        turned = vec[ALL].T
         by_row.put_local(t, jnp.concatenate([turned, jnp.zeros_like(turned)], axis=1))
 
     @pl.when(t == VECTOR_CHUNK + 1)
@@ -897,9 +1003,6 @@
     )(xim, dr, gain, vec, ht, dqkv, w)
 
 
-VECTORS = (80, 80, 240, 80, 80, 80, 320, 80)
-
-
 def to_steps(v):
     rows = v.shape[0]
     return v.reshape(rows, PARTS, MLP_STEPS, UNITS).swapaxes(1, 2).reshape(rows, FFN)
@@ -913,28 +1016,25 @@
 def solution(mesh):
     specs = (P("fsdp"),) * 14
 
-    def gather(shard):
-        return lax.all_gather(shard.astype(BF), "fsdp", axis=0, tiled=True)
-
     def device_step(resid_in, grad_out, ln1_gain, ln1_bias, qkv_weight, qkv_bias, out_weight, out_bias,
                     ln2_gain, ln2_bias, fc_weight, fc_bias, proj_weight, proj_bias):
-        wq, wo, wf, wp = (gather(w) for w in (qkv_weight, out_weight, to_steps(fc_weight.astype(BF)), proj_weight))
-        packed = jnp.concatenate([ln1_gain, ln1_bias, qkv_bias, out_bias, ln2_gain, ln2_bias, fc_bias, proj_bias])
-        packed = gather(packed[None]).astype(F32)
-        cuts = [sum(VECTORS[:i]) for i in range(len(VECTORS) + 1)]
-        g1, b1, bq, bo, g2, b2, bf, bp = (packed[:, a:b].reshape(1, -1) for a, b in zip(cuts, cuts[1:]))
-
+        rows = jnp.concatenate([ln1_gain, ln1_bias, qkv_bias, out_bias, ln2_gain, ln2_bias, fc_bias, proj_bias]).reshape(-1, SHARD)
+        rows = jnp.pad(rows, ((0, VECTOR_ROWS - len(rows)), (0, LANE - SHARD)))
         x = resid_in.transpose(1, 0, 2).reshape(TOKENS, WIDTH)
         dy = grad_out.transpose(1, 0, 2).reshape(TOKENS, WIDTH)
-        xim, ht, qkv = qkv_call(x, g1, b1, wq, bq)
-        o, r, top, inv = attn_call(qkv, xim, wo, bo)
-        y, dr, dr16, dwf, dwp, dbf, small = mlp_call(r, dy, g2, b2, bp, wf, wp, to_steps(bf))
+        xim, h, ht, rows, wq, wo = open_call(x, rows, qkv_weight, out_weight)
+        wq, wo = wq.reshape(WIDTH, QKV), wo.reshape(WIDTH, WIDTH)
+        bo, g2, b2 = rows[5:6], rows[6:7], rows[7:8]
+        joint = lambda v: v.reshape(-1, PARTS, SHARD).swapaxes(0, 1).reshape(1, -1)
+        qkv, wf = qkv_call(h, wq, joint(rows[2:5]), to_steps(fc_weight.astype(BF)))
+        o, r, top, inv, wp = attn_call(qkv, xim, wo, bo, proj_weight)
+        y, dr, dr16, dwf, dwp, dbf, small = mlp_call(r, dy, g2, b2, rows[12:13], wf.reshape(WIDTH, FFN), wp, to_steps(joint(rows[8:12])))
         do, dwo = outb_call(dr16, o, wo)
         dqkv, dbq, dwo = attn_back_call(qkv, do, top, inv, dwo)
         owned = lambda v: v.reshape(PARTS, -1, WIDTH // PARTS).swapaxes(0, 1).reshape(-1, WIDTH)
         vec = jnp.concatenate([jnp.sum(small.reshape(4, 8, WIDTH), axis=1), owned(dbq), owned(from_steps(dbf))])
         vec = jnp.pad(vec, ((0, VECTOR_ROWS - len(vec)), (0, 0)))
-        dx, dwq, vec = qkvb_call(xim, dr, g1, vec, ht, dqkv, wq)
+        dx, dwq, vec = qkvb_call(xim, dr, rows[:1], vec, ht, dqkv, wq)
         dg2, db2, dbp, dbo = vec[:4]
         dbq, dbf = vec[4:7].reshape(-1), vec[7:11].reshape(-1)
         dg1, db1 = vec[VECTOR_ROWS - 2:]

time: 755 us -> 701 us (0.928)
  waiting for transfers between devices: 105 us -> 0 us
  Pallas kernels: 568 us -> 654 us
  blocking collectives: 15 us -> 0 us
  between operations: 14.6 us -> 1.27 us
    all_gather x4 -> x0, waiting for transfers between devices: 105 us -> none  [gather(): return lax.all_gather(shard.astype(BF), 'fsdp', axis=0, tiled=True)]
    pallas_call x0 -> x1, Pallas kernels: none -> 53.6 us  [open_call(): pl.pallas_call(open_kernel, in_specs=[hbm, vmem, vmem, vmem], out_specs=[...]
    pallas_call x1, Pallas kernels: 47.8 us -> 65.3 us  [attn_call(): pl.pallas_call(attn_kernel, grid=(IMAGES,), in_specs=[main(QKV), tail(QKV...]
    pallas_call x1, Pallas kernels: 44.7 us -> 59.7 us  [qkv_call(): pl.pallas_call(qkv_kernel, grid=(QKV // QKV_N,), in_specs=[whole(TOKENS,...]
    all_gather x1 -> x0, blocking collectives: 15 us -> none  [gather(): return lax.all_gather(shard.astype(BF), 'fsdp', axis=0, tiled=True)]
    unnamed x34 -> x17, local copies, waits for them, and re-layouts: 16 us -> 15.9 us
  transfers between devices with their start and end apart: 4 -> 0, of which waited for: 3 -> 0; matrix products, arithmetic and copies ran while one was open for 2% -> 0% of each run, Pallas kernels for 12% -> 0%
where the time goes in v4:
time: 701 us; the launch traced here: 692 us
  Pallas kernels  654 us (93%)
  local copies, waits for them, and re-layouts  32.9 us (5%)
    pallas_call x1, Pallas kernels, mlp_call(): pl.pallas_call(mlp_kernel, grid=(MLP_STEPS + DRAIN,), in_specs=[hbm, hbm,...  279 us
    pallas_call x1, Pallas kernels, qkvb_call(): pl.pallas_call(qkvb_kernel, grid=(QB_GRID,), in_specs=[hbm, hbm, whole(1,...  102 us
    pallas_call x1, Pallas kernels, attn_back_call(): pl.pallas_call(attn_back_kernel, grid=(OUT_STEPS + DRAIN,), in_specs=[mai...  71.9 us
    pallas_call x1, Pallas kernels, attn_call(): pl.pallas_call(attn_kernel, grid=(IMAGES,), in_specs=[main(QKV), tail(QKV...  65.3 us
    pallas_call x1, Pallas kernels, qkv_call(): pl.pallas_call(qkv_kernel, grid=(QKV // QKV_N,), in_specs=[whole(TOKENS,...  59.7 us
    pallas_call x1, Pallas kernels, open_call(): pl.pallas_call(open_kernel, in_specs=[hbm, vmem, vmem, vmem], out_specs=[...  53.6 us
    pallas_call x1, Pallas kernels, outb_call(): pl.pallas_call(outb_kernel, grid=(WIDTH // n,), in_specs=[full, full, by_...  21.6 us
    unnamed x17, local copies, waits for them, and re-layouts  15.9 us

profile of v4, /device:TPU:0, one launch (start us, length us, event | category | flops | bytes accessed | tf_op | source)
XLA Modules:
  0.0 691.6 jit_solution(6742235792548312943)
XLA Ops:
  0.6 0.9 concatenate.6
  1.5 0.1 reshape.101
  1.6 0.6 pad.8.rows_ref
  2.2 53.6 %open.1 = (bf16[2056,1280]{1,0:T(8,128)(2,1)}, bf16[2056,1280]{1,0:T(8,128)(2,1)}, bf16[1280,2056]{1,0:T(8,128)(2,1)}, f32[16,1280]{1,0:T(8,128)}, bf16[2,2,2,2,...) custom-call(bf16[2056,1280]{1,0:T(8,128)(2,1)} %bitcast.52, f32[16,128]{1,0:T(8,128)} %pad.8.rows_ref, ...), custom_call_target="tpu_custom_call" | custom-call | flops 1000000000 | bytes 60000000 | tf_op jit(solution)/shard_map/open/pallas_call | solution.py:388
  55.8 0.8 slice.35
  56.6 0.1 reshape.103
  56.7 0.7 reshape.104.wb_ref
  57.4 1.8 copy.33
  59.2 0.4 copy.34
  59.6 1.3 copy.35.own_ref
  60.9 59.7 %qkv.1 = (bf16[2056,3840]{1,0:T(8,128)(2,1)}, bf16[2,2,2,2,80,5120]{5,4,3,2,1,0:T(8,128)(2,1)}) custom-call(bf16[2056,1280]{1,0:T(8,128)(2,1)} %get-tuple-element.42.h_ref, bf16[1280,3840]{1,0:T(8,128)(2,1)} %bitcast.65, f32[1,3840]{1,0:T(1,128)} %reshape.104.wb_ref, bf16[80,5120]{1,0:T(8,128)(2,1)} %copy.35.own_ref), custom_call_target="tpu_custom_call" | custom-call | flops 20211302400 | bytes 60000000 | tf_op jit(solution)/shard_map/qkv/pallas_call | solution.py:435
  120.7 1.6 fusion
  122.2 65.3 %attn.1 = (bf16[2056,1280]{1,0:T(8,128)(2,1)}, bf16[2056,1280]{1,0:T(8,128)(2,1)}, f32[8,16,256]{2,1,0:T(8,128)}, f32[8,16,256]{2,1,0:T(8,128)}, bf16[2,2,2,2,320,1280]{5,4,3,2,1,0:T(8,128)(2,1)}) custom-call(bf16[2056,3840]{1,0:T(8,128)(2,1)} %get-tuple-element.45.qkv_ref.qkvt_ref, bf16[2056,3840]{1,0:T(8,128)(2,1)} %get-tuple-element.45.qkv_ref.qkvt_ref, ...), custom_call_target="tpu_custom_call" | custom-call | flops 30000001024 | bytes 50000000 | tf_op jit(solution)/shard_map/attn/pallas_call | solution.py:733
  187.5 0.8 slice.40
  188.3 0.1 reshape.111
  188.4 0.1 reshape_reshape.6
  188.6 0.7 reshape.112.fcb_ref
  189.3 279.2 %mlp.1 = (bf16[2056,1280]{1,0:T(8,128)(2,1)}, f32[10,2056,128]{2,1,0:T(8,128)}, bf16[2056,1280]{1,0:T(8,128)(2,1)}, f32[80,5120]{1,0:T(8,128)}, f32[320,1280]{1,...) custom-call(bf16[2056,1280]{1,0:T(8,128)(2,1)} %get-tuple-element.48.r_hbm, bf16[2056,1280]{1,0:T(8,128)(2,1)} %bitcast.67, ...), custom_call_target="tpu_custom_call" | custom-call | flops 161690419200 | bytes 150000000 | tf_op jit(solution)/shard_map/mlp/pallas_call | solution.py:590
  468.6 21.6 %outb.1 = (bf16[2056,1280]{1,0:T(8,128)(2,1)}, f32[1280,1280]{1,0:T(8,128)}) custom-call(bf16[2056,1280]{1,0:T(8,128)(2,1)} %get-tuple-element.54.dr_ref, bf16[2056,1280]{1,0:T(8,128)(2,1)} %get-tuple-element.55.o_ref, bf16[1280,1280]{1,0:T(8,128)(2,1)} %bitcast.69), custom_call_target="tpu_custom_call" | custom-call | flops 13474201600 | bytes 30000000 | tf_op jit(solution)/shard_map/outb/pallas_call | solution.py:762
  490.1 71.9 %attn_back.1 = (bf16[2056,3840]{1,0:T(8,128)(2,1)}, f32[1,3840]{1,0:T(1,128)}, f32[80,1280]{1,0:T(8,128)}) custom-call(bf16[2056,3840]{1,0:T(8,128)(2,1)} %get-tuple-element.45.qkv_ref.qkvt_ref, bf16[2056,3840]{1,0:T(8,128)(2,1)} %get-tuple-element.45.qkv_ref.qkvt_ref, bf16[2056,1280]{1,0:T(8,128)(2,1)} %get-tuple-element.56.do_ref.dot_ref, ...), custom_call_target="tpu_custom_call" | custom-call | flops 60000002048 | bytes 50000000 | tf_op jit(solution)/shard_map/attn_back/pallas_call | solution.py:879
  562.1 0.8 reduce
  562.9 0.1 reshape.115
  563.0 0.1 reshape.116
  563.0 0.5 broadcast.16
  563.6 1.4 reduce.4
  565.0 0.1 reshape.117
  565.1 0.1 copy.39
  565.2 0.1 reshape_reshape.7
  565.3 0.1 reshape.118
  565.4 1.0 bitcast_reduce_fusion
  566.3 0.7 select_maximum_fusion.vec_ref
  567.0 102.2 %qkvb.1 = (bf16[2056,1280]{1,0:T(8,128)(2,1)}, f32[80,3840]{1,0:T(8,128)}, f32[16,80]{1,0:T(8,128)}) custom-call(bf16[2056,1280]{1,0:T(8,128)(2,1)} %get-tuple-element.46.x_ref.xt_ref.xim_hbm, f32[10,2056,128]{2,1,0:T(8,128)} %get-tuple-element.52.dr_hbm, f32[1,1280]{1,0:T(1,128)} %get-tuple-element.84.gain_ref, f32[16,1280]{1,0:T(8,128)} %select_maximum_fusion.vec_ref, ...), custom_call_target="tpu_custom_call" | custom-call | flops 40422604800 | bytes 80000000 | tf_op jit(solution)/shard_map/qkvb/pallas_call | solution.py:988
  669.3 0.7 slice.43
  670.0 0.7 reshape.123
  670.6 1.4 slice_bitcast_fusion
  672.0 0.7 slice.42
  672.7 0.6 reshape.120
  673.3 2.0 copy.41
  675.3 1.8 copy.42
  677.1 0.0 slice-start
  677.1 3.1 copy.43
  680.2 0.0 slice-start.1
  680.2 5.3 copy.53
  685.5 0.0 slice-done
  685.5 0.0 slice-done.1
  685.5 0.0 copy-start.1
  685.5 0.0 copy-start.2
  685.5 0.0 copy-start
  685.5 2.7 copy.54
  688.2 0.0 copy-done.1
  688.2 1.0 copy.55
  689.3 0.0 copy-done.2
  689.3 0.8 copy.56
  690.0 0.0 copy-done
  690.0 1.2 copy.57
  (6 shorter events, 0.1 us)
Async XLA Ops:
  677.1 8.4 %slice-start = ((s8[5263360]{0:T(1024)(128)(4,1)}), s8[1069056]{0:T(1024)(128)(4,1)S(1)}, s32[]{:S(2)}) async-start(s8[5263360]{0:T(1024)(128)(4,1)} %bitcast.54), calls=%async_computation | async-start | bytes 2138112
  680.2 5.4 slice-start.1
  685.5 2.7 copy-start.1
  685.5 3.7 copy-start.2
  685.5 4.5 copy-start

commit v5 on v4

--- a/solution.py
+++ b/solution.py
@@ -323,27 +323,31 @@
 
 PARTS = 16
 SHARD = WIDTH // PARTS
-VECTOR_ROWS = 16
-QKV_ALL = Gather(SHARD, QKV, (0, 1280, 2560, 3840))
-OUT_ALL = Gather(SHARD, WIDTH, (0, 384, 768, 1280))
-FC_ALL = Gather(SHARD, FFN, (0, 1664, 3328, 5120))
-PROJ_ALL = Gather(FFN // PARTS, WIDTH, (0, 384, 896, 1280))
+VECTOR_ROWS = PARTS
+MLP_F = MAIN
+UNITS = MLP_F // PARTS
+MLP_STEPS = FFN // MLP_F
+QKV_ALL = Gather(SHARD, QKV, (0, WIDTH, 2 * WIDTH, QKV))
+WIDTH_CUTS = (0, 384, 896, WIDTH)
+EARLY = 10
+FC_ALL = Gather(SHARD, EARLY * MLP_F, (0, 768, 1664, EARLY * MLP_F))
+PROJ_ALL = Gather(EARLY * UNITS, WIDTH, WIDTH_CUTS)
+FC_STEP = Gather(SHARD, MLP_F, (0, LANE, MLP_F))
+PROJ_STEP = Gather(UNITS, WIDTH, WIDTH_CUTS)
+OUT_ALL = Gather(SHARD, WIDTH, WIDTH_CUTS)
 VECTOR_ALL = Gather(SHARD, LANE, (0, LANE))
 
 
-def open_kernel(x_hbm, rows_ref, wq_ref, wo_ref, xim_hbm, h_hbm, ht_hbm, vec_ref, wq_full, wo_full,
-                x, wide, h, ht, rows, vec_own, vec_full, wq_own, wo_own, sems, *comm):
+def open_kernel(x_hbm, rows_ref, wq_ref, xim_hbm, h_hbm, ht_hbm, vec_ref, wq_full,
+                x, wide, h, ht, rows, vec_own, vec_full, wq_own, sems, *comm):
     loads = pltpu.make_async_copy(x_hbm, x, sems.at[0])
     loads.start()
     clear(rows)
     rows[:VECTOR_ROWS, :] = rows_ref[ALL]
     vec_own[ALL] = rows[ALL].T[:SHARD, :].astype(BF)
     wq_own[ALL] = wq_ref[ALL].astype(BF)
-    wo_own[ALL] = wo_ref[ALL].astype(BF)
-    pairs = [comm[2 * i:2 * i + 2] for i in range(3)]
-    vectors = VECTOR_ALL.bind(vec_own, vec_full, pairs[0])
-    weights = QKV_ALL.bind(wq_own, wq_full, pairs[1]), OUT_ALL.bind(wo_own, wo_full, pairs[2])
-    gathers = (vectors, *weights)
+    vectors, weights = VECTOR_ALL.bind(vec_own, vec_full, comm[:2]), QKV_ALL.bind(wq_own, wq_full, comm[2:])
+    gathers = (vectors, weights)
     vectors.meet()
     for gather in gathers:
         gather.begin()
@@ -375,82 +379,80 @@
     stores = [pltpu.make_async_copy(src, dst, sems.at[i]) for i, (src, dst) in enumerate(((x, xim_hbm), (h, h_hbm), (ht, ht_hbm)))]
     for cp in stores:
         cp.start()
-    for gather in weights:
-        gather.turn(3)
-    for gather in weights:
-        gather.end()
+    weights.turn(3)
+    weights.end()
     for cp in stores:
         cp.wait()
 
 
-def open_call(x, rows, wq, wo):
+def open_call(x, rows, wq):
     hbm, vmem = pl.BlockSpec(memory_space=pl.ANY), pl.BlockSpec(memory_space=pltpu.VMEM)
     return pl.pallas_call(
         open_kernel,
-        in_specs=[hbm, vmem, vmem, vmem],
-        out_specs=[hbm, hbm, hbm, vmem, hbm, hbm],
+        in_specs=[hbm, vmem, vmem],
+        out_specs=[hbm, hbm, hbm, vmem, hbm],
         out_shape=[jax.ShapeDtypeStruct((TOKENS, WIDTH), BF), jax.ShapeDtypeStruct((TOKENS, WIDTH), BF),
                    jax.ShapeDtypeStruct((WIDTH, TOKENS), BF), jax.ShapeDtypeStruct((VECTOR_ROWS, WIDTH), F32),
-                   QKV_ALL.full_shape, OUT_ALL.full_shape],
+                   QKV_ALL.full_shape],
         scratch_shapes=[pltpu.VMEM((TOKENS, WIDTH), BF), pltpu.VMEM((LANES, TOKENS, LANE), F32), pltpu.VMEM((TOKENS, WIDTH), BF),
                         pltpu.VMEM((WIDTH, TOKENS), BF), pltpu.VMEM((LANE, LANE), F32), pltpu.VMEM((SHARD, LANE), BF),
-                        pltpu.VMEM(VECTOR_ALL.full_shape.shape, BF), pltpu.VMEM((SHARD, QKV), BF), pltpu.VMEM((SHARD, WIDTH), BF),
-                        pltpu.SemaphoreType.DMA((3,))] + VECTOR_ALL.scratch() + QKV_ALL.scratch() + OUT_ALL.scratch(),
+                        pltpu.VMEM(VECTOR_ALL.full_shape.shape, BF), pltpu.VMEM((SHARD, QKV), BF),
+                        pltpu.SemaphoreType.DMA((3,))] + VECTOR_ALL.scratch() + QKV_ALL.scratch(),
         compiler_params=pltpu.CompilerParams(vmem_limit_bytes=VMEM_MAX, collective_id=3, has_side_effects=True),
         cost_estimate=cost(1_000_000_000, 60_000_000),
         name="open",
-    )(x, rows, wq, wo)
+    )(x, rows, wq)
 
 
 QKV_N = 768
 
 
-def qkv_kernel(h_ref, w_ref, wb_ref, own_ref, qkv_ref, full, *sems):
+def qkv_kernel(h_ref, w_ref, wb_ref, fc_ref, out_ref, qkv_ref, fc_full, out_full, out_own, *sems):
     t, last = step_id(), pl.num_programs(0) - 1
-    gather = FC_ALL.bind(own_ref, full, sems)
+    gathers = OUT_ALL.bind(out_own, out_full, sems[:2]), FC_ALL.bind(fc_ref, fc_full, sems[2:])
 
     @pl.when(t == 0)
     def _():
-        gather.meet()
-        gather.begin()
-
-    @pl.when(t == 1)
-    def _():
-        gather.turn(1)
-
-    @pl.when(t == 3)
-    def _():
-        gather.turn(2)
+        out_own[ALL] = out_ref[ALL].astype(BF)
+        gathers[0].meet()
+        for gather in gathers:
+            gather.begin()
+
+    for stage in (1, 2):
+        @pl.when(t == stage)
+        def _():
+            for gather in gathers:
+                gather.turn(stage)
     for rows in BLOCKS:
         qkv_ref[rows, :] = (dot(h_ref[rows, :], w_ref[ALL]) + wb_ref[ALL]).astype(BF)
 
     @pl.when(t == last)
     def _():
-        gather.turn(3)
-        gather.end()
-
-
-def qkv_call(h, w, wb, own):
+        for gather in gathers:
+            gather.turn(3)
+        for gather in gathers:
+            gather.end()
+
+
+def qkv_call(h, w, wb, fc, out):
     hbm = pl.BlockSpec(memory_space=pl.ANY)
     return pl.pallas_call(
         qkv_kernel,
         grid=(QKV // QKV_N,),
-        in_specs=[whole(TOKENS, WIDTH, pipeline_mode=pl.Buffered(1)), by_cols(WIDTH, QKV_N), by_cols(1, QKV_N), whole(SHARD, FFN)],
-        out_specs=[by_cols(TOKENS, QKV_N), hbm],
-        out_shape=[jax.ShapeDtypeStruct((TOKENS, QKV), BF), FC_ALL.full_shape],
-        scratch_shapes=FC_ALL.scratch(),
+        in_specs=[whole(TOKENS, WIDTH, pipeline_mode=pl.Buffered(1)), by_cols(WIDTH, QKV_N), by_cols(1, QKV_N),
+                  whole(*fc.shape), whole(*out.shape)],
+        out_specs=[by_cols(TOKENS, QKV_N), hbm, hbm],
+        out_shape=[jax.ShapeDtypeStruct((TOKENS, QKV), BF), FC_ALL.full_shape, OUT_ALL.full_shape],
+        scratch_shapes=[pltpu.VMEM(out.shape, BF)] + OUT_ALL.scratch() + FC_ALL.scratch(),
         compiler_params=comm_params(QUAD),
         cost_estimate=cost(2 * TOKENS * WIDTH * QKV, 60_000_000),
         name="qkv",
-    )(h, w, wb, own)
-
-
-MLP_F = MAIN
-UNITS = MLP_F // PARTS
-MLP_STEPS = FFN // MLP_F
+    )(h, w, wb, fc, out)
+
+
 ROW_CUTS = (0, 24, 48, 80)
-FC_SUM = Exchange(WIDTH // PARTS, MLP_F, ROW_CUTS, 0)
-PROJ_SUM = Exchange(UNITS, WIDTH, (0, 512, 896, 1280), 1)
+FC_SUM = Exchange(SHARD, MLP_F, ROW_CUTS, 0)
+PROJ_SUM = Exchange(UNITS, WIDTH, WIDTH_CUTS, 1)
 CDF_P = 0.33
 CDF_C = (0.1326322871417956, 0.11939570820799192, 0.18103829560051796, -0.08904113226212501,
          0.33075919469138065, -0.22023738432274684, 0.0454530347223348)
@@ -467,11 +469,44 @@
     return u * cdf, cdf + u * bell * ((2.0 * math.pi) ** -0.5)
 
 
-def mlp_kernel(r_hbm, dy_hbm, gain_ref, bias_ref, pb_ref, fc_ref, proj_ref, fcb_ref,
-               y_hbm, dr_hbm, dr16_hbm, dfc_ref, dproj_ref, dfcb_ref, small_ref,
-               n2, dy, y_acc, dn_acc, g, du, ua, ub, da, db, sem, *comm):
+def late_weights(step, own, full, now, sems, *comm):
+    def gathers(c):
+        slot = c % GATHER_SLOTS
+        return [kind.bind(own[i].at[c - EARLY], full[i].at[c - EARLY], [sem.at[slot] for sem in comm[2 * i:2 * i + 2]])
+                for i, kind in enumerate((FC_STEP, PROJ_STEP))]
+
+    def fetches(c):
+        return [pltpu.make_async_copy(full[i].at[c - EARLY], now[i].at[c % 2], sems.at[i]) for i in range(2)]
+
+    @pl.when((step >= EARLY) & (step < MLP_STEPS))
+    def _():
+        for cp in fetches(step):
+            cp.wait()
+    for ahead in range(1, 6):
+        c = step + ahead
+
+        @pl.when((c >= EARLY) & (c < MLP_STEPS))
+        def _():
+            for gather in gathers(c):
+                if ahead == 1:
+                    gather.end()
+                elif ahead == 5:
+                    gather.begin()
+                else:
+                    gather.turn(5 - ahead)
+            if ahead == 1:
+                for cp in fetches(c):
+                    cp.start()
+
+
+GATHER_SLOTS = 6
+
+
+def mlp_kernel(r_hbm, dy_hbm, gain_ref, bias_ref, pb_ref, fc_ref, proj_ref, fcb_ref, fc_own, proj_own,
+               y_hbm, dr_hbm, dr16_hbm, dfc_ref, dproj_ref, dfcb_ref, small_ref, fc_full, proj_full,
+               n2, dy, y_acc, dn_acc, g, du, fc_now, proj_now, ua, ub, da, db, sem, sems, *comm):
     step = step_id()
-    by_row, by_col = FC_SUM.bind(comm[:Exchange.COUNT]), PROJ_SUM.bind(comm[Exchange.COUNT:])
+    by_row, by_col = FC_SUM.bind(comm[:Exchange.COUNT]), PROJ_SUM.bind(comm[Exchange.COUNT:2 * Exchange.COUNT])
 
     @pl.when(step == 0)
     def _():
@@ -502,12 +537,19 @@
         clear(small_ref)
 
     outs = (dfc_ref, dproj_ref)
+    late_weights(step, (fc_own, proj_own), (fc_full, proj_full), (fc_now, proj_now), sems, *comm[2 * Exchange.COUNT:])
     advance((by_row, by_col), step, first_chunks(MLP_STEPS), lambda n, exchange, c: exchange.result(c, outs[n]))
 
     @pl.when(step < MLP_STEPS)
     def _():
+        slot = step % 2
+
+        @pl.when(step < EARLY)
+        def _():
+            fc_now[slot] = fc_ref[ALL].reshape(FC_STEP.full_shape.shape)
+            proj_now[slot] = proj_ref[ALL].reshape(PROJ_STEP.full_shape.shape)
         fcb = fcb_ref[ALL]
-        fc, proj = fc_ref[ALL], proj_ref[ALL].reshape(MLP_F, WIDTH)
+        fc, proj = fc_now[slot].reshape(WIDTH, MLP_F), proj_now[slot].reshape(MLP_F, WIDTH)
         bias_sum = jnp.zeros((SUBLANE, MLP_F), F32)
         tiles = [(b * MAIN, MAIN) for b in range(IMAGES - 1)] + [((IMAGES - 1) * MAIN, MAIN + IMAGES)]
         pairs = ((ua, da), (ub, db))
@@ -535,7 +577,7 @@
         dfcb_ref[ALL] = col_sum(bias_sum)
         y_acc[ALL] += dot(g[ALL], proj)
         for c in range(LANES // 2):
-            part = dot_nt(du[ALL], fc_ref[steps(c, MAIN), :])
+            part = dot_nt(du[ALL], fc[steps(c, MAIN), :])
             dn_acc[2 * c] += part[:, :LANE]
             dn_acc[2 * c + 1] += part[:, LANE:]
         by_col.put_local(step, dot_tn(g[ALL], dy[ALL]))
@@ -582,36 +624,41 @@
         y_copy.wait()
 
 
-def mlp_call(r, dy, gain, bias, pb, fc, proj, fcb):
+def mlp_call(r, dy, gain, bias, pb, fc, proj, fcb, fc_own, proj_own):
     hbm = pl.BlockSpec(memory_space=pl.ANY)
     vec = whole(1, WIDTH)
     now = lambda i: jnp.minimum(i, MLP_STEPS - 1)
+    early = lambda i: jnp.minimum(i, EARLY - 1)
     done = lambda i: jnp.maximum(i - DRAIN, 0)
     return pl.pallas_call(
         mlp_kernel,
         grid=(MLP_STEPS + DRAIN,),
-        in_specs=[hbm, hbm, vec, vec, vec, by_cols(WIDTH, MLP_F, now),
-                  pl.BlockSpec((PARTS, None, UNITS, WIDTH), lambda i: (0, now(i), 0, 0)),
-                  by_cols(1, MLP_F, now)],
-        out_specs=[hbm, hbm, hbm, by_cols(WIDTH // PARTS, MLP_F, done),
+        in_specs=[hbm, hbm, vec, vec, vec, by_cols(WIDTH, MLP_F, early),
+                  pl.BlockSpec((PARTS, None, UNITS, WIDTH), lambda i: (0, early(i), 0, 0)),
+                  by_cols(1, MLP_F, now), whole(*fc_own.shape, pipeline_mode=pl.Buffered(1)),
+                  whole(*proj_own.shape, pipeline_mode=pl.Buffered(1))],
+        out_specs=[hbm, hbm, hbm, by_cols(SHARD, MLP_F, done),
                    by_rows(UNITS, WIDTH, done),
-                   by_cols(1, MLP_F, now), whole(32, WIDTH)],
+                   by_cols(1, MLP_F, now), whole(32, WIDTH), hbm, hbm],
         out_shape=[jax.ShapeDtypeStruct((TOKENS, WIDTH), BF), jax.ShapeDtypeStruct((LANES, TOKENS, LANE), F32),
-                   jax.ShapeDtypeStruct((TOKENS, WIDTH), BF), jax.ShapeDtypeStruct((WIDTH // PARTS, FFN), F32),
+                   jax.ShapeDtypeStruct((TOKENS, WIDTH), BF), jax.ShapeDtypeStruct((SHARD, FFN), F32),
                    jax.ShapeDtypeStruct((FFN // PARTS, WIDTH), F32),
-                   jax.ShapeDtypeStruct((1, FFN), F32), jax.ShapeDtypeStruct((32, WIDTH), F32)],
+                   jax.ShapeDtypeStruct((1, FFN), F32), jax.ShapeDtypeStruct((32, WIDTH), F32),
+                   *(jax.ShapeDtypeStruct((MLP_STEPS - EARLY, *kind.full_shape.shape), BF) for kind in (FC_STEP, PROJ_STEP))],
         scratch_shapes=[pltpu.VMEM((TOKENS, WIDTH), BF), pltpu.VMEM((TOKENS, WIDTH), BF),
                         pltpu.VMEM((TOKENS, WIDTH), F32), pltpu.VMEM((LANES, TOKENS, LANE), F32),
-                        pltpu.VMEM((TOKENS, MLP_F), BF), pltpu.VMEM((TOKENS, MLP_F), BF)]
-                       + [pltpu.VMEM((MAIN + IMAGES, MLP_F), F32)] * QUAD + [pltpu.SemaphoreType.DMA]
-                       + FC_SUM.scratch() + PROJ_SUM.scratch(),
+                        pltpu.VMEM((TOKENS, MLP_F), BF), pltpu.VMEM((TOKENS, MLP_F), BF),
+                        *(pltpu.VMEM((2, *kind.full_shape.shape), BF) for kind in (FC_STEP, PROJ_STEP))]
+                       + [pltpu.VMEM((MAIN + IMAGES, MLP_F), F32)] * QUAD + [pltpu.SemaphoreType.DMA, pltpu.SemaphoreType.DMA((2,))]
+                       + FC_SUM.scratch() + PROJ_SUM.scratch() + [pltpu.SemaphoreType.DMA((GATHER_SLOTS, SEMS))] * QUAD,
         compiler_params=comm_params(0),
         cost_estimate=cost(12 * TOKENS * WIDTH * FFN, 150_000_000, TOKENS * FFN),
         name="mlp",
-    )(r, dy, gain, bias, pb, fc, proj.reshape(PARTS, MLP_STEPS, UNITS, WIDTH), fcb)
+    )(r, dy, gain, bias, pb, fc, proj.reshape(PARTS, EARLY, UNITS, WIDTH), fcb, fc_own, proj_own)
 
 
 SCALE = HEAD ** -0.5
+ATTN_COST = cost(40_000_000_000, 50_000_000, 8_400_000)
 
 
 def window(h):
@@ -661,11 +708,11 @@
     def _():
         gather.turn(1)
 
-    @pl.when(b == 3)
+    @pl.when(b == 2)
     def _():
         gather.turn(2)
 
-    @pl.when(b == last)
+    @pl.when(b == QUAD)
     def _():
         gather.turn(3)
 
@@ -744,7 +791,7 @@
                         pltpu.VMEM((2, MAIN, WIDTH), BF), pltpu.VMEM((2, MAIN, WIDTH), BF), pltpu.SemaphoreType.DMA((2, 2)),
                         pltpu.VMEM(proj.shape, BF)] + PROJ_ALL.scratch(),
         compiler_params=comm_params(5),
-        cost_estimate=cost(30_000_000_000, 50_000_000, 8_400_000),
+        cost_estimate=ATTN_COST,
         name="attn",
     )(qkv, qkv, xim, xim, w, wb, proj)
 
@@ -881,30 +928,31 @@
         grid=(OUT_STEPS + DRAIN,),
         in_specs=[main(QKV), tail(QKV), main(WIDTH), tail(WIDTH), stat, stat,
                   by_cols(WIDTH, MAIN, lambda i: jnp.minimum(i, OUT_STEPS - 1))],
-        out_specs=[hbm, whole(1, QKV), by_cols(WIDTH // PARTS, MAIN, lambda i: jnp.maximum(i - DRAIN, 0))],
+        out_specs=[hbm, whole(1, QKV), by_cols(SHARD, MAIN, lambda i: jnp.maximum(i - DRAIN, 0))],
         out_shape=[jax.ShapeDtypeStruct((TOKENS, QKV), BF), jax.ShapeDtypeStruct((1, QKV), F32),
-                   jax.ShapeDtypeStruct((WIDTH // PARTS, WIDTH), F32)],
+                   jax.ShapeDtypeStruct((SHARD, WIDTH), F32)],
         scratch_shapes=[pltpu.VMEM((IMAGES, QKV), F32), pltpu.VMEM((IMAGES, WIDTH), F32),
                         pltpu.VMEM((IMAGES, QKV), F32), pltpu.VMEM((WIDTH, MAIN), F32),
                         pltpu.VMEM((MAIN, WIDTH), F32), pltpu.VMEM((MAIN, WIDTH), F32), pltpu.VMEM((HEADS, MAIN), F32),
                         pltpu.VMEM((2, MAIN, QKV), BF), pltpu.SemaphoreType.DMA((1, 2))] + FC_SUM.scratch(),
         compiler_params=comm_params(1),
-        cost_estimate=cost(60_000_000_000, 50_000_000, 8_400_000),
+        cost_estimate=ATTN_COST,
         name="attn_back",
     )(qkv, qkv, do, do, top, inv, dw)
 
 
 QB_N = MAIN
 QB_STEPS = QKV // QB_N
-QKV_SUM = Exchange(WIDTH // PARTS, QB_N, ROW_CUTS, 0, 2, 1)
-VECTOR_CHUNK = QB_STEPS + 2
-QB_GRID = VECTOR_CHUNK + 2 + QUAD * QKV_SUM.stride
+QKV_SUM = Exchange(SHARD, QB_N, ROW_CUTS, 0, 2)
+VECTOR_SUM = Exchange(3 * SUBLANE, LANE, (0, SUBLANE, 2 * SUBLANE, 3 * SUBLANE), 0)
+VECTOR_STEP = QB_STEPS + 2
+QB_GRID = QB_STEPS + 1 + QUAD * QKV_SUM.stride
 
 
 def qkvb_kernel(xim_hbm, dr_hbm, gain_ref, vec_ref, ht_ref, dqkv_ref, w_ref, dx_hbm, dw_ref, out_vec_ref,
-                acc, dr, xd, vec, vec_out, sums, sems, *comm):
+                acc, dr, xd, vec, sums, sems, *comm):
     t = step_id()
-    by_row = QKV_SUM.bind(comm)
+    by_row, by_vector = QKV_SUM.bind(comm[:Exchange.COUNT]), VECTOR_SUM.bind(comm[Exchange.COUNT:])
     loads = [pltpu.make_async_copy(dr_hbm, dr, sems.at[0]), pltpu.make_async_copy(xim_hbm, xd, sems.at[1])]
     store = pltpu.make_async_copy(xd, dx_hbm, sems.at[1])
 
@@ -913,19 +961,15 @@
         by_row.meet()
         for cp in loads:
             cp.start()
-        clear(acc, sums, vec)
-        vec[:VECTOR_ROWS, :] = vec_ref[ALL]
-
-    def emit(n, exchange, c):
-        @pl.when(c < QB_STEPS)
-        def _():
-            exchange.result(c, dw_ref)
-
-        @pl.when(c == VECTOR_CHUNK)
-        def _():
-            exchange.result(c, vec_out)
-            out_vec_ref[ALL] = vec_out[:, :LANE].T[:VECTOR_ROWS, :]
-    advance((by_row,), t, lambda c: ((c >= 0) & (c < QB_STEPS)) | (c == VECTOR_CHUNK), emit)
+        clear(acc, sums)
+        by_vector.local[0] = jnp.zeros(by_vector.blocks, F32)
+        vec[ALL] = vec_ref[ALL]
+
+    def emit_vectors(n, exchange, c):
+        for part, (rows, _) in enumerate(exchange.parts[:2]):
+            out_vec_ref[rows, :] = exchange.held[3][part][0, :, :SHARD]
+    advance((by_row,), t, first_chunks(QB_STEPS), lambda n, exchange, c: exchange.result(c, dw_ref))
+    advance((by_vector,), t - VECTOR_STEP, first_chunks(1), emit_vectors)
 
     @pl.when(t < QB_STEPS)
     def _():
@@ -944,7 +988,7 @@
             sums[steps(i, SUBLANE), :] += eights(v)
         acc[pl.ds(r, n), :] = joined(dr, r, n) + norm_back(dn, hat, inv, gain_ref[ALL])
 
-    @pl.when((t >= QB_STEPS) & (t <= VECTOR_CHUNK))
+    @pl.when((t >= QB_STEPS) & (t <= VECTOR_STEP))
     def _():
         part = (t - QB_STEPS) * BACK_TILES
 
@@ -955,19 +999,19 @@
             return carry
         lax.fori_loop(0, BACK_TILES, loop, 0)
 
-    @pl.when(t == VECTOR_CHUNK)
+    @pl.when(t == VECTOR_STEP)
     def _():
         back(TAIL, IMAGES)
         for i in range(2):
-            vec[VECTOR_ROWS - 2 + i:VECTOR_ROWS - 1 + i, :] = col_sum(sums[steps(i, SUBLANE), :])
-        turned = vec[ALL].T
-        by_row.put_local(t, jnp.concatenate([turned, jnp.zeros_like(turned)], axis=1))
-
-    @pl.when(t == VECTOR_CHUNK + 1)
+            vec[steps(VECTOR_ROWS - 2 + i, 1), :] = col_sum(sums[steps(i, SUBLANE), :])
+        for d, place in enumerate(itertools.product(range(2), repeat=QUAD)):
+            by_vector.local[(0, *place, pl.ds(0, VECTOR_ROWS), pl.ds(0, SHARD))] = vec[:, steps(d, SHARD)]
+
+    @pl.when(t == VECTOR_STEP + 1)
     def _():
         from_image_order(acc, dr)
 
-    @pl.when(t == VECTOR_CHUNK + 2)
+    @pl.when(t == VECTOR_STEP + 2)
     def _():
         def narrow(r, n):
             xd[pl.ds(r, n), :] = joined(dr, r, n).astype(BF)
@@ -990,13 +1034,13 @@
         grid=(QB_GRID,),
         in_specs=[hbm, hbm, whole(1, WIDTH), whole(VECTOR_ROWS, WIDTH),
                   whole(WIDTH, TOKENS, pipeline_mode=pl.Buffered(1)), by_cols(TOKENS, QB_N, now), by_cols(WIDTH, QB_N, now)],
-        out_specs=[hbm, by_cols(WIDTH // PARTS, QB_N, lambda i: jnp.clip(i - 1 - QUAD * QKV_SUM.stride, 0, QB_STEPS - 1)),
-                   whole(VECTOR_ROWS, WIDTH // PARTS)],
-        out_shape=[jax.ShapeDtypeStruct((TOKENS, WIDTH), BF), jax.ShapeDtypeStruct((WIDTH // PARTS, QKV), F32),
-                   jax.ShapeDtypeStruct((VECTOR_ROWS, WIDTH // PARTS), F32)],
+        out_specs=[hbm, by_cols(SHARD, QB_N, lambda i: jnp.clip(i - 1 - QUAD * QKV_SUM.stride, 0, QB_STEPS - 1)),
+                   whole(VECTOR_ROWS, SHARD)],
+        out_shape=[jax.ShapeDtypeStruct((TOKENS, WIDTH), BF), jax.ShapeDtypeStruct((SHARD, QKV), F32),
+                   jax.ShapeDtypeStruct((VECTOR_ROWS, SHARD), F32)],
         scratch_shapes=[pltpu.VMEM((TOKENS, WIDTH), F32), pltpu.VMEM((LANES, TOKENS, LANE), F32), pltpu.VMEM((TOKENS, WIDTH), BF),
-                        pltpu.VMEM((LANE, WIDTH), F32), pltpu.VMEM((WIDTH // PARTS, QB_N), F32), pltpu.VMEM((16, WIDTH), F32), pltpu.SemaphoreType.DMA((2,))]
-                       + QKV_SUM.scratch(),
+                        pltpu.VMEM((VECTOR_ROWS, WIDTH), F32), pltpu.VMEM((2 * SUBLANE, WIDTH), F32), pltpu.SemaphoreType.DMA((2,))]
+                       + QKV_SUM.scratch() + VECTOR_SUM.scratch(),
         compiler_params=comm_params(2),
         cost_estimate=cost(QUAD * TOKENS * WIDTH * QKV, 80_000_000),
         name="qkvb",
@@ -1020,15 +1064,20 @@
                     ln2_gain, ln2_bias, fc_weight, fc_bias, proj_weight, proj_bias):
         rows = jnp.concatenate([ln1_gain, ln1_bias, qkv_bias, out_bias, ln2_gain, ln2_bias, fc_bias, proj_bias]).reshape(-1, SHARD)
         rows = jnp.pad(rows, ((0, VECTOR_ROWS - len(rows)), (0, LANE - SHARD)))
-        x = resid_in.transpose(1, 0, 2).reshape(TOKENS, WIDTH)
-        dy = grad_out.transpose(1, 0, 2).reshape(TOKENS, WIDTH)
-        xim, h, ht, rows, wq, wo = open_call(x, rows, qkv_weight, out_weight)
-        wq, wo = wq.reshape(WIDTH, QKV), wo.reshape(WIDTH, WIDTH)
+        x = resid_in.swapaxes(0, 1).reshape(TOKENS, WIDTH)
+        dy = grad_out.swapaxes(0, 1).reshape(TOKENS, WIDTH)
+        xim, h, ht, rows, wq = open_call(x, rows, qkv_weight)
+        wq = wq.reshape(WIDTH, QKV)
         bo, g2, b2 = rows[5:6], rows[6:7], rows[7:8]
         joint = lambda v: v.reshape(-1, PARTS, SHARD).swapaxes(0, 1).reshape(1, -1)
-        qkv, wf = qkv_call(h, wq, joint(rows[2:5]), to_steps(fc_weight.astype(BF)))
-        o, r, top, inv, wp = attn_call(qkv, xim, wo, bo, proj_weight)
-        y, dr, dr16, dwf, dwp, dbf, small = mlp_call(r, dy, g2, b2, rows[12:13], wf.reshape(WIDTH, FFN), wp, to_steps(joint(rows[8:12])))
+        fc, proj = to_steps(fc_weight.astype(BF)), proj_weight.astype(BF)
+        cut = EARLY * UNITS
+        qkv, wf, wo = qkv_call(h, wq, joint(rows[2:5]), fc[:, :EARLY * MLP_F], out_weight)
+        wo = wo.reshape(WIDTH, WIDTH)
+        o, r, top, inv, wp = attn_call(qkv, xim, wo, bo, proj_weight[:cut])
+        y, dr, dr16, dwf, dwp, dbf, small, _, _ = mlp_call(
+            r, dy, g2, b2, rows[12:13], wf.reshape(WIDTH, -1), wp, to_steps(joint(rows[8:12])),
+            fc[:, EARLY * MLP_F:].reshape(SHARD, -1, MLP_F).swapaxes(0, 1), proj[cut:].reshape(-1, UNITS, WIDTH))
         do, dwo = outb_call(dr16, o, wo)
         dqkv, dbq, dwo = attn_back_call(qkv, do, top, inv, dwo)
         owned = lambda v: v.reshape(PARTS, -1, WIDTH // PARTS).swapaxes(0, 1).reshape(-1, WIDTH)
@@ -1039,7 +1088,7 @@
         dbq, dbf = vec[4:7].reshape(-1), vec[7:11].reshape(-1)
         dg1, db1 = vec[VECTOR_ROWS - 2:]
         dwf = from_steps(dwf)
-        unturn = lambda t: t.reshape(SEQ, IMAGES, WIDTH).transpose(1, 0, 2)
+        unturn = lambda t: t.reshape(SEQ, IMAGES, WIDTH).swapaxes(0, 1)
         return (unturn(y), unturn(dx), dg1, db1, dwq, dbq, dwo, dbo, dg2, db2, dwf, dbf, dwp, dbp)
 
     return jax.shard_map(device_step, mesh=mesh, in_specs=specs, out_specs=specs, check_vma=False)

time: 701 us -> 704 us (level)
    pallas_call x1, Pallas kernels: 279 us -> 308 us  [mlp_call(): pl.pallas_call(mlp_kernel, grid=(MLP_STEPS + DRAIN,), in_specs=[hbm, hbm,...]
    pallas_call x1, Pallas kernels: 59.7 us -> 44.8 us  [qkv_call(): pl.pallas_call(qkv_kernel, grid=(QKV // QKV_N,), in_specs=[whole(TOKENS,...]
    unnamed x17 -> x18, local copies, waits for them, and re-layouts: 15.9 us -> 16.9 us
where the time goes in v5:
time: 704 us; the launch traced here: 695 us
  Pallas kernels  651 us (92%)
  local copies, waits for them, and re-layouts  39.6 us (6%)
    pallas_call x1, Pallas kernels, mlp_call(): pl.pallas_call(mlp_kernel, grid=(MLP_STEPS + DRAIN,), in_specs=[hbm, hbm,...  308 us
    pallas_call x1, Pallas kernels, qkvb_call(): pl.pallas_call(qkvb_kernel, grid=(QB_GRID,), in_specs=[hbm, hbm, whole(1,...  99.4 us
    pallas_call x1, Pallas kernels, attn_back_call(): pl.pallas_call(attn_back_kernel, grid=(OUT_STEPS + DRAIN,), in_specs=[mai...  72.2 us
    pallas_call x1, Pallas kernels, attn_call(): pl.pallas_call(attn_kernel, grid=(IMAGES,), in_specs=[main(QKV), tail(QKV...  58.4 us
    pallas_call x1, Pallas kernels, open_call(): pl.pallas_call(open_kernel, in_specs=[hbm, vmem, vmem], out_specs=[hbm, h...  47 us
    pallas_call x1, Pallas kernels, qkv_call(): pl.pallas_call(qkv_kernel, grid=(QKV // QKV_N,), in_specs=[whole(TOKENS,...  44.8 us
    pallas_call x1, Pallas kernels, outb_call(): pl.pallas_call(outb_kernel, grid=(WIDTH // n,), in_specs=[full, full, by_...  21.3 us
    unnamed x18, local copies, waits for them, and re-layouts  16.9 us

profile of v5, /device:TPU:0, one launch (start us, length us, event | category | flops | bytes accessed | tf_op | source)
XLA Modules:
  0.0 695.3 jit_solution(5095587023621626380)
XLA Ops:
  0.6 0.9 concatenate.6
  1.5 0.1 reshape.107
  1.6 0.6 pad.8.rows_ref
  2.2 47.0 %open.1 = (bf16[2056,1280]{1,0:T(8,128)(2,1)}, bf16[2056,1280]{1,0:T(8,128)(2,1)}, bf16[1280,2056]{1,0:T(8,128)(2,1)}, f32[16,1280]{1,0:T(8,128)}, bf16[2,2,2,2,80,3840]{5,4,3,2,1,0:T(8,128)(2,1)}) custom-call(bf16[2056,1280]{1,0:T(8,128)(2,1)} %bitcast.59, f32[16,128]{1,0:T(8,128)} %pad.8.rows_ref, f32[80,3840]{1,0:T(8,128)} %wq_ref.1), custom_call_target="tpu_custom_call" | custom-call | flops 1000000000 | bytes 60000000 | tf_op jit(solution)/shard_map/open/pallas_call | solution.py:390
  49.2 0.8 slice.47
  50.0 0.1 reshape.109
  50.1 0.7 reshape.110.wb_ref
  50.8 1.8 copy.33
  52.6 0.4 copy.34
  53.0 0.9 fusion
  53.9 1.0 copy.48.fc_ref
  54.9 44.8 %qkv.1 = (bf16[2056,3840]{1,0:T(8,128)(2,1)}, bf16[2,2,2,2,80,2560]{5,4,3,2,1,0:T(8,128)(2,1)}, bf16[2,2,2,2,80,1280]{5,4,3,2,1,0:T(8,128)(2,1)}) custom-call(bf16[2056,1280]{1,0:T(8,128)(2,1)} %get-tuple-element.42.h_ref, bf16[1280,3840]{1,0:T(8,128)(2,1)} %bitcast.71, f32[1,3840]{1,0:T(1,128)} %reshape.110.wb_ref, bf16[80,2560]{1,0:T(8,128)(2,1)} %copy.48.fc_ref, ...), custom_call_target="tpu_custom_call" | custom-call | flops 20211302400 | bytes 60000000 | tf_op jit(solution)/shard_map/qkv/pallas_call | solution.py:439
  99.7 1.6 fusion.1
  101.3 2.1 slice.50.proj_ref
  103.4 58.4 %attn.1 = (bf16[2056,1280]{1,0:T(8,128)(2,1)}, bf16[2056,1280]{1,0:T(8,128)(2,1)}, f32[8,16,256]{2,1,0:T(8,128)}, f32[8,16,256]{2,1,0:T(8,128)}, bf16[2,2,2,2,160,1280]{5,4,3,2,1,0:T(8,128)(2,1)}) custom-call(bf16[2056,3840]{1,0:T(8,128)(2,1)} %get-tuple-element.45.qkv_ref.qkvt_ref, bf16[2056,3840]{1,0:T(8,128)(2,1)} %get-tuple-element.45.qkv_ref.qkvt_ref, ...), custom_call_target="tpu_custom_call" | custom-call | flops 40000000000 | bytes 50000000 | tf_op jit(solution)/shard_map/attn/pallas_call | solution.py:780
  161.7 0.8 slice.54
  162.5 0.1 reshape.117
  162.6 0.1 reshape_reshape.6
  162.8 0.7 reshape.118.fcb_ref
  163.5 2.1 copy.39
  165.6 1.9 slice.64
  167.5 307.7 %mlp.1 = (bf16[2056,1280]{1,0:T(8,128)(2,1)}, f32[10,2056,128]{2,1,0:T(8,128)}, bf16[2056,1280]{1,0:T(8,128)(2,1)}, f32[80,5120]{1,0:T(8,128)}, f32[320,1280]{1,...) custom-call(bf16[2056,1280]{1,0:T(8,128)(2,1)} %get-tuple-element.48, ...), custom_call_target="tpu_custom_call" | custom-call | flops 161690419200 | bytes 150000000 | tf_op jit(solution)/shard_map/mlp/pallas_call | solution.py:633
  475.2 21.3 %outb.1 = (bf16[2056,1280]{1,0:T(8,128)(2,1)}, f32[1280,1280]{1,0:T(8,128)}) custom-call(bf16[2056,1280]{1,0:T(8,128)(2,1)} %get-tuple-element.54.dr_ref, bf16[2056,1280]{1,0:T(8,128)(2,1)} %get-tuple-element.55.o_ref, bf16[1280,1280]{1,0:T(8,128)(2,1)} %bitcast.77), custom_call_target="tpu_custom_call" | custom-call | flops 13474201600 | bytes 30000000 | tf_op jit(solution)/shard_map/outb/pallas_call | solution.py:809
  496.5 72.2 %attn_back.1 = (bf16[2056,3840]{1,0:T(8,128)(2,1)}, f32[1,3840]{1,0:T(1,128)}, f32[80,1280]{1,0:T(8,128)}) custom-call(bf16[2056,3840]{1,0:T(8,128)(2,1)} %get-tuple-element.45.qkv_ref.qkvt_ref, bf16[2056,3840]{1,0:T(8,128)(2,1)} %get-tuple-element.45.qkv_ref.qkvt_ref, bf16[2056,1280]{1,0:T(8,128)(2,1)} %get-tuple-element.56.do_ref.dot_ref, ...), custom_call_target="tpu_custom_call" | custom-call | flops 40000000000 | bytes 50000000 | tf_op jit(solution)/shard_map/attn_back/pallas_call | solution.py:926
  568.6 0.8 reduce
  569.4 0.1 reshape.123
  569.5 0.1 reshape.124
  569.6 0.5 broadcast.16
  570.1 1.4 reduce.4
  571.5 0.1 reshape.125
  571.6 0.1 copy.41
  571.7 0.1 reshape_reshape.7
  571.8 0.1 reshape.126
  571.9 1.0 bitcast_reduce_fusion
  572.9 0.7 select_maximum_fusion.vec_ref
  573.5 99.4 %qkvb.1 = (bf16[2056,1280]{1,0:T(8,128)(2,1)}, f32[80,3840]{1,0:T(8,128)}, f32[16,80]{1,0:T(8,128)}) custom-call(bf16[2056,1280]{1,0:T(8,128)(2,1)} %get-tuple-element.46.x_ref.xt_ref.xim_hbm, f32[10,2056,128]{2,1,0:T(8,128)} %get-tuple-element.52.dr_hbm, f32[1,1280]{1,0:T(1,128)} %get-tuple-element.86.gain_ref, f32[16,1280]{1,0:T(8,128)} %select_maximum_fusion.vec_ref, ...), custom_call_target="tpu_custom_call" | custom-call | flops 40422604800 | bytes 80000000 | tf_op jit(solution)/shard_map/qkvb/pallas_call | solution.py:1032
  672.9 0.7 slice.59
  673.6 0.7 reshape.131
  674.3 1.4 slice_bitcast_fusion
  675.7 0.7 slice.58
  676.4 0.6 reshape.128
  677.0 2.0 copy.43
  679.0 1.8 copy.44
  680.8 0.0 slice-start
  680.8 3.1 copy.45
  683.9 0.0 slice-start.1
  683.9 5.3 copy.58
  689.2 0.0 slice-done
  689.2 0.0 slice-done.1
  689.2 0.0 copy-start.1
  689.2 0.0 copy-start.2
  689.2 0.0 copy-start
  689.2 2.7 copy.59
  691.9 0.0 copy-done.1
  691.9 1.0 copy.60
  693.0 0.0 copy-done.2
  693.0 0.8 copy.61
  693.7 0.0 copy-done
  693.7 1.2 copy.62
  (6 shorter events, 0.1 us)
Async XLA Ops:
  680.8 8.4 %slice-start = ((s8[5263360]{0:T(1024)(128)(4,1)}), s8[1069056]{0:T(1024)(128)(4,1)S(1)}, s32[]{:S(2)}) async-start(s8[5263360]{0:T(1024)(128)(4,1)} %bitcast.56), calls=%async_computation | async-start | bytes 2138112
  683.9 5.4 slice-start.1
  689.2 2.7 copy-start.1
  689.2 3.7 copy-start.2
  689.2 4.5 copy-start

commit v6 on v4

--- a/solution.py
+++ b/solution.py
@@ -96,6 +96,19 @@
         return carry
     lax.fori_loop(0, TAIL // step, loop, 0)
     body(TAIL, IMAGES)
+
+
+def back_part(body, part):
+    tiles = -(-TAIL // ROWS // 3)
+
+    def loop(i, carry):
+        tile = part * tiles + i
+
+        @pl.when(tile < TAIL // ROWS)
+        def _():
+            body(pl.multiple_of(tile * ROWS, ROWS), ROWS)
+        return carry
+    lax.fori_loop(0, tiles, loop, 0)
 
 
 def to_image_order(wide, place, step=LANE):
@@ -323,18 +336,23 @@
 
 PARTS = 16
 SHARD = WIDTH // PARTS
-VECTOR_ROWS = 16
-QKV_ALL = Gather(SHARD, QKV, (0, 1280, 2560, 3840))
-OUT_ALL = Gather(SHARD, WIDTH, (0, 384, 768, 1280))
+VECTOR_ROWS = PARTS
+MLP_F = MAIN
+UNITS = MLP_F // PARTS
+MLP_STEPS = FFN // MLP_F
+WIDTH_CUTS = (0, 384, 896, WIDTH)
+QKV_ALL = Gather(SHARD, QKV, (0, WIDTH, 2 * WIDTH, QKV))
+OUT_ALL = Gather(SHARD, WIDTH, WIDTH_CUTS)
 FC_ALL = Gather(SHARD, FFN, (0, 1664, 3328, 5120))
-PROJ_ALL = Gather(FFN // PARTS, WIDTH, (0, 384, 896, 1280))
+PROJ_ALL = Gather(FFN // PARTS, WIDTH, WIDTH_CUTS)
 VECTOR_ALL = Gather(SHARD, LANE, (0, LANE))
 
 
-def open_kernel(x_hbm, rows_ref, wq_ref, wo_ref, xim_hbm, h_hbm, ht_hbm, vec_ref, wq_full, wo_full,
-                x, wide, h, ht, rows, vec_own, vec_full, wq_own, wo_own, sems, *comm):
-    loads = pltpu.make_async_copy(x_hbm, x, sems.at[0])
-    loads.start()
+def open_kernel(x_hbm, dy_hbm, rows_ref, wq_ref, wo_ref, xim_hbm, dyim_hbm, h_hbm, ht_hbm, vec_ref, wq_full, wo_full,
+                x, dy, wide, h, ht, rows, vec_own, vec_full, wq_own, wo_own, sems, *comm):
+    loads = [pltpu.make_async_copy(src, dst, sems.at[i]) for i, (src, dst) in enumerate(((x_hbm, x), (dy_hbm, dy)))]
+    for cp in loads:
+        cp.start()
     clear(rows)
     rows[:VECTOR_ROWS, :] = rows_ref[ALL]
     vec_own[ALL] = rows[ALL].T[:SHARD, :].astype(BF)
@@ -347,17 +365,21 @@
     vectors.meet()
     for gather in gathers:
         gather.begin()
-    loads.wait()
-
-    def widen(r, n):
-        put(wide, r, n, x[pl.ds(r, n), :].astype(F32))
-    row_tiles(widen)
+    for cp in loads:
+        cp.wait()
+
+    def reorder(tokens):
+        def widen(r, n):
+            put(wide, r, n, tokens[pl.ds(r, n), :].astype(F32))
+        row_tiles(widen)
+
+        def place(r, n, values):
+            tokens[pl.ds(r, n), :] = values.astype(BF)
+        to_image_order(wide, place)
+    reorder(x)
     for gather in gathers:
         gather.turn(1)
-
-    def place(r, n, values):
-        x[pl.ds(r, n), :] = values.astype(BF)
-    to_image_order(wide, place)
+    reorder(dy)
     for gather in gathers:
         gather.turn(2)
     vectors.turn(3)
@@ -371,8 +393,8 @@
     row_tiles(norm, ROWS)
     for b in range(IMAGES):
         ht[:, steps(b, MAIN)] = h[steps(b, MAIN), :].T
-    ht[:, TAIL:TOKENS] = h[TAIL:TOKENS, :].T
-    stores = [pltpu.make_async_copy(src, dst, sems.at[i]) for i, (src, dst) in enumerate(((x, xim_hbm), (h, h_hbm), (ht, ht_hbm)))]
+    ht[:, TAIL:] = h[TAIL:, :].T
+    stores = [pltpu.make_async_copy(src, dst, sems.at[i]) for i, (src, dst) in enumerate(((x, xim_hbm), (dy, dyim_hbm), (h, h_hbm), (ht, ht_hbm)))]
     for cp in stores:
         cp.start()
     for gather in weights:
@@ -383,23 +405,23 @@
         cp.wait()
 
 
-def open_call(x, rows, wq, wo):
+def open_call(x, dy, rows, wq, wo):
     hbm, vmem = pl.BlockSpec(memory_space=pl.ANY), pl.BlockSpec(memory_space=pltpu.VMEM)
     return pl.pallas_call(
         open_kernel,
-        in_specs=[hbm, vmem, vmem, vmem],
-        out_specs=[hbm, hbm, hbm, vmem, hbm, hbm],
-        out_shape=[jax.ShapeDtypeStruct((TOKENS, WIDTH), BF), jax.ShapeDtypeStruct((TOKENS, WIDTH), BF),
+        in_specs=[hbm, hbm, vmem, vmem, vmem],
+        out_specs=[hbm, hbm, hbm, hbm, vmem, hbm, hbm],
+        out_shape=[*[jax.ShapeDtypeStruct((TOKENS, WIDTH), BF)] * 3,
                    jax.ShapeDtypeStruct((WIDTH, TOKENS), BF), jax.ShapeDtypeStruct((VECTOR_ROWS, WIDTH), F32),
                    QKV_ALL.full_shape, OUT_ALL.full_shape],
-        scratch_shapes=[pltpu.VMEM((TOKENS, WIDTH), BF), pltpu.VMEM((LANES, TOKENS, LANE), F32), pltpu.VMEM((TOKENS, WIDTH), BF),
-                        pltpu.VMEM((WIDTH, TOKENS), BF), pltpu.VMEM((LANE, LANE), F32), pltpu.VMEM((SHARD, LANE), BF),
+        scratch_shapes=[pltpu.VMEM((TOKENS, WIDTH), BF), pltpu.VMEM((TOKENS, WIDTH), BF), pltpu.VMEM((LANES, TOKENS, LANE), F32),
+                        pltpu.VMEM((TOKENS, WIDTH), BF), pltpu.VMEM((WIDTH, TOKENS), BF), pltpu.VMEM((LANE, LANE), F32), pltpu.VMEM((SHARD, LANE), BF),
                         pltpu.VMEM(VECTOR_ALL.full_shape.shape, BF), pltpu.VMEM((SHARD, QKV), BF), pltpu.VMEM((SHARD, WIDTH), BF),
-                        pltpu.SemaphoreType.DMA((3,))] + VECTOR_ALL.scratch() + QKV_ALL.scratch() + OUT_ALL.scratch(),
+                        pltpu.SemaphoreType.DMA((QUAD,))] + VECTOR_ALL.scratch() + QKV_ALL.scratch() + OUT_ALL.scratch(),
         compiler_params=pltpu.CompilerParams(vmem_limit_bytes=VMEM_MAX, collective_id=3, has_side_effects=True),
         cost_estimate=cost(1_000_000_000, 60_000_000),
         name="open",
-    )(x, rows, wq, wo)
+    )(x, dy, rows, wq, wo)
 
 
 QKV_N = 768
@@ -445,12 +467,9 @@
     )(h, w, wb, own)
 
 
-MLP_F = MAIN
-UNITS = MLP_F // PARTS
-MLP_STEPS = FFN // MLP_F
 ROW_CUTS = (0, 24, 48, 80)
-FC_SUM = Exchange(WIDTH // PARTS, MLP_F, ROW_CUTS, 0)
-PROJ_SUM = Exchange(UNITS, WIDTH, (0, 512, 896, 1280), 1)
+FC_SUM = Exchange(SHARD, MLP_F, ROW_CUTS, 0)
+PROJ_SUM = Exchange(UNITS, WIDTH, WIDTH_CUTS, 1)
 CDF_P = 0.33
 CDF_C = (0.1326322871417956, 0.11939570820799192, 0.18103829560051796, -0.08904113226212501,
          0.33075919469138065, -0.22023738432274684, 0.0454530347223348)
@@ -467,7 +486,7 @@
     return u * cdf, cdf + u * bell * ((2.0 * math.pi) ** -0.5)
 
 
-def mlp_kernel(r_hbm, dy_hbm, gain_ref, bias_ref, pb_ref, fc_ref, proj_ref, fcb_ref,
+def mlp_kernel(r_hbm, n_hbm, dy_hbm, gain_ref, pb_ref, fc_ref, proj_ref, fcb_ref,
                y_hbm, dr_hbm, dr16_hbm, dfc_ref, dproj_ref, dfcb_ref, small_ref,
                n2, dy, y_acc, dn_acc, g, du, ua, ub, da, db, sem, *comm):
     step = step_id()
@@ -475,31 +494,13 @@
 
     @pl.when(step == 0)
     def _():
+        loads = [pltpu.make_async_copy(n_hbm, n2, sem), pltpu.make_async_copy(dy_hbm, dy, sem)]
+        for cp in loads:
+            cp.start()
         by_row.meet()
-        cp = pltpu.make_async_copy(dy_hbm, n2, sem)
-        cp.start()
-        cp.wait()
-
-        def widen(r, n):
-            put(dn_acc, r, n, n2[pl.ds(r, n), :].astype(F32))
-        row_tiles(widen)
-        cp = pltpu.make_async_copy(r_hbm, n2, sem)
-        cp.start()
-
-        def place(r, n, values):
-            dy[pl.ds(r, n), :] = values.astype(BF)
-        to_image_order(dn_acc, place, ROWS)
-        cp.wait()
-        gain, bias, pb = gain_ref[ALL], bias_ref[ALL], pb_ref[ALL]
-
-        def norm(r, n):
-            wide_r = n2[pl.ds(r, n), :].astype(F32)
-            hat, _ = norm_stats(wide_r)
-            n2[pl.ds(r, n), :] = (hat * gain + bias).astype(BF)
-            y_acc[pl.ds(r, n), :] = wide_r + pb
-            put(dn_acc, r, n, jnp.zeros((n, WIDTH), F32))
-        row_tiles(norm, ROWS)
-        clear(small_ref)
+        clear(small_ref, y_acc, dn_acc)
+        for cp in loads:
+            cp.wait()
 
     outs = (dfc_ref, dproj_ref)
     advance((by_row, by_col), step, first_chunks(MLP_STEPS), lambda n, exchange, c: exchange.result(c, outs[n]))
@@ -541,48 +542,55 @@
         by_col.put_local(step, dot_tn(g[ALL], dy[ALL]))
         by_row.put_local(step, dot_tn(n2[ALL], du[ALL]))
 
+    after = step - MLP_STEPS
+    r_copy = pltpu.make_async_copy(r_hbm, n2, sem)
     out_copies = [pltpu.make_async_copy(dn_acc, dr_hbm, sem), pltpu.make_async_copy(n2, dr16_hbm, sem)]
     y_copy = pltpu.make_async_copy(dy, y_hbm, sem)
 
-    @pl.when(step == MLP_STEPS)
-    def _():
-        cp = pltpu.make_async_copy(r_hbm, n2, sem)
-        cp.start()
-        cp.wait()
-        gain = gain_ref[ALL]
-
-        def back(r, n):
-            hat, inv = norm_stats(n2[pl.ds(r, n), :].astype(F32))
-            dn = joined(dn_acc, r, n)
-            wide_dy = dy[pl.ds(r, n), :].astype(F32)
-            dr = wide_dy + norm_back(dn, hat, inv, gain)
-            put(dn_acc, r, n, dr)
-            n2[pl.ds(r, n), :] = dr.astype(BF)
-            for i, v in enumerate((dn * hat, dn, wide_dy, dr)):
-                small_ref[steps(i, SUBLANE), :] += eights(v)
-        row_tiles(back, ROWS)
+    def back(r, n):
+        wide_r = n2[pl.ds(r, n), :].astype(F32)
+        hat, inv = norm_stats(wide_r)
+        dn = joined(dn_acc, r, n)
+        wide_dy = dy[pl.ds(r, n), :].astype(F32)
+        dr = wide_dy + norm_back(dn, hat, inv, gain_ref[ALL])
+        put(dn_acc, r, n, dr)
+        n2[pl.ds(r, n), :] = dr.astype(BF)
+        y_acc[pl.ds(r, n), :] += wide_r + pb_ref[ALL]
+        for i, v in enumerate((dn * hat, dn, wide_dy, dr)):
+            small_ref[steps(i, SUBLANE), :] += eights(v)
+
+    @pl.when(after == 0)
+    def _():
+        r_copy.start()
+        r_copy.wait()
+        back(TAIL, IMAGES)
+
+    @pl.when((after >= 0) & (after < 3))
+    def _():
+        back_part(back, after)
+
+    @pl.when(after == 2)
+    def _():
         for cp in out_copies:
             cp.start()
 
-    @pl.when(step == MLP_STEPS + 1)
+    @pl.when(after == 3)
     def _():
         for cp in out_copies:
             cp.wait()
         from_image_order(y_acc, dn_acc)
 
-    @pl.when(step == MLP_STEPS + 2)
-    def _():
         def narrow(r, n):
             dy[pl.ds(r, n), :] = joined(dn_acc, r, n).astype(BF)
         row_tiles(narrow)
         y_copy.start()
 
-    @pl.when(step == MLP_STEPS + 3)
+    @pl.when(after == QUAD)
     def _():
         y_copy.wait()
 
 
-def mlp_call(r, dy, gain, bias, pb, fc, proj, fcb):
+def mlp_call(r, n2, dy, gain, pb, fc, proj, fcb):
     hbm = pl.BlockSpec(memory_space=pl.ANY)
     vec = whole(1, WIDTH)
     now = lambda i: jnp.minimum(i, MLP_STEPS - 1)
@@ -590,14 +598,14 @@
     return pl.pallas_call(
         mlp_kernel,
         grid=(MLP_STEPS + DRAIN,),
-        in_specs=[hbm, hbm, vec, vec, vec, by_cols(WIDTH, MLP_F, now),
+        in_specs=[hbm, hbm, hbm, vec, vec, by_cols(WIDTH, MLP_F, now),
                   pl.BlockSpec((PARTS, None, UNITS, WIDTH), lambda i: (0, now(i), 0, 0)),
                   by_cols(1, MLP_F, now)],
-        out_specs=[hbm, hbm, hbm, by_cols(WIDTH // PARTS, MLP_F, done),
+        out_specs=[hbm, hbm, hbm, by_cols(SHARD, MLP_F, done),
                    by_rows(UNITS, WIDTH, done),
                    by_cols(1, MLP_F, now), whole(32, WIDTH)],
         out_shape=[jax.ShapeDtypeStruct((TOKENS, WIDTH), BF), jax.ShapeDtypeStruct((LANES, TOKENS, LANE), F32),
-                   jax.ShapeDtypeStruct((TOKENS, WIDTH), BF), jax.ShapeDtypeStruct((WIDTH // PARTS, FFN), F32),
+                   jax.ShapeDtypeStruct((TOKENS, WIDTH), BF), jax.ShapeDtypeStruct((SHARD, FFN), F32),
                    jax.ShapeDtypeStruct((FFN // PARTS, WIDTH), F32),
                    jax.ShapeDtypeStruct((1, FFN), F32), jax.ShapeDtypeStruct((32, WIDTH), F32)],
         scratch_shapes=[pltpu.VMEM((TOKENS, WIDTH), BF), pltpu.VMEM((TOKENS, WIDTH), BF),
@@ -608,10 +616,11 @@
         compiler_params=comm_params(0),
         cost_estimate=cost(12 * TOKENS * WIDTH * FFN, 150_000_000, TOKENS * FFN),
         name="mlp",
-    )(r, dy, gain, bias, pb, fc, proj.reshape(PARTS, MLP_STEPS, UNITS, WIDTH), fcb)
+    )(r, n2, dy, gain, pb, fc, proj.reshape(PARTS, MLP_STEPS, UNITS, WIDTH), fcb)
 
 
 SCALE = HEAD ** -0.5
+ATTN_COST = cost(40_000_000_000, 50_000_000, 8_400_000)
 
 
 def window(h):
@@ -644,8 +653,9 @@
     return e * inv, e_self * inv
 
 
-def attn_kernel(qkv_ref, qkvt_ref, x_ref, xt_ref, w_ref, wb_ref, proj_ref, o_hbm, r_hbm, max_ref, inv_ref, full,
-                tails, o_tail, o_t, ptail, o_buf, r_buf, sems, own, *comm):
+def attn_kernel(qkv_ref, qkvt_ref, x_ref, xt_ref, w_ref, wb_ref, gain_ref, bias_ref, proj_ref, o_hbm, r_hbm, n_hbm,
+                max_ref, inv_ref, full,
+                tails, o_tail, o_t, ptail, o_buf, r_buf, n_buf, sa, sb, sems, own, *comm):
     b, last = step_id(), pl.num_programs(0) - 1
     slot = b % 2
     gather = PROJ_ALL.bind(own, full, comm)
@@ -679,44 +689,57 @@
 
     s_tail = dot_nt(k_t.astype(BF), q)
     v_turned = v.T
+    scores = sa, sb
+
+    def next_scores(h):
+        first, wide, _ = window(h)
+        q_h = jnp.where(lane_mask(h), qkv_ref[:, pl.ds(first, wide)], jnp.zeros((), BF))
+        scores[h % 2][ALL] = dot_nt(qkv_ref[:, pl.ds(WIDTH + first, wide)], q_h)
+    next_scores(0)
     for h in range(HEADS):
-        first, wide, _ = window(h)
-        q_h = jnp.where(lane_mask(h), qkv_ref[:, first:first + wide], jnp.zeros((), BF))
-        s = dot_nt(qkv_ref[:, pl.ds(WIDTH + first, wide)], q_h)
-        top = jnp.maximum(col_max(s), s_tail[steps(h, 1), :])
-        e = jnp.exp((s - top) * SCALE)
-        e_tail = jnp.exp((s_tail[steps(h, 1), :] - top) * SCALE)
+        if h + 1 < HEADS:
+            next_scores(h + 1)
+        s, mine = scores[h % 2], steps(h, 1)
+        top = jnp.maximum(col_max(s[ALL]), s_tail[mine, :])
+        e = jnp.exp((s[ALL] - top) * SCALE)
+        e_tail = jnp.exp((s_tail[mine, :] - top) * SCALE)
         inv = 1.0 / (col_sum(e) + e_tail)
-        max_ref[0, steps(h, 1), :] = top
-        inv_ref[0, steps(h, 1), :] = inv
-        ptail[steps(h, 1), :] = e_tail * inv
+        max_ref[0, mine, :] = top
+        inv_ref[0, mine, :] = inv
+        ptail[mine, :] = e_tail * inv
         o_t[steps(h, HEAD), :] = dot(v_turned[steps(h, HEAD), :], (e * inv).astype(BF))
 
+    outs = (o_buf, o_hbm), (r_buf, r_hbm), (n_buf, n_hbm)
+
+    def write(slot, rows, o, x):
+        o_buf[slot, rows, :] = o
+        r = (x.astype(F32) + dot(o, w_ref[ALL]) + wb_ref[ALL]).astype(BF)
+        r_buf[slot, rows, :] = r
+        hat, _ = norm_stats(r.astype(F32))
+        n_buf[slot, rows, :] = (hat * gain_ref[ALL] + bias_ref[ALL]).astype(BF)
+
     @pl.when(b >= 2)
     def _():
-        out_copy(o_buf, o_hbm, slot, b - 2, sems, 0).wait()
-        out_copy(r_buf, r_hbm, slot, b - 2, sems, 1).wait()
+        for n, (buf, hbm) in enumerate(outs):
+            out_copy(buf, hbm, slot, b - 2, sems, n).wait()
 
     o = (o_t[ALL].T + dot_tn(ptail[ALL].astype(BF), v_t.astype(BF))).astype(BF)
-    o_buf[slot] = o
-    r_buf[slot] = (x_ref[ALL].astype(F32) + dot(o, w_ref[ALL]) + wb_ref[ALL]).astype(BF)
-    out_copy(o_buf, o_hbm, slot, b, sems, 0).start()
-    out_copy(r_buf, r_hbm, slot, b, sems, 1).start()
+    write(slot, slice(None), o, x_ref[ALL])
+    for n, (buf, hbm) in enumerate(outs):
+        out_copy(buf, hbm, slot, b, sems, n).start()
 
     @pl.when(b == last)
     def _():
-        for buf, hbm, n in ((o_buf, o_hbm, 0), (r_buf, r_hbm, 1)):
+        for n, (buf, hbm) in enumerate(outs):
             out_copy(buf, hbm, 1 - slot, b - 1, sems, n).wait()
-        o = o_tail[ALL].astype(BF)
-        o_buf[1 - slot, 0:IMAGES, :] = o
-        r_buf[1 - slot, 0:IMAGES, :] = (xt_ref[ALL].astype(F32) + dot(o, w_ref[ALL]) + wb_ref[ALL]).astype(BF)
+        write(1 - slot, slice(IMAGES), o_tail[ALL].astype(BF), xt_ref[ALL])
         copies = [pltpu.make_async_copy(buf.at[1 - slot, pl.ds(0, IMAGES)], hbm.at[pl.ds(TAIL, IMAGES)], sems.at[n, 1 - slot])
-                  for buf, hbm, n in ((o_buf, o_hbm, 0), (r_buf, r_hbm, 1))]
+                  for n, (buf, hbm) in enumerate(outs)]
         for cp in copies:
             cp.start()
         for cp in copies:
             cp.wait()
-        for buf, hbm, n in ((o_buf, o_hbm, 0), (r_buf, r_hbm, 1)):
+        for n, (buf, hbm) in enumerate(outs):
             out_copy(buf, hbm, slot, b, sems, n).wait()
         gather.end()
 
@@ -725,7 +748,7 @@
     return pltpu.make_async_copy(buf.at[slot], hbm.at[pl.ds(pl.multiple_of(b * MAIN, MAIN), MAIN)], sems.at[n, slot])
 
 
-def attn_call(qkv, xim, w, wb, proj):
+def attn_call(qkv, xim, w, wb, gain, bias, proj):
     hbm = pl.BlockSpec(memory_space=pl.ANY)
     main = lambda n: by_rows(MAIN, n)
     tail = lambda n: by_rows(IMAGES, n, lambda i: TAIL // IMAGES)
@@ -734,19 +757,19 @@
         attn_kernel,
         grid=(IMAGES,),
         in_specs=[main(QKV), tail(QKV), main(WIDTH), tail(WIDTH),
-                  whole(WIDTH, WIDTH), whole(1, WIDTH), whole(*proj.shape)],
-        out_specs=[hbm, hbm, stat, stat, hbm],
-        out_shape=[jax.ShapeDtypeStruct((TOKENS, WIDTH), BF), jax.ShapeDtypeStruct((TOKENS, WIDTH), BF),
+                  whole(WIDTH, WIDTH), *[whole(1, WIDTH)] * 3, whole(*proj.shape)],
+        out_specs=[hbm, hbm, hbm, stat, stat, hbm],
+        out_shape=[*[jax.ShapeDtypeStruct((TOKENS, WIDTH), BF)] * 3,
                    jax.ShapeDtypeStruct((IMAGES, HEADS, MAIN), F32), jax.ShapeDtypeStruct((IMAGES, HEADS, MAIN), F32),
                    PROJ_ALL.full_shape],
         scratch_shapes=[pltpu.VMEM((IMAGES, QKV), F32), pltpu.VMEM((IMAGES, WIDTH), F32),
                         pltpu.VMEM((WIDTH, MAIN), F32), pltpu.VMEM((HEADS, MAIN), F32),
-                        pltpu.VMEM((2, MAIN, WIDTH), BF), pltpu.VMEM((2, MAIN, WIDTH), BF), pltpu.SemaphoreType.DMA((2, 2)),
+                        *[pltpu.VMEM((2, MAIN, WIDTH), BF)] * 3, *[pltpu.VMEM((MAIN, MAIN), F32)] * 2, pltpu.SemaphoreType.DMA((3, 2)),
                         pltpu.VMEM(proj.shape, BF)] + PROJ_ALL.scratch(),
         compiler_params=comm_params(5),
-        cost_estimate=cost(30_000_000_000, 50_000_000, 8_400_000),
+        cost_estimate=ATTN_COST,
         name="attn",
-    )(qkv, qkv, xim, xim, w, wb, proj)
+    )(qkv, qkv, xim, xim, w, wb, gain, bias, proj)
 
 
 def outb_kernel(dr_ref, o_ref, w_ref, do_ref, dw_ref):
@@ -772,7 +795,7 @@
 
 
 def attn_back_kernel(qkv_ref, qkvt_ref, do_ref, dot_ref, max_ref, inv_ref, dw_ref, dqkv_hbm, dwb_ref, dwout_ref,
-                     tails, do_tails, grad_tails, dq_t, dk, dv, ds_tail, buf, sems, *comm):
+                     tails, do_tails, grad_tails, dq_t, dk, dv, ds_tail, sa, da, sb, db, buf, sems, *comm):
     b = step_id()
     by_row = FC_SUM.bind(comm)
 
@@ -788,14 +811,14 @@
     @pl.when(b < IMAGES)
     def _():
         image_back(b, qkv_ref, qkvt_ref, do_ref, dot_ref, max_ref, inv_ref, dqkv_hbm, dwb_ref,
-                   tails, do_tails, grad_tails, dq_t, dk, dv, ds_tail, buf, sems)
+                   tails, do_tails, grad_tails, dq_t, dk, dv, ds_tail, ((sa, da), (sb, db)), buf, sems)
 
 
 OUT_STEPS = WIDTH // MAIN
 
 
 def image_back(b, qkv_ref, qkvt_ref, do_ref, dot_ref, max_ref, inv_ref, dqkv_hbm, dwb_ref,
-               tails, do_tails, grad_tails, dq_t, dk, dv, ds_tail, buf, sems):
+               tails, do_tails, grad_tails, dq_t, dk, dv, ds_tail, ahead, buf, sems):
     last = IMAGES - 1
     slot = b % 2
 
@@ -828,21 +851,31 @@
     inner_tail = p_tail * dp_tail
 
     k_turned = k.T
+
+    def masked(h):
+        first, wide, _ = window(h)
+        here, mask = pl.ds(first, wide), lane_mask(h)
+        return here, jnp.where(mask, qkv_ref[:, here], jnp.zeros((), BF)), jnp.where(mask, do_ref[:, here], jnp.zeros((), BF))
+
+    def next_products(h):
+        first, wide, _ = window(h)
+        _, q_h, do_h = masked(h)
+        ahead[h % 2][0][ALL] = dot_nt(qkv_ref[:, pl.ds(WIDTH + first, wide)], q_h)
+        ahead[h % 2][1][ALL] = dot_nt(qkv_ref[:, pl.ds(2 * WIDTH + first, wide)], do_h)
+    next_products(0)
     for h in range(HEADS):
-        first, wide, _ = window(h)
-        here = slice(first, first + wide)
-        mask = lane_mask(h)
-        q_h = jnp.where(mask, qkv_ref[:, here], jnp.zeros((), BF))
-        do_h = jnp.where(mask, do_ref[:, here], jnp.zeros((), BF))
-        s = dot_nt(qkv_ref[:, pl.ds(WIDTH + first, wide)], q_h)
-        dp = dot_nt(qkv_ref[:, pl.ds(2 * WIDTH + first, wide)], do_h)
-        p = jnp.exp((s - max_ref[0, steps(h, 1), :]) * SCALE) * inv_ref[0, steps(h, 1), :]
-        inner = col_sum(p * dp) + inner_tail[steps(h, 1), :]
+        if h + 1 < HEADS:
+            next_products(h + 1)
+        here, q_h, do_h = masked(h)
+        mine = steps(h, 1)
+        s, dp = (ref[ALL] for ref in ahead[h % 2])
+        p = jnp.exp((s - max_ref[0, mine, :]) * SCALE) * inv_ref[0, mine, :]
+        inner = col_sum(p * dp) + inner_tail[mine, :]
         ds = (p * (dp - inner) * SCALE).astype(BF)
         dv[:, here] += dot(p.astype(BF), do_h)
         dk[:, here] += dot(ds, q_h)
         dq_t[steps(h, HEAD), :] = dot(k_turned[steps(h, HEAD), :], ds)
-        ds_tail[steps(h, 1), :] = p_tail[steps(h, 1), :] * (dp_tail[steps(h, 1), :] - inner) * SCALE
+        ds_tail[mine, :] = p_tail[mine, :] * (dp_tail[mine, :] - inner) * SCALE
 
     ds_tail16 = ds_tail[ALL].astype(BF)
     grad_k = col_sum(grad_k + dot(ds_tail16, q) * heads)
@@ -881,30 +914,31 @@
         grid=(OUT_STEPS + DRAIN,),
         in_specs=[main(QKV), tail(QKV), main(WIDTH), tail(WIDTH), stat, stat,
                   by_cols(WIDTH, MAIN, lambda i: jnp.minimum(i, OUT_STEPS - 1))],
-        out_specs=[hbm, whole(1, QKV), by_cols(WIDTH // PARTS, MAIN, lambda i: jnp.maximum(i - DRAIN, 0))],
+        out_specs=[hbm, whole(1, QKV), by_cols(SHARD, MAIN, lambda i: jnp.maximum(i - DRAIN, 0))],
         out_shape=[jax.ShapeDtypeStruct((TOKENS, QKV), BF), jax.ShapeDtypeStruct((1, QKV), F32),
-                   jax.ShapeDtypeStruct((WIDTH // PARTS, WIDTH), F32)],
+                   jax.ShapeDtypeStruct((SHARD, WIDTH), F32)],
         scratch_shapes=[pltpu.VMEM((IMAGES, QKV), F32), pltpu.VMEM((IMAGES, WIDTH), F32),
                         pltpu.VMEM((IMAGES, QKV), F32), pltpu.VMEM((WIDTH, MAIN), F32),
                         pltpu.VMEM((MAIN, WIDTH), F32), pltpu.VMEM((MAIN, WIDTH), F32), pltpu.VMEM((HEADS, MAIN), F32),
-                        pltpu.VMEM((2, MAIN, QKV), BF), pltpu.SemaphoreType.DMA((1, 2))] + FC_SUM.scratch(),
+                        *[pltpu.VMEM((MAIN, MAIN), F32)] * QUAD, pltpu.VMEM((2, MAIN, QKV), BF), pltpu.SemaphoreType.DMA((1, 2))] + FC_SUM.scratch(),
         compiler_params=comm_params(1),
-        cost_estimate=cost(60_000_000_000, 50_000_000, 8_400_000),
+        cost_estimate=ATTN_COST,
         name="attn_back",
     )(qkv, qkv, do, do, top, inv, dw)
 
 
 QB_N = MAIN
 QB_STEPS = QKV // QB_N
-QKV_SUM = Exchange(WIDTH // PARTS, QB_N, ROW_CUTS, 0, 2, 1)
-VECTOR_CHUNK = QB_STEPS + 2
-QB_GRID = VECTOR_CHUNK + 2 + QUAD * QKV_SUM.stride
+QKV_SUM = Exchange(SHARD, QB_N, ROW_CUTS, 0, 2)
+VECTOR_SUM = Exchange(3 * SUBLANE, LANE, (0, SUBLANE, 2 * SUBLANE, 3 * SUBLANE), 0)
+VECTOR_STEP = QB_STEPS + 2
+QB_GRID = QB_STEPS + 1 + QUAD * QKV_SUM.stride
 
 
 def qkvb_kernel(xim_hbm, dr_hbm, gain_ref, vec_ref, ht_ref, dqkv_ref, w_ref, dx_hbm, dw_ref, out_vec_ref,
-                acc, dr, xd, vec, vec_out, sums, sems, *comm):
+                acc, dr, xd, vec, sums, sems, *comm):
     t = step_id()
-    by_row = QKV_SUM.bind(comm)
+    by_row, by_vector = QKV_SUM.bind(comm[:Exchange.COUNT]), VECTOR_SUM.bind(comm[Exchange.COUNT:])
     loads = [pltpu.make_async_copy(dr_hbm, dr, sems.at[0]), pltpu.make_async_copy(xim_hbm, xd, sems.at[1])]
     store = pltpu.make_async_copy(xd, dx_hbm, sems.at[1])
 
@@ -913,19 +947,15 @@
         by_row.meet()
         for cp in loads:
             cp.start()
-        clear(acc, sums, vec)
-        vec[:VECTOR_ROWS, :] = vec_ref[ALL]
-
-    def emit(n, exchange, c):
-        @pl.when(c < QB_STEPS)
-        def _():
-            exchange.result(c, dw_ref)
-
-        @pl.when(c == VECTOR_CHUNK)
-        def _():
-            exchange.result(c, vec_out)
-            out_vec_ref[ALL] = vec_out[:, :LANE].T[:VECTOR_ROWS, :]
-    advance((by_row,), t, lambda c: ((c >= 0) & (c < QB_STEPS)) | (c == VECTOR_CHUNK), emit)
+        clear(acc, sums)
+        by_vector.local[0] = jnp.zeros(by_vector.blocks, F32)
+        vec[ALL] = vec_ref[ALL]
+
+    def emit_vectors(n, exchange, c):
+        for part, (rows, _) in enumerate(exchange.parts[:2]):
+            out_vec_ref[rows, :] = exchange.held[3][part][0, :, :SHARD]
+    advance((by_row,), t, first_chunks(QB_STEPS), lambda n, exchange, c: exchange.result(c, dw_ref))
+    advance((by_vector,), t - VECTOR_STEP, first_chunks(1), emit_vectors)
 
     @pl.when(t < QB_STEPS)
     def _():
@@ -944,30 +974,23 @@
             sums[steps(i, SUBLANE), :] += eights(v)
         acc[pl.ds(r, n), :] = joined(dr, r, n) + norm_back(dn, hat, inv, gain_ref[ALL])
 
-    @pl.when((t >= QB_STEPS) & (t <= VECTOR_CHUNK))
-    def _():
-        part = (t - QB_STEPS) * BACK_TILES
-
-        def loop(i, carry):
-            @pl.when(part + i < TAIL // ROWS)
-            def _():
-                back(pl.multiple_of((part + i) * ROWS, ROWS), ROWS)
-            return carry
-        lax.fori_loop(0, BACK_TILES, loop, 0)
-
-    @pl.when(t == VECTOR_CHUNK)
+    @pl.when((t >= QB_STEPS) & (t <= VECTOR_STEP))
+    def _():
+        back_part(back, t - QB_STEPS)
+
+    @pl.when(t == VECTOR_STEP)
     def _():
         back(TAIL, IMAGES)
         for i in range(2):
-            vec[VECTOR_ROWS - 2 + i:VECTOR_ROWS - 1 + i, :] = col_sum(sums[steps(i, SUBLANE), :])
-        turned = vec[ALL].T
-        by_row.put_local(t, jnp.concatenate([turned, jnp.zeros_like(turned)], axis=1))
-
-    @pl.when(t == VECTOR_CHUNK + 1)
+            vec[steps(VECTOR_ROWS - 2 + i, 1), :] = col_sum(sums[steps(i, SUBLANE), :])
+        for d, place in enumerate(itertools.product(range(2), repeat=QUAD)):
+            by_vector.local[(0, *place, pl.ds(0, VECTOR_ROWS), pl.ds(0, SHARD))] = vec[:, steps(d, SHARD)]
+
+    @pl.when(t == VECTOR_STEP + 1)
     def _():
         from_image_order(acc, dr)
 
-    @pl.when(t == VECTOR_CHUNK + 2)
+    @pl.when(t == VECTOR_STEP + 2)
     def _():
         def narrow(r, n):
             xd[pl.ds(r, n), :] = joined(dr, r, n).astype(BF)
@@ -977,9 +1000,6 @@
     @pl.when(t == QB_GRID - 1)
     def _():
         store.wait()
-
-
-BACK_TILES = -(-TAIL // ROWS // 3)
 
 
 def qkvb_call(xim, dr, gain, vec, ht, dqkv, w):
@@ -990,13 +1010,13 @@
         grid=(QB_GRID,),
         in_specs=[hbm, hbm, whole(1, WIDTH), whole(VECTOR_ROWS, WIDTH),
                   whole(WIDTH, TOKENS, pipeline_mode=pl.Buffered(1)), by_cols(TOKENS, QB_N, now), by_cols(WIDTH, QB_N, now)],
-        out_specs=[hbm, by_cols(WIDTH // PARTS, QB_N, lambda i: jnp.clip(i - 1 - QUAD * QKV_SUM.stride, 0, QB_STEPS - 1)),
-                   whole(VECTOR_ROWS, WIDTH // PARTS)],
-        out_shape=[jax.ShapeDtypeStruct((TOKENS, WIDTH), BF), jax.ShapeDtypeStruct((WIDTH // PARTS, QKV), F32),
-                   jax.ShapeDtypeStruct((VECTOR_ROWS, WIDTH // PARTS), F32)],
+        out_specs=[hbm, by_cols(SHARD, QB_N, lambda i: jnp.clip(i - 1 - QUAD * QKV_SUM.stride, 0, QB_STEPS - 1)),
+                   whole(VECTOR_ROWS, SHARD)],
+        out_shape=[jax.ShapeDtypeStruct((TOKENS, WIDTH), BF), jax.ShapeDtypeStruct((SHARD, QKV), F32),
+                   jax.ShapeDtypeStruct((VECTOR_ROWS, SHARD), F32)],
         scratch_shapes=[pltpu.VMEM((TOKENS, WIDTH), F32), pltpu.VMEM((LANES, TOKENS, LANE), F32), pltpu.VMEM((TOKENS, WIDTH), BF),
-                        pltpu.VMEM((LANE, WIDTH), F32), pltpu.VMEM((WIDTH // PARTS, QB_N), F32), pltpu.VMEM((16, WIDTH), F32), pltpu.SemaphoreType.DMA((2,))]
-                       + QKV_SUM.scratch(),
+                        pltpu.VMEM((VECTOR_ROWS, WIDTH), F32), pltpu.VMEM((2 * SUBLANE, WIDTH), F32), pltpu.SemaphoreType.DMA((2,))]
+                       + QKV_SUM.scratch() + VECTOR_SUM.scratch(),
         compiler_params=comm_params(2),
         cost_estimate=cost(QUAD * TOKENS * WIDTH * QKV, 80_000_000),
         name="qkvb",
@@ -1020,15 +1040,15 @@
                     ln2_gain, ln2_bias, fc_weight, fc_bias, proj_weight, proj_bias):
         rows = jnp.concatenate([ln1_gain, ln1_bias, qkv_bias, out_bias, ln2_gain, ln2_bias, fc_bias, proj_bias]).reshape(-1, SHARD)
         rows = jnp.pad(rows, ((0, VECTOR_ROWS - len(rows)), (0, LANE - SHARD)))
-        x = resid_in.transpose(1, 0, 2).reshape(TOKENS, WIDTH)
-        dy = grad_out.transpose(1, 0, 2).reshape(TOKENS, WIDTH)
-        xim, h, ht, rows, wq, wo = open_call(x, rows, qkv_weight, out_weight)
+        x = resid_in.swapaxes(0, 1).reshape(TOKENS, WIDTH)
+        dy = grad_out.swapaxes(0, 1).reshape(TOKENS, WIDTH)
+        xim, dyim, h, ht, rows, wq, wo = open_call(x, dy, rows, qkv_weight, out_weight)
         wq, wo = wq.reshape(WIDTH, QKV), wo.reshape(WIDTH, WIDTH)
         bo, g2, b2 = rows[5:6], rows[6:7], rows[7:8]
         joint = lambda v: v.reshape(-1, PARTS, SHARD).swapaxes(0, 1).reshape(1, -1)
         qkv, wf = qkv_call(h, wq, joint(rows[2:5]), to_steps(fc_weight.astype(BF)))
-        o, r, top, inv, wp = attn_call(qkv, xim, wo, bo, proj_weight)
-        y, dr, dr16, dwf, dwp, dbf, small = mlp_call(r, dy, g2, b2, rows[12:13], wf.reshape(WIDTH, FFN), wp, to_steps(joint(rows[8:12])))
+        o, r, n2, top, inv, wp = attn_call(qkv, xim, wo, bo, g2, b2, proj_weight)
+        y, dr, dr16, dwf, dwp, dbf, small = mlp_call(r, n2, dyim, g2, rows[12:13], wf.reshape(WIDTH, FFN), wp, to_steps(joint(rows[8:12])))
         do, dwo = outb_call(dr16, o, wo)
         dqkv, dbq, dwo = attn_back_call(qkv, do, top, inv, dwo)
         owned = lambda v: v.reshape(PARTS, -1, WIDTH // PARTS).swapaxes(0, 1).reshape(-1, WIDTH)
@@ -1039,7 +1059,7 @@
         dbq, dbf = vec[4:7].reshape(-1), vec[7:11].reshape(-1)
         dg1, db1 = vec[VECTOR_ROWS - 2:]
         dwf = from_steps(dwf)
-        unturn = lambda t: t.reshape(SEQ, IMAGES, WIDTH).transpose(1, 0, 2)
+        unturn = lambda t: t.reshape(SEQ, IMAGES, WIDTH).swapaxes(0, 1)
         return (unturn(y), unturn(dx), dg1, db1, dwq, dbq, dwo, dbo, dg2, db2, dwf, dbf, dwp, dbp)
 
     return jax.shard_map(device_step, mesh=mesh, in_specs=specs, out_specs=specs, check_vma=False)

time: 701 us -> 663 us (0.946)
  Pallas kernels: 654 us -> 619 us
    pallas_call x1, Pallas kernels: 279 us -> 259 us  [mlp_call(): pl.pallas_call(mlp_kernel, grid=(MLP_STEPS + DRAIN,), in_specs=[hbm, hbm,...]
    pallas_call x1, Pallas kernels: 71.9 us -> 58.3 us  [attn_back_call(): pl.pallas_call(attn_back_kernel, grid=(OUT_STEPS + DRAIN,), in_specs=[mai...]
where the time goes in v6:
time: 663 us; the launch traced here: 656 us
  Pallas kernels  619 us (93%)
  local copies, waits for them, and re-layouts  32.9 us (5%)
    pallas_call x1, Pallas kernels, mlp_call(): pl.pallas_call(mlp_kernel, grid=(MLP_STEPS + DRAIN,), in_specs=[hbm, hbm,...  259 us
    pallas_call x1, Pallas kernels, qkvb_call(): pl.pallas_call(qkvb_kernel, grid=(QB_GRID,), in_specs=[hbm, hbm, whole(1,...  99.6 us
    pallas_call x1, Pallas kernels, attn_call(): pl.pallas_call(attn_kernel, grid=(IMAGES,), in_specs=[main(QKV), tail(QKV...  65.5 us
    pallas_call x1, Pallas kernels, qkv_call(): pl.pallas_call(qkv_kernel, grid=(QKV // QKV_N,), in_specs=[whole(TOKENS,...  60.3 us
    pallas_call x1, Pallas kernels, attn_back_call(): pl.pallas_call(attn_back_kernel, grid=(OUT_STEPS + DRAIN,), in_specs=[mai...  58.3 us
    pallas_call x1, Pallas kernels, open_call(): pl.pallas_call(open_kernel, in_specs=[hbm, hbm, vmem, vmem, vmem], out_sp...  54.6 us
    pallas_call x1, Pallas kernels, outb_call(): pl.pallas_call(outb_kernel, grid=(WIDTH // n,), in_specs=[full, full, by_...  21.4 us
    unnamed x17, local copies, waits for them, and re-layouts  15.9 us

profile of v6, /device:TPU:0, one launch (start us, length us, event | category | flops | bytes accessed | tf_op | source)
XLA Modules:
  0.0 656.3 jit_solution(15578625699157813822)
XLA Ops:
  0.6 0.9 concatenate.6
  1.5 0.1 reshape.102
  1.6 0.6 pad.8.rows_ref
  2.2 54.6 %open.1 = (bf16[2056,1280]{1,0:T(8,128)(2,1)}, bf16[2056,1280]{1,0:T(8,128)(2,1)}, bf16[2056,1280]{1,0:T(8,128)(2,1)}, bf16[1280,2056]{1,0:T(8,128)(2,1)}, f32[1...) custom-call(bf16[2056,1280]{1,0:T(8,128)(2,1)} %bitcast.52, ...), custom_call_target="tpu_custom_call" | custom-call | flops 1000000000 | bytes 60000000 | tf_op jit(solution)/shard_map/open/pallas_call | solution.py:410
  56.8 0.8 slice.35
  57.5 0.1 reshape.104
  57.7 0.7 reshape.105.wb_ref
  58.4 1.8 copy.33
  60.2 0.4 copy.34
  60.6 1.3 copy.35.own_ref
  61.9 60.3 %qkv.1 = (bf16[2056,3840]{1,0:T(8,128)(2,1)}, bf16[2,2,2,2,80,5120]{5,4,3,2,1,0:T(8,128)(2,1)}) custom-call(bf16[2056,1280]{1,0:T(8,128)(2,1)} %get-tuple-element.44.h_ref, bf16[1280,3840]{1,0:T(8,128)(2,1)} %bitcast.66, f32[1,3840]{1,0:T(1,128)} %reshape.105.wb_ref, bf16[80,5120]{1,0:T(8,128)(2,1)} %copy.35.own_ref), custom_call_target="tpu_custom_call" | custom-call | flops 20211302400 | bytes 60000000 | tf_op jit(solution)/shard_map/qkv/pallas_call | solution.py:457
  122.2 1.6 fusion
  123.8 65.5 %attn.1 = (bf16[2056,1280]{1,0:T(8,128)(2,1)}, bf16[2056,1280]{1,0:T(8,128)(2,1)}, bf16[2056,1280]{1,0:T(8,128)(2,1)}, f32[8,16,256]{2,1,0:T(8,128)}, f32[8,16,2...) custom-call(bf16[2056,3840]{1,0:T(8,128)(2,1)} %get-tuple-element.47.qkv_ref.qkvt_ref, ...), custom_call_target="tpu_custom_call" | custom-call | flops 40000000000 | bytes 50000000 | tf_op jit(solution)/shard_map/attn/pallas_call | solution.py:756
  189.3 0.8 slice.40
  190.1 0.1 reshape.111
  190.2 0.1 reshape_reshape.6
  190.4 0.7 reshape.112.fcb_ref
  191.1 258.8 %mlp.1 = (bf16[2056,1280]{1,0:T(8,128)(2,1)}, f32[10,2056,128]{2,1,0:T(8,128)}, bf16[2056,1280]{1,0:T(8,128)(2,1)}, f32[80,5120]{1,0:T(8,128)}, f32[320,1280]{1,...) custom-call(bf16[2056,1280]{1,0:T(8,128)(2,1)} %get-tuple-element.50.r_hbm, ...), custom_call_target="tpu_custom_call" | custom-call | flops 161690419200 | bytes 150000000 | tf_op jit(solution)/shard_map/mlp/pallas_call | solution.py:598
  449.9 21.4 %outb.1 = (bf16[2056,1280]{1,0:T(8,128)(2,1)}, f32[1280,1280]{1,0:T(8,128)}) custom-call(bf16[2056,1280]{1,0:T(8,128)(2,1)} %get-tuple-element.58.dr_ref, bf16[2056,1280]{1,0:T(8,128)(2,1)} %get-tuple-element.59.o_ref, bf16[1280,1280]{1,0:T(8,128)(2,1)} %bitcast.69), custom_call_target="tpu_custom_call" | custom-call | flops 13474201600 | bytes 30000000 | tf_op jit(solution)/shard_map/outb/pallas_call | solution.py:785
  471.3 58.3 %attn_back.1 = (bf16[2056,3840]{1,0:T(8,128)(2,1)}, f32[1,3840]{1,0:T(1,128)}, f32[80,1280]{1,0:T(8,128)}) custom-call(bf16[2056,3840]{1,0:T(8,128)(2,1)} %get-tuple-element.47.qkv_ref.qkvt_ref, bf16[2056,3840]{1,0:T(8,128)(2,1)} %get-tuple-element.47.qkv_ref.qkvt_ref, bf16[2056,1280]{1,0:T(8,128)(2,1)} %get-tuple-element.60.do_ref.dot_ref, ...), custom_call_target="tpu_custom_call" | custom-call | flops 40000000000 | bytes 50000000 | tf_op jit(solution)/shard_map/attn_back/pallas_call | solution.py:912
  529.6 0.8 reduce
  530.4 0.1 reshape.115
  530.5 0.1 reshape.116
  530.6 0.5 broadcast.16
  531.1 1.4 reduce.4
  532.5 0.1 reshape.117
  532.6 0.1 copy.39
  532.7 0.1 reshape_reshape.7
  532.8 0.1 reshape.118
  532.9 1.0 bitcast_reduce_fusion
  533.9 0.7 select_maximum_fusion.vec_ref
  534.5 99.6 %qkvb.1 = (bf16[2056,1280]{1,0:T(8,128)(2,1)}, f32[80,3840]{1,0:T(8,128)}, f32[16,80]{1,0:T(8,128)}) custom-call(bf16[2056,1280]{1,0:T(8,128)(2,1)} %get-tuple-element.48.x_ref.xt_ref.xim_hbm, f32[10,2056,128]{2,1,0:T(8,128)} %get-tuple-element.56.dr_hbm, f32[1,1280]{1,0:T(1,128)} %get-tuple-element.88.gain_ref, f32[16,1280]{1,0:T(8,128)} %select_maximum_fusion.vec_ref, ...), custom_call_target="tpu_custom_call" | custom-call | flops 40422604800 | bytes 80000000 | tf_op jit(solution)/shard_map/qkvb/pallas_call | solution.py:1008
  634.2 0.7 slice.43
  634.9 0.7 reshape.123
  635.5 1.4 slice_bitcast_fusion
  636.9 0.7 slice.42
  637.6 0.6 reshape.120
  638.2 2.0 copy.41
  640.2 1.8 copy.42
  642.0 0.0 slice-start
  642.0 3.1 copy.43
  645.1 0.0 slice-start.1
  645.1 5.3 copy.53
  650.4 0.0 slice-done
  650.4 0.0 slice-done.1
  650.4 0.0 copy-start.1
  650.4 0.0 copy-start.2
  650.4 0.0 copy-start
  650.5 2.7 copy.54
  653.1 0.0 copy-done.1
  653.1 1.0 copy.55
  654.2 0.0 copy-done.2
  654.2 0.8 copy.56
  654.9 0.0 copy-done
  654.9 1.2 copy.57
  (6 shorter events, 0.1 us)
Async XLA Ops:
  642.0 8.4 %slice-start = ((s8[5263360]{0:T(1024)(128)(4,1)}), s8[1069056]{0:T(1024)(128)(4,1)S(1)}, s32[]{:S(2)}) async-start(s8[5263360]{0:T(1024)(128)(4,1)} %bitcast.55), calls=%async_computation | async-start | bytes 2138112
  645.1 5.4 slice-start.1
  650.4 2.7 copy-start.1
  650.4 3.7 copy-start.2
  650.4 4.5 copy-start

commit v7 on v6

--- a/solution.py
+++ b/solution.py
@@ -80,6 +80,21 @@
     return slice(first * wide, (first + 1) * wide)
 
 
+def regroup(rows, source, load, store):
+    groups = LANE // UNITS
+    lane = lax.broadcasted_iota(jnp.int32, (rows, LANE), 1) // UNITS
+    for tile in range(FFN // LANE):
+        out = None
+        for i in range(groups):
+            n = source(tile * groups + i)
+            piece = load(n // groups)
+            shift = (i - n) % groups
+            if shift:
+                piece = pltpu.roll(piece, shift * UNITS, 1)
+            out = piece if out is None else jnp.where(lane == i, piece, out)
+        store(tile, out)
+
+
 def norm_stats(values):
     mean = row_mean(values)
     centered = values - mean
@@ -193,11 +208,11 @@
         place = [slice(None) if a in done else self.at[a] for a in range(3)]
         if arrived:
             place[done[-1]] = 1 - self.at[done[-1]]
-        return (*place, self.core, slice(None), pl.ds(self.cuts[part], self.cuts[part + 1] - self.cuts[part]))
+        return (*place, self.core, pl.ds(self.cuts[part], self.cuts[part + 1] - self.cuts[part]))
 
     def hop(self, stage, part):
         where = self.full.at[self.region(part, stage - 1)]
-        source = self.own.at[self.region(part, 0)[-2:]] if stage == 1 else where
+        source = self.own.at[self.region(part, 0)[-1]] if stage == 1 else where
         return self.remote(source, where, QUAD * stage + part, self.other[ORDERS[part][stage - 1]])
 
     def forward(self, stage, part):
@@ -341,14 +356,15 @@
 UNITS = MLP_F // PARTS
 MLP_STEPS = FFN // MLP_F
 WIDTH_CUTS = (0, 384, 896, WIDTH)
-QKV_ALL = Gather(SHARD, QKV, (0, WIDTH, 2 * WIDTH, QKV))
-OUT_ALL = Gather(SHARD, WIDTH, WIDTH_CUTS)
-FC_ALL = Gather(SHARD, FFN, (0, 1664, 3328, 5120))
-PROJ_ALL = Gather(FFN // PARTS, WIDTH, WIDTH_CUTS)
-VECTOR_ALL = Gather(SHARD, LANE, (0, LANE))
-
-
-def open_kernel(x_hbm, dy_hbm, rows_ref, wq_ref, wo_ref, xim_hbm, dyim_hbm, h_hbm, ht_hbm, vec_ref, wq_full, wo_full,
+GATHER_CUTS = (0, 32, 64, SHARD)
+QKV_ALL = Gather(SHARD, QKV, GATHER_CUTS)
+OUT_ALL = Gather(SHARD, WIDTH, GATHER_CUTS)
+FC_ALL = Gather(SHARD, FFN, GATHER_CUTS)
+PROJ_ALL = Gather(FFN // PARTS, WIDTH, (0, 112, 208, FFN // PARTS))
+VECTOR_ALL = Gather(SHARD, LANE, (0, SHARD))
+
+
+def open_kernel(x_hbm, dy_hbm, rows_ref, fc_ref, wq_ref, wo_ref, xim_hbm, dyim_hbm, h_hbm, ht_hbm, vec_ref, fc_own, wq_full, wo_full,
                 x, dy, wide, h, ht, rows, vec_own, vec_full, wq_own, wo_own, sems, *comm):
     loads = [pltpu.make_async_copy(src, dst, sems.at[i]) for i, (src, dst) in enumerate(((x_hbm, x), (dy_hbm, dy)))]
     for cp in loads:
@@ -380,6 +396,10 @@
     for gather in gathers:
         gather.turn(1)
     reorder(dy)
+
+    def store_fc(tile, values):
+        fc_own[:, steps(tile, LANE)] = values.astype(BF)
+    regroup(SHARD, lambda n: n % PARTS * MLP_STEPS + n // PARTS, lambda tile: fc_ref[:, steps(tile, LANE)], store_fc)
     for gather in gathers:
         gather.turn(2)
     vectors.turn(3)
@@ -405,15 +425,15 @@
         cp.wait()
 
 
-def open_call(x, dy, rows, wq, wo):
+def open_call(x, dy, rows, fc, wq, wo):
     hbm, vmem = pl.BlockSpec(memory_space=pl.ANY), pl.BlockSpec(memory_space=pltpu.VMEM)
     return pl.pallas_call(
         open_kernel,
-        in_specs=[hbm, hbm, vmem, vmem, vmem],
-        out_specs=[hbm, hbm, hbm, hbm, vmem, hbm, hbm],
+        in_specs=[hbm, hbm, vmem, vmem, vmem, vmem],
+        out_specs=[hbm, hbm, hbm, hbm, vmem, vmem, hbm, hbm],
         out_shape=[*[jax.ShapeDtypeStruct((TOKENS, WIDTH), BF)] * 3,
                    jax.ShapeDtypeStruct((WIDTH, TOKENS), BF), jax.ShapeDtypeStruct((VECTOR_ROWS, WIDTH), F32),
-                   QKV_ALL.full_shape, OUT_ALL.full_shape],
+                   jax.ShapeDtypeStruct(fc.shape, BF), QKV_ALL.full_shape, OUT_ALL.full_shape],
         scratch_shapes=[pltpu.VMEM((TOKENS, WIDTH), BF), pltpu.VMEM((TOKENS, WIDTH), BF), pltpu.VMEM((LANES, TOKENS, LANE), F32),
                         pltpu.VMEM((TOKENS, WIDTH), BF), pltpu.VMEM((WIDTH, TOKENS), BF), pltpu.VMEM((LANE, LANE), F32), pltpu.VMEM((SHARD, LANE), BF),
                         pltpu.VMEM(VECTOR_ALL.full_shape.shape, BF), pltpu.VMEM((SHARD, QKV), BF), pltpu.VMEM((SHARD, WIDTH), BF),
@@ -421,7 +441,7 @@
         compiler_params=pltpu.CompilerParams(vmem_limit_bytes=VMEM_MAX, collective_id=3, has_side_effects=True),
         cost_estimate=cost(1_000_000_000, 60_000_000),
         name="open",
-    )(x, dy, rows, wq, wo)
+    )(x, dy, rows, fc, wq, wo)
 
 
 QKV_N = 768
@@ -772,26 +792,49 @@
     )(qkv, qkv, xim, xim, w, wb, gain, bias, proj)
 
 
-def outb_kernel(dr_ref, o_ref, w_ref, do_ref, dw_ref):
-    n = MAIN
-    c = step_id()
+def outb_kernel(dr_ref, o_ref, w_ref, dfc_ref, y_in, dproj_in, do_ref, dw_ref, dfc_out, y_out, dproj_out, y, dproj, sems):
+    c, last = step_id(), pl.num_programs(0) - 1
+    loads = [pltpu.make_async_copy(src, dst, sems.at[i]) for i, (src, dst) in enumerate(((y_in, y), (dproj_in, dproj)))]
+    stores = [pltpu.make_async_copy(src, dst, sems.at[i]) for i, (src, dst) in enumerate(((y, y_out), (dproj, dproj_out)))]
+
+    @pl.when(c == 0)
+    def _():
+        for cp in loads:
+            cp.start()
+
+    @pl.when(c == 1)
+    def _():
+        for cp in loads:
+            cp.wait()
+        for cp in stores:
+            cp.start()
+
+        def store_fc(tile, values):
+            dfc_out[:, steps(tile, LANE)] = values
+        regroup(SHARD, lambda n: n % MLP_STEPS * PARTS + n // MLP_STEPS, lambda tile: dfc_ref[:, steps(tile, LANE)], store_fc)
     do_ref[ALL] = dot_nt(dr_ref[ALL], w_ref[ALL]).astype(BF)
-    dw_ref[ALL] = dot_tn(o_ref[ALL], dr_ref[:, pl.ds(pl.multiple_of(c * n, n), n)])
-
-
-def outb_call(dr, o, w):
-    n = MAIN
-    full = whole(TOKENS, WIDTH)
+    dw_ref[ALL] = dot_tn(o_ref[ALL], dr_ref[:, pl.ds(pl.multiple_of(c * MAIN, MAIN), MAIN)])
+
+    @pl.when(c == last)
+    def _():
+        for cp in stores:
+            cp.wait()
+
+
+def outb_call(dr, o, w, dfc, y, dproj):
+    full, hbm = whole(TOKENS, WIDTH), pl.BlockSpec(memory_space=pl.ANY)
+    like = lambda v: jax.ShapeDtypeStruct(v.shape, v.dtype)
     return pl.pallas_call(
         outb_kernel,
-        grid=(WIDTH // n,),
-        in_specs=[full, full, by_rows(n, WIDTH)],
-        out_specs=[by_cols(TOKENS, n), by_cols(WIDTH, n)],
-        out_shape=[jax.ShapeDtypeStruct((TOKENS, WIDTH), BF), jax.ShapeDtypeStruct((WIDTH, WIDTH), F32)],
+        grid=(WIDTH // MAIN,),
+        in_specs=[full, full, by_rows(MAIN, WIDTH), whole(*dfc.shape), hbm, hbm],
+        out_specs=[by_cols(TOKENS, MAIN), by_cols(WIDTH, MAIN), whole(*dfc.shape), hbm, hbm],
+        out_shape=[like(dr), jax.ShapeDtypeStruct((WIDTH, WIDTH), F32), like(dfc), like(y), like(dproj)],
+        scratch_shapes=[pltpu.VMEM(y.shape, BF), pltpu.VMEM(dproj.shape, F32), pltpu.SemaphoreType.DMA((2,))],
         compiler_params=pltpu.CompilerParams(dimension_semantics=("arbitrary",), vmem_limit_bytes=VMEM_MAX),
-        cost_estimate=cost(QUAD * TOKENS * WIDTH * WIDTH, 30_000_000),
+        cost_estimate=cost(QUAD * TOKENS * WIDTH * WIDTH, 50_000_000),
         name="outb",
-    )(dr, o, w)
+    )(dr, o, w, dfc, y, dproj)
 
 
 def attn_back_kernel(qkv_ref, qkvt_ref, do_ref, dot_ref, max_ref, inv_ref, dw_ref, dqkv_hbm, dwb_ref, dwout_ref,
@@ -1042,14 +1085,14 @@
         rows = jnp.pad(rows, ((0, VECTOR_ROWS - len(rows)), (0, LANE - SHARD)))
         x = resid_in.swapaxes(0, 1).reshape(TOKENS, WIDTH)
         dy = grad_out.swapaxes(0, 1).reshape(TOKENS, WIDTH)
-        xim, dyim, h, ht, rows, wq, wo = open_call(x, dy, rows, qkv_weight, out_weight)
+        xim, dyim, h, ht, rows, fc, wq, wo = open_call(x, dy, rows, fc_weight, qkv_weight, out_weight)
         wq, wo = wq.reshape(WIDTH, QKV), wo.reshape(WIDTH, WIDTH)
         bo, g2, b2 = rows[5:6], rows[6:7], rows[7:8]
         joint = lambda v: v.reshape(-1, PARTS, SHARD).swapaxes(0, 1).reshape(1, -1)
-        qkv, wf = qkv_call(h, wq, joint(rows[2:5]), to_steps(fc_weight.astype(BF)))
+        qkv, wf = qkv_call(h, wq, joint(rows[2:5]), fc)
         o, r, n2, top, inv, wp = attn_call(qkv, xim, wo, bo, g2, b2, proj_weight)
         y, dr, dr16, dwf, dwp, dbf, small = mlp_call(r, n2, dyim, g2, rows[12:13], wf.reshape(WIDTH, FFN), wp, to_steps(joint(rows[8:12])))
-        do, dwo = outb_call(dr16, o, wo)
+        do, dwo, dwf, y, dwp = outb_call(dr16, o, wo, dwf, y, dwp)
         dqkv, dbq, dwo = attn_back_call(qkv, do, top, inv, dwo)
         owned = lambda v: v.reshape(PARTS, -1, WIDTH // PARTS).swapaxes(0, 1).reshape(-1, WIDTH)
         vec = jnp.concatenate([jnp.sum(small.reshape(4, 8, WIDTH), axis=1), owned(dbq), owned(from_steps(dbf))])
@@ -1058,7 +1101,6 @@
         dg2, db2, dbp, dbo = vec[:4]
         dbq, dbf = vec[4:7].reshape(-1), vec[7:11].reshape(-1)
         dg1, db1 = vec[VECTOR_ROWS - 2:]
-        dwf = from_steps(dwf)
         unturn = lambda t: t.reshape(SEQ, IMAGES, WIDTH).swapaxes(0, 1)
         return (unturn(y), unturn(dx), dg1, db1, dwq, dbq, dwo, dbo, dg2, db2, dwf, dbf, dwp, dbp)
 

time: 663 us -> 662 us (level)
  local copies, waits for them, and re-layouts: 32.9 us -> 18.7 us
  Pallas kernels: 619 us -> 631 us
    pallas_call x2, Pallas kernels: 75.9 us -> 88.3 us  [the longest x1 62.8 us: open_call(): pl.pallas_call(open_kernel, in_specs=[hbm, hbm, vmem, vmem, vmem, vmem],...]
    unnamed x17 -> x7, local copies, waits for them, and re-layouts: 15.9 us -> 7.11 us
where the time goes in v7:
time: 662 us; the launch traced here: 655 us
  Pallas kernels  631 us (95%)
  local copies, waits for them, and re-layouts  18.7 us (3%)
    pallas_call x1, Pallas kernels, mlp_call(): pl.pallas_call(mlp_kernel, grid=(MLP_STEPS + DRAIN,), in_specs=[hbm, hbm,...  258 us
    pallas_call x1, Pallas kernels, qkvb_call(): pl.pallas_call(qkvb_kernel, grid=(QB_GRID,), in_specs=[hbm, hbm, whole(1,...  100 us
    pallas_call x1, Pallas kernels, qkv_call(): pl.pallas_call(qkv_kernel, grid=(QKV // QKV_N,), in_specs=[whole(TOKENS,...  66 us
    pallas_call x1, Pallas kernels, open_call(): pl.pallas_call(open_kernel, in_specs=[hbm, hbm, vmem, vmem, vmem, vmem],...  62.8 us
    pallas_call x1, Pallas kernels, attn_call(): pl.pallas_call(attn_kernel, grid=(IMAGES,), in_specs=[main(QKV), tail(QKV...  60.3 us
    pallas_call x1, Pallas kernels, attn_back_call(): pl.pallas_call(attn_back_kernel, grid=(OUT_STEPS + DRAIN,), in_specs=[mai...  58.3 us
    pallas_call x1, Pallas kernels, outb_call(): pl.pallas_call(outb_kernel, grid=(WIDTH // MAIN,), in_specs=[full, full,...  25.5 us

profile of v7, /device:TPU:0, one launch (start us, length us, event | category | flops | bytes accessed | tf_op | source)
XLA Modules:
  0.0 655.2 jit_solution(14592397205221877549)
XLA Ops:
  0.6 0.9 concatenate.6
  1.5 0.1 reshape.90
  1.6 0.6 pad.8.rows_ref
  2.2 62.8 %open.1 = (bf16[2056,1280]{1,0:T(8,128)(2,1)}, bf16[2056,1280]{1,0:T(8,128)(2,1)}, bf16[2056,1280]{1,0:T(8,128)(2,1)}, bf16[1280,2056]{1,0:T(8,128)(2,1)}, f32[1...) custom-call(bf16[2056,1280]{1,0:T(8,128)(2,1)} %bitcast.43, ...), custom_call_target="tpu_custom_call" | custom-call | flops 1000000000 | bytes 60000000 | tf_op jit(solution)/shard_map/open/pallas_call | solution.py:430
  65.0 0.8 slice.35
  65.8 0.1 reshape.92
  65.9 0.7 reshape.93.wb_ref
  66.6 66.0 %qkv.1 = (bf16[2056,3840]{1,0:T(8,128)(2,1)}, bf16[2,2,2,2,80,5120]{5,4,3,2,1,0:T(8,128)(2,1)}) custom-call(bf16[2056,1280]{1,0:T(8,128)(2,1)} %get-tuple-element.48.h_ref, bf16[1280,3840]{1,0:T(8,128)(2,1)} %bitcast.51, f32[1,3840]{1,0:T(1,128)} %reshape.93.wb_ref, bf16[80,5120]{1,0:T(8,128)(2,1)} %get-tuple-element.51.own_ref), custom_call_target="tpu_custom_call" | custom-call | flops 20211302400 | bytes 60000000 | tf_op jit(solution)/shard_map/qkv/pallas_call | solution.py:477
  132.6 1.6 fusion
  134.2 60.3 %attn.1 = (bf16[2056,1280]{1,0:T(8,128)(2,1)}, bf16[2056,1280]{1,0:T(8,128)(2,1)}, bf16[2056,1280]{1,0:T(8,128)(2,1)}, f32[8,16,256]{2,1,0:T(8,128)}, f32[8,16,2...) custom-call(bf16[2056,3840]{1,0:T(8,128)(2,1)} %get-tuple-element.52.qkv_ref.qkvt_ref, ...), custom_call_target="tpu_custom_call" | custom-call | flops 40000000000 | bytes 50000000 | tf_op jit(solution)/shard_map/attn/pallas_call | solution.py:776
  194.4 0.8 slice.40
  195.2 0.1 reshape.97
  195.3 0.1 reshape_reshape.6
  195.5 0.7 reshape.98.fcb_ref
  196.2 258.3 %mlp.1 = (bf16[2056,1280]{1,0:T(8,128)(2,1)}, f32[10,2056,128]{2,1,0:T(8,128)}, bf16[2056,1280]{1,0:T(8,128)(2,1)}, f32[80,5120]{1,0:T(8,128)}, f32[320,1280]{1,...) custom-call(bf16[2056,1280]{1,0:T(8,128)(2,1)} %get-tuple-element.55.r_hbm, ...), custom_call_target="tpu_custom_call" | custom-call | flops 161690419200 | bytes 150000000 | tf_op jit(solution)/shard_map/mlp/pallas_call | solution.py:618
  454.5 25.5 %outb.1 = (bf16[2056,1280]{1,0:T(8,128)(2,1)}, f32[1280,1280]{1,0:T(8,128)}, f32[80,5120]{1,0:T(8,128)}, bf16[2056,1280]{1,0:T(8,128)(2,1)}, f32[320,1280]{1,0:T(8,128)}) custom-call(bf16[2056,1280]{1,0:T(8,128)(2,1)} %get-tuple-element.60.dr_ref, bf16[2056,1280]{1,0:T(8,128)(2,1)} %get-tuple-element.61.o_ref, bf16[1280,1280]{1,0:T(8,128)(2,1)} %bitcast.54, ...), custom_call_target="tpu_custom_call" | custom-call | flops 13474201600 | bytes 50000000 | tf_op jit(solution)/shard_map/outb/pallas_call | solution.py:827
  480.1 58.3 %attn_back.1 = (bf16[2056,3840]{1,0:T(8,128)(2,1)}, f32[1,3840]{1,0:T(1,128)}, f32[80,1280]{1,0:T(8,128)}) custom-call(bf16[2056,3840]{1,0:T(8,128)(2,1)} %get-tuple-element.52.qkv_ref.qkvt_ref, bf16[2056,3840]{1,0:T(8,128)(2,1)} %get-tuple-element.52.qkv_ref.qkvt_ref, bf16[2056,1280]{1,0:T(8,128)(2,1)} %get-tuple-element.68.do_ref.dot_ref, ...), custom_call_target="tpu_custom_call" | custom-call | flops 40000000000 | bytes 50000000 | tf_op jit(solution)/shard_map/attn_back/pallas_call | solution.py:955
  538.4 0.8 reduce
  539.2 0.1 reshape.101
  539.3 0.1 reshape.102
  539.4 0.5 broadcast.16
  539.9 1.4 reduce.4
  541.3 0.1 reshape.103
  541.4 0.1 copy.34
  541.5 0.1 reshape_reshape.7
  541.6 0.1 reshape.104
  541.7 1.0 bitcast_reduce_fusion
  542.7 0.7 select_maximum_fusion.vec_ref
  543.3 100.2 %qkvb.1 = (bf16[2056,1280]{1,0:T(8,128)(2,1)}, f32[80,3840]{1,0:T(8,128)}, f32[16,80]{1,0:T(8,128)}) custom-call(bf16[2056,1280]{1,0:T(8,128)(2,1)} %get-tuple-element.53.x_ref.xt_ref.xim_hbm, f32[10,2056,128]{2,1,0:T(8,128)} %get-tuple-element.66.dr_hbm, f32[1,1280]{1,0:T(1,128)} %get-tuple-element.82.gain_ref, f32[16,1280]{1,0:T(8,128)} %select_maximum_fusion.vec_ref, ...), custom_call_target="tpu_custom_call" | custom-call | flops 40422604800 | bytes 80000000 | tf_op jit(solution)/shard_map/qkvb/pallas_call | solution.py:1051
  643.6 0.7 slice.43
  644.3 0.7 reshape.107
  645.0 1.4 slice_bitcast_fusion
  646.3 0.7 slice.42
  647.0 0.6 reshape.106
  647.7 0.0 copy-start
  647.7 0.0 copy-start.1
  647.7 5.3 copy.43
  653.0 0.0 copy-done
  653.0 1.0 copy.44
  654.0 0.0 copy-done.1
  654.0 0.8 copy.45
  (5 shorter events, 0.1 us)
Async XLA Ops:
  647.7 5.3 copy-start
  647.7 6.4 copy-start.1

commit v8 on v7

--- a/solution.py
+++ b/solution.py
@@ -191,8 +191,8 @@
 class Gather(Links):
     COUNT = 2
 
-    def __init__(self, rows, cols, cuts):
-        self.rows, self.cols, self.cuts = rows, cols, cuts
+    def __init__(self, rows, cols, cuts, by_rows):
+        self.rows, self.cols, self.cuts, self.by_rows = rows, cols, cuts, by_rows
         self.parts = range(len(cuts) - 1)
         self.full_shape = jax.ShapeDtypeStruct((2, 2, 2, 2, rows, cols), BF)
 
@@ -203,51 +203,63 @@
         self.own, self.full = own, full
         return self.find(*sems)
 
-    def region(self, part, known, arrived=False):
+    def region(self, part, known, arrived=False, half=None):
         done = ORDERS[part][:known]
         place = [slice(None) if a in done else self.at[a] for a in range(3)]
+        if half is not None:
+            place[done[0]] = half
         if arrived:
             place[done[-1]] = 1 - self.at[done[-1]]
-        return (*place, self.core, pl.ds(self.cuts[part], self.cuts[part + 1] - self.cuts[part]))
-
-    def hop(self, stage, part):
-        where = self.full.at[self.region(part, stage - 1)]
-        source = self.own.at[self.region(part, 0)[-1]] if stage == 1 else where
-        return self.remote(source, where, QUAD * stage + part, self.other[ORDERS[part][stage - 1]])
-
-    def forward(self, stage, part):
+        cut = pl.ds(self.cuts[part], self.cuts[part + 1] - self.cuts[part])
+        return (*place, self.core, cut, slice(None)) if self.by_rows else (*place, self.core, slice(None), cut)
+
+    def hop(self, stage, part, half):
+        where = self.full.at[self.region(part, stage - 1, half=half)]
+        source = self.own.at[self.region(part, 0)[-2:]] if stage == 1 else where
+        return self.remote(source, where, self.sem(stage, part, half), self.other[ORDERS[part][stage - 1]])
+
+    def forward(self, stage, part, half=None):
         if stage == 0:
             return self.remote(self.own, self.full.at[(*self.at, self.core)], 0, self.other_core)
-        where = self.full.at[self.region(part, stage, True)]
-        return self.remote(where, where, QUAD * (stage + 3) + part, self.other_core)
+        where = self.full.at[self.region(part, stage, True, half)]
+        return self.remote(where, where, self.sem(stage + QUAD, part, half), self.other_core)
+
+    def sem(self, row, part, half):
+        return QUAD * (row + (half or 0)) + part
+
+    def halves(self, stage):
+        return (None,) if stage < 3 else range(2)
 
     def keep(self):
         return pltpu.make_async_copy(self.own, self.full.at[(*self.at, self.core)], self.send.at[1])
 
     def begin(self):
         for part in self.parts:
-            self.hop(1, part).start()
+            self.hop(1, part, None).start()
         self.forward(0, 0).start()
         self.keep().start()
 
     def turn(self, stage):
         if stage == 1:
             self.keep().wait()
-        for part in self.parts:
-            self.hop(stage, part).wait()
-            if stage < 3:
-                self.hop(stage + 1, part).start()
-        for part in self.parts:
-            self.forward(stage, part).start()
+        for half in self.halves(stage):
+            for part in self.parts:
+                self.hop(stage, part, half).wait()
+                if stage < 3:
+                    for onward in self.halves(stage + 1):
+                        self.hop(stage + 1, part, onward).start()
+            for part in self.parts:
+                self.forward(stage, part, half).start()
 
     def end(self):
         self.forward(0, 0).wait()
         for stage in range(1, QUAD):
-            for part in self.parts:
-                self.forward(stage, part).wait()
-
-
-SEMS = 28
+            for half in self.halves(stage):
+                for part in self.parts:
+                    self.forward(stage, part, half).wait()
+
+
+SEMS = 36
 
 
 class Exchange(Links):
@@ -356,12 +368,11 @@
 UNITS = MLP_F // PARTS
 MLP_STEPS = FFN // MLP_F
 WIDTH_CUTS = (0, 384, 896, WIDTH)
-GATHER_CUTS = (0, 32, 64, SHARD)
-QKV_ALL = Gather(SHARD, QKV, GATHER_CUTS)
-OUT_ALL = Gather(SHARD, WIDTH, GATHER_CUTS)
-FC_ALL = Gather(SHARD, FFN, GATHER_CUTS)
-PROJ_ALL = Gather(FFN // PARTS, WIDTH, (0, 112, 208, FFN // PARTS))
-VECTOR_ALL = Gather(SHARD, LANE, (0, SHARD))
+QKV_ALL = Gather(SHARD, QKV, (0, WIDTH, 2 * WIDTH, QKV), False)
+OUT_ALL = Gather(SHARD, WIDTH, (0, 384, 768, WIDTH), False)
+FC_ALL = Gather(SHARD, FFN, (0, 1664, 3328, FFN), False)
+PROJ_ALL = Gather(FFN // PARTS, WIDTH, (0, 112, 208, FFN // PARTS), True)
+VECTOR_ALL = Gather(SHARD, LANE, (0, SHARD), True)
 
 
 def open_kernel(x_hbm, dy_hbm, rows_ref, fc_ref, wq_ref, wo_ref, xim_hbm, dyim_hbm, h_hbm, ht_hbm, vec_ref, fc_own, wq_full, wo_full,
@@ -396,10 +407,6 @@
     for gather in gathers:
         gather.turn(1)
     reorder(dy)
-
-    def store_fc(tile, values):
-        fc_own[:, steps(tile, LANE)] = values.astype(BF)
-    regroup(SHARD, lambda n: n % PARTS * MLP_STEPS + n // PARTS, lambda tile: fc_ref[:, steps(tile, LANE)], store_fc)
     for gather in gathers:
         gather.turn(2)
     vectors.turn(3)
@@ -417,6 +424,9 @@
     stores = [pltpu.make_async_copy(src, dst, sems.at[i]) for i, (src, dst) in enumerate(((x, xim_hbm), (dy, dyim_hbm), (h, h_hbm), (ht, ht_hbm)))]
     for cp in stores:
         cp.start()
+    def store_fc(tile, values):
+        fc_own[:, steps(tile, LANE)] = values.astype(BF)
+    regroup(SHARD, lambda n: n % PARTS * MLP_STEPS + n // PARTS, lambda tile: fc_ref[:, steps(tile, LANE)], store_fc)
     for gather in weights:
         gather.turn(3)
     for gather in weights:
@@ -840,7 +850,7 @@
 def attn_back_kernel(qkv_ref, qkvt_ref, do_ref, dot_ref, max_ref, inv_ref, dw_ref, dqkv_hbm, dwb_ref, dwout_ref,
                      tails, do_tails, grad_tails, dq_t, dk, dv, ds_tail, sa, da, sb, db, buf, sems, *comm):
     b = step_id()
-    by_row = FC_SUM.bind(comm)
+    by_row = OUT_SUM.bind(comm)
 
     @pl.when(b == 0)
     def _():
@@ -857,7 +867,9 @@
                    tails, do_tails, grad_tails, dq_t, dk, dv, ds_tail, ((sa, da), (sb, db)), buf, sems)
 
 
-OUT_STEPS = WIDTH // MAIN
+OUT_N = WIDTH // 2
+OUT_STEPS = WIDTH // OUT_N
+OUT_SUM = Exchange(SHARD, OUT_N, ROW_CUTS, 0)
 
 
 def image_back(b, qkv_ref, qkvt_ref, do_ref, dot_ref, max_ref, inv_ref, dqkv_hbm, dwb_ref,
@@ -954,16 +966,16 @@
     stat = pl.BlockSpec((1, HEADS, MAIN), lambda i: (image(i), 0, 0))
     return pl.pallas_call(
         attn_back_kernel,
-        grid=(OUT_STEPS + DRAIN,),
+        grid=(max(IMAGES, OUT_STEPS + DRAIN),),
         in_specs=[main(QKV), tail(QKV), main(WIDTH), tail(WIDTH), stat, stat,
-                  by_cols(WIDTH, MAIN, lambda i: jnp.minimum(i, OUT_STEPS - 1))],
-        out_specs=[hbm, whole(1, QKV), by_cols(SHARD, MAIN, lambda i: jnp.maximum(i - DRAIN, 0))],
+                  by_cols(WIDTH, OUT_N, lambda i: jnp.minimum(i, OUT_STEPS - 1))],
+        out_specs=[hbm, whole(1, QKV), by_cols(SHARD, OUT_N, lambda i: jnp.clip(i - DRAIN, 0, OUT_STEPS - 1))],
         out_shape=[jax.ShapeDtypeStruct((TOKENS, QKV), BF), jax.ShapeDtypeStruct((1, QKV), F32),
                    jax.ShapeDtypeStruct((SHARD, WIDTH), F32)],
         scratch_shapes=[pltpu.VMEM((IMAGES, QKV), F32), pltpu.VMEM((IMAGES, WIDTH), F32),
                         pltpu.VMEM((IMAGES, QKV), F32), pltpu.VMEM((WIDTH, MAIN), F32),
                         pltpu.VMEM((MAIN, WIDTH), F32), pltpu.VMEM((MAIN, WIDTH), F32), pltpu.VMEM((HEADS, MAIN), F32),
-                        *[pltpu.VMEM((MAIN, MAIN), F32)] * QUAD, pltpu.VMEM((2, MAIN, QKV), BF), pltpu.SemaphoreType.DMA((1, 2))] + FC_SUM.scratch(),
+                        *[pltpu.VMEM((MAIN, MAIN), F32)] * QUAD, pltpu.VMEM((2, MAIN, QKV), BF), pltpu.SemaphoreType.DMA((1, 2))] + OUT_SUM.scratch(),
         compiler_params=comm_params(1),
         cost_estimate=ATTN_COST,
         name="attn_back",
@@ -978,12 +990,19 @@
 QB_GRID = QB_STEPS + 1 + QUAD * QKV_SUM.stride
 
 
-def qkvb_kernel(xim_hbm, dr_hbm, gain_ref, vec_ref, ht_ref, dqkv_ref, w_ref, dx_hbm, dw_ref, out_vec_ref,
-                acc, dr, xd, vec, sums, sems, *comm):
+def qkvb_kernel(xim_hbm, dr_hbm, gain_ref, sums_ref, qb_ref, fb_ref, ht_ref, dqkv_ref, w_ref, dx_hbm, dw_ref, out_vec_ref,
+                acc, dr, xd, sums, sems, *comm):
     t = step_id()
     by_row, by_vector = QKV_SUM.bind(comm[:Exchange.COUNT]), VECTOR_SUM.bind(comm[Exchange.COUNT:])
     loads = [pltpu.make_async_copy(dr_hbm, dr, sems.at[0]), pltpu.make_async_copy(xim_hbm, xd, sems.at[1])]
     store = pltpu.make_async_copy(xd, dx_hbm, sems.at[1])
+
+    def put_row(place, row, lane, values):
+        by_vector.local[(0, *place, pl.ds(row, len(values)), pl.ds(lane, values.shape[1]))] = values
+
+    def share(row, values):
+        for d, place in enumerate(DEVICES):
+            put_row(place, row, 0, values[:, steps(d, SHARD)])
 
     @pl.when(t == 0)
     def _():
@@ -992,7 +1011,12 @@
             cp.start()
         clear(acc, sums)
         by_vector.local[0] = jnp.zeros(by_vector.blocks, F32)
-        vec[ALL] = vec_ref[ALL]
+        share(0, jnp.concatenate([col_sum(sums_ref[steps(i, SUBLANE), :]) for i in range(QUAD)], axis=0))
+        for d, place in enumerate(DEVICES):
+            for i in range(3):
+                put_row(place, QUAD + i, 0, qb_ref[:, pl.ds((3 * d + i) * SHARD, SHARD)])
+            for n in range(MLP_STEPS):
+                put_row(place, QUAD + 3 + n * UNITS // SHARD, n * UNITS % SHARD, fb_ref[:, pl.ds(n * MLP_F + d * UNITS, UNITS)])
 
     def emit_vectors(n, exchange, c):
         for part, (rows, _) in enumerate(exchange.parts[:2]):
@@ -1024,10 +1048,7 @@
     @pl.when(t == VECTOR_STEP)
     def _():
         back(TAIL, IMAGES)
-        for i in range(2):
-            vec[steps(VECTOR_ROWS - 2 + i, 1), :] = col_sum(sums[steps(i, SUBLANE), :])
-        for d, place in enumerate(itertools.product(range(2), repeat=QUAD)):
-            by_vector.local[(0, *place, pl.ds(0, VECTOR_ROWS), pl.ds(0, SHARD))] = vec[:, steps(d, SHARD)]
+        share(VECTOR_ROWS - 2, jnp.concatenate([col_sum(sums[steps(i, SUBLANE), :]) for i in range(2)], axis=0))
 
     @pl.when(t == VECTOR_STEP + 1)
     def _():
@@ -1045,35 +1066,33 @@
         store.wait()
 
 
-def qkvb_call(xim, dr, gain, vec, ht, dqkv, w):
+DEVICES = list(itertools.product(range(2), repeat=QUAD))
+
+
+def qkvb_call(xim, dr, gain, sums, qb, fb, ht, dqkv, w):
     hbm = pl.BlockSpec(memory_space=pl.ANY)
     now = lambda i: jnp.minimum(i, QB_STEPS - 1)
     return pl.pallas_call(
         qkvb_kernel,
         grid=(QB_GRID,),
-        in_specs=[hbm, hbm, whole(1, WIDTH), whole(VECTOR_ROWS, WIDTH),
+        in_specs=[hbm, hbm, whole(1, WIDTH), *(whole(*v.shape) for v in (sums, qb, fb)),
                   whole(WIDTH, TOKENS, pipeline_mode=pl.Buffered(1)), by_cols(TOKENS, QB_N, now), by_cols(WIDTH, QB_N, now)],
         out_specs=[hbm, by_cols(SHARD, QB_N, lambda i: jnp.clip(i - 1 - QUAD * QKV_SUM.stride, 0, QB_STEPS - 1)),
                    whole(VECTOR_ROWS, SHARD)],
         out_shape=[jax.ShapeDtypeStruct((TOKENS, WIDTH), BF), jax.ShapeDtypeStruct((SHARD, QKV), F32),
                    jax.ShapeDtypeStruct((VECTOR_ROWS, SHARD), F32)],
         scratch_shapes=[pltpu.VMEM((TOKENS, WIDTH), F32), pltpu.VMEM((LANES, TOKENS, LANE), F32), pltpu.VMEM((TOKENS, WIDTH), BF),
-                        pltpu.VMEM((VECTOR_ROWS, WIDTH), F32), pltpu.VMEM((2 * SUBLANE, WIDTH), F32), pltpu.SemaphoreType.DMA((2,))]
+                        pltpu.VMEM((2 * SUBLANE, WIDTH), F32), pltpu.SemaphoreType.DMA((2,))]
                        + QKV_SUM.scratch() + VECTOR_SUM.scratch(),
         compiler_params=comm_params(2),
         cost_estimate=cost(QUAD * TOKENS * WIDTH * QKV, 80_000_000),
         name="qkvb",
-    )(xim, dr, gain, vec, ht, dqkv, w)
+    )(xim, dr, gain, sums, qb, fb, ht, dqkv, w)
 
 
 def to_steps(v):
     rows = v.shape[0]
     return v.reshape(rows, PARTS, MLP_STEPS, UNITS).swapaxes(1, 2).reshape(rows, FFN)
-
-
-def from_steps(v):
-    rows = v.shape[0]
-    return v.reshape(rows, MLP_STEPS, PARTS, UNITS).swapaxes(1, 2).reshape(rows, FFN)
 
 
 def solution(mesh):
@@ -1094,10 +1113,7 @@
         y, dr, dr16, dwf, dwp, dbf, small = mlp_call(r, n2, dyim, g2, rows[12:13], wf.reshape(WIDTH, FFN), wp, to_steps(joint(rows[8:12])))
         do, dwo, dwf, y, dwp = outb_call(dr16, o, wo, dwf, y, dwp)
         dqkv, dbq, dwo = attn_back_call(qkv, do, top, inv, dwo)
-        owned = lambda v: v.reshape(PARTS, -1, WIDTH // PARTS).swapaxes(0, 1).reshape(-1, WIDTH)
-        vec = jnp.concatenate([jnp.sum(small.reshape(4, 8, WIDTH), axis=1), owned(dbq), owned(from_steps(dbf))])
-        vec = jnp.pad(vec, ((0, VECTOR_ROWS - len(vec)), (0, 0)))
-        dx, dwq, vec = qkvb_call(xim, dr, rows[:1], vec, ht, dqkv, wq)
+        dx, dwq, vec = qkvb_call(xim, dr, rows[:1], small, dbq, dbf, ht, dqkv, wq)
         dg2, db2, dbp, dbo = vec[:4]
         dbq, dbf = vec[4:7].reshape(-1), vec[7:11].reshape(-1)
         dg1, db1 = vec[VECTOR_ROWS - 2:]

time: 662 us -> 649 us (0.980)
  Pallas kernels: 631 us -> 620 us
    pallas_call x1, Pallas kernels: 66 us -> 58.1 us  [qkv_call(): pl.pallas_call(qkv_kernel, grid=(QKV // QKV_N,), in_specs=[whole(TOKENS,...]
    pallas_call x1, Pallas kernels: 62.8 us -> 55.1 us  [open_call(): pl.pallas_call(open_kernel, in_specs=[hbm, hbm, vmem, vmem, vmem, vmem],...]
where the time goes in v8:
time: 649 us; the launch traced here: 638 us
  Pallas kernels  620 us (96%)
  local copies, waits for them, and re-layouts  17.6 us (3%)
    pallas_call x1, Pallas kernels, mlp_call(): pl.pallas_call(mlp_kernel, grid=(MLP_STEPS + DRAIN,), in_specs=[hbm, hbm,...  257 us
    pallas_call x1, Pallas kernels, qkvb_call(): pl.pallas_call(qkvb_kernel, grid=(QB_GRID,), in_specs=[hbm, hbm, whole(1,...  102 us
    pallas_call x1, Pallas kernels, attn_back_call(): pl.pallas_call(attn_back_kernel, grid=(max(IMAGES, OUT_STEPS + DRAIN),),...  61.7 us
    pallas_call x1, Pallas kernels, attn_call(): pl.pallas_call(attn_kernel, grid=(IMAGES,), in_specs=[main(QKV), tail(QKV...  60.1 us
    pallas_call x1, Pallas kernels, qkv_call(): pl.pallas_call(qkv_kernel, grid=(QKV // QKV_N,), in_specs=[whole(TOKENS,...  58.1 us
    pallas_call x1, Pallas kernels, open_call(): pl.pallas_call(open_kernel, in_specs=[hbm, hbm, vmem, vmem, vmem, vmem],...  55.1 us
    pallas_call x1, Pallas kernels, outb_call(): pl.pallas_call(outb_kernel, grid=(WIDTH // MAIN,), in_specs=[full, full,...  25.5 us

profile of v8, /device:TPU:0, one launch (start us, length us, event | category | flops | bytes accessed | tf_op | source)
XLA Modules:
  0.0 638.4 jit_solution(17735534566889434282)
XLA Ops:
  0.6 0.9 concatenate.3
  1.5 0.1 reshape.75
  1.6 0.6 pad.4.rows_ref
  2.2 55.1 %open.1 = (bf16[2056,1280]{1,0:T(8,128)(2,1)}, bf16[2056,1280]{1,0:T(8,128)(2,1)}, bf16[2056,1280]{1,0:T(8,128)(2,1)}, bf16[1280,2056]{1,0:T(8,128)(2,1)}, f32[1...) custom-call(bf16[2056,1280]{1,0:T(8,128)(2,1)} %bitcast.38, ...), custom_call_target="tpu_custom_call" | custom-call | flops 1000000000 | bytes 60000000 | tf_op jit(solution)/shard_map/open/pallas_call | solution.py:440
  57.3 0.8 slice.40
  58.0 0.1 reshape.82
  58.2 0.8 slice.35
  58.9 1.6 fusion
  60.5 0.1 reshape.77
  60.6 0.7 reshape.78.wb_ref
  61.3 0.1 reshape_reshape.3
  61.5 0.7 reshape.83.fcb_ref
  62.2 58.1 %qkv.1 = (bf16[2056,3840]{1,0:T(8,128)(2,1)}, bf16[2,2,2,2,80,5120]{5,4,3,2,1,0:T(8,128)(2,1)}) custom-call(bf16[2056,1280]{1,0:T(8,128)(2,1)} %get-tuple-element.48.h_ref, bf16[1280,3840]{1,0:T(8,128)(2,1)} %bitcast.43, f32[1,3840]{1,0:T(1,128)} %reshape.78.wb_ref, bf16[80,5120]{1,0:T(8,128)(2,1)} %get-tuple-element.51.own_ref), custom_call_target="tpu_custom_call" | custom-call | flops 20211302400 | bytes 60000000 | tf_op jit(solution)/shard_map/qkv/pallas_call | solution.py:487
  120.4 60.1 %attn.1 = (bf16[2056,1280]{1,0:T(8,128)(2,1)}, bf16[2056,1280]{1,0:T(8,128)(2,1)}, bf16[2056,1280]{1,0:T(8,128)(2,1)}, f32[8,16,256]{2,1,0:T(8,128)}, f32[8,16,2...) custom-call(bf16[2056,3840]{1,0:T(8,128)(2,1)} %get-tuple-element.52.qkv_ref.qkvt_ref, ...), custom_call_target="tpu_custom_call" | custom-call | flops 40000000000 | bytes 50000000 | tf_op jit(solution)/shard_map/attn/pallas_call | solution.py:786
  180.4 257.5 %mlp.1 = (bf16[2056,1280]{1,0:T(8,128)(2,1)}, f32[10,2056,128]{2,1,0:T(8,128)}, bf16[2056,1280]{1,0:T(8,128)(2,1)}, f32[80,5120]{1,0:T(8,128)}, f32[320,1280]{1,...) custom-call(bf16[2056,1280]{1,0:T(8,128)(2,1)} %get-tuple-element.55.r_hbm, ...), custom_call_target="tpu_custom_call" | custom-call | flops 161690419200 | bytes 150000000 | tf_op jit(solution)/shard_map/mlp/pallas_call | solution.py:628
  437.9 25.5 %outb.1 = (bf16[2056,1280]{1,0:T(8,128)(2,1)}, f32[1280,1280]{1,0:T(8,128)}, f32[80,5120]{1,0:T(8,128)}, bf16[2056,1280]{1,0:T(8,128)(2,1)}, f32[320,1280]{1,0:T(8,128)}) custom-call(bf16[2056,1280]{1,0:T(8,128)(2,1)} %get-tuple-element.60.dr_ref, bf16[2056,1280]{1,0:T(8,128)(2,1)} %get-tuple-element.61.o_ref, bf16[1280,1280]{1,0:T(8,128)(2,1)} %bitcast.46, ...), custom_call_target="tpu_custom_call" | custom-call | flops 13474201600 | bytes 50000000 | tf_op jit(solution)/shard_map/outb/pallas_call | solution.py:837
  463.5 61.7 %attn_back.1 = (bf16[2056,3840]{1,0:T(8,128)(2,1)}, f32[1,3840]{1,0:T(1,128)}, f32[80,1280]{1,0:T(8,128)}) custom-call(bf16[2056,3840]{1,0:T(8,128)(2,1)} %get-tuple-element.52.qkv_ref.qkvt_ref, bf16[2056,3840]{1,0:T(8,128)(2,1)} %get-tuple-element.52.qkv_ref.qkvt_ref, bf16[2056,1280]{1,0:T(8,128)(2,1)} %get-tuple-element.68.do_ref.dot_ref, ...), custom_call_target="tpu_custom_call" | custom-call | flops 40000000000 | bytes 50000000 | tf_op jit(solution)/shard_map/attn_back/pallas_call | solution.py:967
  525.2 101.6 %qkvb.1 = (bf16[2056,1280]{1,0:T(8,128)(2,1)}, f32[80,3840]{1,0:T(8,128)}, f32[16,80]{1,0:T(8,128)}) custom-call(bf16[2056,1280]{1,0:T(8,128)(2,1)} %get-tuple-element.53.x_ref.xt_ref.xim_hbm, f32[10,2056,128]{2,1,0:T(8,128)} %get-tuple-element.66.dr_hbm, f32[1,1280]{1,0:T(1,128)} %get-tuple-element.82.gain_ref, f32[32,1280]{1,0:T(8,128)} %get-tuple-element.67.sums_ref, ...), custom_call_target="tpu_custom_call" | custom-call | flops 40422604800 | bytes 80000000 | tf_op jit(solution)/shard_map/qkvb/pallas_call | solution.py:1075
  626.8 0.7 slice.42
  627.4 0.6 reshape.86
  628.1 0.7 slice.43
  628.8 1.4 slice_bitcast_fusion
  630.2 0.7 reshape.87
  630.8 0.0 copy-start
  630.8 0.0 copy-start.1
  630.8 5.3 copy.39
  636.1 0.0 copy-done
  636.1 1.0 copy.40
  637.2 0.0 copy-done.1
  637.2 0.8 copy.41
  (3 shorter events, 0.1 us)
Async XLA Ops:
  630.8 5.3 copy-start
  630.8 6.4 copy-start.1

commit v9 on v8

--- a/solution.py
+++ b/solution.py
@@ -113,8 +113,8 @@
     body(TAIL, IMAGES)
 
 
-def back_part(body, part):
-    tiles = -(-TAIL // ROWS // 3)
+def back_part(body, part, parts):
+    tiles = -(-TAIL // ROWS // parts)
 
     def loop(i, carry):
         tile = part * tiles + i
@@ -364,6 +364,7 @@
 PARTS = 16
 SHARD = WIDTH // PARTS
 VECTOR_ROWS = PARTS
+LN1_GAIN, LN1_BIAS, QKV_BIAS, OUT_BIAS, LN2_GAIN, LN2_BIAS, FC_BIAS, PROJ_BIAS = 0, 1, 2, 5, 6, 7, 8, 12
 MLP_F = MAIN
 UNITS = MLP_F // PARTS
 MLP_STEPS = FFN // MLP_F
@@ -375,7 +376,7 @@
 VECTOR_ALL = Gather(SHARD, LANE, (0, SHARD), True)
 
 
-def open_kernel(x_hbm, dy_hbm, rows_ref, fc_ref, wq_ref, wo_ref, xim_hbm, dyim_hbm, h_hbm, ht_hbm, vec_ref, fc_own, wq_full, wo_full,
+def open_kernel(x_hbm, dy_hbm, rows_ref, fc_ref, wq_ref, wo_ref, xim_hbm, dyim_hbm, h_hbm, ht_hbm, vec_ref, qb_ref, fb_ref, fc_own, wq_full, wo_full,
                 x, dy, wide, h, ht, rows, vec_own, vec_full, wq_own, wo_own, sems, *comm):
     loads = [pltpu.make_async_copy(src, dst, sems.at[i]) for i, (src, dst) in enumerate(((x_hbm, x), (dy_hbm, dy)))]
     for cp in loads:
@@ -412,7 +413,13 @@
     vectors.turn(3)
     vectors.end()
     vec_ref[ALL] = vec_full[ALL].reshape(WIDTH, LANE).astype(F32).T[:VECTOR_ROWS, :]
-    gain, bias = vec_ref[0:1, :], vec_ref[1:2, :]
+    gain, bias = vec_ref[steps(LN1_GAIN, 1), :], vec_ref[steps(LN1_BIAS, 1), :]
+    for d in range(PARTS):
+        for i in range(3):
+            qb_ref[:, steps(3 * d + i, SHARD)] = vec_ref[steps(QKV_BIAS + i, 1), steps(d, SHARD)]
+        for n in range(MLP_STEPS):
+            place = pl.ds(d * SHARD + n * UNITS % SHARD, UNITS)
+            fb_ref[:, pl.ds(n * MLP_F + d * UNITS, UNITS)] = vec_ref[steps(FC_BIAS + n * UNITS // SHARD, 1), place]
 
     def norm(r, n):
         hat, _ = norm_stats(x[pl.ds(r, n), :].astype(F32))
@@ -440,10 +447,10 @@
     return pl.pallas_call(
         open_kernel,
         in_specs=[hbm, hbm, vmem, vmem, vmem, vmem],
-        out_specs=[hbm, hbm, hbm, hbm, vmem, vmem, hbm, hbm],
+        out_specs=[hbm, hbm, hbm, hbm, vmem, vmem, vmem, vmem, hbm, hbm],
         out_shape=[*[jax.ShapeDtypeStruct((TOKENS, WIDTH), BF)] * 3,
                    jax.ShapeDtypeStruct((WIDTH, TOKENS), BF), jax.ShapeDtypeStruct((VECTOR_ROWS, WIDTH), F32),
-                   jax.ShapeDtypeStruct(fc.shape, BF), QKV_ALL.full_shape, OUT_ALL.full_shape],
+                   *(jax.ShapeDtypeStruct((1, n), F32) for n in (QKV, FFN)), jax.ShapeDtypeStruct(fc.shape, BF), QKV_ALL.full_shape, OUT_ALL.full_shape],
         scratch_shapes=[pltpu.VMEM((TOKENS, WIDTH), BF), pltpu.VMEM((TOKENS, WIDTH), BF), pltpu.VMEM((LANES, TOKENS, LANE), F32),
                         pltpu.VMEM((TOKENS, WIDTH), BF), pltpu.VMEM((WIDTH, TOKENS), BF), pltpu.VMEM((LANE, LANE), F32), pltpu.VMEM((SHARD, LANE), BF),
                         pltpu.VMEM(VECTOR_ALL.full_shape.shape, BF), pltpu.VMEM((SHARD, QKV), BF), pltpu.VMEM((SHARD, WIDTH), BF),
@@ -516,7 +523,7 @@
     return u * cdf, cdf + u * bell * ((2.0 * math.pi) ** -0.5)
 
 
-def mlp_kernel(r_hbm, n_hbm, dy_hbm, gain_ref, pb_ref, fc_ref, proj_ref, fcb_ref,
+def mlp_kernel(r_hbm, n_hbm, dy_hbm, vec_ref, fc_ref, proj_ref, fcb_ref,
                y_hbm, dr_hbm, dr16_hbm, dfc_ref, dproj_ref, dfcb_ref, small_ref,
                n2, dy, y_acc, dn_acc, g, du, ua, ub, da, db, sem, *comm):
     step = step_id()
@@ -582,10 +589,10 @@
         hat, inv = norm_stats(wide_r)
         dn = joined(dn_acc, r, n)
         wide_dy = dy[pl.ds(r, n), :].astype(F32)
-        dr = wide_dy + norm_back(dn, hat, inv, gain_ref[ALL])
+        dr = wide_dy + norm_back(dn, hat, inv, vec_ref[steps(LN2_GAIN, 1), :])
         put(dn_acc, r, n, dr)
         n2[pl.ds(r, n), :] = dr.astype(BF)
-        y_acc[pl.ds(r, n), :] += wide_r + pb_ref[ALL]
+        y_acc[pl.ds(r, n), :] += wide_r + vec_ref[steps(PROJ_BIAS, 1), :]
         for i, v in enumerate((dn * hat, dn, wide_dy, dr)):
             small_ref[steps(i, SUBLANE), :] += eights(v)
 
@@ -597,7 +604,7 @@
 
     @pl.when((after >= 0) & (after < 3))
     def _():
-        back_part(back, after)
+        back_part(back, after, 3)
 
     @pl.when(after == 2)
     def _():
@@ -620,15 +627,14 @@
         y_copy.wait()
 
 
-def mlp_call(r, n2, dy, gain, pb, fc, proj, fcb):
+def mlp_call(r, n2, dy, vec, fc, proj, fcb):
     hbm = pl.BlockSpec(memory_space=pl.ANY)
-    vec = whole(1, WIDTH)
     now = lambda i: jnp.minimum(i, MLP_STEPS - 1)
     done = lambda i: jnp.maximum(i - DRAIN, 0)
     return pl.pallas_call(
         mlp_kernel,
         grid=(MLP_STEPS + DRAIN,),
-        in_specs=[hbm, hbm, hbm, vec, vec, by_cols(WIDTH, MLP_F, now),
+        in_specs=[hbm, hbm, hbm, whole(*vec.shape), by_cols(WIDTH, MLP_F, now),
                   pl.BlockSpec((PARTS, None, UNITS, WIDTH), lambda i: (0, now(i), 0, 0)),
                   by_cols(1, MLP_F, now)],
         out_specs=[hbm, hbm, hbm, by_cols(SHARD, MLP_F, done),
@@ -646,7 +652,7 @@
         compiler_params=comm_params(0),
         cost_estimate=cost(12 * TOKENS * WIDTH * FFN, 150_000_000, TOKENS * FFN),
         name="mlp",
-    )(r, n2, dy, gain, pb, fc, proj.reshape(PARTS, MLP_STEPS, UNITS, WIDTH), fcb)
+    )(r, n2, dy, vec, fc, proj.reshape(PARTS, MLP_STEPS, UNITS, WIDTH), fcb)
 
 
 SCALE = HEAD ** -0.5
@@ -683,7 +689,7 @@
     return e * inv, e_self * inv
 
 
-def attn_kernel(qkv_ref, qkvt_ref, x_ref, xt_ref, w_ref, wb_ref, gain_ref, bias_ref, proj_ref, o_hbm, r_hbm, n_hbm,
+def attn_kernel(qkv_ref, qkvt_ref, x_ref, xt_ref, w_ref, vec_ref, proj_ref, o_hbm, r_hbm, n_hbm,
                 max_ref, inv_ref, full,
                 tails, o_tail, o_t, ptail, o_buf, r_buf, n_buf, sa, sb, sems, own, *comm):
     b, last = step_id(), pl.num_programs(0) - 1
@@ -740,13 +746,14 @@
         o_t[steps(h, HEAD), :] = dot(v_turned[steps(h, HEAD), :], (e * inv).astype(BF))
 
     outs = (o_buf, o_hbm), (r_buf, r_hbm), (n_buf, n_hbm)
+    out_bias, gain, bias = (vec_ref[steps(i, 1), :] for i in (OUT_BIAS, LN2_GAIN, LN2_BIAS))
 
     def write(slot, rows, o, x):
         o_buf[slot, rows, :] = o
-        r = (x.astype(F32) + dot(o, w_ref[ALL]) + wb_ref[ALL]).astype(BF)
+        r = (x.astype(F32) + dot(o, w_ref[ALL]) + out_bias).astype(BF)
         r_buf[slot, rows, :] = r
         hat, _ = norm_stats(r.astype(F32))
-        n_buf[slot, rows, :] = (hat * gain_ref[ALL] + bias_ref[ALL]).astype(BF)
+        n_buf[slot, rows, :] = (hat * gain + bias).astype(BF)
 
     @pl.when(b >= 2)
     def _():
@@ -778,7 +785,7 @@
     return pltpu.make_async_copy(buf.at[slot], hbm.at[pl.ds(pl.multiple_of(b * MAIN, MAIN), MAIN)], sems.at[n, slot])
 
 
-def attn_call(qkv, xim, w, wb, gain, bias, proj):
+def attn_call(qkv, xim, w, vec, proj):
     hbm = pl.BlockSpec(memory_space=pl.ANY)
     main = lambda n: by_rows(MAIN, n)
     tail = lambda n: by_rows(IMAGES, n, lambda i: TAIL // IMAGES)
@@ -787,7 +794,7 @@
         attn_kernel,
         grid=(IMAGES,),
         in_specs=[main(QKV), tail(QKV), main(WIDTH), tail(WIDTH),
-                  whole(WIDTH, WIDTH), *[whole(1, WIDTH)] * 3, whole(*proj.shape)],
+                  whole(WIDTH, WIDTH), whole(*vec.shape), whole(*proj.shape)],
         out_specs=[hbm, hbm, hbm, stat, stat, hbm],
         out_shape=[*[jax.ShapeDtypeStruct((TOKENS, WIDTH), BF)] * 3,
                    jax.ShapeDtypeStruct((IMAGES, HEADS, MAIN), F32), jax.ShapeDtypeStruct((IMAGES, HEADS, MAIN), F32),
@@ -799,7 +806,7 @@
         compiler_params=comm_params(5),
         cost_estimate=ATTN_COST,
         name="attn",
-    )(qkv, qkv, xim, xim, w, wb, gain, bias, proj)
+    )(qkv, qkv, xim, xim, w, vec, proj)
 
 
 def outb_kernel(dr_ref, o_ref, w_ref, dfc_ref, y_in, dproj_in, do_ref, dw_ref, dfc_out, y_out, dproj_out, y, dproj, sems):
@@ -855,11 +862,11 @@
     @pl.when(b == 0)
     def _():
         by_row.meet()
-    advance((by_row,), b, first_chunks(OUT_STEPS), lambda n, exchange, c: exchange.result(c, dwout_ref))
 
     @pl.when(b < OUT_STEPS)
     def _():
         by_row.put_local(b, dw_ref[ALL])
+    advance((by_row,), b + 1, first_chunks(OUT_STEPS), lambda n, exchange, c: exchange.result(c, dwout_ref))
 
     @pl.when(b < IMAGES)
     def _():
@@ -867,7 +874,7 @@
                    tails, do_tails, grad_tails, dq_t, dk, dv, ds_tail, ((sa, da), (sb, db)), buf, sems)
 
 
-OUT_N = WIDTH // 2
+OUT_N = MAIN
 OUT_STEPS = WIDTH // OUT_N
 OUT_SUM = Exchange(SHARD, OUT_N, ROW_CUTS, 0)
 
@@ -966,10 +973,10 @@
     stat = pl.BlockSpec((1, HEADS, MAIN), lambda i: (image(i), 0, 0))
     return pl.pallas_call(
         attn_back_kernel,
-        grid=(max(IMAGES, OUT_STEPS + DRAIN),),
+        grid=(OUT_STEPS + DRAIN - 1,),
         in_specs=[main(QKV), tail(QKV), main(WIDTH), tail(WIDTH), stat, stat,
                   by_cols(WIDTH, OUT_N, lambda i: jnp.minimum(i, OUT_STEPS - 1))],
-        out_specs=[hbm, whole(1, QKV), by_cols(SHARD, OUT_N, lambda i: jnp.clip(i - DRAIN, 0, OUT_STEPS - 1))],
+        out_specs=[hbm, whole(1, QKV), by_cols(SHARD, OUT_N, lambda i: jnp.clip(i + 1 - DRAIN, 0, OUT_STEPS - 1))],
         out_shape=[jax.ShapeDtypeStruct((TOKENS, QKV), BF), jax.ShapeDtypeStruct((1, QKV), F32),
                    jax.ShapeDtypeStruct((SHARD, WIDTH), F32)],
         scratch_shapes=[pltpu.VMEM((IMAGES, QKV), F32), pltpu.VMEM((IMAGES, WIDTH), F32),
@@ -986,11 +993,12 @@
 QB_STEPS = QKV // QB_N
 QKV_SUM = Exchange(SHARD, QB_N, ROW_CUTS, 0, 2)
 VECTOR_SUM = Exchange(3 * SUBLANE, LANE, (0, SUBLANE, 2 * SUBLANE, 3 * SUBLANE), 0)
-VECTOR_STEP = QB_STEPS + 2
+VECTOR_STEP = QB_STEPS - 1
+BACK_STEP = VECTOR_STEP - 4
 QB_GRID = QB_STEPS + 1 + QUAD * QKV_SUM.stride
 
 
-def qkvb_kernel(xim_hbm, dr_hbm, gain_ref, sums_ref, qb_ref, fb_ref, ht_ref, dqkv_ref, w_ref, dx_hbm, dw_ref, out_vec_ref,
+def qkvb_kernel(xim_hbm, dr_hbm, vec_ref, sums_ref, qb_ref, fb_ref, ht_ref, dqkv_ref, wide_ref, w_ref, dx_hbm, dw_ref, out_vec_ref,
                 acc, dr, xd, sums, sems, *comm):
     t = step_id()
     by_row, by_vector = QKV_SUM.bind(comm[:Exchange.COUNT]), VECTOR_SUM.bind(comm[Exchange.COUNT:])
@@ -1027,9 +1035,12 @@
     @pl.when(t < QB_STEPS)
     def _():
         by_row.put_local(t, dot(ht_ref[ALL], dqkv_ref[ALL]))
-        acc[ALL] += dot_nt(dqkv_ref[ALL], w_ref[ALL])
-
-    @pl.when(t == QB_STEPS)
+
+    @pl.when((t < BACK_STEP) & (t % 2 == 0))
+    def _():
+        acc[ALL] += dot_nt(wide_ref[ALL], w_ref[ALL])
+
+    @pl.when(t == BACK_STEP)
     def _():
         for cp in loads:
             cp.wait()
@@ -1039,11 +1050,11 @@
         dn = acc[pl.ds(r, n), :]
         for i, v in enumerate((dn * hat, dn)):
             sums[steps(i, SUBLANE), :] += eights(v)
-        acc[pl.ds(r, n), :] = joined(dr, r, n) + norm_back(dn, hat, inv, gain_ref[ALL])
-
-    @pl.when((t >= QB_STEPS) & (t <= VECTOR_STEP))
-    def _():
-        back_part(back, t - QB_STEPS)
+        acc[pl.ds(r, n), :] = joined(dr, r, n) + norm_back(dn, hat, inv, vec_ref[steps(LN1_GAIN, 1), :])
+
+    @pl.when((t >= BACK_STEP) & (t <= VECTOR_STEP))
+    def _():
+        back_part(back, t - BACK_STEP, 5)
 
     @pl.when(t == VECTOR_STEP)
     def _():
@@ -1069,14 +1080,15 @@
 DEVICES = list(itertools.product(range(2), repeat=QUAD))
 
 
-def qkvb_call(xim, dr, gain, sums, qb, fb, ht, dqkv, w):
+def qkvb_call(xim, dr, vec, sums, qb, fb, ht, dqkv, w):
     hbm = pl.BlockSpec(memory_space=pl.ANY)
     now = lambda i: jnp.minimum(i, QB_STEPS - 1)
+    wide = lambda i: jnp.minimum(i // 2, QKV // QKV_N - 1)
     return pl.pallas_call(
         qkvb_kernel,
         grid=(QB_GRID,),
-        in_specs=[hbm, hbm, whole(1, WIDTH), *(whole(*v.shape) for v in (sums, qb, fb)),
-                  whole(WIDTH, TOKENS, pipeline_mode=pl.Buffered(1)), by_cols(TOKENS, QB_N, now), by_cols(WIDTH, QB_N, now)],
+        in_specs=[hbm, hbm, *(whole(*v.shape) for v in (vec, sums, qb, fb)),
+                  whole(WIDTH, TOKENS, pipeline_mode=pl.Buffered(1)), by_cols(TOKENS, QB_N, now), by_cols(TOKENS, QKV_N, wide), by_cols(WIDTH, QKV_N, wide)],
         out_specs=[hbm, by_cols(SHARD, QB_N, lambda i: jnp.clip(i - 1 - QUAD * QKV_SUM.stride, 0, QB_STEPS - 1)),
                    whole(VECTOR_ROWS, SHARD)],
         out_shape=[jax.ShapeDtypeStruct((TOKENS, WIDTH), BF), jax.ShapeDtypeStruct((SHARD, QKV), F32),
@@ -1087,12 +1099,7 @@
         compiler_params=comm_params(2),
         cost_estimate=cost(QUAD * TOKENS * WIDTH * QKV, 80_000_000),
         name="qkvb",
-    )(xim, dr, gain, sums, qb, fb, ht, dqkv, w)
-
-
-def to_steps(v):
-    rows = v.shape[0]
-    return v.reshape(rows, PARTS, MLP_STEPS, UNITS).swapaxes(1, 2).reshape(rows, FFN)
+    )(xim, dr, vec, sums, qb, fb, ht, dqkv, dqkv, w)
 
 
 def solution(mesh):
@@ -1104,16 +1111,14 @@
         rows = jnp.pad(rows, ((0, VECTOR_ROWS - len(rows)), (0, LANE - SHARD)))
         x = resid_in.swapaxes(0, 1).reshape(TOKENS, WIDTH)
         dy = grad_out.swapaxes(0, 1).reshape(TOKENS, WIDTH)
-        xim, dyim, h, ht, rows, fc, wq, wo = open_call(x, dy, rows, fc_weight, qkv_weight, out_weight)
+        xim, dyim, h, ht, rows, bq, bf, fc, wq, wo = open_call(x, dy, rows, fc_weight, qkv_weight, out_weight)
         wq, wo = wq.reshape(WIDTH, QKV), wo.reshape(WIDTH, WIDTH)
-        bo, g2, b2 = rows[5:6], rows[6:7], rows[7:8]
-        joint = lambda v: v.reshape(-1, PARTS, SHARD).swapaxes(0, 1).reshape(1, -1)
-        qkv, wf = qkv_call(h, wq, joint(rows[2:5]), fc)
-        o, r, n2, top, inv, wp = attn_call(qkv, xim, wo, bo, g2, b2, proj_weight)
-        y, dr, dr16, dwf, dwp, dbf, small = mlp_call(r, n2, dyim, g2, rows[12:13], wf.reshape(WIDTH, FFN), wp, to_steps(joint(rows[8:12])))
+        qkv, wf = qkv_call(h, wq, bq, fc)
+        o, r, n2, top, inv, wp = attn_call(qkv, xim, wo, rows, proj_weight)
+        y, dr, dr16, dwf, dwp, dbf, small = mlp_call(r, n2, dyim, rows, wf.reshape(WIDTH, FFN), wp, bf)
         do, dwo, dwf, y, dwp = outb_call(dr16, o, wo, dwf, y, dwp)
         dqkv, dbq, dwo = attn_back_call(qkv, do, top, inv, dwo)
-        dx, dwq, vec = qkvb_call(xim, dr, rows[:1], small, dbq, dbf, ht, dqkv, wq)
+        dx, dwq, vec = qkvb_call(xim, dr, rows, small, dbq, dbf, ht, dqkv, wq)
         dg2, db2, dbp, dbo = vec[:4]
         dbq, dbf = vec[4:7].reshape(-1), vec[7:11].reshape(-1)
         dg1, db1 = vec[VECTOR_ROWS - 2:]

time: 649 us -> 641 us (0.988)
  no operation moved by 1% of the time
where the time goes in v9:
time: 641 us; the launch traced here: 635 us
  Pallas kernels  621 us (97%)
  local copies, waits for them, and re-layouts  12.7 us (2%)
    pallas_call x1, Pallas kernels, mlp_call(): pl.pallas_call(mlp_kernel, grid=(MLP_STEPS + DRAIN,), in_specs=[hbm, hbm,...  258 us
    pallas_call x1, Pallas kernels, qkvb_call(): pl.pallas_call(qkvb_kernel, grid=(QB_GRID,), in_specs=[hbm, hbm, *(whole(...  109 us
    pallas_call x1, Pallas kernels, attn_call(): pl.pallas_call(attn_kernel, grid=(IMAGES,), in_specs=[main(QKV), tail(QKV...  60.1 us
    pallas_call x1, Pallas kernels, qkv_call(): pl.pallas_call(qkv_kernel, grid=(QKV // QKV_N,), in_specs=[whole(TOKENS,...  57.8 us
    pallas_call x1, Pallas kernels, attn_back_call(): pl.pallas_call(attn_back_kernel, grid=(OUT_STEPS + DRAIN - 1,), in_specs=...  56 us
    pallas_call x1, Pallas kernels, open_call(): pl.pallas_call(open_kernel, in_specs=[hbm, hbm, vmem, vmem, vmem, vmem],...  55.5 us
    pallas_call x1, Pallas kernels, outb_call(): pl.pallas_call(outb_kernel, grid=(WIDTH // MAIN,), in_specs=[full, full,...  25.5 us

profile of v9, /device:TPU:0, one launch (start us, length us, event | category | flops | bytes accessed | tf_op | source)
XLA Modules:
  0.0 634.8 jit_solution(11841525421216321001)
XLA Ops:
  0.6 0.9 concatenate.3
  1.5 0.1 reshape.63
  1.6 0.6 pad.4.rows_ref
  2.2 55.5 %open.1 = (bf16[2056,1280]{1,0:T(8,128)(2,1)}, bf16[2056,1280]{1,0:T(8,128)(2,1)}, bf16[2056,1280]{1,0:T(8,128)(2,1)}, bf16[1280,2056]{1,0:T(8,128)(2,1)}, f32[1...) custom-call(bf16[2056,1280]{1,0:T(8,128)(2,1)} %bitcast.29, ...), custom_call_target="tpu_custom_call" | custom-call | flops 1000000000 | bytes 60000000 | tf_op jit(solution)/shard_map/open/pallas_call | solution.py:447
  57.7 57.8 %qkv.1 = (bf16[2056,3840]{1,0:T(8,128)(2,1)}, bf16[2,2,2,2,80,5120]{5,4,3,2,1,0:T(8,128)(2,1)}) custom-call(bf16[2056,1280]{1,0:T(8,128)(2,1)} %get-tuple-element.50.h_ref, bf16[1280,3840]{1,0:T(8,128)(2,1)} %bitcast.31, f32[1,3840]{1,0:T(1,128)} %get-tuple-element.52.wb_ref, bf16[80,5120]{1,0:T(8,128)(2,1)} %get-tuple-element.53.own_ref), custom_call_target="tpu_custom_call" | custom-call | flops 20211302400 | bytes 60000000 | tf_op jit(solution)/shard_map/qkv/pallas_call | solution.py:494
  115.5 60.1 %attn.1 = (bf16[2056,1280]{1,0:T(8,128)(2,1)}, bf16[2056,1280]{1,0:T(8,128)(2,1)}, bf16[2056,1280]{1,0:T(8,128)(2,1)}, f32[8,16,256]{2,1,0:T(8,128)}, f32[8,16,2...) custom-call(bf16[2056,3840]{1,0:T(8,128)(2,1)} %get-tuple-element.54.qkv_ref.qkvt_ref, ...), custom_call_target="tpu_custom_call" | custom-call | flops 40000000000 | bytes 50000000 | tf_op jit(solution)/shard_map/attn/pallas_call | solution.py:793
  175.6 257.7 %mlp.1 = (bf16[2056,1280]{1,0:T(8,128)(2,1)}, f32[10,2056,128]{2,1,0:T(8,128)}, bf16[2056,1280]{1,0:T(8,128)(2,1)}, f32[80,5120]{1,0:T(8,128)}, f32[320,1280]{1,...) custom-call(bf16[2056,1280]{1,0:T(8,128)(2,1)} %get-tuple-element.58.r_hbm, ...), custom_call_target="tpu_custom_call" | custom-call | flops 161690419200 | bytes 150000000 | tf_op jit(solution)/shard_map/mlp/pallas_call | solution.py:634
  433.3 25.5 %outb.1 = (bf16[2056,1280]{1,0:T(8,128)(2,1)}, f32[1280,1280]{1,0:T(8,128)}, f32[80,5120]{1,0:T(8,128)}, bf16[2056,1280]{1,0:T(8,128)(2,1)}, f32[320,1280]{1,0:T(8,128)}) custom-call(bf16[2056,1280]{1,0:T(8,128)(2,1)} %get-tuple-element.64.dr_ref, bf16[2056,1280]{1,0:T(8,128)(2,1)} %get-tuple-element.65.o_ref, bf16[1280,1280]{1,0:T(8,128)(2,1)} %bitcast.34, ...), custom_call_target="tpu_custom_call" | custom-call | flops 13474201600 | bytes 50000000 | tf_op jit(solution)/shard_map/outb/pallas_call | solution.py:844
  458.8 56.0 %attn_back.1 = (bf16[2056,3840]{1,0:T(8,128)(2,1)}, f32[1,3840]{1,0:T(1,128)}, f32[80,1280]{1,0:T(8,128)}) custom-call(bf16[2056,3840]{1,0:T(8,128)(2,1)} %get-tuple-element.54.qkv_ref.qkvt_ref, bf16[2056,3840]{1,0:T(8,128)(2,1)} %get-tuple-element.54.qkv_ref.qkvt_ref, bf16[2056,1280]{1,0:T(8,128)(2,1)} %get-tuple-element.72.do_ref.dot_ref, ...), custom_call_target="tpu_custom_call" | custom-call | flops 40000000000 | bytes 50000000 | tf_op jit(solution)/shard_map/attn_back/pallas_call | solution.py:974
  514.8 108.6 %qkvb.1 = (bf16[2056,1280]{1,0:T(8,128)(2,1)}, f32[80,3840]{1,0:T(8,128)}, f32[16,80]{1,0:T(8,128)}) custom-call(bf16[2056,1280]{1,0:T(8,128)(2,1)} %get-tuple-element.55.x_ref.xt_ref.xim_hbm, f32[10,2056,128]{2,1,0:T(8,128)} %get-tuple-element.70.dr_hbm, f32[16,1280]{1,0:T(8,128)} %get-tuple-element.57.vec_ref, f32[32,1280]{1,0:T(8,128)} %get-tuple-element.71.sums_ref, ...), custom_call_target="tpu_custom_call" | custom-call | flops 40422604800 | bytes 80000000 | tf_op jit(solution)/shard_map/qkvb/pallas_call | solution.py:1087
  623.4 0.7 slice.14
  624.1 0.6 reshape.70
  624.8 0.7 slice.15
  625.5 1.4 slice_bitcast_fusion
  626.8 0.7 reshape.71
  627.5 0.0 copy-start
  627.5 0.0 copy-start.1
  627.5 5.3 copy.31
  632.8 0.0 copy-done
  632.8 1.0 copy.32
  633.8 0.0 copy-done.1
  633.9 0.8 copy.33
Async XLA Ops:
  627.5 5.3 copy-start
  627.5 6.4 %copy-start.1 = (f32[80,1280]{1,0:T(8,128)S(1)}, f32[80,1280]{1,0:T(8,128)}, u32[]{:S(2)}) copy-start(f32[80,1280]{1,0:T(8,128)} %get-tuple-element.112) | copy-start | bytes 1228804

commit v10 on v9

--- a/solution.py
+++ b/solution.py
@@ -15,6 +15,7 @@
 VMEM_MAX = 67043328
 LANE, SUBLANE, QUAD, QKV = 128, 8, 4, 3 * WIDTH
 ALL = ...
+TORUS = (2,) * QUAD
 LANES = WIDTH // LANE
 ROWS = 32
 
@@ -102,7 +103,7 @@
     return centered * inv, inv
 
 
-BLOCKS = [slice(a, b) for a, b in ((0, 512), (512, 1024), (1024, 1536), (1536, TOKENS))]
+BLOCKS = [slice(i * 512, i * 512 + 512) for i in range(3)] + [slice(1536, TOKENS)]
 
 
 def row_tiles(body, step=LANE):
@@ -166,6 +167,10 @@
 ORDERS = ((2, 1, 0), (1, 0, 2), (0, 2, 1))
 
 
+def all_blocks(rows, cols):
+    return jax.ShapeDtypeStruct((*TORUS, rows, cols), BF)
+
+
 class Links:
     def find(self, send, recv):
         self.send, self.recv = send, recv
@@ -194,7 +199,7 @@
     def __init__(self, rows, cols, cuts, by_rows):
         self.rows, self.cols, self.cuts, self.by_rows = rows, cols, cuts, by_rows
         self.parts = range(len(cuts) - 1)
-        self.full_shape = jax.ShapeDtypeStruct((2, 2, 2, 2, rows, cols), BF)
+        self.full_shape = all_blocks(rows, cols)
 
     def scratch(self):
         return [pltpu.SemaphoreType.DMA((SEMS,))] * self.COUNT
@@ -266,23 +271,22 @@
     def __init__(self, rows, cols, cuts, along, stride=1, spare=0):
         self.rows, self.cols, self.stride = rows, cols, stride
         self.slots, self.locals = 3 * stride + spare, 1 + stride
-        self.blocks = (2, 2, 2, 2, rows, cols)
+        self.blocks = (*TORUS, rows, cols)
         self.parts = [((slice(a, b), slice(None)) if along == 0 else (slice(None), slice(a, b))) for a, b in zip(cuts, cuts[1:])]
         self.shapes = [((b - a, cols) if along == 0 else (rows, b - a)) for a, b in zip(cuts, cuts[1:])]
 
     def scratch(self):
-        two = (2, 2, 2)
-        out = [pltpu.VMEM((self.locals, *self.blocks), F32), pltpu.VMEM((self.slots, *two, self.rows, self.cols), F32)]
+        out = [pltpu.VMEM((self.locals, *self.blocks), F32), pltpu.VMEM((self.slots, *TORUS[1:], self.rows, self.cols), F32)]
         for axes in (2, 1, 0):
-            out += [pltpu.VMEM((self.slots, *two[:axes], *shape), F32) for shape in self.shapes]
+            out += [pltpu.VMEM((self.slots, *TORUS[:axes], *shape), F32) for shape in self.shapes]
         return out + [pltpu.SemaphoreType.DMA((10, self.slots))] * 2
 
     COUNT = 13
 
     def bind(self, refs):
-        self.local, self.pair = refs[0], refs[1]
-        self.held = [None, refs[2:5], refs[5:SUBLANE], refs[SUBLANE:11]]
-        return self.find(*refs[11:])
+        self.local, self.pair, *rest = refs
+        self.held = [None, *(rest[steps(i, 3)] for i in range(3))]
+        return self.find(*rest[9:])
 
     def index(self, stage, part, side):
         order = ORDERS[part]
@@ -371,8 +375,10 @@
 WIDTH_CUTS = (0, 384, 896, WIDTH)
 QKV_ALL = Gather(SHARD, QKV, (0, WIDTH, 2 * WIDTH, QKV), False)
 OUT_ALL = Gather(SHARD, WIDTH, (0, 384, 768, WIDTH), False)
-FC_ALL = Gather(SHARD, FFN, (0, 1664, 3328, FFN), False)
-PROJ_ALL = Gather(FFN // PARTS, WIDTH, (0, 112, 208, FFN // PARTS), True)
+FC_HALF = FFN // 2
+FC_ALL = [Gather(SHARD, FC_HALF, (0, 896, 1792, FC_HALF), False) for _ in range(2)]
+PROJ_FIRST = 144
+PROJ_ALL = [Gather(PROJ_FIRST, WIDTH, (0, 48, 96, PROJ_FIRST), True), Gather(FFN // PARTS - PROJ_FIRST, WIDTH, (0, 64, 128, 176), True)]
 VECTOR_ALL = Gather(SHARD, LANE, (0, SHARD), True)
 
 
@@ -386,7 +392,7 @@
     vec_own[ALL] = rows[ALL].T[:SHARD, :].astype(BF)
     wq_own[ALL] = wq_ref[ALL].astype(BF)
     wo_own[ALL] = wo_ref[ALL].astype(BF)
-    pairs = [comm[2 * i:2 * i + 2] for i in range(3)]
+    pairs = [comm[steps(i, 2)] for i in range(3)]
     vectors = VECTOR_ALL.bind(vec_own, vec_full, pairs[0])
     weights = QKV_ALL.bind(wq_own, wq_full, pairs[1]), OUT_ALL.bind(wo_own, wo_full, pairs[2])
     gathers = (vectors, *weights)
@@ -466,27 +472,37 @@
 
 def qkv_kernel(h_ref, w_ref, wb_ref, own_ref, qkv_ref, full, *sems):
     t, last = step_id(), pl.num_programs(0) - 1
-    gather = FC_ALL.bind(own_ref, full, sems)
+    gathers = []
+    for i, kind in enumerate(FC_ALL):
+        part = pl.ds(i * FC_HALF, FC_HALF)
+        gathers.append(kind.bind(own_ref.at[:, part], full.at[(*EVERY, part)], sems[steps(i, 2)]))
 
     @pl.when(t == 0)
     def _():
-        gather.meet()
-        gather.begin()
+        gathers[0].meet()
+        for gather in gathers:
+            gather.begin()
 
     @pl.when(t == 1)
     def _():
-        gather.turn(1)
-
-    @pl.when(t == 3)
-    def _():
-        gather.turn(2)
+        for gather in gathers:
+            gather.turn(1)
+    for i in range(2):
+        @pl.when(t == i + 2)
+        def _():
+            gathers[i].turn(2)
     for rows in BLOCKS:
         qkv_ref[rows, :] = (dot(h_ref[rows, :], w_ref[ALL]) + wb_ref[ALL]).astype(BF)
 
     @pl.when(t == last)
     def _():
-        gather.turn(3)
-        gather.end()
+        for gather in gathers:
+            gather.turn(3)
+        for gather in gathers:
+            gather.end()
+
+
+EVERY = [slice(None)] * 5
 
 
 def qkv_call(h, w, wb, own):
@@ -496,8 +512,8 @@
         grid=(QKV // QKV_N,),
         in_specs=[whole(TOKENS, WIDTH, pipeline_mode=pl.Buffered(1)), by_cols(WIDTH, QKV_N), by_cols(1, QKV_N), whole(SHARD, FFN)],
         out_specs=[by_cols(TOKENS, QKV_N), hbm],
-        out_shape=[jax.ShapeDtypeStruct((TOKENS, QKV), BF), FC_ALL.full_shape],
-        scratch_shapes=FC_ALL.scratch(),
+        out_shape=[jax.ShapeDtypeStruct((TOKENS, QKV), BF), all_blocks(SHARD, FFN)],
+        scratch_shapes=FC_ALL[0].scratch() * 2,
         compiler_params=comm_params(QUAD),
         cost_estimate=cost(2 * TOKENS * WIDTH * QKV, 60_000_000),
         name="qkv",
@@ -694,26 +710,23 @@
                 tails, o_tail, o_t, ptail, o_buf, r_buf, n_buf, sa, sb, sems, own, *comm):
     b, last = step_id(), pl.num_programs(0) - 1
     slot = b % 2
-    gather = PROJ_ALL.bind(own, full, comm)
+    gathers = []
+    for i, kind in enumerate(PROJ_ALL):
+        part = pl.ds(i * PROJ_FIRST, kind.rows)
+        gathers.append(kind.bind(own.at[part], full.at[(*EVERY[1:], part)], comm[steps(i, 2)]))
 
     @pl.when(b == 0)
     def _():
         tails[ALL] = qkvt_ref[ALL].astype(F32)
         own[ALL] = proj_ref[ALL].astype(BF)
-        gather.meet()
-        gather.begin()
-
-    @pl.when(b == 1)
-    def _():
-        gather.turn(1)
-
-    @pl.when(b == 3)
-    def _():
-        gather.turn(2)
-
-    @pl.when(b == last)
-    def _():
-        gather.turn(3)
+        gathers[0].meet()
+        for gather in gathers:
+            gather.begin()
+
+    for turn, (stage, i) in enumerate(itertools.product((1, 2, 3), range(2))):
+        @pl.when(b == turn + 1 + stage // 3)
+        def _():
+            gathers[i].turn(stage)
 
     heads = head_rows()
     q_t, k_t, v_t = (heads * z for z in thirds(tails, pl.ds(b, 1)))
@@ -778,7 +791,8 @@
             cp.wait()
         for n, (buf, hbm) in enumerate(outs):
             out_copy(buf, hbm, slot, b, sems, n).wait()
-        gather.end()
+        for gather in gathers:
+            gather.end()
 
 
 def out_copy(buf, hbm, slot, b, sems, n):
@@ -798,11 +812,11 @@
         out_specs=[hbm, hbm, hbm, stat, stat, hbm],
         out_shape=[*[jax.ShapeDtypeStruct((TOKENS, WIDTH), BF)] * 3,
                    jax.ShapeDtypeStruct((IMAGES, HEADS, MAIN), F32), jax.ShapeDtypeStruct((IMAGES, HEADS, MAIN), F32),
-                   PROJ_ALL.full_shape],
+                   all_blocks(*proj.shape)],
         scratch_shapes=[pltpu.VMEM((IMAGES, QKV), F32), pltpu.VMEM((IMAGES, WIDTH), F32),
                         pltpu.VMEM((WIDTH, MAIN), F32), pltpu.VMEM((HEADS, MAIN), F32),
                         *[pltpu.VMEM((2, MAIN, WIDTH), BF)] * 3, *[pltpu.VMEM((MAIN, MAIN), F32)] * 2, pltpu.SemaphoreType.DMA((3, 2)),
-                        pltpu.VMEM(proj.shape, BF)] + PROJ_ALL.scratch(),
+                        pltpu.VMEM(proj.shape, BF)] + PROJ_ALL[0].scratch() * 2,
         compiler_params=comm_params(5),
         cost_estimate=ATTN_COST,
         name="attn",
@@ -993,12 +1007,11 @@
 QB_STEPS = QKV // QB_N
 QKV_SUM = Exchange(SHARD, QB_N, ROW_CUTS, 0, 2)
 VECTOR_SUM = Exchange(3 * SUBLANE, LANE, (0, SUBLANE, 2 * SUBLANE, 3 * SUBLANE), 0)
-VECTOR_STEP = QB_STEPS - 1
-BACK_STEP = VECTOR_STEP - 4
+VECTOR_STEP = QB_STEPS + 2
 QB_GRID = QB_STEPS + 1 + QUAD * QKV_SUM.stride
 
 
-def qkvb_kernel(xim_hbm, dr_hbm, vec_ref, sums_ref, qb_ref, fb_ref, ht_ref, dqkv_ref, wide_ref, w_ref, dx_hbm, dw_ref, out_vec_ref,
+def qkvb_kernel(xim_hbm, dr_hbm, vec_ref, sums_ref, qb_ref, fb_ref, ht_ref, dqkv_ref, w_ref, dx_hbm, dw_ref, out_vec_ref,
                 acc, dr, xd, sums, sems, *comm):
     t = step_id()
     by_row, by_vector = QKV_SUM.bind(comm[:Exchange.COUNT]), VECTOR_SUM.bind(comm[Exchange.COUNT:])
@@ -1035,12 +1048,9 @@
     @pl.when(t < QB_STEPS)
     def _():
         by_row.put_local(t, dot(ht_ref[ALL], dqkv_ref[ALL]))
-
-    @pl.when((t < BACK_STEP) & (t % 2 == 0))
-    def _():
-        acc[ALL] += dot_nt(wide_ref[ALL], w_ref[ALL])
-
-    @pl.when(t == BACK_STEP)
+        acc[ALL] += dot_nt(dqkv_ref[ALL], w_ref[ALL])
+
+    @pl.when(t == QB_STEPS)
     def _():
         for cp in loads:
             cp.wait()
@@ -1052,9 +1062,9 @@
             sums[steps(i, SUBLANE), :] += eights(v)
         acc[pl.ds(r, n), :] = joined(dr, r, n) + norm_back(dn, hat, inv, vec_ref[steps(LN1_GAIN, 1), :])
 
-    @pl.when((t >= BACK_STEP) & (t <= VECTOR_STEP))
-    def _():
-        back_part(back, t - BACK_STEP, 5)
+    @pl.when((t >= QB_STEPS) & (t <= VECTOR_STEP))
+    def _():
+        back_part(back, t - QB_STEPS, 3)
 
     @pl.when(t == VECTOR_STEP)
     def _():
@@ -1083,12 +1093,11 @@
 def qkvb_call(xim, dr, vec, sums, qb, fb, ht, dqkv, w):
     hbm = pl.BlockSpec(memory_space=pl.ANY)
     now = lambda i: jnp.minimum(i, QB_STEPS - 1)
-    wide = lambda i: jnp.minimum(i // 2, QKV // QKV_N - 1)
     return pl.pallas_call(
         qkvb_kernel,
         grid=(QB_GRID,),
         in_specs=[hbm, hbm, *(whole(*v.shape) for v in (vec, sums, qb, fb)),
-                  whole(WIDTH, TOKENS, pipeline_mode=pl.Buffered(1)), by_cols(TOKENS, QB_N, now), by_cols(TOKENS, QKV_N, wide), by_cols(WIDTH, QKV_N, wide)],
+                  whole(WIDTH, TOKENS, pipeline_mode=pl.Buffered(1)), by_cols(TOKENS, QB_N, now), by_cols(WIDTH, QB_N, now)],
         out_specs=[hbm, by_cols(SHARD, QB_N, lambda i: jnp.clip(i - 1 - QUAD * QKV_SUM.stride, 0, QB_STEPS - 1)),
                    whole(VECTOR_ROWS, SHARD)],
         out_shape=[jax.ShapeDtypeStruct((TOKENS, WIDTH), BF), jax.ShapeDtypeStruct((SHARD, QKV), F32),
@@ -1099,7 +1108,7 @@
         compiler_params=comm_params(2),
         cost_estimate=cost(QUAD * TOKENS * WIDTH * QKV, 80_000_000),
         name="qkvb",
-    )(xim, dr, vec, sums, qb, fb, ht, dqkv, dqkv, w)
+    )(xim, dr, vec, sums, qb, fb, ht, dqkv, w)
 
 
 def solution(mesh):

time: 641 us -> 632 us (0.986)
  Pallas kernels: 621 us -> 608 us
    pallas_call x1, Pallas kernels: 109 us -> 99.9 us  [qkvb_call(): pl.pallas_call(qkvb_kernel, grid=(QB_GRID,), in_specs=[hbm, hbm, *(whole(...]
where the time goes in v10:
time: 632 us; the launch traced here: 622 us
  Pallas kernels  608 us (96%)
  local copies, waits for them, and re-layouts  12.7 us (2%)
    pallas_call x1, Pallas kernels, mlp_call(): pl.pallas_call(mlp_kernel, grid=(MLP_STEPS + DRAIN,), in_specs=[hbm, hbm,...  258 us
    pallas_call x1, Pallas kernels, qkvb_call(): pl.pallas_call(qkvb_kernel, grid=(QB_GRID,), in_specs=[hbm, hbm, *(whole(...  99.9 us
    pallas_call x1, Pallas kernels, attn_call(): pl.pallas_call(attn_kernel, grid=(IMAGES,), in_specs=[main(QKV), tail(QKV...  58.3 us
    pallas_call x1, Pallas kernels, attn_back_call(): pl.pallas_call(attn_back_kernel, grid=(OUT_STEPS + DRAIN - 1,), in_specs=...  56 us
    pallas_call x1, Pallas kernels, open_call(): pl.pallas_call(open_kernel, in_specs=[hbm, hbm, vmem, vmem, vmem, vmem],...  55.5 us
    pallas_call x1, Pallas kernels, qkv_call(): pl.pallas_call(qkv_kernel, grid=(QKV // QKV_N,), in_specs=[whole(TOKENS,...  54 us
    pallas_call x1, Pallas kernels, outb_call(): pl.pallas_call(outb_kernel, grid=(WIDTH // MAIN,), in_specs=[full, full,...  25.5 us

profile of v10, /device:TPU:0, one launch (start us, length us, event | category | flops | bytes accessed | tf_op | source)
XLA Modules:
  0.0 621.5 jit_solution(7404505318830087272)
XLA Ops:
  0.6 0.9 concatenate.3
  1.5 0.1 reshape.63
  1.6 0.6 pad.4.rows_ref
  2.2 55.5 %open.1 = (bf16[2056,1280]{1,0:T(8,128)(2,1)}, bf16[2056,1280]{1,0:T(8,128)(2,1)}, bf16[2056,1280]{1,0:T(8,128)(2,1)}, bf16[1280,2056]{1,0:T(8,128)(2,1)}, f32[1...) custom-call(bf16[2056,1280]{1,0:T(8,128)(2,1)} %bitcast.29, ...), custom_call_target="tpu_custom_call" | custom-call | flops 1000000000 | bytes 60000000 | tf_op jit(solution)/shard_map/open/pallas_call | solution.py:453
  57.7 54.0 %qkv.1 = (bf16[2056,3840]{1,0:T(8,128)(2,1)}, bf16[2,2,2,2,80,5120]{5,4,3,2,1,0:T(8,128)(2,1)}) custom-call(bf16[2056,1280]{1,0:T(8,128)(2,1)} %get-tuple-element.50.h_ref, bf16[1280,3840]{1,0:T(8,128)(2,1)} %bitcast.31, f32[1,3840]{1,0:T(1,128)} %get-tuple-element.52.wb_ref, bf16[80,5120]{1,0:T(8,128)(2,1)} %get-tuple-element.53.own_ref), custom_call_target="tpu_custom_call" | custom-call | flops 20211302400 | bytes 60000000 | tf_op jit(solution)/shard_map/qkv/pallas_call | solution.py:510
  111.7 58.3 %attn.1 = (bf16[2056,1280]{1,0:T(8,128)(2,1)}, bf16[2056,1280]{1,0:T(8,128)(2,1)}, bf16[2056,1280]{1,0:T(8,128)(2,1)}, f32[8,16,256]{2,1,0:T(8,128)}, f32[8,16,2...) custom-call(bf16[2056,3840]{1,0:T(8,128)(2,1)} %get-tuple-element.54.qkv_ref.qkvt_ref, ...), custom_call_target="tpu_custom_call" | custom-call | flops 40000000000 | bytes 50000000 | tf_op jit(solution)/shard_map/attn/pallas_call | solution.py:807
  170.0 258.5 %mlp.1 = (bf16[2056,1280]{1,0:T(8,128)(2,1)}, f32[10,2056,128]{2,1,0:T(8,128)}, bf16[2056,1280]{1,0:T(8,128)(2,1)}, f32[80,5120]{1,0:T(8,128)}, f32[320,1280]{1,...) custom-call(bf16[2056,1280]{1,0:T(8,128)(2,1)} %get-tuple-element.58.r_hbm, ...), custom_call_target="tpu_custom_call" | custom-call | flops 161690419200 | bytes 150000000 | tf_op jit(solution)/shard_map/mlp/pallas_call | solution.py:650
  428.5 25.5 %outb.1 = (bf16[2056,1280]{1,0:T(8,128)(2,1)}, f32[1280,1280]{1,0:T(8,128)}, f32[80,5120]{1,0:T(8,128)}, bf16[2056,1280]{1,0:T(8,128)(2,1)}, f32[320,1280]{1,0:T(8,128)}) custom-call(bf16[2056,1280]{1,0:T(8,128)(2,1)} %get-tuple-element.64.dr_ref, bf16[2056,1280]{1,0:T(8,128)(2,1)} %get-tuple-element.65.o_ref, bf16[1280,1280]{1,0:T(8,128)(2,1)} %bitcast.34, ...), custom_call_target="tpu_custom_call" | custom-call | flops 13474201600 | bytes 50000000 | tf_op jit(solution)/shard_map/outb/pallas_call | solution.py:858
  454.0 56.0 %attn_back.1 = (bf16[2056,3840]{1,0:T(8,128)(2,1)}, f32[1,3840]{1,0:T(1,128)}, f32[80,1280]{1,0:T(8,128)}) custom-call(bf16[2056,3840]{1,0:T(8,128)(2,1)} %get-tuple-element.54.qkv_ref.qkvt_ref, bf16[2056,3840]{1,0:T(8,128)(2,1)} %get-tuple-element.54.qkv_ref.qkvt_ref, bf16[2056,1280]{1,0:T(8,128)(2,1)} %get-tuple-element.72.do_ref.dot_ref, ...), custom_call_target="tpu_custom_call" | custom-call | flops 40000000000 | bytes 50000000 | tf_op jit(solution)/shard_map/attn_back/pallas_call | solution.py:988
  510.0 99.9 %qkvb.1 = (bf16[2056,1280]{1,0:T(8,128)(2,1)}, f32[80,3840]{1,0:T(8,128)}, f32[16,80]{1,0:T(8,128)}) custom-call(bf16[2056,1280]{1,0:T(8,128)(2,1)} %get-tuple-element.55.x_ref.xt_ref.xim_hbm, f32[10,2056,128]{2,1,0:T(8,128)} %get-tuple-element.70.dr_hbm, f32[16,1280]{1,0:T(8,128)} %get-tuple-element.57.vec_ref, f32[32,1280]{1,0:T(8,128)} %get-tuple-element.71.sums_ref, ...), custom_call_target="tpu_custom_call" | custom-call | flops 40422604800 | bytes 80000000 | tf_op jit(solution)/shard_map/qkvb/pallas_call | solution.py:1096
  609.9 0.7 slice.14
  610.6 0.6 reshape.70
  611.3 0.7 slice.15
  612.0 1.4 slice_bitcast_fusion
  613.3 0.7 reshape.71
  614.0 0.0 copy-start
  614.0 0.0 copy-start.1
  614.0 5.3 copy.31
  619.3 0.0 copy-done
  619.3 1.0 copy.32
  620.3 0.0 copy-done.1
  620.3 0.8 copy.33
Async XLA Ops:
  614.0 5.3 copy-start
  614.0 6.4 %copy-start.1 = (f32[80,1280]{1,0:T(8,128)S(1)}, f32[80,1280]{1,0:T(8,128)}, u32[]{:S(2)}) copy-start(f32[80,1280]{1,0:T(8,128)} %get-tuple-element.112) | copy-start | bytes 1228804

commit v11 on v10

--- a/solution.py
+++ b/solution.py
@@ -12,6 +12,7 @@
 TOKENS = IMAGES * SEQ
 TAIL = IMAGES * MAIN
 LN_EPS = 1e-5
+LOG2E = math.log2(math.e)
 VMEM_MAX = 67043328
 LANE, SUBLANE, QUAD, QKV = 128, 8, 4, 3 * WIDTH
 ALL = ...
@@ -373,7 +374,8 @@
 UNITS = MLP_F // PARTS
 MLP_STEPS = FFN // MLP_F
 WIDTH_CUTS = (0, 384, 896, WIDTH)
-QKV_ALL = Gather(SHARD, QKV, (0, WIDTH, 2 * WIDTH, QKV), False)
+QKV_HALF = QKV // 2
+QKV_ALL = [Gather(SHARD, QKV_HALF, (0, MLP_F * 5 // 2, WIDTH, QKV_HALF), False) for _ in range(2)]
 OUT_ALL = Gather(SHARD, WIDTH, (0, 384, 768, WIDTH), False)
 FC_HALF = FFN // 2
 FC_ALL = [Gather(SHARD, FC_HALF, (0, 896, 1792, FC_HALF), False) for _ in range(2)]
@@ -382,19 +384,26 @@
 VECTOR_ALL = Gather(SHARD, LANE, (0, SHARD), True)
 
 
-def open_kernel(x_hbm, dy_hbm, rows_ref, fc_ref, wq_ref, wo_ref, xim_hbm, dyim_hbm, h_hbm, ht_hbm, vec_ref, qb_ref, fb_ref, fc_own, wq_full, wo_full,
+def open_kernel(x_hbm, dy_hbm, lg_ref, lb_ref, qv_ref, ov_ref, mg_ref, mb_ref, fv_ref, pv_ref, fc_ref, wq_ref, wo_ref, xim_hbm, dyim_hbm, h_hbm, ht_hbm, vec_ref, qb_ref, fb_ref, fc_own, wq_full, wo_full,
                 x, dy, wide, h, ht, rows, vec_own, vec_full, wq_own, wo_own, sems, *comm):
     loads = [pltpu.make_async_copy(src, dst, sems.at[i]) for i, (src, dst) in enumerate(((x_hbm, x), (dy_hbm, dy)))]
     for cp in loads:
         cp.start()
     clear(rows)
-    rows[:VECTOR_ROWS, :] = rows_ref[ALL]
+    row = 0
+    for ref in (lg_ref, lb_ref, qv_ref, ov_ref, mg_ref, mb_ref, fv_ref, pv_ref):
+        for i in range(ref.shape[1] // SHARD):
+            rows[steps(row, 1), :SHARD] = ref[:, steps(i, SHARD)]
+            row += 1
     vec_own[ALL] = rows[ALL].T[:SHARD, :].astype(BF)
     wq_own[ALL] = wq_ref[ALL].astype(BF)
     wo_own[ALL] = wo_ref[ALL].astype(BF)
-    pairs = [comm[steps(i, 2)] for i in range(3)]
+    pairs = [comm[steps(i, 2)] for i in range(QUAD)]
     vectors = VECTOR_ALL.bind(vec_own, vec_full, pairs[0])
-    weights = QKV_ALL.bind(wq_own, wq_full, pairs[1]), OUT_ALL.bind(wo_own, wo_full, pairs[2])
+    weights = [OUT_ALL.bind(wo_own, wo_full, pairs[1])]
+    for i, kind in enumerate(QKV_ALL):
+        part = pl.ds(i * QKV_HALF, QKV_HALF)
+        weights.append(kind.bind(wq_own.at[:, part], wq_full.at[(*EVERY, part)], pairs[2 + i]))
     gathers = (vectors, *weights)
     vectors.meet()
     for gather in gathers:
@@ -448,23 +457,23 @@
         cp.wait()
 
 
-def open_call(x, dy, rows, fc, wq, wo):
+def open_call(x, dy, vectors, fc, wq, wo):
     hbm, vmem = pl.BlockSpec(memory_space=pl.ANY), pl.BlockSpec(memory_space=pltpu.VMEM)
     return pl.pallas_call(
         open_kernel,
-        in_specs=[hbm, hbm, vmem, vmem, vmem, vmem],
+        in_specs=[hbm, hbm] + [vmem] * (len(vectors) + 3),
         out_specs=[hbm, hbm, hbm, hbm, vmem, vmem, vmem, vmem, hbm, hbm],
         out_shape=[*[jax.ShapeDtypeStruct((TOKENS, WIDTH), BF)] * 3,
                    jax.ShapeDtypeStruct((WIDTH, TOKENS), BF), jax.ShapeDtypeStruct((VECTOR_ROWS, WIDTH), F32),
-                   *(jax.ShapeDtypeStruct((1, n), F32) for n in (QKV, FFN)), jax.ShapeDtypeStruct(fc.shape, BF), QKV_ALL.full_shape, OUT_ALL.full_shape],
+                   *(jax.ShapeDtypeStruct((1, n), F32) for n in (QKV, FFN)), jax.ShapeDtypeStruct(fc.shape, BF), all_blocks(SHARD, QKV), OUT_ALL.full_shape],
         scratch_shapes=[pltpu.VMEM((TOKENS, WIDTH), BF), pltpu.VMEM((TOKENS, WIDTH), BF), pltpu.VMEM((LANES, TOKENS, LANE), F32),
                         pltpu.VMEM((TOKENS, WIDTH), BF), pltpu.VMEM((WIDTH, TOKENS), BF), pltpu.VMEM((LANE, LANE), F32), pltpu.VMEM((SHARD, LANE), BF),
                         pltpu.VMEM(VECTOR_ALL.full_shape.shape, BF), pltpu.VMEM((SHARD, QKV), BF), pltpu.VMEM((SHARD, WIDTH), BF),
-                        pltpu.SemaphoreType.DMA((QUAD,))] + VECTOR_ALL.scratch() + QKV_ALL.scratch() + OUT_ALL.scratch(),
+                        pltpu.SemaphoreType.DMA((QUAD,))] + VECTOR_ALL.scratch() * QUAD,
         compiler_params=pltpu.CompilerParams(vmem_limit_bytes=VMEM_MAX, collective_id=3, has_side_effects=True),
         cost_estimate=cost(1_000_000_000, 60_000_000),
         name="open",
-    )(x, dy, rows, fc, wq, wo)
+    )(x, dy, *vectors, fc, wq, wo)
 
 
 QKV_N = 768
@@ -529,7 +538,7 @@
 
 
 def gelu_pair(u):
-    bell = jnp.exp(u * u * -0.5)
+    bell = jnp.exp2(u * u * (-0.5 * LOG2E))
     t = 1.0 / (1.0 + CDF_P * jnp.abs(u))
     poly = CDF_C[6]
     for c in CDF_C[5::-1]:
@@ -672,6 +681,7 @@
 
 
 SCALE = HEAD ** -0.5
+SCALE2 = SCALE * LOG2E
 ATTN_COST = cost(40_000_000_000, 50_000_000, 8_400_000)
 
 
@@ -699,8 +709,8 @@
 
 def tail_softmax(s, s_self):
     m = jnp.maximum(jnp.max(s, axis=1, keepdims=True), s_self)
-    e = jnp.exp((s - m) * SCALE)
-    e_self = jnp.exp((s_self - m) * SCALE)
+    e = jnp.exp2((s - m) * SCALE2)
+    e_self = jnp.exp2((s_self - m) * SCALE2)
     inv = 1.0 / (row_sum(e) + e_self)
     return e * inv, e_self * inv
 
@@ -750,8 +760,8 @@
             next_scores(h + 1)
         s, mine = scores[h % 2], steps(h, 1)
         top = jnp.maximum(col_max(s[ALL]), s_tail[mine, :])
-        e = jnp.exp((s[ALL] - top) * SCALE)
-        e_tail = jnp.exp((s_tail[mine, :] - top) * SCALE)
+        e = jnp.exp2((s[ALL] - top) * SCALE2)
+        e_tail = jnp.exp2((s_tail[mine, :] - top) * SCALE2)
         inv = 1.0 / (col_sum(e) + e_tail)
         max_ref[0, mine, :] = top
         inv_ref[0, mine, :] = inv
@@ -922,7 +932,7 @@
     dk[ALL] = dot_tn(ds16, q_t16)
     dv[ALL] = dot_tn(p.astype(BF), do_t16)
 
-    p_tail = jnp.exp((dot_nt(k_t16, q) - max_ref[0]) * SCALE) * inv_ref[0]
+    p_tail = jnp.exp2((dot_nt(k_t16, q) - max_ref[0]) * SCALE2) * inv_ref[0]
     dp_tail = dot_nt(v_t16, do)
     inner_tail = p_tail * dp_tail
 
@@ -945,7 +955,7 @@
         here, q_h, do_h = masked(h)
         mine = steps(h, 1)
         s, dp = (ref[ALL] for ref in ahead[h % 2])
-        p = jnp.exp((s - max_ref[0, mine, :]) * SCALE) * inv_ref[0, mine, :]
+        p = jnp.exp2((s - max_ref[0, mine, :]) * SCALE2) * inv_ref[0, mine, :]
         inner = col_sum(p * dp) + inner_tail[mine, :]
         ds = (p * (dp - inner) * SCALE).astype(BF)
         dv[:, here] += dot(p.astype(BF), do_h)
@@ -1116,11 +1126,10 @@
 
     def device_step(resid_in, grad_out, ln1_gain, ln1_bias, qkv_weight, qkv_bias, out_weight, out_bias,
                     ln2_gain, ln2_bias, fc_weight, fc_bias, proj_weight, proj_bias):
-        rows = jnp.concatenate([ln1_gain, ln1_bias, qkv_bias, out_bias, ln2_gain, ln2_bias, fc_bias, proj_bias]).reshape(-1, SHARD)
-        rows = jnp.pad(rows, ((0, VECTOR_ROWS - len(rows)), (0, LANE - SHARD)))
+        vectors = [v.reshape(1, -1) for v in (ln1_gain, ln1_bias, qkv_bias, out_bias, ln2_gain, ln2_bias, fc_bias, proj_bias)]
         x = resid_in.swapaxes(0, 1).reshape(TOKENS, WIDTH)
         dy = grad_out.swapaxes(0, 1).reshape(TOKENS, WIDTH)
-        xim, dyim, h, ht, rows, bq, bf, fc, wq, wo = open_call(x, dy, rows, fc_weight, qkv_weight, out_weight)
+        xim, dyim, h, ht, rows, bq, bf, fc, wq, wo = open_call(x, dy, vectors, fc_weight, qkv_weight, out_weight)
         wq, wo = wq.reshape(WIDTH, QKV), wo.reshape(WIDTH, WIDTH)
         qkv, wf = qkv_call(h, wq, bq, fc)
         o, r, n2, top, inv, wp = attn_call(qkv, xim, wo, rows, proj_weight)

time: 632 us -> 637 us (level)
  Pallas kernels: 608 us -> 619 us
    pallas_call x1, Pallas kernels: 58.3 us -> 70 us  [attn_call(): pl.pallas_call(attn_kernel, grid=(IMAGES,), in_specs=[main(QKV), tail(QKV...]
where the time goes in v11:
time: 637 us; the launch traced here: 632 us
  Pallas kernels  619 us (97%)
  local copies, waits for them, and re-layouts  12.4 us (2%)
    pallas_call x1, Pallas kernels, mlp_call(): pl.pallas_call(mlp_kernel, grid=(MLP_STEPS + DRAIN,), in_specs=[hbm, hbm,...  257 us
    pallas_call x1, Pallas kernels, qkvb_call(): pl.pallas_call(qkvb_kernel, grid=(QB_GRID,), in_specs=[hbm, hbm, *(whole(...  99.9 us
    pallas_call x1, Pallas kernels, attn_call(): pl.pallas_call(attn_kernel, grid=(IMAGES,), in_specs=[main(QKV), tail(QKV...  70 us
    pallas_call x1, Pallas kernels, open_call(): pl.pallas_call(open_kernel, in_specs=[hbm, hbm] + [vmem] * (len(vectors)...  56.1 us
    pallas_call x1, Pallas kernels, attn_back_call(): pl.pallas_call(attn_back_kernel, grid=(OUT_STEPS + DRAIN - 1,), in_specs=...  55.4 us
    pallas_call x1, Pallas kernels, qkv_call(): pl.pallas_call(qkv_kernel, grid=(QKV // QKV_N,), in_specs=[whole(TOKENS,...  54.5 us
    pallas_call x1, Pallas kernels, outb_call(): pl.pallas_call(outb_kernel, grid=(WIDTH // MAIN,), in_specs=[full, full,...  25.7 us

profile of v11, /device:TPU:0, one launch (start us, length us, event | category | flops | bytes accessed | tf_op | source)
XLA Modules:
  0.0 632.5 jit_solution(3628347009343466178)
XLA Ops:
  0.6 1.2 reshape.90.fv_ref
  1.9 56.1 %open.1 = (bf16[2056,1280]{1,0:T(8,128)(2,1)}, bf16[2056,1280]{1,0:T(8,128)(2,1)}, bf16[2056,1280]{1,0:T(8,128)(2,1)}, bf16[1280,2056]{1,0:T(8,128)(2,1)}, f32[1...) custom-call(bf16[2056,1280]{1,0:T(8,128)(2,1)} %bitcast.35, ...), custom_call_target="tpu_custom_call" | custom-call | flops 1000000000 | bytes 60000000 | tf_op jit(solution)/shard_map/open/pallas_call | solution.py:462
  58.0 54.5 %qkv.1 = (bf16[2056,3840]{1,0:T(8,128)(2,1)}, bf16[2,2,2,2,80,5120]{5,4,3,2,1,0:T(8,128)(2,1)}) custom-call(bf16[2056,1280]{1,0:T(8,128)(2,1)} %get-tuple-element.50.h_ref, bf16[1280,3840]{1,0:T(8,128)(2,1)} %bitcast.45, f32[1,3840]{1,0:T(1,128)} %get-tuple-element.52.wb_ref, bf16[80,5120]{1,0:T(8,128)(2,1)} %get-tuple-element.53.own_ref), custom_call_target="tpu_custom_call" | custom-call | flops 20211302400 | bytes 60000000 | tf_op jit(solution)/shard_map/qkv/pallas_call | solution.py:519
  112.5 70.0 %attn.1 = (bf16[2056,1280]{1,0:T(8,128)(2,1)}, bf16[2056,1280]{1,0:T(8,128)(2,1)}, bf16[2056,1280]{1,0:T(8,128)(2,1)}, f32[8,16,256]{2,1,0:T(8,128)}, f32[8,16,2...) custom-call(bf16[2056,3840]{1,0:T(8,128)(2,1)} %get-tuple-element.54.qkv_ref.qkvt_ref, ...), custom_call_target="tpu_custom_call" | custom-call | flops 40000000000 | bytes 50000000 | tf_op jit(solution)/shard_map/attn/pallas_call | solution.py:817
  182.5 257.4 %mlp.1 = (bf16[2056,1280]{1,0:T(8,128)(2,1)}, f32[10,2056,128]{2,1,0:T(8,128)}, bf16[2056,1280]{1,0:T(8,128)(2,1)}, f32[80,5120]{1,0:T(8,128)}, f32[320,1280]{1,...) custom-call(bf16[2056,1280]{1,0:T(8,128)(2,1)} %get-tuple-element.58.r_hbm, ...), custom_call_target="tpu_custom_call" | custom-call | flops 161690419200 | bytes 150000000 | tf_op jit(solution)/shard_map/mlp/pallas_call | solution.py:659
  439.8 25.7 %outb.1 = (bf16[2056,1280]{1,0:T(8,128)(2,1)}, f32[1280,1280]{1,0:T(8,128)}, f32[80,5120]{1,0:T(8,128)}, bf16[2056,1280]{1,0:T(8,128)(2,1)}, f32[320,1280]{1,0:T(8,128)}) custom-call(bf16[2056,1280]{1,0:T(8,128)(2,1)} %get-tuple-element.64.dr_ref, bf16[2056,1280]{1,0:T(8,128)(2,1)} %get-tuple-element.65.o_ref, bf16[1280,1280]{1,0:T(8,128)(2,1)} %bitcast.48, ...), custom_call_target="tpu_custom_call" | custom-call | flops 13474201600 | bytes 50000000 | tf_op jit(solution)/shard_map/outb/pallas_call | solution.py:868
  465.6 55.4 %attn_back.1 = (bf16[2056,3840]{1,0:T(8,128)(2,1)}, f32[1,3840]{1,0:T(1,128)}, f32[80,1280]{1,0:T(8,128)}) custom-call(bf16[2056,3840]{1,0:T(8,128)(2,1)} %get-tuple-element.54.qkv_ref.qkvt_ref, bf16[2056,3840]{1,0:T(8,128)(2,1)} %get-tuple-element.54.qkv_ref.qkvt_ref, bf16[2056,1280]{1,0:T(8,128)(2,1)} %get-tuple-element.72.do_ref.dot_ref, ...), custom_call_target="tpu_custom_call" | custom-call | flops 40000000000 | bytes 50000000 | tf_op jit(solution)/shard_map/attn_back/pallas_call | solution.py:998
  520.9 99.9 %qkvb.1 = (bf16[2056,1280]{1,0:T(8,128)(2,1)}, f32[80,3840]{1,0:T(8,128)}, f32[16,80]{1,0:T(8,128)}) custom-call(bf16[2056,1280]{1,0:T(8,128)(2,1)} %get-tuple-element.55.x_ref.xt_ref.xim_hbm, f32[10,2056,128]{2,1,0:T(8,128)} %get-tuple-element.70.dr_hbm, f32[16,1280]{1,0:T(8,128)} %get-tuple-element.57.vec_ref, f32[32,1280]{1,0:T(8,128)} %get-tuple-element.71.sums_ref, ...), custom_call_target="tpu_custom_call" | custom-call | flops 40422604800 | bytes 80000000 | tf_op jit(solution)/shard_map/qkvb/pallas_call | solution.py:1106
  620.9 0.7 slice.14
  621.6 0.6 reshape.98
  622.2 0.7 slice.15
  622.9 1.4 slice_bitcast_fusion
  624.3 0.7 reshape.99
  624.9 0.0 copy-start
  624.9 0.0 copy-start.1
  624.9 5.3 copy.31
  630.2 0.0 copy-done
  630.2 1.0 copy.32
  631.3 0.0 copy-done.1
  631.3 0.8 copy.33
Async XLA Ops:
  624.9 5.3 copy-start
  624.9 6.4 %copy-start.1 = (f32[80,1280]{1,0:T(8,128)S(1)}, f32[80,1280]{1,0:T(8,128)}, u32[]{:S(2)}) copy-start(f32[80,1280]{1,0:T(8,128)} %get-tuple-element.112) | copy-start | bytes 1228804

commit v12 on v10

--- a/solution.py
+++ b/solution.py
@@ -12,6 +12,7 @@
 TOKENS = IMAGES * SEQ
 TAIL = IMAGES * MAIN
 LN_EPS = 1e-5
+LOG2E = math.log2(math.e)
 VMEM_MAX = 67043328
 LANE, SUBLANE, QUAD, QKV = 128, 8, 4, 3 * WIDTH
 ALL = ...
@@ -529,7 +530,7 @@
 
 
 def gelu_pair(u):
-    bell = jnp.exp(u * u * -0.5)
+    bell = jnp.exp2(u * u * (-0.5 * LOG2E))
     t = 1.0 / (1.0 + CDF_P * jnp.abs(u))
     poly = CDF_C[6]
     for c in CDF_C[5::-1]:
@@ -672,6 +673,7 @@
 
 
 SCALE = HEAD ** -0.5
+SCALE2 = SCALE * LOG2E
 ATTN_COST = cost(40_000_000_000, 50_000_000, 8_400_000)
 
 
@@ -922,7 +924,7 @@
     dk[ALL] = dot_tn(ds16, q_t16)
     dv[ALL] = dot_tn(p.astype(BF), do_t16)
 
-    p_tail = jnp.exp((dot_nt(k_t16, q) - max_ref[0]) * SCALE) * inv_ref[0]
+    p_tail = jnp.exp2((dot_nt(k_t16, q) - max_ref[0]) * SCALE2) * inv_ref[0]
     dp_tail = dot_nt(v_t16, do)
     inner_tail = p_tail * dp_tail
 
@@ -945,7 +947,7 @@
         here, q_h, do_h = masked(h)
         mine = steps(h, 1)
         s, dp = (ref[ALL] for ref in ahead[h % 2])
-        p = jnp.exp((s - max_ref[0, mine, :]) * SCALE) * inv_ref[0, mine, :]
+        p = jnp.exp2((s - max_ref[0, mine, :]) * SCALE2) * inv_ref[0, mine, :]
         inner = col_sum(p * dp) + inner_tail[mine, :]
         ds = (p * (dp - inner) * SCALE).astype(BF)
         dv[:, here] += dot(p.astype(BF), do_h)

time: 632 us -> 637 us (level)
  Pallas kernels: 608 us -> 618 us
    pallas_call x1, Pallas kernels: 58.3 us -> 70.3 us  [attn_call(): pl.pallas_call(attn_kernel, grid=(IMAGES,), in_specs=[main(QKV), tail(QKV...]
where the time goes in v12:
time: 637 us; the launch traced here: 632 us
  Pallas kernels  618 us (97%)
  local copies, waits for them, and re-layouts  12.7 us (2%)
    pallas_call x1, Pallas kernels, mlp_call(): pl.pallas_call(mlp_kernel, grid=(MLP_STEPS + DRAIN,), in_specs=[hbm, hbm,...  257 us
    pallas_call x1, Pallas kernels, qkvb_call(): pl.pallas_call(qkvb_kernel, grid=(QB_GRID,), in_specs=[hbm, hbm, *(whole(...  99.9 us
    pallas_call x1, Pallas kernels, attn_call(): pl.pallas_call(attn_kernel, grid=(IMAGES,), in_specs=[main(QKV), tail(QKV...  70.3 us
    pallas_call x1, Pallas kernels, open_call(): pl.pallas_call(open_kernel, in_specs=[hbm, hbm, vmem, vmem, vmem, vmem],...  55.5 us
    pallas_call x1, Pallas kernels, attn_back_call(): pl.pallas_call(attn_back_kernel, grid=(OUT_STEPS + DRAIN - 1,), in_specs=...  55.3 us
    pallas_call x1, Pallas kernels, qkv_call(): pl.pallas_call(qkv_kernel, grid=(QKV // QKV_N,), in_specs=[whole(TOKENS,...  54 us
    pallas_call x1, Pallas kernels, outb_call(): pl.pallas_call(outb_kernel, grid=(WIDTH // MAIN,), in_specs=[full, full,...  25.7 us

profile of v12, /device:TPU:0, one launch (start us, length us, event | category | flops | bytes accessed | tf_op | source)
XLA Modules:
  0.0 632.0 jit_solution(3217939090885069970)
XLA Ops:
  0.6 0.9 concatenate.3
  1.5 0.1 reshape.63
  1.6 0.6 pad.4.rows_ref
  2.2 55.5 %open.1 = (bf16[2056,1280]{1,0:T(8,128)(2,1)}, bf16[2056,1280]{1,0:T(8,128)(2,1)}, bf16[2056,1280]{1,0:T(8,128)(2,1)}, bf16[1280,2056]{1,0:T(8,128)(2,1)}, f32[1...) custom-call(bf16[2056,1280]{1,0:T(8,128)(2,1)} %bitcast.29, ...), custom_call_target="tpu_custom_call" | custom-call | flops 1000000000 | bytes 60000000 | tf_op jit(solution)/shard_map/open/pallas_call | solution.py:454
  57.7 54.0 %qkv.1 = (bf16[2056,3840]{1,0:T(8,128)(2,1)}, bf16[2,2,2,2,80,5120]{5,4,3,2,1,0:T(8,128)(2,1)}) custom-call(bf16[2056,1280]{1,0:T(8,128)(2,1)} %get-tuple-element.50.h_ref, bf16[1280,3840]{1,0:T(8,128)(2,1)} %bitcast.31, f32[1,3840]{1,0:T(1,128)} %get-tuple-element.52.wb_ref, bf16[80,5120]{1,0:T(8,128)(2,1)} %get-tuple-element.53.own_ref), custom_call_target="tpu_custom_call" | custom-call | flops 20211302400 | bytes 60000000 | tf_op jit(solution)/shard_map/qkv/pallas_call | solution.py:511
  111.7 70.3 %attn.1 = (bf16[2056,1280]{1,0:T(8,128)(2,1)}, bf16[2056,1280]{1,0:T(8,128)(2,1)}, bf16[2056,1280]{1,0:T(8,128)(2,1)}, f32[8,16,256]{2,1,0:T(8,128)}, f32[8,16,2...) custom-call(bf16[2056,3840]{1,0:T(8,128)(2,1)} %get-tuple-element.54.qkv_ref.qkvt_ref, ...), custom_call_target="tpu_custom_call" | custom-call | flops 40000000000 | bytes 50000000 | tf_op jit(solution)/shard_map/attn/pallas_call | solution.py:809
  182.0 257.4 %mlp.1 = (bf16[2056,1280]{1,0:T(8,128)(2,1)}, f32[10,2056,128]{2,1,0:T(8,128)}, bf16[2056,1280]{1,0:T(8,128)(2,1)}, f32[80,5120]{1,0:T(8,128)}, f32[320,1280]{1,...) custom-call(bf16[2056,1280]{1,0:T(8,128)(2,1)} %get-tuple-element.58.r_hbm, ...), custom_call_target="tpu_custom_call" | custom-call | flops 161690419200 | bytes 150000000 | tf_op jit(solution)/shard_map/mlp/pallas_call | solution.py:651
  439.4 25.7 %outb.1 = (bf16[2056,1280]{1,0:T(8,128)(2,1)}, f32[1280,1280]{1,0:T(8,128)}, f32[80,5120]{1,0:T(8,128)}, bf16[2056,1280]{1,0:T(8,128)(2,1)}, f32[320,1280]{1,0:T(8,128)}) custom-call(bf16[2056,1280]{1,0:T(8,128)(2,1)} %get-tuple-element.64.dr_ref, bf16[2056,1280]{1,0:T(8,128)(2,1)} %get-tuple-element.65.o_ref, bf16[1280,1280]{1,0:T(8,128)(2,1)} %bitcast.34, ...), custom_call_target="tpu_custom_call" | custom-call | flops 13474201600 | bytes 50000000 | tf_op jit(solution)/shard_map/outb/pallas_call | solution.py:860
  465.1 55.3 %attn_back.1 = (bf16[2056,3840]{1,0:T(8,128)(2,1)}, f32[1,3840]{1,0:T(1,128)}, f32[80,1280]{1,0:T(8,128)}) custom-call(bf16[2056,3840]{1,0:T(8,128)(2,1)} %get-tuple-element.54.qkv_ref.qkvt_ref, bf16[2056,3840]{1,0:T(8,128)(2,1)} %get-tuple-element.54.qkv_ref.qkvt_ref, bf16[2056,1280]{1,0:T(8,128)(2,1)} %get-tuple-element.72.do_ref.dot_ref, ...), custom_call_target="tpu_custom_call" | custom-call | flops 40000000000 | bytes 50000000 | tf_op jit(solution)/shard_map/attn_back/pallas_call | solution.py:990
  520.4 99.9 %qkvb.1 = (bf16[2056,1280]{1,0:T(8,128)(2,1)}, f32[80,3840]{1,0:T(8,128)}, f32[16,80]{1,0:T(8,128)}) custom-call(bf16[2056,1280]{1,0:T(8,128)(2,1)} %get-tuple-element.55.x_ref.xt_ref.xim_hbm, f32[10,2056,128]{2,1,0:T(8,128)} %get-tuple-element.70.dr_hbm, f32[16,1280]{1,0:T(8,128)} %get-tuple-element.57.vec_ref, f32[32,1280]{1,0:T(8,128)} %get-tuple-element.71.sums_ref, ...), custom_call_target="tpu_custom_call" | custom-call | flops 40422604800 | bytes 80000000 | tf_op jit(solution)/shard_map/qkvb/pallas_call | solution.py:1098
  620.4 0.7 slice.14
  621.1 0.6 reshape.70
  621.7 0.7 slice.15
  622.4 1.4 slice_bitcast_fusion
  623.8 0.7 reshape.71
  624.5 0.0 copy-start
  624.5 0.0 copy-start.1
  624.5 5.3 copy.31
  629.8 0.0 copy-done
  629.8 1.0 copy.32
  630.8 0.0 copy-done.1
  630.8 0.8 copy.33
Async XLA Ops:
  624.5 5.3 copy-start
  624.5 6.4 %copy-start.1 = (f32[80,1280]{1,0:T(8,128)S(1)}, f32[80,1280]{1,0:T(8,128)}, u32[]{:S(2)}) copy-start(f32[80,1280]{1,0:T(8,128)} %get-tuple-element.112) | copy-start | bytes 1228804

commit v13 on v12

--- a/solution.py
+++ b/solution.py
@@ -432,8 +432,12 @@
         hat, _ = norm_stats(x[pl.ds(r, n), :].astype(F32))
         h[pl.ds(r, n), :] = (hat * gain + bias).astype(BF)
     row_tiles(norm, ROWS)
-    for b in range(IMAGES):
-        ht[:, steps(b, MAIN)] = h[steps(b, MAIN), :].T
+
+    def turn(b, carry):
+        image = pl.ds(pl.multiple_of(b * MAIN, MAIN), MAIN)
+        ht[:, image] = h[image, :].T
+        return carry
+    lax.fori_loop(0, IMAGES, turn, 0)
     ht[:, TAIL:] = h[TAIL:, :].T
     stores = [pltpu.make_async_copy(src, dst, sems.at[i]) for i, (src, dst) in enumerate(((x, xim_hbm), (dy, dyim_hbm), (h, h_hbm), (ht, ht_hbm)))]
     for cp in stores:

time: 637 us -> 626 us (0.983)
  Pallas kernels: 618 us -> 607 us
    pallas_call x1, Pallas kernels: 70.3 us -> 58.6 us  [attn_call(): pl.pallas_call(attn_kernel, grid=(IMAGES,), in_specs=[main(QKV), tail(QKV...]
where the time goes in v13:
time: 626 us; the launch traced here: 621 us
  Pallas kernels  607 us (97%)
  local copies, waits for them, and re-layouts  12.7 us (2%)
    pallas_call x1, Pallas kernels, mlp_call(): pl.pallas_call(mlp_kernel, grid=(MLP_STEPS + DRAIN,), in_specs=[hbm, hbm,...  258 us
    pallas_call x1, Pallas kernels, qkvb_call(): pl.pallas_call(qkvb_kernel, grid=(QB_GRID,), in_specs=[hbm, hbm, *(whole(...  100 us
    pallas_call x1, Pallas kernels, attn_call(): pl.pallas_call(attn_kernel, grid=(IMAGES,), in_specs=[main(QKV), tail(QKV...  58.6 us
    pallas_call x1, Pallas kernels, open_call(): pl.pallas_call(open_kernel, in_specs=[hbm, hbm, vmem, vmem, vmem, vmem],...  55.9 us
    pallas_call x1, Pallas kernels, attn_back_call(): pl.pallas_call(attn_back_kernel, grid=(OUT_STEPS + DRAIN - 1,), in_specs=...  55.1 us
    pallas_call x1, Pallas kernels, qkv_call(): pl.pallas_call(qkv_kernel, grid=(QKV // QKV_N,), in_specs=[whole(TOKENS,...  53.6 us
    pallas_call x1, Pallas kernels, outb_call(): pl.pallas_call(outb_kernel, grid=(WIDTH // MAIN,), in_specs=[full, full,...  25.7 us

profile of v13, /device:TPU:0, one launch (start us, length us, event | category | flops | bytes accessed | tf_op | source)
XLA Modules:
  0.0 620.7 jit_solution(6774805580726880791)
XLA Ops:
  0.6 0.9 concatenate.3
  1.5 0.1 reshape.63
  1.6 0.6 pad.4.rows_ref
  2.2 55.9 %open.1 = (bf16[2056,1280]{1,0:T(8,128)(2,1)}, bf16[2056,1280]{1,0:T(8,128)(2,1)}, bf16[2056,1280]{1,0:T(8,128)(2,1)}, bf16[1280,2056]{1,0:T(8,128)(2,1)}, f32[1...) custom-call(bf16[2056,1280]{1,0:T(8,128)(2,1)} %bitcast.29, ...), custom_call_target="tpu_custom_call" | custom-call | flops 1000000000 | bytes 60000000 | tf_op jit(solution)/shard_map/open/pallas_call | solution.py:458
  58.1 53.6 %qkv.1 = (bf16[2056,3840]{1,0:T(8,128)(2,1)}, bf16[2,2,2,2,80,5120]{5,4,3,2,1,0:T(8,128)(2,1)}) custom-call(bf16[2056,1280]{1,0:T(8,128)(2,1)} %get-tuple-element.50.h_ref, bf16[1280,3840]{1,0:T(8,128)(2,1)} %bitcast.31, f32[1,3840]{1,0:T(1,128)} %get-tuple-element.52.wb_ref, bf16[80,5120]{1,0:T(8,128)(2,1)} %get-tuple-element.53.own_ref), custom_call_target="tpu_custom_call" | custom-call | flops 20211302400 | bytes 60000000 | tf_op jit(solution)/shard_map/qkv/pallas_call | solution.py:515
  111.7 58.6 %attn.1 = (bf16[2056,1280]{1,0:T(8,128)(2,1)}, bf16[2056,1280]{1,0:T(8,128)(2,1)}, bf16[2056,1280]{1,0:T(8,128)(2,1)}, f32[8,16,256]{2,1,0:T(8,128)}, f32[8,16,2...) custom-call(bf16[2056,3840]{1,0:T(8,128)(2,1)} %get-tuple-element.54.qkv_ref.qkvt_ref, ...), custom_call_target="tpu_custom_call" | custom-call | flops 40000000000 | bytes 50000000 | tf_op jit(solution)/shard_map/attn/pallas_call | solution.py:813
  170.4 257.9 %mlp.1 = (bf16[2056,1280]{1,0:T(8,128)(2,1)}, f32[10,2056,128]{2,1,0:T(8,128)}, bf16[2056,1280]{1,0:T(8,128)(2,1)}, f32[80,5120]{1,0:T(8,128)}, f32[320,1280]{1,...) custom-call(bf16[2056,1280]{1,0:T(8,128)(2,1)} %get-tuple-element.58.r_hbm, ...), custom_call_target="tpu_custom_call" | custom-call | flops 161690419200 | bytes 150000000 | tf_op jit(solution)/shard_map/mlp/pallas_call | solution.py:655
  428.2 25.7 %outb.1 = (bf16[2056,1280]{1,0:T(8,128)(2,1)}, f32[1280,1280]{1,0:T(8,128)}, f32[80,5120]{1,0:T(8,128)}, bf16[2056,1280]{1,0:T(8,128)(2,1)}, f32[320,1280]{1,0:T(8,128)}) custom-call(bf16[2056,1280]{1,0:T(8,128)(2,1)} %get-tuple-element.64.dr_ref, bf16[2056,1280]{1,0:T(8,128)(2,1)} %get-tuple-element.65.o_ref, bf16[1280,1280]{1,0:T(8,128)(2,1)} %bitcast.34, ...), custom_call_target="tpu_custom_call" | custom-call | flops 13474201600 | bytes 50000000 | tf_op jit(solution)/shard_map/outb/pallas_call | solution.py:864
  454.0 55.1 %attn_back.1 = (bf16[2056,3840]{1,0:T(8,128)(2,1)}, f32[1,3840]{1,0:T(1,128)}, f32[80,1280]{1,0:T(8,128)}) custom-call(bf16[2056,3840]{1,0:T(8,128)(2,1)} %get-tuple-element.54.qkv_ref.qkvt_ref, bf16[2056,3840]{1,0:T(8,128)(2,1)} %get-tuple-element.54.qkv_ref.qkvt_ref, bf16[2056,1280]{1,0:T(8,128)(2,1)} %get-tuple-element.72.do_ref.dot_ref, ...), custom_call_target="tpu_custom_call" | custom-call | flops 40000000000 | bytes 50000000 | tf_op jit(solution)/shard_map/attn_back/pallas_call | solution.py:994
  509.0 100.0 %qkvb.1 = (bf16[2056,1280]{1,0:T(8,128)(2,1)}, f32[80,3840]{1,0:T(8,128)}, f32[16,80]{1,0:T(8,128)}) custom-call(bf16[2056,1280]{1,0:T(8,128)(2,1)} %get-tuple-element.55.x_ref.xt_ref.xim_hbm, f32[10,2056,128]{2,1,0:T(8,128)} %get-tuple-element.70.dr_hbm, f32[16,1280]{1,0:T(8,128)} %get-tuple-element.57.vec_ref, f32[32,1280]{1,0:T(8,128)} %get-tuple-element.71.sums_ref, ...), custom_call_target="tpu_custom_call" | custom-call | flops 40422604800 | bytes 80000000 | tf_op jit(solution)/shard_map/qkvb/pallas_call | solution.py:1102
  609.1 0.7 slice.14
  609.8 0.6 reshape.70
  610.4 0.7 slice.15
  611.1 1.4 slice_bitcast_fusion
  612.5 0.7 reshape.71
  613.1 0.0 copy-start
  613.1 0.0 copy-start.1
  613.1 5.3 copy.31
  618.5 0.0 copy-done
  618.5 1.0 copy.32
  619.5 0.0 copy-done.1
  619.5 0.8 copy.33
Async XLA Ops:
  613.1 5.3 copy-start
  613.1 6.4 %copy-start.1 = (f32[80,1280]{1,0:T(8,128)S(1)}, f32[80,1280]{1,0:T(8,128)}, u32[]{:S(2)}) copy-start(f32[80,1280]{1,0:T(8,128)} %get-tuple-element.112) | copy-start | bytes 1228804
